TPU v7x, 32 devices: a whole 2x2x4 slice. The times are simulated.
32 devices in a mesh: dp: 16 (over z, y, x), rep: 2 (over core).
Axes of the slice: x: 2, y: 2, z: 4, core: 2. Of those that a mesh axis runs over, the one named last changes fastest.
Arguments:
- queries: bfloat16 [2048, 2048], P(('dp', 'rep')), may hold values from -24 to 24
- documents: bfloat16 [2048, 2048], P(('dp', 'rep')), may hold values from -24 to 24
- partner: int32 [2048], P(('dp', 'rep')), may hold values from 0 to 2047, each once
Outputs:
- grad_queries: float32 [2048, 2048], P(('dp', 'rep'))
- grad_documents: float32 [2048, 2048], P(('dp', 'rep'))
Inputs may be any that keep to these rules, and one draw needn't show every extreme that they name: `partner`: every document index appears exactly once.
All inputs are finite; a program needn't handle non-finite values.
Results may differ from a plain program's by a relative error of at most 0.0031.
Values may be sent and summed in bfloat16 or wider, within the bound.
No kernel may reach another device: no remote copies, remote signals or barrier semaphores. Data moves between devices by JAX's collectives and lax.ppermute only.
A program may use at most 256 MiB of HBM per device.

v0:
```python
import functools
import math

import jax
import jax.numpy as jnp
from jax import lax
from jax.experimental import pallas as pl
from jax.experimental.pallas import tpu as pltpu
from jax.sharding import PartitionSpec as P


WIDTHS = 9
AXES = ("dp", "rep")
LOG2E = 1.4426950408889634
STATS = 16
LANES = 128


logit_gain = 3.0


def width_list(feature_dim):
    return [feature_dim >> WIDTHS - 1 - nested for nested in range(WIDTHS)]


def transposed_dot(a, b):
    return lax.dot_general(a, b, (((1,), (1,)), ((), ())), preferred_element_type=jnp.float32)


def prefix_scores(v_ref, w_ref, rows, uppers):
    narrow = [m for m in uppers if m <= LANES]
    count = rows.size
    head = v_ref[rows, :LANES]
    lane = lax.broadcasted_iota(jnp.int32, head.shape, 1)
    masked = [jnp.where(lane < m, head, jnp.zeros_like(head)) for m in narrow]
    stacked = transposed_dot(jnp.concatenate(masked, axis=0), w_ref[:, :LANES])
    result = [stacked[k * count:(k + 1) * count] for k in range(len(narrow))]
    lower = narrow[-1]
    for upper in uppers[len(narrow):]:
        part = transposed_dot(v_ref[rows, lower:upper], w_ref[:, lower:upper])
        result.append(result[-1] + part)
        lower = upper
    return result


def block_of(total):
    return min(total, 256)


def load_tile(refs, scratch):
    at = 0
    for ref in refs:
        scratch[at:at + ref.shape[0], :] = ref[...]
        at += ref.shape[0]


def stats_kernel(pieces, uppers, *refs):
    role_ref, partner_ref = refs[:2]
    v_refs, w_refs = refs[2:2 + pieces], refs[2 + pieces:2 + 2 * pieces]
    out_ref, v_ref, w_ref, col_ref = refs[2 + 2 * pieces:]
    load_tile(v_refs, v_ref)
    load_tile(w_refs, w_ref)
    total = v_ref.shape[0]
    block = block_of(total)
    steps = total // block
    gains = [logit_gain * m ** -0.5 * LOG2E for m in uppers]
    own = partner_ref.shape[1]
    out_ref[...] = jnp.zeros_like(out_ref)

    @pl.when((role_ref[0] & 1) == 0)
    def _():
        for step in range(steps):
            rows = pl.ds(step * block, block)
            col_ref[rows, :] = jnp.zeros((block, LANES), jnp.float32)
            for k, s in enumerate(prefix_scores(v_ref, w_ref, rows, uppers)):
                logits = s * gains[k]
                peak = jnp.max(logits, axis=1, keepdims=True)
                mass = jnp.sum(jnp.exp2(logits - peak), axis=1, keepdims=True)
                col_ref[rows, k:k + 1] = peak + jnp.log(mass) * LOG2E
        out_ref[...] = col_ref[...].T[:STATS]

    @pl.when((role_ref[0] & 1) != 0)
    def _():
        peaks, masses = [None] * len(uppers), [None] * len(uppers)
        for step in range(steps):
            rows = pl.ds(step * block, block)
            for k, s in enumerate(prefix_scores(v_ref, w_ref, rows, uppers)):
                logits = s * gains[k]
                peak = jnp.max(logits, axis=0, keepdims=True)
                mass = jnp.sum(jnp.exp2(logits - peak), axis=0, keepdims=True)
                if step:
                    top = jnp.maximum(peak, peaks[k])
                    mass = mass * jnp.exp2(peak - top) + masses[k] * jnp.exp2(peaks[k] - top)
                    peak = top
                peaks[k], masses[k] = peak, mass
        for k in range(len(uppers)):
            out_ref[k:k + 1, :] = peaks[k] + jnp.log(masses[k]) * LOG2E

    out_ref[len(uppers):len(uppers) + 1, :own] = partner_ref[...]


def document_ids(shape, axis, first, own_rows, masks, start=0):
    at = lax.broadcasted_iota(jnp.int32, shape, axis) + start
    shift = own_rows.bit_length() - 1
    piece = at >> shift
    device = first ^ (piece & 1)
    for s, mask in enumerate(masks):
        device = device ^ (((piece >> (1 + s)) & 1) * mask)
    return (device * own_rows + (at & (own_rows - 1))).astype(jnp.float32)


def grads_kernel(pieces, uppers, own_rows, masks, *refs):
    me_ref = refs[0]
    groups = pieces // 2
    stat_refs = refs[1:1 + groups]
    v_refs = refs[1 + groups:1 + groups + pieces]
    w_refs = refs[1 + groups + pieces:1 + groups + 2 * pieces]
    out_refs = refs[1 + groups + 2 * pieces:1 + 2 * groups + 2 * pieces]
    v_ref, w_ref, score_ref, col_ref = refs[1 + 2 * groups + 2 * pieces:]
    load_tile(v_refs, v_ref)
    load_tile(w_refs, w_ref)
    total = v_ref.shape[0]
    block = block_of(total)
    chip_rows = total // groups
    count = len(uppers)
    scales = [logit_gain * m ** -0.5 for m in uppers]
    me = me_ref[0]
    lead = (me & 1) == 0

    parts = []
    partners = []
    for j, ref in enumerate(stat_refs):
        parts.append(jnp.concatenate(
            [ref[:, (i ^ j) * chip_rows:((i ^ j) + 1) * chip_rows] for i in range(groups)], axis=1))
        partners.append(ref[count:count + 1, :chip_rows])
    peak = functools.reduce(jnp.maximum, parts)
    mass = functools.reduce(lambda a, b: a + b, [jnp.exp2(part - peak) for part in parts])
    totals = peak + jnp.log(mass) * LOG2E
    partner_row = jnp.concatenate(partners, axis=1)
    packed = jnp.concatenate(
        [totals[:count], partner_row, jnp.zeros((LANES - count - 1, total), jnp.float32)], axis=0)
    col_ref[...] = packed.T
    zero_or = lambda keep, x: jnp.where(keep, x, jnp.zeros_like(x))
    document_row = document_ids((1, total), 1, me | 1, own_rows, masks)
    id_row = jnp.where(lead, document_row, partner_row)
    shifts = [math.log2(s) for s in scales]
    total_rows = [zero_or(jnp.logical_not(lead), totals[k:k + 1]) - shifts[k] for k in range(count)]

    narrow = [m for m in uppers if m <= LANES]
    for step in range(total // block):
        rows = pl.ds(step * block, block)
        document_col = document_ids((block, 1), 0, me | 1, own_rows, masks, step * block)
        id_col = jnp.where(lead, col_ref[rows, count:count + 1], document_col)
        hit = id_col == id_row
        for k, s in enumerate(prefix_scores(v_ref, w_ref, rows, uppers)):
            score_ref[k] = s
        running = None
        stack = []
        for k in reversed(range(count)):
            gain = scales[k] * LOG2E
            total_col = zero_or(lead, col_ref[rows, k:k + 1])
            weight = jnp.exp2(score_ref[k] * gain - total_col - total_rows[k])
            weight = weight - jnp.where(hit, scales[k], 0.0)
            running = weight if running is None else running + weight
            band = running.astype(jnp.bfloat16)
            if k >= len(narrow):
                lower, upper = uppers[k - 1], uppers[k]
                product = jnp.dot(band, w_ref[:, lower:upper], preferred_element_type=jnp.float32)
                store(out_refs, product, step * block, lower, upper, chip_rows)
            else:
                stack.append(band)
        product = jnp.dot(
            jnp.concatenate(stack, axis=0), w_ref[:, :LANES], preferred_element_type=jnp.float32)
        lane = lax.broadcasted_iota(jnp.int32, (block, LANES), 1)
        chosen = product[:block]
        for at_stack in range(1, len(stack)):
            k = len(narrow) - 1 - at_stack
            chosen = jnp.where(
                lane < uppers[k], product[at_stack * block:(at_stack + 1) * block], chosen)
        store(out_refs, chosen, step * block, 0, LANES, chip_rows)


def rows_of(refs, lower, upper):
    return jnp.concatenate([ref[:, lower:upper] for ref in refs], axis=0)


def subtile_scores(v_refs, w_refs, uppers):
    narrow = [m for m in uppers if m <= LANES]
    head = rows_of(v_refs, 0, LANES)
    count = head.shape[0]
    lane = lax.broadcasted_iota(jnp.int32, head.shape, 1)
    masked = [jnp.where(lane < m, head, jnp.zeros_like(head)) for m in narrow]
    stacked = transposed_dot(jnp.concatenate(masked, axis=0), rows_of(w_refs, 0, LANES))
    for k in range(len(narrow)):
        yield stacked[k * count:(k + 1) * count]
    lower, running = narrow[-1], stacked[-count:]
    for upper in uppers[len(narrow):]:
        running = running + transposed_dot(
            rows_of(v_refs, lower, upper), rows_of(w_refs, lower, upper))
        yield running
        lower = upper


def subtile(lead, v_refs, w_refs, uppers, refs):
    power_ref, col_peak, col_mass, row_peak, row_mass = refs
    gains = [logit_gain * m ** -0.5 * LOG2E for m in uppers]
    count = power_ref.shape[1]

    @pl.when(lead)
    def _():
        lane = lax.broadcasted_iota(jnp.int32, (count, LANES), 1)
        peaks = jnp.zeros((count, LANES), jnp.float32)
        masses = jnp.ones((count, LANES), jnp.float32)
        for k, s in enumerate(subtile_scores(v_refs, w_refs, uppers)):
            logits = s * gains[k]
            peak = jnp.max(logits, axis=1, keepdims=True)
            power = jnp.exp2(logits - peak)
            power_ref[k] = power
            peaks = jnp.where(lane == k, peak, peaks)
            masses = jnp.where(lane == k, jnp.sum(power, axis=1, keepdims=True), masses)
        col_peak[...] = peaks
        col_mass[...] = masses

    @pl.when(jnp.logical_not(lead))
    def _():
        row_peak[...] = jnp.zeros_like(row_peak)
        row_mass[...] = jnp.ones_like(row_mass)
        for k, s in enumerate(subtile_scores(v_refs, w_refs, uppers)):
            logits = s * gains[k]
            peak = jnp.max(logits, axis=0, keepdims=True)
            power = jnp.exp2(logits - peak)
            power_ref[k] = power
            row_peak[k:k + 1, :] = peak
            row_mass[k:k + 1, :] = jnp.sum(power, axis=0, keepdims=True)


def log_sum(pairs):
    top = functools.reduce(jnp.maximum, [peak for peak, _ in pairs])
    mass = functools.reduce(
        lambda a, b: a + b, [mass * jnp.exp2(peak - top) for peak, mass in pairs])
    return top + jnp.log(mass) * LOG2E


def tile_kernel(tiles, uppers, own_rows, pieces, finish, *refs):
    me_ref, partner_ref = refs[:2]
    v_refs, w_refs = refs[2:2 + pieces], refs[2 + pieces:2 + 2 * pieces]
    at = 2 + 2 * pieces
    earlier = refs[at:at + 4 * finish]
    outs = refs[at + 4 * finish:]
    lead = (me_ref[0] & 1) == 0
    for i, (r0, r1, c0, c1) in enumerate(tiles):
        subtile(
            lead, v_refs[2 * r0:2 * r1], w_refs[2 * c0:2 * c1], uppers, outs[5 * i:5 * i + 5])
    if not finish:
        outs[-1][...] = partner_ref[...]
        return
    stats_ref = outs[-1]
    every = [earlier[4 * i:4 * i + 4] for i in range(finish)]
    every += [outs[5 * i + 1:5 * i + 5] for i in range(len(tiles))]
    shapes = subtiles(pieces // 2)
    segments = segments_of(pieces // 2)
    chip_rows = 2 * own_rows

    @pl.when(lead)
    def _():
        merged = []
        for s0, s1 in segments:
            pairs = []
            for (r0, r1, _, _), tile in zip(shapes, every):
                if r0 <= s0 and s1 <= r1:
                    rows = slice((s0 - r0) * chip_rows, (s1 - r0) * chip_rows)
                    pairs.append((tile[0][rows, :], tile[1][rows, :]))
            merged.append(log_sum(pairs))
        stats_ref[...] = jnp.concatenate(merged, axis=0).T[:STATS]

    @pl.when(jnp.logical_not(lead))
    def _():
        for s0, s1 in segments:
            pairs = []
            for (_, _, c0, c1), tile in zip(shapes, every):
                if c0 <= s0 and s1 <= c1:
                    across = slice((s0 - c0) * chip_rows, (s1 - c0) * chip_rows)
                    pairs.append((tile[2][:, across], tile[3][:, across]))
            stats_ref[:, s0 * chip_rows:s1 * chip_rows] = log_sum(pairs)

    count = len(uppers)
    stats_ref[count:count + 1, :chip_rows] = partner_ref[...]


def segments_of(groups):
    low, middle = groups // 2, groups // 2 + groups // 4
    return [(0, low), (low, middle), (middle, groups)]


def subtiles(groups):
    (_, low), (_, middle), _ = segments_of(groups)
    return [(0, low, 0, low), (0, low, low, middle), (low, middle, 0, middle),
            (0, middle, middle, groups), (middle, groups, 0, groups)]


def band_kernel(groups, uppers, widths, own_rows, masks, follows, *refs):
    me_ref = refs[0]
    stat_refs = refs[1:1 + groups]
    at = 1 + groups
    shapes = subtiles(groups)
    tiles = len(shapes)
    power_refs, col_refs, row_refs = [refs[at + i * tiles:at + (i + 1) * tiles] for i in range(3)]
    at += 3 * tiles
    w_refs = refs[at:at + 2 * groups]
    at += 2 * groups
    before_ref = None
    if follows:
        before_ref, at = refs[at], at + 1
    out_refs = refs[at:at + groups]
    at += groups
    after_ref = None
    if not follows:
        after_ref, at = refs[at], at + 1
    w_ref, = refs[at:]
    base = 0 if widths[-1] == 0 else uppers[widths[-1] - 1]
    top = uppers[widths[0]]
    for i, ref in enumerate(w_refs):
        w_ref[i * own_rows:(i + 1) * own_rows, :] = ref[:, base:top]

    total = w_ref.shape[0]
    chip_rows = total // groups
    count = len(uppers)
    scales = [logit_gain * m ** -0.5 for m in uppers]
    me = me_ref[0]
    lead = (me & 1) == 0
    parts, partners = [], []
    for j, ref in enumerate(stat_refs):
        parts.append(jnp.concatenate(
            [ref[:, (i ^ j) * chip_rows:((i ^ j) + 1) * chip_rows] for i in range(groups)], axis=1))
        partners.append(ref[count:count + 1, :chip_rows])
    peak = functools.reduce(jnp.maximum, parts)
    mass = functools.reduce(lambda a, b: a + b, [jnp.exp2(part - peak) for part in parts])
    partner_row = jnp.concatenate(partners, axis=1)
    sub = lax.broadcasted_iota(jnp.int32, (STATS, total), 0)
    totals = peak + jnp.log(mass) * LOG2E
    for k in range(count):
        totals = jnp.where(sub == k, totals - math.log2(scales[k]), totals)
    packed = jnp.concatenate(
        [totals[:count], partner_row, jnp.zeros((LANES - count - 1, total), jnp.float32)], axis=0)
    cols = packed.T
    id_row = jnp.where(
        lead, document_ids((1, total), 1, me | 1, own_rows, masks), partner_row)
    id_col = jnp.where(
        lead, cols[:, count:count + 1],
        document_ids((total, 1), 0, me | 1, own_rows, masks))

    segments = segments_of(groups)
    narrow = [k for k in widths if uppers[k] <= LANES]
    for block in (segments[1:], segments[:1]):
        first = block[0][0] * chip_rows
        rows = slice(first, block[-1][1] * chip_rows)
        height = rows.stop - first
        hit = id_col[rows] == id_row
        strips = []
        for s0, s1 in block:
            strip = []
            for (r0, r1, c0, c1), power, col_peak, row_peak in zip(
                    shapes, power_refs, col_refs, row_refs):
                if r0 <= s0 and s1 <= r1:
                    inner = slice((s0 - r0) * chip_rows, (s1 - r0) * chip_rows)
                    outer = slice(s0 * chip_rows, s1 * chip_rows)
                    across = slice(c0 * chip_rows, c1 * chip_rows)
                    strip.append((
                        c0, power, inner,
                        jnp.where(lead, jnp.exp2(col_peak[inner, :] - cols[outer]), 1.0),
                        jnp.where(lead, 1.0, jnp.exp2(row_peak[...] - totals[:, across]))))
            strips.append(sorted(strip, key=lambda item: item[0]))
        running = before_ref[rows, :] if follows else None
        stack = []
        for k in widths:
            weight = jnp.concatenate([
                jnp.concatenate([
                    power[k, inner] * col_gain[:, k:k + 1] * row_gain[k:k + 1, :]
                    for _, power, inner, col_gain, row_gain in strip], axis=1)
                for strip in strips], axis=0)
            weight = weight - jnp.where(hit, scales[k], 0.0)
            running = weight if running is None else running + weight
            band = running.astype(jnp.bfloat16)
            if k not in narrow:
                lower, upper = uppers[k - 1] - base, uppers[k] - base
                product = jnp.dot(band, w_ref[:, lower:upper], preferred_element_type=jnp.float32)
                store(out_refs, product, first, lower, upper, chip_rows)
            else:
                stack.append(band)
        if not follows:
            after_ref[rows, :] = running
        if narrow:
            product = jnp.dot(
                jnp.concatenate(stack, axis=0), w_ref[:, :LANES],
                preferred_element_type=jnp.float32)
            lane = lax.broadcasted_iota(jnp.int32, (height, LANES), 1)
            chosen = product[:height]
            for i in range(1, len(stack)):
                chosen = jnp.where(
                    lane < uppers[narrow[i]], product[i * height:(i + 1) * height], chosen)
            store(out_refs, chosen, first, 0, LANES, chip_rows)


def store(out_refs, value, first_row, lower, upper, chip_rows):
    for at in range(0, value.shape[0], chip_rows):
        ref = out_refs[(first_row + at) // chip_rows]
        ref[:, lower:upper] = value[at:at + chip_rows].astype(ref.dtype)


def on_device(queries, documents, partner):
    own_rows, feature_dim = queries.shape
    uppers = width_list(feature_dim)
    dp_size, rep_size = lax.axis_size("dp"), lax.axis_size("rep")
    devices = dp_size * rep_size
    bits = devices.bit_length() - 1
    assert rep_size == 2 and devices == 1 << bits and bits % 2 == 1
    stages = (bits - 1) // 2
    groups = 1 << stages
    pieces = 2 * groups
    query_masks = [1 << (2 * s + 1) for s in range(stages)]
    document_masks = [1 << (2 * s + 2) for s in range(stages)]
    total = pieces * own_rows
    chip_rows = 2 * own_rows

    role = lax.axis_index("rep")
    me = (lax.axis_index("dp") * rep_size + role).astype(jnp.int32).reshape(1)
    lead = role == 0

    def exchange(x, masks_of):
        return lax.ppermute(x, AXES, [(i, i ^ masks_of(i)) for i in range(devices)])

    def swap(x):
        return exchange(x, lambda i: 1)

    def along(x, stage):
        return exchange(x, lambda i: document_masks[stage] if i & 1 else query_masks[stage])

    mine = jnp.where(lead, queries, documents)
    other = jnp.where(lead, documents, queries)
    v = {(0, 0): mine, (0, 1): swap(other)}
    w = {(0, 0): swap(mine), (0, 1): other}
    for stage in reversed(range(stages)):
        for j in [j for j in range(groups) if (j, 0) in v]:
            for t in range(2):
                v[j | 1 << stage, t] = along(v[j, t], stage)
    for j, t in sorted(v):
        if j:
            w[j, t] = swap(v[j, t])
    order = [(j, t) for j in range(groups) for t in range(2)]
    v_list, w_list = [v[key] for key in order], [w[key] for key in order]

    own_partner = partner.astype(jnp.float32).reshape(1, own_rows)
    far_partner = swap(own_partner)
    chip_partner = jnp.where(
        lead,
        jnp.concatenate([own_partner, far_partner], axis=1),
        jnp.concatenate([far_partner, own_partner], axis=1))

    vmem = pl.BlockSpec(memory_space=pltpu.VMEM)
    smem = pl.BlockSpec(memory_space=pltpu.SMEM)

    def query_mask(j):
        return sum(mask for s, mask in enumerate(query_masks) if j >> s & 1)

    def gathered(stats):
        return [stats] + [exchange(stats, lambda i: query_mask(j)) for j in range(1, groups)]

    shape = lambda *dims: jax.ShapeDtypeStruct(dims, jnp.float32)

    def gradient_shapes(columns):
        return [
            jax.ShapeDtypeStruct((chip_rows, columns), jnp.bfloat16 if j & 1 else jnp.float32)
            for j in range(groups)]

    if WIDTHS * total * total * 4 > 16 << 20:
        limit = 60 << 20
        stats = pl.pallas_call(
            functools.partial(stats_kernel, pieces, uppers),
            out_shape=shape(STATS, total),
            in_specs=[smem] + [vmem] * (1 + 2 * pieces),
            out_specs=vmem,
            scratch_shapes=[
                pltpu.VMEM((total, feature_dim), jnp.bfloat16),
                pltpu.VMEM((total, feature_dim), jnp.bfloat16),
                pltpu.VMEM((total, LANES), jnp.float32),
            ],
            compiler_params=pltpu.CompilerParams(vmem_limit_bytes=limit),
            name="tile_stats",
        )(me, chip_partner, *v_list, *w_list)
        whole = pl.pallas_call(
            functools.partial(grads_kernel, pieces, uppers, own_rows, document_masks),
            out_shape=gradient_shapes(feature_dim),
            in_specs=[smem] + [vmem] * (groups + 2 * pieces),
            out_specs=[vmem] * groups,
            scratch_shapes=[
                pltpu.VMEM((total, feature_dim), jnp.bfloat16),
                pltpu.VMEM((total, feature_dim), jnp.bfloat16),
                pltpu.VMEM((WIDTHS, block_of(total), total), jnp.float32),
                pltpu.VMEM((total, LANES), jnp.float32),
            ],
            compiler_params=pltpu.CompilerParams(vmem_limit_bytes=limit),
            name="tile_grads",
        )(me, *gathered(stats), *v_list, *w_list)
        chunks = [whole]
    else:
        shapes = subtiles(groups)
        limit = 20 << 20
        params = pltpu.CompilerParams(vmem_limit_bytes=limit)

        def tile(span, partner_row, earlier=()):
            reach = 2 * max(max(shapes[i][1], shapes[i][3]) for i in span)
            stat_shapes = [shape(STATS, total)] if earlier else [shape(1, chip_rows)]
            result, area = [], 0
            for i in span:
                r0, r1, c0, c1 = shapes[i]
                tall, wide = (r1 - r0) * chip_rows, (c1 - c0) * chip_rows
                area += tall * wide
                result += [shape(WIDTHS, tall, wide), shape(tall, LANES), shape(tall, LANES),
                           shape(STATS, wide), shape(STATS, wide)]
            *arrays, last_array = pl.pallas_call(
                functools.partial(
                    tile_kernel, [shapes[i] for i in span], uppers, own_rows, reach,
                    len(earlier)),
                out_shape=result + stat_shapes,
                in_specs=[smem] + [vmem] * (1 + 2 * reach + 4 * len(earlier)),
                out_specs=[vmem] * (len(result) + 1),
                compiler_params=params,
                cost_estimate=pl.CostEstimate(
                    flops=6 * area * feature_dim, transcendentals=0,
                    bytes_accessed=2 * total * feature_dim),
            )(me, partner_row, *v_list[:reach], *w_list[:reach],
              *[a for one in earlier for a in one[1:]])
            return [arrays[5 * i:5 * i + 5] for i in range(len(span))], last_array

        done, chip_partner = tile([0], chip_partner)
        more, chip_partner = tile([1, 2], chip_partner)
        done += more
        more, stats = tile([3, 4], chip_partner, done)
        done += more
        common = [me, *gathered(stats), *[t[0] for t in done], *[t[1] for t in done],
                  *[t[3] for t in done], *w_list]
        last = WIDTHS - 1

        def bands(widths, more, follows):
            base = 0 if widths[-1] == 0 else uppers[widths[-1] - 1]
            columns = uppers[widths[0]] - base
            return pl.pallas_call(
                functools.partial(
                    band_kernel, groups, uppers, widths, own_rows, document_masks, follows),
                out_shape=gradient_shapes(columns) + ([] if follows else [shape(total, total)]),
                in_specs=[smem] + [vmem] * (len(common) - 1 + len(more)),
                out_specs=[vmem] * (groups + (not follows)),
                scratch_shapes=[pltpu.VMEM((total, columns), jnp.bfloat16)],
                compiler_params=params,
                cost_estimate=pl.CostEstimate(
                    flops=2 * total * total * feature_dim, transcendentals=0,
                    bytes_accessed=4 * total * feature_dim),
            )(*common, *more)

        *widest, running = bands([last], [], False)
        others = bands(list(reversed(range(last))), [running], True)
        chunks = [widest, others]

    mine_parts, other_parts = [], []
    for c, chunk in enumerate(chunks):
        partial = dict(enumerate(chunk))
        for stage in range(stages - 1):
            step = 1 << stage
            for j in sorted([j for j in partial if j & step], reverse=True):
                arrived = along(partial.pop(j).astype(jnp.bfloat16), stage)
                partial[j ^ step] = partial[j ^ step] + arrived.astype(jnp.float32)
        stage = stages - 1
        outgoing = partial[1 << stage].astype(jnp.bfloat16)
        kept = partial[0]
        if c < len(chunks) - 1:
            arrived = along(outgoing, stage)
            kept = kept + arrived.astype(jnp.float32)
            mine_parts.append(kept[:own_rows])
            other_parts.append(swap(kept[own_rows:]))
        else:
            far = lambda i: document_masks[stage] ^ 1 if i & 1 else query_masks[stage] ^ 1
            near_arrived = along(outgoing[:own_rows], stage)
            far_arrived = exchange(outgoing[own_rows:], far)
            mine_parts.append(kept[:own_rows] + near_arrived.astype(jnp.float32))
            other_parts.append(
                swap(kept[own_rows:]) + far_arrived.astype(jnp.float32))
    mine_parts, other_parts = mine_parts[::-1], other_parts[::-1]
    ours = jnp.concatenate(mine_parts, axis=1)
    theirs = jnp.concatenate(other_parts, axis=1)
    return jnp.where(lead, ours, theirs), jnp.where(lead, theirs, ours)


def solution(mesh):
    return jax.shard_map(
        on_device,
        mesh=mesh,
        in_specs=(P(AXES, None), P(AXES, None), P(AXES)),
        out_specs=(P(AXES, None), P(AXES, None)),
        check_vma=False,
    )
```

profile of v0, /device:TPU:0, one launch (start us, length us, event | category | flops | bytes accessed | tf_op | source)
XLA Modules:
  0.0 65.5 jit_solution(3769252507902691359)
XLA Ops:
  0.6 1.1 %broadcast_select_fusion = (bf16[64,2048]{1,0:T(8,128)(2,1)S(1)}, bf16[64,2048]{1,0:T(8,128)(2,1)S(1)}) fusion(bf16[64,2048]{1,0:T(8,128)(2,1)} %param.4, bf16[64,2048]{1,0:T(8,128)(2,1)} %param.3, pred[]{:T(512)S(6)} %eq.3), kind=kLoop, calls=%fused_computation.10 | loop fusion | flops 262144 | bytes 1048577 | tf_op jit(solution)/shard_map/jit(_where)/select_n | solution.py:439
  2.3 2.6 %collective-permute-start.2 = (bf16[64,2048]{1,0:T(8,128)(2,1)S(1)}, bf16[64,2048]{1,0:T(8,128)(2,1)S(1)}, u32[]{:S(2)}, u32[]{:S(2)}) collective-permute-start(bf16[64,2048]{1,0:T(8,128)(2,1)S(1)} %get-tuple-element.75.refs_2_), channel_id=1, source_target_pairs={{0,2},{1,5},{2,0},{3,7},{4,6},{5,1},{6,4},{7,3},{8,10},{9,13},{10,... | collective-permute-start | bytes 786440 | tf_op jit(solution)/shard_map/ppermute | solution.py:430
  4.8 1.6 %collective-permute-start.7 = (bf16[64,2048]{1,0:T(8,128)(2,1)S(1)}, bf16[64,2048]{1,0:T(8,128)(2,1)S(1)}, u32[]{:S(2)}, u32[]{:S(2)}) collective-permute-start(bf16[64,2048]{1,0:T(8,128)(2,1)S(1)} %get-tuple-element.75.refs_2_), channel_id=1, source_target_pairs={{0,8},{1,17},{2,10},{3,19},{4,12},{5,21},{6,14},{7,23},{8,0},{9,25... | collective-permute-start | bytes 786440 | tf_op jit(solution)/shard_map/ppermute | solution.py:430
  6.9 0.9 %collective-permute-start.8 = (bf16[64,2048]{1,0:T(8,128)(2,1)S(1)}, bf16[64,2048]{1,0:T(8,128)(2,1)S(1)}, u32[]{:S(2)}, u32[]{:S(2)}) collective-permute-start(bf16[64,2048]{1,0:T(8,128)(2,1)S(1)} %collective-permute-done.1.refs_3_), channel_id=1, source_target_pairs={{0,8},{1,17},{2,10},{3,19},{4,12},{5,21},{6,14},{7,23},{8,0},{9,25... | collective-permute-start | bytes 786440 | tf_op jit(solution)/shard_map/ppermute | solution.py:430
  7.9 0.7 %convert_bitcast_fusion = f32[1,64]{1,0:T(1,128)S(1)} fusion(s32[64]{0:T(128)} %param.5), kind=kLoop, calls=%fused_computation.13 | loop fusion | flops 64 | bytes 512 | tf_op jit(solution)/shard_map/concatenate | solution.py:456
  9.1 0.8 %collective-permute-done = f32[1,64]{1,0:T(1,128)S(1)} collective-permute-done((f32[1,64]{1,0:T(1,128)S(1)}, f32[1,64]{1,0:T(1,128)S(1)}, u32[]{:S(2)}, u32[]{:S(2)}) %collective-permute-start) | collective-permute-done | bytes 288 | tf_op jit(solution)/shard_map/ppermute | solution.py:430
  10.5 3.4 %collective-permute-done.7.refs_6_ = bf16[64,2048]{1,0:T(8,128)(2,1)S(1)} collective-permute-done((bf16[64,2048]{1,0:T(8,128)(2,1)S(1)}, bf16[64,2048]{1,0:T(8,128)(2,1)S(1)}, u32[]{:S(2)}, u32[]{:S(2)}) %collective-permute-start.7) | collective-permute-done | bytes 262176 | tf_op jit(solution)/shard_map/ppermute | solution.py:430
  13.9 5.6 %collective-permute-done.8.refs_7_ = bf16[64,2048]{1,0:T(8,128)(2,1)S(1)} collective-permute-done((bf16[64,2048]{1,0:T(8,128)(2,1)S(1)}, bf16[64,2048]{1,0:T(8,128)(2,1)S(1)}, u32[]{:S(2)}, u32[]{:S(2)}) %collective-permute-start.8) | collective-permute-done | bytes 262176 | tf_op jit(solution)/shard_map/ppermute | solution.py:430
  20.6 5.4 %collective-permute-done.12.refs_9_ = bf16[64,2048]{1,0:T(8,128)(2,1)} collective-permute-done((bf16[64,2048]{1,0:T(8,128)(2,1)S(1)}, bf16[64,2048]{1,0:T(8,128)(2,1)}, u32[]{:S(2)}, u32[]{:S(2)}) %collective-permute-start.12) | collective-permute-done | bytes 262176 | tf_op jit(solution)/shard_map/ppermute | solution.py:430
  26.1 1.0 %shard_map.50 = (f32[9,256,256]{2,1,0:T(8,128)S(1)}, f32[256,128]{1,0:T(8,128)S(1)}, f32[256,128]{1,0:T(8,128)S(1)}, f32[16,256]{1,0:T(8,128)S(1)}, f32[16,256]{1,0:T(8,128)S(1)}, /*index=5*/f32[1,128]{1,0:T(1,128)S(1)}) custom-call(s32[1]{0:T(128)} %bitcast.refs_0_, f32[1,128]{1,0:T(1,128)S(1)} %broadcast_select_fusion.2.refs_1_, ...), custom_call_target="tpu_custom_call" | custom-call | flops 805306368 | bytes 2097152 | tf_op jit(solution)/shard_map/pallas_call | solution.py:520
  27.1 2.1 %shard_map.51 = (f32[9,256,128]{2,1,0:T(8,128)S(1)}, f32[256,128]{1,0:T(8,128)S(1)}, f32[256,128]{1,0:T(8,128)S(1)}, f32[16,128]{1,0:T(8,128)S(1)}, f32[16,128]{...) custom-call(s32[1]{0:T(128)} %bitcast.refs_0_, ...), custom_call_target="tpu_custom_call" | custom-call | flops 1006632960 | bytes 2097152 | tf_op jit(solution)/shard_map/pallas_call | solution.py:520
  29.2 4.7 %shard_map.52 = (f32[9,384,128]{2,1,0:T(8,128)S(1)}, f32[384,128]{1,0:T(8,128)S(1)}, f32[384,128]{1,0:T(8,128)}, f32[16,128]{1,0:T(8,128)S(1)}, f32[16,128]{1,0:...) custom-call(s32[1]{0:T(128)} %bitcast.refs_0_, ...), custom_call_target="tpu_custom_call" | custom-call | flops 1409286144 | bytes 2097152 | tf_op jit(solution)/shard_map/pallas_call | solution.py:520
  33.9 1.9 %collective-permute-start.16 = (f32[16,512]{1,0:T(8,128)S(1)}, f32[16,512]{1,0:T(8,128)S(1)}, u32[]{:S(2)}, u32[]{:S(2)}) collective-permute-start(f32[16,512]{1,0:T(8,128)S(1)} %get-tuple-element.49.refs_1_), channel_id=1, source_target_pairs={{0,8},{1,9},{2,10},{3,11},{4,12},{5,13},{6,14},{7,15},{8,0},{9,1},... | collective-permute-start | bytes 98312 | tf_op jit(solution)/shard_map/ppermute | solution.py:430
  35.8 1.6 %collective-permute-start.17 = (f32[16,512]{1,0:T(8,128)S(1)}, f32[16,512]{1,0:T(8,128)S(1)}, u32[]{:S(2)}, u32[]{:S(2)}) collective-permute-start(f32[16,512]{1,0:T(8,128)S(1)} %get-tuple-element.49.refs_1_), channel_id=1, source_target_pairs={{0,10},{1,11},{2,8},{3,9},{4,14},{5,15},{6,12},{7,13},{8,2},{9,3},... | collective-permute-start | bytes 98312 | tf_op jit(solution)/shard_map/ppermute | solution.py:430
  37.8 2.8 %collective-permute-done.17.refs_4_ = f32[16,512]{1,0:T(8,128)S(1)} collective-permute-done((f32[16,512]{1,0:T(8,128)S(1)}, f32[16,512]{1,0:T(8,128)S(1)}, u32[]{:S(2)}, u32[]{:S(2)}) %collective-permute-start.17) | collective-permute-done | bytes 32800 | tf_op jit(solution)/shard_map/ppermute | solution.py:430
  40.6 1.0 %shard_map.53 = (f32[128,1024]{1,0:T(8,128)S(1)}, bf16[128,1024]{1,0:T(8,128)(2,1)S(1)}, f32[128,1024]{1,0:T(8,128)S(1)}, bf16[128,1024]{1,0:T(8,128)(2,1)S(1)}, f32[512,512]{1,0:T(8,128)S(1)}) custom-call(s32[1]{0:T(128)} %bitcast.refs_0_, f32[16,512]{1,0:T(8,128)S(1)} %get-tuple-element.49.refs_1_, f32[16,512]{1,0:T(8,128)S(1)} %collective-permute-done.15.refs_2_, ...), custom_call_target="tpu_custom_call" | custom-call | flops 1073741824 | bytes 4194304 | tf_op jit(solution)/shard_map/pallas_call | solution.py:547
  41.6 1.7 %collective-permute-start.22 = (bf16[128,1024]{1,0:T(8,128)(2,1)S(1)}, bf16[128,1024]{1,0:T(8,128)(2,1)S(1)}, u32[]{:S(2)}, u32[]{:S(2)}) collective-permute-start(bf16[128,1024]{1,0:T(8,128)(2,1)S(1)} %get-tuple-element.67), channel_id=1, source_target_pairs={{0,2},{1,5},{2,0},{3,7},{4,6},{5,1},{6,4},{7,3},{8,10},{9,13},{10,... | collective-permute-start | bytes 786440 | tf_op jit(solution)/shard_map/ppermute | solution.py:430
  43.3 3.4 %shard_map.54 = (f32[128,1024]{1,0:T(8,128)S(1)}, bf16[128,1024]{1,0:T(8,128)(2,1)S(1)}, f32[128,1024]{1,0:T(8,128)S(1)}, bf16[128,1024]{1,0:T(8,128)(2,1)S(1)}) custom-call(s32[1]{0:T(128)} %bitcast.refs_0_, f32[16,512]{1,0:T(8,128)S(1)} %get-tuple-element.49.refs_1_, f32[16,512]{1,0:T(8,128)S(1)} %collective-permute-done.15.refs_2_, ...), custom_call_target="tpu_custom_call" | custom-call | flops 1073741824 | bytes 4194304 | tf_op jit(solution)/shard_map/pallas_call | solution.py:547
  47.2 1.6 %collective-permute-start.21 = (bf16[128,1024]{1,0:T(8,128)(2,1)S(1)}, bf16[128,1024]{1,0:T(8,128)(2,1)S(1)}, u32[]{:S(2)}, u32[]{:S(2)}) collective-permute-start(bf16[128,1024]{1,0:T(8,128)(2,1)S(1)} %get-tuple-element.65), channel_id=1, source_target_pairs={{0,2},{1,5},{2,0},{3,7},{4,6},{5,1},{6,4},{7,3},{8,10},{9,13},{10,... | collective-permute-start | bytes 786440 | tf_op jit(solution)/shard_map/ppermute | solution.py:430
  49.8 3.3 %collective-permute-done.19 = bf16[128,1024]{1,0:T(8,128)(2,1)S(1)} collective-permute-done((bf16[128,1024]{1,0:T(8,128)(2,1)S(1)}, bf16[128,1024]{1,0:T(8,128)(2,1)S(1)}, u32[]{:S(2)}, u32[]{:S(2)}) %collective-permute-start.19) | collective-permute-done | bytes 262176 | tf_op jit(solution)/shard_map/ppermute | solution.py:430
  53.9 4.9 %collective-permute-done.18 = bf16[128,1024]{1,0:T(8,128)(2,1)S(1)} collective-permute-done((bf16[128,1024]{1,0:T(8,128)(2,1)S(1)}, bf16[128,1024]{1,0:T(8,128)(2,1)S(1)}, u32[]{:S(2)}, u32[]{:S(2)}) %collective-permute-start.18) | collective-permute-done | bytes 262176 | tf_op jit(solution)/shard_map/ppermute | solution.py:430
  58.8 3.6 %collective-permute-done.20 = bf16[64,1024]{1,0:T(8,128)(2,1)S(1)} collective-permute-done((bf16[64,1024]{1,0:T(8,128)(2,1)S(1)}, bf16[64,1024]{1,0:T(8,128)(2,1)S(1)}, u32[]{:S(2)}, u32[]{:S(2)}) %collective-permute-start.20) | collective-permute-done | bytes 131104 | tf_op jit(solution)/shard_map/ppermute | solution.py:430
  63.3 0.8 %collective-permute-done.24 = f32[64,1024]{1,0:T(8,128)S(1)} collective-permute-done((f32[64,1024]{1,0:T(8,128)S(1)}, f32[64,1024]{1,0:T(8,128)S(1)}, u32[]{:S(2)}, u32[]{:S(2)}) %collective-permute-start.24) | collective-permute-done | bytes 262176 | tf_op jit(solution)/shard_map/ppermute | solution.py:430
  64.4 1.1 %fusion = (f32[64,2048]{1,0:T(8,128)}, f32[64,2048]{1,0:T(8,128)}) fusion(f32[64,1024]{1,0:T(8,128)S(1)} %collective-permute-done.26, f32[64,1024]{1,0:T(8,128)S(1)} %convert_add_fusion.2, f32[64,1024]{1,0:T(8,128)S(1)} %get-tuple-element.72, f32[64,1024]{1,0:T(8,128)S(1)} %get-tuple-element.70, pred[]{:T(512)S(6)} %eq.3), kind=kLoop, calls=%fused_computation.6 | loop fusion | flops 524288 | bytes 2097153 | tf_op jit(solution)/shard_map/jit(_where)/select_n | solution.py:590
  (47 shorter events, 7.3 us)
Async XLA Ops:
  1.7 4.7 %collective-permute-start.1 = (bf16[64,2048]{1,0:T(8,128)(2,1)S(1)}, bf16[64,2048]{1,0:T(8,128)(2,1)S(1)}, u32[]{:S(2)}, u32[]{:S(2)}) collective-permute-start(bf16[64,2048]{1,0:T(8,128)(2,1)S(1)} %get-tuple-element.74.refs_7_.refs_9_.refs_11_.refs_21_), channel_id=1, source_target_pairs={{0,1},{1,0},{2,3},{3,2},{4,5},{5,4},{6,7},{7,6},{8,9},{9,8},{10,11... | collective-permute-start | bytes 786440 | tf_op jit(solution)/shard_map/ppermute | solution.py:430
  2.3 8.0 %collective-permute-start.2 = (bf16[64,2048]{1,0:T(8,128)(2,1)S(1)}, bf16[64,2048]{1,0:T(8,128)(2,1)S(1)}, u32[]{:S(2)}, u32[]{:S(2)}) collective-permute-start(bf16[64,2048]{1,0:T(8,128)(2,1)S(1)} %get-tuple-element.75.refs_2_), channel_id=1, source_target_pairs={{0,2},{1,5},{2,0},{3,7},{4,6},{5,1},{6,4},{7,3},{8,10},{9,13},{10,... | collective-permute-start | bytes 786440 | tf_op jit(solution)/shard_map/ppermute | solution.py:430
  4.8 9.1 %collective-permute-start.7 = (bf16[64,2048]{1,0:T(8,128)(2,1)S(1)}, bf16[64,2048]{1,0:T(8,128)(2,1)S(1)}, u32[]{:S(2)}, u32[]{:S(2)}) collective-permute-start(bf16[64,2048]{1,0:T(8,128)(2,1)S(1)} %get-tuple-element.75.refs_2_), channel_id=1, source_target_pairs={{0,8},{1,17},{2,10},{3,19},{4,12},{5,21},{6,14},{7,23},{8,0},{9,25... | collective-permute-start | bytes 786440 | tf_op jit(solution)/shard_map/ppermute | solution.py:430
  6.4 13.1 %collective-permute-start.3 = (bf16[64,2048]{1,0:T(8,128)(2,1)S(1)}, bf16[64,2048]{1,0:T(8,128)(2,1)S(1)}, u32[]{:S(2)}, u32[]{:S(2)}) collective-permute-start(bf16[64,2048]{1,0:T(8,128)(2,1)S(1)} %collective-permute-done.1.refs_3_), channel_id=1, source_target_pairs={{0,2},{1,5},{2,0},{3,7},{4,6},{5,1},{6,4},{7,3},{8,10},{9,13},{10,... | collective-permute-start | bytes 786440 | tf_op jit(solution)/shard_map/ppermute | solution.py:430
  6.9 12.6 %collective-permute-start.8 = (bf16[64,2048]{1,0:T(8,128)(2,1)S(1)}, bf16[64,2048]{1,0:T(8,128)(2,1)S(1)}, u32[]{:S(2)}, u32[]{:S(2)}) collective-permute-start(bf16[64,2048]{1,0:T(8,128)(2,1)S(1)} %collective-permute-done.1.refs_3_), channel_id=1, source_target_pairs={{0,8},{1,17},{2,10},{3,19},{4,12},{5,21},{6,14},{7,23},{8,0},{9,25... | collective-permute-start | bytes 786440 | tf_op jit(solution)/shard_map/ppermute | solution.py:430
  9.9 9.8 %collective-permute-start.4 = (bf16[64,2048]{1,0:T(8,128)(2,1)S(1)}, bf16[64,2048]{1,0:T(8,128)(2,1)S(1)}, u32[]{:S(2)}, u32[]{:S(2)}) collective-permute-start(bf16[64,2048]{1,0:T(8,128)(2,1)S(1)} %get-tuple-element.75.refs_2_), channel_id=1, source_target_pairs={{0,1},{1,0},{2,3},{3,2},{4,5},{5,4},{6,7},{7,6},{8,9},{9,8},{10,11... | collective-permute-start | bytes 786440 | tf_op jit(solution)/shard_map/ppermute | solution.py:430
  10.3 9.8 %collective-permute-start.5 = (bf16[64,2048]{1,0:T(8,128)(2,1)S(1)}, bf16[64,2048]{1,0:T(8,128)(2,1)S(1)}, u32[]{:S(2)}, u32[]{:S(2)}) collective-permute-start(bf16[64,2048]{1,0:T(8,128)(2,1)S(1)} %collective-permute-done.2.refs_4_), channel_id=1, source_target_pairs={{0,1},{1,0},{2,3},{3,2},{4,5},{5,4},{6,7},{7,6},{8,9},{9,8},{10,11... | collective-permute-start | bytes 786440 | tf_op jit(solution)/shard_map/ppermute | solution.py:430
  13.9 6.4 %collective-permute-start.11 = (bf16[64,2048]{1,0:T(8,128)(2,1)S(1)}, bf16[64,2048]{1,0:T(8,128)(2,1)S(1)}, u32[]{:S(2)}, u32[]{:S(2)}) collective-permute-start(bf16[64,2048]{1,0:T(8,128)(2,1)S(1)} %collective-permute-done.7.refs_6_), channel_id=1, source_target_pairs={{0,2},{1,5},{2,0},{3,7},{4,6},{5,1},{6,4},{7,3},{8,10},{9,13},{10,... | collective-permute-start | bytes 786440 | tf_op jit(solution)/shard_map/ppermute | solution.py:430
  19.5 6.5 %collective-permute-start.12 = (bf16[64,2048]{1,0:T(8,128)(2,1)S(1)}, bf16[64,2048]{1,0:T(8,128)(2,1)}, u32[]{:S(2)}, u32[]{:S(2)}) collective-permute-start(bf16[64,2048]{1,0:T(8,128)(2,1)S(1)} %collective-permute-done.8.refs_7_), channel_id=1, source_target_pairs={{0,2},{1,5},{2,0},{3,7},{4,6},{5,1},{6,4},{7,3},{8,10},{9,13},{10,... | collective-permute-start | bytes 786440 | tf_op jit(solution)/shard_map/ppermute | solution.py:430
  19.5 6.6 %collective-permute-start.6 = (bf16[64,2048]{1,0:T(8,128)(2,1)S(1)}, bf16[64,2048]{1,0:T(8,128)(2,1)S(1)}, u32[]{:S(2)}, u32[]{:S(2)}) collective-permute-start(bf16[64,2048]{1,0:T(8,128)(2,1)S(1)} %collective-permute-done.3.refs_5_), channel_id=1, source_target_pairs={{0,1},{1,0},{2,3},{3,2},{4,5},{5,4},{6,7},{7,6},{8,9},{9,8},{10,11... | collective-permute-start | bytes 786440 | tf_op jit(solution)/shard_map/ppermute | solution.py:430
  19.7 7.4 %collective-permute-start.9 = (bf16[64,2048]{1,0:T(8,128)(2,1)S(1)}, bf16[64,2048]{1,0:T(8,128)(2,1)S(1)}, u32[]{:S(2)}, u32[]{:S(2)}) collective-permute-start(bf16[64,2048]{1,0:T(8,128)(2,1)S(1)} %collective-permute-done.7.refs_6_), channel_id=1, source_target_pairs={{0,1},{1,0},{2,3},{3,2},{4,5},{5,4},{6,7},{7,6},{8,9},{9,8},{10,11... | collective-permute-start | bytes 786440 | tf_op jit(solution)/shard_map/ppermute | solution.py:430
  20.1 7.1 %collective-permute-start.10 = (bf16[64,2048]{1,0:T(8,128)(2,1)S(1)}, bf16[64,2048]{1,0:T(8,128)(2,1)S(1)}, u32[]{:S(2)}, u32[]{:S(2)}) collective-permute-start(bf16[64,2048]{1,0:T(8,128)(2,1)S(1)} %collective-permute-done.8.refs_7_), channel_id=1, source_target_pairs={{0,1},{1,0},{2,3},{3,2},{4,5},{5,4},{6,7},{7,6},{8,9},{9,8},{10,11... | collective-permute-start | bytes 786440 | tf_op jit(solution)/shard_map/ppermute | solution.py:430
  20.3 8.9 %collective-permute-start.13 = (bf16[64,2048]{1,0:T(8,128)(2,1)S(1)}, bf16[64,2048]{1,0:T(8,128)(2,1)S(1)}, u32[]{:S(2)}, u32[]{:S(2)}) collective-permute-start(bf16[64,2048]{1,0:T(8,128)(2,1)S(1)} %collective-permute-done.11.refs_8_), channel_id=1, source_target_pairs={{0,1},{1,0},{2,3},{3,2},{4,5},{5,4},{6,7},{7,6},{8,9},{9,8},{10,11... | collective-permute-start | bytes 786440 | tf_op jit(solution)/shard_map/ppermute | solution.py:430
  26.0 3.2 %collective-permute-start.14 = (bf16[64,2048]{1,0:T(8,128)(2,1)}, bf16[64,2048]{1,0:T(8,128)(2,1)S(1)}, u32[]{:S(2)}, u32[]{:S(2)}) collective-permute-start(bf16[64,2048]{1,0:T(8,128)(2,1)} %collective-permute-done.12.refs_9_), channel_id=1, source_target_pairs={{0,1},{1,0},{2,3},{3,2},{4,5},{5,4},{6,7},{7,6},{8,9},{9,8},{10,11... | collective-permute-start | bytes 786440 | tf_op jit(solution)/shard_map/ppermute | solution.py:430
  33.9 3.9 %collective-permute-start.15 = (f32[16,512]{1,0:T(8,128)S(1)}, f32[16,512]{1,0:T(8,128)S(1)}, u32[]{:S(2)}, u32[]{:S(2)}) collective-permute-start(f32[16,512]{1,0:T(8,128)S(1)} %get-tuple-element.49.refs_1_), channel_id=1, source_target_pairs={{0,2},{1,3},{2,0},{3,1},{4,6},{5,7},{6,4},{7,5},{8,10},{9,11},{10,... | collective-permute-start | bytes 98312 | tf_op jit(solution)/shard_map/ppermute | solution.py:430
  33.9 3.9 %collective-permute-start.16 = (f32[16,512]{1,0:T(8,128)S(1)}, f32[16,512]{1,0:T(8,128)S(1)}, u32[]{:S(2)}, u32[]{:S(2)}) collective-permute-start(f32[16,512]{1,0:T(8,128)S(1)} %get-tuple-element.49.refs_1_), channel_id=1, source_target_pairs={{0,8},{1,9},{2,10},{3,11},{4,12},{5,13},{6,14},{7,15},{8,0},{9,1},... | collective-permute-start | bytes 98312 | tf_op jit(solution)/shard_map/ppermute | solution.py:430
  35.8 4.8 %collective-permute-start.17 = (f32[16,512]{1,0:T(8,128)S(1)}, f32[16,512]{1,0:T(8,128)S(1)}, u32[]{:S(2)}, u32[]{:S(2)}) collective-permute-start(f32[16,512]{1,0:T(8,128)S(1)} %get-tuple-element.49.refs_1_), channel_id=1, source_target_pairs={{0,10},{1,11},{2,8},{3,9},{4,14},{5,15},{6,12},{7,13},{8,2},{9,3},... | collective-permute-start | bytes 98312 | tf_op jit(solution)/shard_map/ppermute | solution.py:430
  41.6 7.6 %collective-permute-start.22 = (bf16[128,1024]{1,0:T(8,128)(2,1)S(1)}, bf16[128,1024]{1,0:T(8,128)(2,1)S(1)}, u32[]{:S(2)}, u32[]{:S(2)}) collective-permute-start(bf16[128,1024]{1,0:T(8,128)(2,1)S(1)} %get-tuple-element.67), channel_id=1, source_target_pairs={{0,2},{1,5},{2,0},{3,7},{4,6},{5,1},{6,4},{7,3},{8,10},{9,13},{10,... | collective-permute-start | bytes 786440 | tf_op jit(solution)/shard_map/ppermute | solution.py:430
  46.7 6.4 %collective-permute-start.19 = (bf16[128,1024]{1,0:T(8,128)(2,1)S(1)}, bf16[128,1024]{1,0:T(8,128)(2,1)S(1)}, u32[]{:S(2)}, u32[]{:S(2)}) collective-permute-start(bf16[128,1024]{1,0:T(8,128)(2,1)S(1)} %get-tuple-element.63), channel_id=1, source_target_pairs={{0,2},{1,5},{2,0},{3,7},{4,6},{5,1},{6,4},{7,3},{8,10},{9,13},{10,... | collective-permute-start | bytes 786440 | tf_op jit(solution)/shard_map/ppermute | solution.py:430
  47.2 15.4 %collective-permute-start.21 = (bf16[128,1024]{1,0:T(8,128)(2,1)S(1)}, bf16[128,1024]{1,0:T(8,128)(2,1)S(1)}, u32[]{:S(2)}, u32[]{:S(2)}) collective-permute-start(bf16[128,1024]{1,0:T(8,128)(2,1)S(1)} %get-tuple-element.65), channel_id=1, source_target_pairs={{0,2},{1,5},{2,0},{3,7},{4,6},{5,1},{6,4},{7,3},{8,10},{9,13},{10,... | collective-permute-start | bytes 786440 | tf_op jit(solution)/shard_map/ppermute | solution.py:430
  48.8 10.0 %collective-permute-start.18 = (bf16[128,1024]{1,0:T(8,128)(2,1)S(1)}, bf16[128,1024]{1,0:T(8,128)(2,1)S(1)}, u32[]{:S(2)}, u32[]{:S(2)}) collective-permute-start(bf16[128,1024]{1,0:T(8,128)(2,1)S(1)} %get-tuple-element.61), channel_id=1, source_target_pairs={{0,2},{1,5},{2,0},{3,7},{4,6},{5,1},{6,4},{7,3},{8,10},{9,13},{10,... | collective-permute-start | bytes 786440 | tf_op jit(solution)/shard_map/ppermute | solution.py:430
  49.3 13.3 %collective-permute-start.23 = (bf16[128,1024]{1,0:T(8,128)(2,1)S(1)}, bf16[128,1024]{1,0:T(8,128)(2,1)S(1)}, u32[]{:S(2)}, u32[]{:S(2)}) collective-permute-start(bf16[128,1024]{1,0:T(8,128)(2,1)S(1)} %add_convert_fusion), channel_id=1, source_target_pairs={{0,8},{1,17},{2,10},{3,19},{4,12},{5,21},{6,14},{7,23},{8,0},{9,25... | collective-permute-start | bytes 786440 | tf_op jit(solution)/shard_map/ppermute | solution.py:430
  53.2 9.2 %collective-permute-start.20 = (bf16[64,1024]{1,0:T(8,128)(2,1)S(1)}, bf16[64,1024]{1,0:T(8,128)(2,1)S(1)}, u32[]{:S(2)}, u32[]{:S(2)}) collective-permute-start(bf16[64,1024]{1,0:T(8,128)(2,1)S(1)} %get-tuple-element.76), channel_id=1, source_target_pairs={{0,8},{1,17},{2,10},{3,19},{4,12},{5,21},{6,14},{7,23},{8,0},{9,25... | collective-permute-start | bytes 393224 | tf_op jit(solution)/shard_map/ppermute | solution.py:430
  53.9 9.4 %collective-permute-start.25 = (bf16[64,1024]{1,0:T(8,128)(2,1)S(1)}, bf16[64,1024]{1,0:T(8,128)(2,1)S(1)}, u32[]{:S(2)}, u32[]{:S(2)}) collective-permute-start(bf16[64,1024]{1,0:T(8,128)(2,1)S(1)} %get-tuple-element.77), channel_id=1, source_target_pairs={{0,9},{1,16},{2,11},{3,18},{4,13},{5,20},{6,15},{7,22},{8,1},{9,24... | collective-permute-start | bytes 393224 | tf_op jit(solution)/shard_map/ppermute | solution.py:430
  (3 other events, 4.8 us)
where the time goes:
time: 65.7 us; the launch traced here: 65.5 us
  waiting for transfers between devices  31.5 us (48%)
  starting transfers between devices  17.7 us (27%)
  Pallas kernels  12.2 us (19%)
  other arithmetic  3.24 us (5%)
  between operations  0.8 us (1%)
    ppermute x27, waiting for transfers between devices, exchange(): return lax.ppermute(x, AXES, [(i, i ^ masks_of(i)) for i in range(devices)])  31.5 us
    ppermute x27, starting transfers between devices, exchange(): return lax.ppermute(x, AXES, [(i, i ^ masks_of(i)) for i in range(devices)])  17.7 us
    pallas_call x3, Pallas kernels, tile(): pl.pallas_call(functools.partial(tile_kernel, [shapes[i] for i in span],...  7.75 us
    pallas_call x2, Pallas kernels, bands(): pl.pallas_call(functools.partial(band_kernel, groups, uppers, widths, own...  4.41 us
  transfers between devices with their start and end apart: 27, of which 11 were waited for; matrix products, arithmetic and copies ran while one was open for 2% of the time, Pallas kernels for 10%

commit v1 on v0

--- a/solution.py
+++ b/solution.py
@@ -186,14 +186,21 @@
 
 def subtile_scores(v_refs, w_refs, uppers):
     narrow = [m for m in uppers if m <= LANES]
-    head = rows_of(v_refs, 0, LANES)
+    left, right = rows_of(v_refs, 0, LANES), rows_of(w_refs, 0, LANES)
+    slim = right.shape[0] < 2 * LANES
+    head = right if slim else left
     count = head.shape[0]
     lane = lax.broadcasted_iota(jnp.int32, head.shape, 1)
-    masked = [jnp.where(lane < m, head, jnp.zeros_like(head)) for m in narrow]
-    stacked = transposed_dot(jnp.concatenate(masked, axis=0), rows_of(w_refs, 0, LANES))
-    for k in range(len(narrow)):
-        yield stacked[k * count:(k + 1) * count]
-    lower, running = narrow[-1], stacked[-count:]
+    masked = jnp.concatenate(
+        [jnp.where(lane < m, head, jnp.zeros_like(head)) for m in narrow], axis=0)
+    if slim:
+        stacked = transposed_dot(left, masked)
+        parts = [stacked[:, k * count:(k + 1) * count] for k in range(len(narrow))]
+    else:
+        stacked = transposed_dot(masked, right)
+        parts = [stacked[k * count:(k + 1) * count] for k in range(len(narrow))]
+    yield from parts
+    lower, running = narrow[-1], parts[-1]
     for upper in uppers[len(narrow):]:
         running = running + transposed_dot(
             rows_of(v_refs, lower, upper), rows_of(w_refs, lower, upper))
@@ -241,24 +248,28 @@
     return top + jnp.log(mass) * LOG2E
 
 
-def tile_kernel(tiles, uppers, own_rows, pieces, finish, *refs):
+def tile_kernel(span, groups, uppers, own_rows, finish, *refs):
+    shapes = subtiles(groups)
+    tiles = [shapes[i] for i in span]
+    r0, r1, c0, c1 = extent(tiles)
     me_ref, partner_ref = refs[:2]
-    v_refs, w_refs = refs[2:2 + pieces], refs[2 + pieces:2 + 2 * pieces]
-    at = 2 + 2 * pieces
+    at = 2 + 2 * (r1 - r0)
+    v_refs, w_refs = refs[2:at], refs[at:at + 2 * (c1 - c0)]
+    at += 2 * (c1 - c0)
     earlier = refs[at:at + 4 * finish]
     outs = refs[at + 4 * finish:]
     lead = (me_ref[0] & 1) == 0
-    for i, (r0, r1, c0, c1) in enumerate(tiles):
+    for i, (t0, t1, u0, u1) in enumerate(tiles):
         subtile(
-            lead, v_refs[2 * r0:2 * r1], w_refs[2 * c0:2 * c1], uppers, outs[5 * i:5 * i + 5])
+            lead, v_refs[2 * (t0 - r0):2 * (t1 - r0)], w_refs[2 * (u0 - c0):2 * (u1 - c0)],
+            uppers, outs[5 * i:5 * i + 5])
     if not finish:
         outs[-1][...] = partner_ref[...]
         return
     stats_ref = outs[-1]
     every = [earlier[4 * i:4 * i + 4] for i in range(finish)]
     every += [outs[5 * i + 1:5 * i + 5] for i in range(len(tiles))]
-    shapes = subtiles(pieces // 2)
-    segments = segments_of(pieces // 2)
+    segments = segments_of(groups)
     chip_rows = 2 * own_rows
 
     @pl.when(lead)
@@ -295,7 +306,12 @@
 def subtiles(groups):
     (_, low), (_, middle), _ = segments_of(groups)
     return [(0, low, 0, low), (0, low, low, middle), (low, middle, 0, middle),
-            (0, middle, middle, groups), (middle, groups, 0, groups)]
+            (middle, groups, 0, middle), (0, groups, middle, groups)]
+
+
+def extent(tiles):
+    first, second, third, fourth = zip(*tiles)
+    return min(first), max(second), min(third), max(fourth)
 
 
 def band_kernel(groups, uppers, widths, own_rows, masks, follows, *refs):
@@ -508,7 +524,8 @@
         params = pltpu.CompilerParams(vmem_limit_bytes=limit)
 
         def tile(span, partner_row, earlier=()):
-            reach = 2 * max(max(shapes[i][1], shapes[i][3]) for i in span)
+            first, end, left, right = extent([shapes[i] for i in span])
+            operands = v_list[2 * first:2 * end] + w_list[2 * left:2 * right]
             stat_shapes = [shape(STATS, total)] if earlier else [shape(1, chip_rows)]
             result, area = [], 0
             for i in span:
@@ -519,23 +536,23 @@
                            shape(STATS, wide), shape(STATS, wide)]
             *arrays, last_array = pl.pallas_call(
                 functools.partial(
-                    tile_kernel, [shapes[i] for i in span], uppers, own_rows, reach,
-                    len(earlier)),
+                    tile_kernel, span, groups, uppers, own_rows, len(earlier)),
                 out_shape=result + stat_shapes,
-                in_specs=[smem] + [vmem] * (1 + 2 * reach + 4 * len(earlier)),
+                in_specs=[smem] + [vmem] * (1 + len(operands) + 4 * len(earlier)),
                 out_specs=[vmem] * (len(result) + 1),
                 compiler_params=params,
                 cost_estimate=pl.CostEstimate(
                     flops=6 * area * feature_dim, transcendentals=0,
                     bytes_accessed=2 * total * feature_dim),
-            )(me, partner_row, *v_list[:reach], *w_list[:reach],
-              *[a for one in earlier for a in one[1:]])
+            )(me, partner_row, *operands, *[a for one in earlier for a in one[1:]])
             return [arrays[5 * i:5 * i + 5] for i in range(len(span))], last_array
 
         done, chip_partner = tile([0], chip_partner)
         more, chip_partner = tile([1, 2], chip_partner)
         done += more
-        more, stats = tile([3, 4], chip_partner, done)
+        more, chip_partner = tile([3], chip_partner)
+        done += more
+        more, stats = tile([4], chip_partner, done)
         done += more
         common = [me, *gathered(stats), *[t[0] for t in done], *[t[1] for t in done],
                   *[t[3] for t in done], *w_list]
@@ -569,8 +586,10 @@
             for j in sorted([j for j in partial if j & step], reverse=True):
                 arrived = along(partial.pop(j).astype(jnp.bfloat16), stage)
                 partial[j ^ step] = partial[j ^ step] + arrived.astype(jnp.float32)
+                if stage == stages - 2 and j ^ step:
+                    partial[j ^ step] = partial[j ^ step].astype(jnp.bfloat16)
         stage = stages - 1
-        outgoing = partial[1 << stage].astype(jnp.bfloat16)
+        outgoing = partial[1 << stage]
         kept = partial[0]
         if c < len(chunks) - 1:
             arrived = along(outgoing, stage)
@@ -581,9 +600,9 @@
             far = lambda i: document_masks[stage] ^ 1 if i & 1 else query_masks[stage] ^ 1
             near_arrived = along(outgoing[:own_rows], stage)
             far_arrived = exchange(outgoing[own_rows:], far)
-            mine_parts.append(kept[:own_rows] + near_arrived.astype(jnp.float32))
-            other_parts.append(
-                swap(kept[own_rows:]) + far_arrived.astype(jnp.float32))
+            ours, theirs = lax.optimization_barrier((kept[:own_rows], kept[own_rows:]))
+            mine_parts.append(ours + near_arrived.astype(jnp.float32))
+            other_parts.append(swap(theirs) + far_arrived.astype(jnp.float32))
     mine_parts, other_parts = mine_parts[::-1], other_parts[::-1]
     ours = jnp.concatenate(mine_parts, axis=1)
     theirs = jnp.concatenate(other_parts, axis=1)

time: 65.7 us -> 70 us (1.065)
  the two profiles are of different devices: /device:TPU:0 before, /device:TPU:1 now
where the time goes in v1:
time: 70 us; the launch traced here: 69.8 us
  starting transfers between devices  29.4 us (42%)
  waiting for transfers between devices  24.3 us (35%)
  Pallas kernels  11.9 us (17%)
  other arithmetic  3.23 us (5%)
  between operations  0.79 us (1%)
    ppermute x27, starting transfers between devices, exchange(): return lax.ppermute(x, AXES, [(i, i ^ masks_of(i)) for i in range(devices)])  29.4 us
    ppermute x27, waiting for transfers between devices, exchange(): return lax.ppermute(x, AXES, [(i, i ^ masks_of(i)) for i in range(devices)])  24.3 us
    pallas_call x4, Pallas kernels, tile(): pl.pallas_call(functools.partial(tile_kernel, span, groups, uppers, own_r...  7.6 us
    pallas_call x2, Pallas kernels, bands(): pl.pallas_call(functools.partial(band_kernel, groups, uppers, widths, own...  4.32 us
  transfers between devices with their start and end apart: 27, of which 9 were waited for; matrix products, arithmetic and copies ran while one was open for 2% of the time, Pallas kernels for 11%

profile of v1, /device:TPU:1, one launch (start us, length us, event | category | flops | bytes accessed | tf_op | source)
XLA Modules:
  0.0 69.8 jit_solution(5045940168994070135)
XLA Ops:
  0.6 1.1 %broadcast_select_fusion = (bf16[64,2048]{1,0:T(8,128)(2,1)S(1)}, bf16[64,2048]{1,0:T(8,128)(2,1)S(1)}) fusion(bf16[64,2048]{1,0:T(8,128)(2,1)} %param.4, bf16[64,2048]{1,0:T(8,128)(2,1)} %param.3, pred[]{:T(512)S(6)} %eq.3), kind=kLoop, calls=%fused_computation.10 | loop fusion | flops 262144 | bytes 1048577 | tf_op jit(solution)/shard_map/jit(_where)/select_n | solution.py:455
  1.8 2.7 %collective-permute-start.2 = (bf16[64,2048]{1,0:T(8,128)(2,1)S(1)}, bf16[64,2048]{1,0:T(8,128)(2,1)S(1)}, u32[]{:S(2)}, u32[]{:S(2)}) collective-permute-start(bf16[64,2048]{1,0:T(8,128)(2,1)S(1)} %get-tuple-element.85.refs_2_), channel_id=1, source_target_pairs={{0,2},{1,5},{2,0},{3,7},{4,6},{5,1},{6,4},{7,3},{8,10},{9,13},{10,... | collective-permute-start | bytes 786440 | tf_op jit(solution)/shard_map/ppermute | solution.py:446
  4.5 2.3 %collective-permute-start.7 = (bf16[64,2048]{1,0:T(8,128)(2,1)S(1)}, bf16[64,2048]{1,0:T(8,128)(2,1)S(1)}, u32[]{:S(2)}, u32[]{:S(2)}) collective-permute-start(bf16[64,2048]{1,0:T(8,128)(2,1)S(1)} %get-tuple-element.85.refs_2_), channel_id=1, source_target_pairs={{0,8},{1,17},{2,10},{3,19},{4,12},{5,21},{6,14},{7,23},{8,0},{9,25... | collective-permute-start | bytes 786440 | tf_op jit(solution)/shard_map/ppermute | solution.py:446
  8.6 1.2 %collective-permute-done = f32[1,64]{1,0:T(1,128)S(1)} collective-permute-done((f32[1,64]{1,0:T(1,128)S(1)}, f32[1,64]{1,0:T(1,128)S(1)}, u32[]{:S(2)}, u32[]{:S(2)}) %collective-permute-start) | collective-permute-done | bytes 288 | tf_op jit(solution)/shard_map/ppermute | solution.py:446
  10.3 3.1 %collective-permute-done.7.refs_6_ = bf16[64,2048]{1,0:T(8,128)(2,1)S(1)} collective-permute-done((bf16[64,2048]{1,0:T(8,128)(2,1)S(1)}, bf16[64,2048]{1,0:T(8,128)(2,1)S(1)}, u32[]{:S(2)}, u32[]{:S(2)}) %collective-permute-start.7) | collective-permute-done | bytes 262176 | tf_op jit(solution)/shard_map/ppermute | solution.py:446
  14.4 4.7 %collective-permute-done.8.refs_7_ = bf16[64,2048]{1,0:T(8,128)(2,1)S(1)} collective-permute-done((bf16[64,2048]{1,0:T(8,128)(2,1)S(1)}, bf16[64,2048]{1,0:T(8,128)(2,1)S(1)}, u32[]{:S(2)}, u32[]{:S(2)}) %collective-permute-start.8) | collective-permute-done | bytes 262176 | tf_op jit(solution)/shard_map/ppermute | solution.py:446
  20.3 4.3 %collective-permute-done.12.refs_3_.refs_9_ = bf16[64,2048]{1,0:T(8,128)(2,1)} collective-permute-done((bf16[64,2048]{1,0:T(8,128)(2,1)S(1)}, bf16[64,2048]{1,0:T(8,128)(2,1)}, u32[]{:S(2)}, u32[]{:S(2)}) %collective-permute-start.12) | collective-permute-done | bytes 262176 | tf_op jit(solution)/shard_map/ppermute | solution.py:446
  24.7 1.4 %collective-permute-start.14 = (bf16[64,2048]{1,0:T(8,128)(2,1)}, bf16[64,2048]{1,0:T(8,128)(2,1)S(1)}, u32[]{:S(2)}, u32[]{:S(2)}) collective-permute-start(bf16[64,2048]{1,0:T(8,128)(2,1)} %collective-permute-done.12.refs_3_.refs_9_), channel_id=1, source_target_pairs={{0,1},{1,0},{2,3},{3,2},{4,5},{5,4},{6,7},{7,6},{8,9},{9,8},{10,11... | collective-permute-start | bytes 786440 | tf_op jit(solution)/shard_map/ppermute | solution.py:446
  27.1 1.7 %shard_map.51 = (f32[9,256,128]{2,1,0:T(8,128)S(1)}, f32[256,128]{1,0:T(8,128)S(1)}, f32[256,128]{1,0:T(8,128)S(1)}, f32[16,128]{1,0:T(8,128)S(1)}, f32[16,128]{...) custom-call(s32[1]{0:T(128)} %bitcast.refs_0_, ...), custom_call_target="tpu_custom_call" | custom-call | flops 1006632960 | bytes 2097152 | tf_op jit(solution)/shard_map/pallas_call | solution.py:537
  28.7 1.9 %shard_map.52 = (f32[9,128,384]{2,1,0:T(8,128)S(1)}, f32[128,128]{1,0:T(8,128)S(1)}, f32[128,128]{1,0:T(8,128)S(1)}, f32[16,384]{1,0:T(8,128)S(1)}, f32[16,384]{1,0:T(8,128)S(1)}, /*index=5*/f32[1,128]{1,0:T(1,128)S(1)}) custom-call(s32[1]{0:T(128)} %bitcast.refs_0_, f32[1,128]{1,0:T(1,128)S(1)} %get-tuple-element.41.refs_1_, ...), custom_call_target="tpu_custom_call" | custom-call | flops 603979776 | bytes 2097152 | tf_op jit(solution)/shard_map/pallas_call | solution.py:537
  30.6 3.1 %shard_map.53 = (f32[9,512,128]{2,1,0:T(8,128)S(1)}, f32[512,128]{1,0:T(8,128)S(1)}, f32[512,128]{1,0:T(8,128)}, f32[16,128]{1,0:T(8,128)S(1)}, f32[16,128]{1,0:T(8,128)}, /*index=5*/f32[16,512]{1,0:T(8,128)S(1)}) custom-call(s32[1]{0:T(128)} %bitcast.refs_0_, f32[1,128]{1,0:T(1,128)S(1)} %get-tuple-element.42.refs_1_, ...), custom_call_target="tpu_custom_call" | custom-call | flops 805306368 | bytes 2097152 | tf_op jit(solution)/shard_map/pallas_call | solution.py:537
  33.7 1.2 %collective-permute-start.16 = (f32[16,512]{1,0:T(8,128)S(1)}, f32[16,512]{1,0:T(8,128)S(1)}, u32[]{:S(2)}, u32[]{:S(2)}) collective-permute-start(f32[16,512]{1,0:T(8,128)S(1)} %get-tuple-element.59.refs_1_), channel_id=1, source_target_pairs={{0,8},{1,9},{2,10},{3,11},{4,12},{5,13},{6,14},{7,15},{8,0},{9,1},... | collective-permute-start | bytes 98312 | tf_op jit(solution)/shard_map/ppermute | solution.py:446
  34.9 1.5 %collective-permute-start.17 = (f32[16,512]{1,0:T(8,128)S(1)}, f32[16,512]{1,0:T(8,128)S(1)}, u32[]{:S(2)}, u32[]{:S(2)}) collective-permute-start(f32[16,512]{1,0:T(8,128)S(1)} %get-tuple-element.59.refs_1_), channel_id=1, source_target_pairs={{0,10},{1,11},{2,8},{3,9},{4,14},{5,15},{6,12},{7,13},{8,2},{9,3},... | collective-permute-start | bytes 98312 | tf_op jit(solution)/shard_map/ppermute | solution.py:446
  36.5 2.1 %collective-permute-done.17.refs_4_ = f32[16,512]{1,0:T(8,128)S(1)} collective-permute-done((f32[16,512]{1,0:T(8,128)S(1)}, f32[16,512]{1,0:T(8,128)S(1)}, u32[]{:S(2)}, u32[]{:S(2)}) %collective-permute-start.17) | collective-permute-done | bytes 32800 | tf_op jit(solution)/shard_map/ppermute | solution.py:446
  38.6 1.0 %shard_map.54 = (f32[128,1024]{1,0:T(8,128)S(1)}, bf16[128,1024]{1,0:T(8,128)(2,1)S(1)}, f32[128,1024]{1,0:T(8,128)S(1)}, bf16[128,1024]{1,0:T(8,128)(2,1)S(1)}, f32[512,512]{1,0:T(8,128)S(1)}) custom-call(s32[1]{0:T(128)} %bitcast.refs_0_, f32[16,512]{1,0:T(8,128)S(1)} %get-tuple-element.59.refs_1_, f32[16,512]{1,0:T(8,128)S(1)} %collective-permute-done.15.refs_2_, ...), custom_call_target="tpu_custom_call" | custom-call | flops 1073741824 | bytes 4194304 | tf_op jit(solution)/shard_map/pallas_call | solution.py:564
  39.6 1.6 %collective-permute-start.22 = (bf16[128,1024]{1,0:T(8,128)(2,1)S(1)}, bf16[128,1024]{1,0:T(8,128)(2,1)S(1)}, u32[]{:S(2)}, u32[]{:S(2)}) collective-permute-start(bf16[128,1024]{1,0:T(8,128)(2,1)S(1)} %get-tuple-element.76), channel_id=1, source_target_pairs={{0,2},{1,5},{2,0},{3,7},{4,6},{5,1},{6,4},{7,3},{8,10},{9,13},{10,... | collective-permute-start | bytes 786440 | tf_op jit(solution)/shard_map/ppermute | solution.py:446
  41.2 3.3 %shard_map.55 = (f32[128,1024]{1,0:T(8,128)S(1)}, bf16[128,1024]{1,0:T(8,128)(2,1)S(1)}, f32[128,1024]{1,0:T(8,128)S(1)}, bf16[128,1024]{1,0:T(8,128)(2,1)S(1)}) custom-call(s32[1]{0:T(128)} %bitcast.refs_0_, f32[16,512]{1,0:T(8,128)S(1)} %get-tuple-element.59.refs_1_, f32[16,512]{1,0:T(8,128)S(1)} %collective-permute-done.15.refs_2_, ...), custom_call_target="tpu_custom_call" | custom-call | flops 1073741824 | bytes 4194304 | tf_op jit(solution)/shard_map/pallas_call | solution.py:564
  44.6 1.4 %collective-permute-start.21 = (bf16[128,1024]{1,0:T(8,128)(2,1)S(1)}, bf16[128,1024]{1,0:T(8,128)(2,1)S(1)}, u32[]{:S(2)}, u32[]{:S(2)}) collective-permute-start(bf16[128,1024]{1,0:T(8,128)(2,1)S(1)} %get-tuple-element.74), channel_id=1, source_target_pairs={{0,2},{1,5},{2,0},{3,7},{4,6},{5,1},{6,4},{7,3},{8,10},{9,13},{10,... | collective-permute-start | bytes 786440 | tf_op jit(solution)/shard_map/ppermute | solution.py:446
  46.2 2.6 %collective-permute-start.23 = (bf16[128,1024]{1,0:T(8,128)(2,1)S(1)}, bf16[128,1024]{1,0:T(8,128)(2,1)S(1)}, u32[]{:S(2)}, u32[]{:S(2)}) collective-permute-start(bf16[128,1024]{1,0:T(8,128)(2,1)S(1)} %add_convert_fusion), channel_id=1, source_target_pairs={{0,8},{1,17},{2,10},{3,19},{4,12},{5,21},{6,14},{7,23},{8,0},{9,25... | collective-permute-start | bytes 786440 | tf_op jit(solution)/shard_map/ppermute | solution.py:446
  49.9 4.3 %collective-permute-start.24 = (f32[64,1024]{1,0:T(8,128)S(1)}, f32[64,1024]{1,0:T(8,128)S(1)}, u32[]{:S(2)}, u32[]{:S(2)}) collective-permute-start(f32[64,1024]{1,0:T(8,128)S(1)} %get-tuple-element.77), channel_id=1, source_target_pairs={{0,1},{1,0},{2,3},{3,2},{4,5},{5,4},{6,7},{7,6},{8,9},{9,8},{10,11... | collective-permute-start | bytes 786440 | tf_op jit(solution)/shard_map/ppermute | solution.py:446
  54.2 1.5 %collective-permute-done.19 = bf16[128,1024]{1,0:T(8,128)(2,1)S(1)} collective-permute-done((bf16[128,1024]{1,0:T(8,128)(2,1)S(1)}, bf16[128,1024]{1,0:T(8,128)(2,1)S(1)}, u32[]{:S(2)}, u32[]{:S(2)}) %collective-permute-start.19) | collective-permute-done | bytes 262176 | tf_op jit(solution)/shard_map/ppermute | solution.py:446
  55.8 6.2 %collective-permute-start.25 = (bf16[64,1024]{1,0:T(8,128)(2,1)S(1)}, bf16[64,1024]{1,0:T(8,128)(2,1)S(1)}, u32[]{:S(2)}, u32[]{:S(2)}) collective-permute-start(bf16[64,1024]{1,0:T(8,128)(2,1)S(1)} %get-tuple-element.87), channel_id=1, source_target_pairs={{0,9},{1,16},{2,11},{3,18},{4,13},{5,20},{6,15},{7,22},{8,1},{9,24... | collective-permute-start | bytes 393224 | tf_op jit(solution)/shard_map/ppermute | solution.py:446
  62.3 6.3 %collective-permute-done.20 = bf16[64,1024]{1,0:T(8,128)(2,1)S(1)} collective-permute-done((bf16[64,1024]{1,0:T(8,128)(2,1)S(1)}, bf16[64,1024]{1,0:T(8,128)(2,1)S(1)}, u32[]{:S(2)}, u32[]{:S(2)}) %collective-permute-start.20) | collective-permute-done | bytes 131104 | tf_op jit(solution)/shard_map/ppermute | solution.py:446
  68.7 1.1 %fusion = (f32[64,2048]{1,0:T(8,128)}, f32[64,2048]{1,0:T(8,128)}) fusion(f32[64,1024]{1,0:T(8,128)S(1)} %collective-permute-done.26, f32[64,1024]{1,0:T(8,128)S(1)} %convert_add_fusion.2, f32[64,1024]{1,0:T(8,128)S(1)} %get-tuple-element.80, f32[64,1024]{1,0:T(8,128)S(1)} %convert_add_fusion.3, pred[]{:T(512)S(6)} %eq.3), kind=kLoop, calls=%fused_computation.6 | loop fusion | flops 524288 | bytes 2097153 | tf_op jit(solution)/shard_map/jit(_where)/select_n | solution.py:609
  (49 shorter events, 7.5 us)
Async XLA Ops:
  1.7 5.1 %collective-permute-start.1 = (bf16[64,2048]{1,0:T(8,128)(2,1)S(1)}, bf16[64,2048]{1,0:T(8,128)(2,1)S(1)}, u32[]{:S(2)}, u32[]{:S(2)}) collective-permute-start(bf16[64,2048]{1,0:T(8,128)(2,1)S(1)} %get-tuple-element.84.refs_7_.refs_9_.refs_5_.refs_21_), channel_id=1, source_target_pairs={{0,1},{1,0},{2,3},{3,2},{4,5},{5,4},{6,7},{7,6},{8,9},{9,8},{10,11... | collective-permute-start | bytes 786440 | tf_op jit(solution)/shard_map/ppermute | solution.py:446
  1.8 8.2 %collective-permute-start.2 = (bf16[64,2048]{1,0:T(8,128)(2,1)S(1)}, bf16[64,2048]{1,0:T(8,128)(2,1)S(1)}, u32[]{:S(2)}, u32[]{:S(2)}) collective-permute-start(bf16[64,2048]{1,0:T(8,128)(2,1)S(1)} %get-tuple-element.85.refs_2_), channel_id=1, source_target_pairs={{0,2},{1,5},{2,0},{3,7},{4,6},{5,1},{6,4},{7,3},{8,10},{9,13},{10,... | collective-permute-start | bytes 786440 | tf_op jit(solution)/shard_map/ppermute | solution.py:446
  4.5 8.9 %collective-permute-start.7 = (bf16[64,2048]{1,0:T(8,128)(2,1)S(1)}, bf16[64,2048]{1,0:T(8,128)(2,1)S(1)}, u32[]{:S(2)}, u32[]{:S(2)}) collective-permute-start(bf16[64,2048]{1,0:T(8,128)(2,1)S(1)} %get-tuple-element.85.refs_2_), channel_id=1, source_target_pairs={{0,8},{1,17},{2,10},{3,19},{4,12},{5,21},{6,14},{7,23},{8,0},{9,25... | collective-permute-start | bytes 786440 | tf_op jit(solution)/shard_map/ppermute | solution.py:446
  6.8 12.4 %collective-permute-start.3 = (bf16[64,2048]{1,0:T(8,128)(2,1)S(1)}, bf16[64,2048]{1,0:T(8,128)(2,1)S(1)}, u32[]{:S(2)}, u32[]{:S(2)}) collective-permute-start(bf16[64,2048]{1,0:T(8,128)(2,1)S(1)} %collective-permute-done.1.refs_3_), channel_id=1, source_target_pairs={{0,2},{1,5},{2,0},{3,7},{4,6},{5,1},{6,4},{7,3},{8,10},{9,13},{10,... | collective-permute-start | bytes 786440 | tf_op jit(solution)/shard_map/ppermute | solution.py:446
  7.0 12.0 %collective-permute-start.8 = (bf16[64,2048]{1,0:T(8,128)(2,1)S(1)}, bf16[64,2048]{1,0:T(8,128)(2,1)S(1)}, u32[]{:S(2)}, u32[]{:S(2)}) collective-permute-start(bf16[64,2048]{1,0:T(8,128)(2,1)S(1)} %collective-permute-done.1.refs_3_), channel_id=1, source_target_pairs={{0,8},{1,17},{2,10},{3,19},{4,12},{5,21},{6,14},{7,23},{8,0},{9,25... | collective-permute-start | bytes 786440 | tf_op jit(solution)/shard_map/ppermute | solution.py:446
  9.8 9.8 %collective-permute-start.4 = (bf16[64,2048]{1,0:T(8,128)(2,1)S(1)}, bf16[64,2048]{1,0:T(8,128)(2,1)S(1)}, u32[]{:S(2)}, u32[]{:S(2)}) collective-permute-start(bf16[64,2048]{1,0:T(8,128)(2,1)S(1)} %get-tuple-element.85.refs_2_), channel_id=1, source_target_pairs={{0,1},{1,0},{2,3},{3,2},{4,5},{5,4},{6,7},{7,6},{8,9},{9,8},{10,11... | collective-permute-start | bytes 786440 | tf_op jit(solution)/shard_map/ppermute | solution.py:446
  10.0 9.8 %collective-permute-start.5 = (bf16[64,2048]{1,0:T(8,128)(2,1)S(1)}, bf16[64,2048]{1,0:T(8,128)(2,1)S(1)}, u32[]{:S(2)}, u32[]{:S(2)}) collective-permute-start(bf16[64,2048]{1,0:T(8,128)(2,1)S(1)} %collective-permute-done.2.refs_4_), channel_id=1, source_target_pairs={{0,1},{1,0},{2,3},{3,2},{4,5},{5,4},{6,7},{7,6},{8,9},{9,8},{10,11... | collective-permute-start | bytes 786440 | tf_op jit(solution)/shard_map/ppermute | solution.py:446
  13.4 6.7 %collective-permute-start.11 = (bf16[64,2048]{1,0:T(8,128)(2,1)S(1)}, bf16[64,2048]{1,0:T(8,128)(2,1)S(1)}, u32[]{:S(2)}, u32[]{:S(2)}) collective-permute-start(bf16[64,2048]{1,0:T(8,128)(2,1)S(1)} %collective-permute-done.7.refs_6_), channel_id=1, source_target_pairs={{0,2},{1,5},{2,0},{3,7},{4,6},{5,1},{6,4},{7,3},{8,10},{9,13},{10,... | collective-permute-start | bytes 786440 | tf_op jit(solution)/shard_map/ppermute | solution.py:446
  19.0 5.6 %collective-permute-start.12 = (bf16[64,2048]{1,0:T(8,128)(2,1)S(1)}, bf16[64,2048]{1,0:T(8,128)(2,1)}, u32[]{:S(2)}, u32[]{:S(2)}) collective-permute-start(bf16[64,2048]{1,0:T(8,128)(2,1)S(1)} %collective-permute-done.8.refs_7_), channel_id=1, source_target_pairs={{0,2},{1,5},{2,0},{3,7},{4,6},{5,1},{6,4},{7,3},{8,10},{9,13},{10,... | collective-permute-start | bytes 786440 | tf_op jit(solution)/shard_map/ppermute | solution.py:446
  19.2 6.9 %collective-permute-start.6 = (bf16[64,2048]{1,0:T(8,128)(2,1)S(1)}, bf16[64,2048]{1,0:T(8,128)(2,1)S(1)}, u32[]{:S(2)}, u32[]{:S(2)}) collective-permute-start(bf16[64,2048]{1,0:T(8,128)(2,1)S(1)} %collective-permute-done.3.refs_5_), channel_id=1, source_target_pairs={{0,1},{1,0},{2,3},{3,2},{4,5},{5,4},{6,7},{7,6},{8,9},{9,8},{10,11... | collective-permute-start | bytes 786440 | tf_op jit(solution)/shard_map/ppermute | solution.py:446
  19.6 7.5 %collective-permute-start.9 = (bf16[64,2048]{1,0:T(8,128)(2,1)S(1)}, bf16[64,2048]{1,0:T(8,128)(2,1)S(1)}, u32[]{:S(2)}, u32[]{:S(2)}) collective-permute-start(bf16[64,2048]{1,0:T(8,128)(2,1)S(1)} %collective-permute-done.7.refs_6_), channel_id=1, source_target_pairs={{0,1},{1,0},{2,3},{3,2},{4,5},{5,4},{6,7},{7,6},{8,9},{9,8},{10,11... | collective-permute-start | bytes 786440 | tf_op jit(solution)/shard_map/ppermute | solution.py:446
  19.8 7.3 %collective-permute-start.10 = (bf16[64,2048]{1,0:T(8,128)(2,1)S(1)}, bf16[64,2048]{1,0:T(8,128)(2,1)S(1)}, u32[]{:S(2)}, u32[]{:S(2)}) collective-permute-start(bf16[64,2048]{1,0:T(8,128)(2,1)S(1)} %collective-permute-done.8.refs_7_), channel_id=1, source_target_pairs={{0,1},{1,0},{2,3},{3,2},{4,5},{5,4},{6,7},{7,6},{8,9},{9,8},{10,11... | collective-permute-start | bytes 786440 | tf_op jit(solution)/shard_map/ppermute | solution.py:446
  20.1 10.5 %collective-permute-start.13 = (bf16[64,2048]{1,0:T(8,128)(2,1)S(1)}, bf16[64,2048]{1,0:T(8,128)(2,1)S(1)}, u32[]{:S(2)}, u32[]{:S(2)}) collective-permute-start(bf16[64,2048]{1,0:T(8,128)(2,1)S(1)} %collective-permute-done.11.refs_2_.refs_8_), channel_id=1, source_target_pairs={{0,1},{1,0},{2,3},{3,2},{4,5},{5,4},{6,7},{7,6},{8,9},{9,8},{10,11... | collective-permute-start | bytes 786440 | tf_op jit(solution)/shard_map/ppermute | solution.py:446
  24.7 6.0 %collective-permute-start.14 = (bf16[64,2048]{1,0:T(8,128)(2,1)}, bf16[64,2048]{1,0:T(8,128)(2,1)S(1)}, u32[]{:S(2)}, u32[]{:S(2)}) collective-permute-start(bf16[64,2048]{1,0:T(8,128)(2,1)} %collective-permute-done.12.refs_3_.refs_9_), channel_id=1, source_target_pairs={{0,1},{1,0},{2,3},{3,2},{4,5},{5,4},{6,7},{7,6},{8,9},{9,8},{10,11... | collective-permute-start | bytes 786440 | tf_op jit(solution)/shard_map/ppermute | solution.py:446
  34.9 3.7 %collective-permute-start.17 = (f32[16,512]{1,0:T(8,128)S(1)}, f32[16,512]{1,0:T(8,128)S(1)}, u32[]{:S(2)}, u32[]{:S(2)}) collective-permute-start(f32[16,512]{1,0:T(8,128)S(1)} %get-tuple-element.59.refs_1_), channel_id=1, source_target_pairs={{0,10},{1,11},{2,8},{3,9},{4,14},{5,15},{6,12},{7,13},{8,2},{9,3},... | collective-permute-start | bytes 98312 | tf_op jit(solution)/shard_map/ppermute | solution.py:446
  39.6 6.5 %collective-permute-start.22 = (bf16[128,1024]{1,0:T(8,128)(2,1)S(1)}, bf16[128,1024]{1,0:T(8,128)(2,1)S(1)}, u32[]{:S(2)}, u32[]{:S(2)}) collective-permute-start(bf16[128,1024]{1,0:T(8,128)(2,1)S(1)} %get-tuple-element.76), channel_id=1, source_target_pairs={{0,2},{1,5},{2,0},{3,7},{4,6},{5,1},{6,4},{7,3},{8,10},{9,13},{10,... | collective-permute-start | bytes 786440 | tf_op jit(solution)/shard_map/ppermute | solution.py:446
  44.5 5.3 %collective-permute-start.18 = (bf16[128,1024]{1,0:T(8,128)(2,1)S(1)}, bf16[128,1024]{1,0:T(8,128)(2,1)S(1)}, u32[]{:S(2)}, u32[]{:S(2)}) collective-permute-start(bf16[128,1024]{1,0:T(8,128)(2,1)S(1)} %get-tuple-element.69), channel_id=1, source_target_pairs={{0,2},{1,5},{2,0},{3,7},{4,6},{5,1},{6,4},{7,3},{8,10},{9,13},{10,... | collective-permute-start | bytes 786440 | tf_op jit(solution)/shard_map/ppermute | solution.py:446
  44.6 17.4 %collective-permute-start.21 = (bf16[128,1024]{1,0:T(8,128)(2,1)S(1)}, bf16[128,1024]{1,0:T(8,128)(2,1)S(1)}, u32[]{:S(2)}, u32[]{:S(2)}) collective-permute-start(bf16[128,1024]{1,0:T(8,128)(2,1)S(1)} %get-tuple-element.74), channel_id=1, source_target_pairs={{0,2},{1,5},{2,0},{3,7},{4,6},{5,1},{6,4},{7,3},{8,10},{9,13},{10,... | collective-permute-start | bytes 786440 | tf_op jit(solution)/shard_map/ppermute | solution.py:446
  46.0 9.7 %collective-permute-start.19 = (bf16[128,1024]{1,0:T(8,128)(2,1)S(1)}, bf16[128,1024]{1,0:T(8,128)(2,1)S(1)}, u32[]{:S(2)}, u32[]{:S(2)}) collective-permute-start(bf16[128,1024]{1,0:T(8,128)(2,1)S(1)} %get-tuple-element.72), channel_id=1, source_target_pairs={{0,2},{1,5},{2,0},{3,7},{4,6},{5,1},{6,4},{7,3},{8,10},{9,13},{10,... | collective-permute-start | bytes 786440 | tf_op jit(solution)/shard_map/ppermute | solution.py:446
  46.2 15.8 %collective-permute-start.23 = (bf16[128,1024]{1,0:T(8,128)(2,1)S(1)}, bf16[128,1024]{1,0:T(8,128)(2,1)S(1)}, u32[]{:S(2)}, u32[]{:S(2)}) collective-permute-start(bf16[128,1024]{1,0:T(8,128)(2,1)S(1)} %add_convert_fusion), channel_id=1, source_target_pairs={{0,8},{1,17},{2,10},{3,19},{4,12},{5,21},{6,14},{7,23},{8,0},{9,25... | collective-permute-start | bytes 786440 | tf_op jit(solution)/shard_map/ppermute | solution.py:446
  49.9 18.7 %collective-permute-start.24 = (f32[64,1024]{1,0:T(8,128)S(1)}, f32[64,1024]{1,0:T(8,128)S(1)}, u32[]{:S(2)}, u32[]{:S(2)}) collective-permute-start(f32[64,1024]{1,0:T(8,128)S(1)} %get-tuple-element.77), channel_id=1, source_target_pairs={{0,1},{1,0},{2,3},{3,2},{4,5},{5,4},{6,7},{7,6},{8,9},{9,8},{10,11... | collective-permute-start | bytes 786440 | tf_op jit(solution)/shard_map/ppermute | solution.py:446
  55.8 12.8 %collective-permute-start.25 = (bf16[64,1024]{1,0:T(8,128)(2,1)S(1)}, bf16[64,1024]{1,0:T(8,128)(2,1)S(1)}, u32[]{:S(2)}, u32[]{:S(2)}) collective-permute-start(bf16[64,1024]{1,0:T(8,128)(2,1)S(1)} %get-tuple-element.87), channel_id=1, source_target_pairs={{0,9},{1,16},{2,11},{3,18},{4,13},{5,20},{6,15},{7,22},{8,1},{9,24... | collective-permute-start | bytes 393224 | tf_op jit(solution)/shard_map/ppermute | solution.py:446
  62.0 6.6 %collective-permute-start.20 = (bf16[64,1024]{1,0:T(8,128)(2,1)S(1)}, bf16[64,1024]{1,0:T(8,128)(2,1)S(1)}, u32[]{:S(2)}, u32[]{:S(2)}) collective-permute-start(bf16[64,1024]{1,0:T(8,128)(2,1)S(1)} %get-tuple-element.86), channel_id=1, source_target_pairs={{0,8},{1,17},{2,10},{3,19},{4,12},{5,21},{6,14},{7,23},{8,0},{9,25... | collective-permute-start | bytes 393224 | tf_op jit(solution)/shard_map/ppermute | solution.py:446
  62.2 6.5 %collective-permute-start.26 = (f32[64,1024]{1,0:T(8,128)S(1)}, f32[64,1024]{1,0:T(8,128)S(1)}, u32[]{:S(2)}, u32[]{:S(2)}) collective-permute-start(f32[64,1024]{1,0:T(8,128)S(1)} %get-tuple-element.81), channel_id=1, source_target_pairs={{0,1},{1,0},{2,3},{3,2},{4,5},{5,4},{6,7},{7,6},{8,9},{9,8},{10,11... | collective-permute-start | bytes 786440 | tf_op jit(solution)/shard_map/ppermute | solution.py:446
  (3 other events, 6.7 us)

commit v2 on v1

--- a/solution.py
+++ b/solution.py
@@ -248,21 +248,22 @@
     return top + jnp.log(mass) * LOG2E
 
 
-def tile_kernel(span, groups, uppers, own_rows, finish, *refs):
+def tile_kernel(span, counts, uppers, own_rows, finish, *refs):
+    groups = len(counts)
     shapes = subtiles(groups)
     tiles = [shapes[i] for i in span]
     r0, r1, c0, c1 = extent(tiles)
     me_ref, partner_ref = refs[:2]
-    at = 2 + 2 * (r1 - r0)
-    v_refs, w_refs = refs[2:at], refs[at:at + 2 * (c1 - c0)]
-    at += 2 * (c1 - c0)
+    at = 2 + sum(counts[r0:r1])
+    v_refs, w_refs = refs[2:at], refs[at:at + sum(counts[c0:c1])]
+    at += sum(counts[c0:c1])
     earlier = refs[at:at + 4 * finish]
     outs = refs[at + 4 * finish:]
     lead = (me_ref[0] & 1) == 0
     for i, (t0, t1, u0, u1) in enumerate(tiles):
         subtile(
-            lead, v_refs[2 * (t0 - r0):2 * (t1 - r0)], w_refs[2 * (u0 - c0):2 * (u1 - c0)],
-            uppers, outs[5 * i:5 * i + 5])
+            lead, v_refs[sum(counts[r0:t0]):sum(counts[r0:t1])],
+            w_refs[sum(counts[c0:u0]):sum(counts[c0:u1])], uppers, outs[5 * i:5 * i + 5])
     if not finish:
         outs[-1][...] = partner_ref[...]
         return
@@ -305,7 +306,7 @@
 
 def subtiles(groups):
     (_, low), (_, middle), _ = segments_of(groups)
-    return [(0, low, 0, low), (0, low, low, middle), (low, middle, 0, middle),
+    return [(0, low, 0, low), (low, middle, 0, low), (0, middle, low, middle),
             (middle, groups, 0, middle), (0, groups, middle, groups)]
 
 
@@ -314,34 +315,10 @@
     return min(first), max(second), min(third), max(fourth)
 
 
-def band_kernel(groups, uppers, widths, own_rows, masks, follows, *refs):
-    me_ref = refs[0]
-    stat_refs = refs[1:1 + groups]
-    at = 1 + groups
-    shapes = subtiles(groups)
-    tiles = len(shapes)
-    power_refs, col_refs, row_refs = [refs[at + i * tiles:at + (i + 1) * tiles] for i in range(3)]
-    at += 3 * tiles
-    w_refs = refs[at:at + 2 * groups]
-    at += 2 * groups
-    before_ref = None
-    if follows:
-        before_ref, at = refs[at], at + 1
-    out_refs = refs[at:at + groups]
-    at += groups
-    after_ref = None
-    if not follows:
-        after_ref, at = refs[at], at + 1
-    w_ref, = refs[at:]
-    base = 0 if widths[-1] == 0 else uppers[widths[-1] - 1]
-    top = uppers[widths[0]]
-    for i, ref in enumerate(w_refs):
-        w_ref[i * own_rows:(i + 1) * own_rows, :] = ref[:, base:top]
-
-    total = w_ref.shape[0]
+def band_setup(groups, uppers, own_rows, masks, me_ref, stat_refs):
+    count = len(uppers)
+    total = stat_refs[0].shape[1]
     chip_rows = total // groups
-    count = len(uppers)
-    scales = [logit_gain * m ** -0.5 for m in uppers]
     me = me_ref[0]
     lead = (me & 1) == 0
     parts, partners = [], []
@@ -355,7 +332,7 @@
     sub = lax.broadcasted_iota(jnp.int32, (STATS, total), 0)
     totals = peak + jnp.log(mass) * LOG2E
     for k in range(count):
-        totals = jnp.where(sub == k, totals - math.log2(scales[k]), totals)
+        totals = jnp.where(sub == k, totals - math.log2(logit_gain * uppers[k] ** -0.5), totals)
     packed = jnp.concatenate(
         [totals[:count], partner_row, jnp.zeros((LANES - count - 1, total), jnp.float32)], axis=0)
     cols = packed.T
@@ -364,57 +341,102 @@
     id_col = jnp.where(
         lead, cols[:, count:count + 1],
         document_ids((total, 1), 0, me | 1, own_rows, masks))
-
+    return lead, totals, cols, id_row, id_col
+
+
+def weights_of(segment, groups, setup, power_refs, col_refs, row_refs):
+    lead, totals, cols, _, _ = setup
+    chip_rows = totals.shape[1] // groups
+    s0, s1 = segment
+    strip = []
+    for (r0, r1, c0, c1), power, col_peak, row_peak in zip(
+            subtiles(groups), power_refs, col_refs, row_refs):
+        if r0 <= s0 and s1 <= r1:
+            inner = slice((s0 - r0) * chip_rows, (s1 - r0) * chip_rows)
+            outer = slice(s0 * chip_rows, s1 * chip_rows)
+            across = slice(c0 * chip_rows, c1 * chip_rows)
+            strip.append((
+                c0, power, inner,
+                jnp.where(lead, jnp.exp2(col_peak[inner, :] - cols[outer]), 1.0),
+                jnp.where(lead, 1.0, jnp.exp2(row_peak[...] - totals[:, across]))))
+    strip.sort(key=lambda item: item[0])
+    return lambda k: jnp.concatenate([
+        power[k, inner] * col_gain[:, k:k + 1] * row_gain[k:k + 1, :]
+        for _, power, inner, col_gain, row_gain in strip], axis=1)
+
+
+def last_band_kernel(groups, uppers, own_rows, masks, *refs):
+    tiles = len(subtiles(groups))
+    setup = band_setup(groups, uppers, own_rows, masks, refs[0], refs[1:1 + groups])
+    at = 1 + groups
+    power_refs, col_refs, row_refs = [refs[at + i * tiles:at + (i + 1) * tiles] for i in range(3)]
+    segment = segments_of(groups)[-1]
+    farthest = segment[1] - segment[0]
+    w_refs, out_refs, after_ref = refs[at + 3 * tiles:-farthest - 1], refs[-farthest - 1:-1], refs[-1]
+    _, totals, _, id_row, id_col = setup
+    chip_rows = totals.shape[1] // groups
+    k = len(uppers) - 1
+    rows = slice(segment[0] * chip_rows, segment[1] * chip_rows)
+    weight = weights_of(segment, groups, setup, power_refs, col_refs, row_refs)(k)
+    weight = weight - jnp.where(id_col[rows] == id_row, logit_gain * uppers[k] ** -0.5, 0.0)
+    after_ref[...] = weight
+    product = jnp.dot(
+        weight.astype(jnp.bfloat16), rows_of(w_refs, uppers[k - 1], uppers[k]),
+        preferred_element_type=jnp.float32)
+    store(out_refs, product, 0, 0, uppers[k] - uppers[k - 1], chip_rows)
+
+
+def bands_kernel(groups, uppers, own_rows, masks, *refs):
+    tiles = len(subtiles(groups))
+    setup = band_setup(groups, uppers, own_rows, masks, refs[0], refs[1:1 + groups])
+    at = 1 + groups
+    power_refs, col_refs, row_refs = [refs[at + i * tiles:at + (i + 1) * tiles] for i in range(3)]
     segments = segments_of(groups)
-    narrow = [k for k in widths if uppers[k] <= LANES]
+    outs = groups + segments[-1][0]
+    before_ref = refs[-outs - 1]
+    w_refs, others, widest = refs[at + 3 * tiles:-outs - 1], refs[-outs:-outs + groups], refs[-outs + groups:]
+    _, totals, _, id_row, id_col = setup
+    chip_rows = totals.shape[1] // groups
+    scales = [logit_gain * m ** -0.5 for m in uppers]
+    last = len(uppers) - 1
+    narrow = [k for k in range(last, -1, -1) if uppers[k] <= LANES]
     for block in (segments[1:], segments[:1]):
         first = block[0][0] * chip_rows
         rows = slice(first, block[-1][1] * chip_rows)
         height = rows.stop - first
         hit = id_col[rows] == id_row
-        strips = []
-        for s0, s1 in block:
-            strip = []
-            for (r0, r1, c0, c1), power, col_peak, row_peak in zip(
-                    shapes, power_refs, col_refs, row_refs):
-                if r0 <= s0 and s1 <= r1:
-                    inner = slice((s0 - r0) * chip_rows, (s1 - r0) * chip_rows)
-                    outer = slice(s0 * chip_rows, s1 * chip_rows)
-                    across = slice(c0 * chip_rows, c1 * chip_rows)
-                    strip.append((
-                        c0, power, inner,
-                        jnp.where(lead, jnp.exp2(col_peak[inner, :] - cols[outer]), 1.0),
-                        jnp.where(lead, 1.0, jnp.exp2(row_peak[...] - totals[:, across]))))
-            strips.append(sorted(strip, key=lambda item: item[0]))
-        running = before_ref[rows, :] if follows else None
+        weights = [
+            weights_of(segment, groups, setup, power_refs, col_refs, row_refs) for segment in block]
+        tall = (block[0][1] - block[0][0]) * chip_rows
+        running = weights[0](last) - jnp.where(hit[:tall], scales[last], 0.0)
+        lower, upper = uppers[last - 1], uppers[last]
+        product = jnp.dot(
+            running.astype(jnp.bfloat16), rows_of(w_refs, lower, upper),
+            preferred_element_type=jnp.float32)
+        store(widest, product, first, 0, upper - lower, chip_rows)
+        if len(block) > 1:
+            running = jnp.concatenate([running, before_ref[...]], axis=0)
         stack = []
-        for k in widths:
-            weight = jnp.concatenate([
-                jnp.concatenate([
-                    power[k, inner] * col_gain[:, k:k + 1] * row_gain[k:k + 1, :]
-                    for _, power, inner, col_gain, row_gain in strip], axis=1)
-                for strip in strips], axis=0)
-            weight = weight - jnp.where(hit, scales[k], 0.0)
-            running = weight if running is None else running + weight
+        for k in range(last - 1, -1, -1):
+            weight = jnp.concatenate([part(k) for part in weights], axis=0)
+            running = running + (weight - jnp.where(hit, scales[k], 0.0))
             band = running.astype(jnp.bfloat16)
-            if k not in narrow:
-                lower, upper = uppers[k - 1] - base, uppers[k] - base
-                product = jnp.dot(band, w_ref[:, lower:upper], preferred_element_type=jnp.float32)
-                store(out_refs, product, first, lower, upper, chip_rows)
-            else:
+            if k in narrow:
                 stack.append(band)
-        if not follows:
-            after_ref[rows, :] = running
-        if narrow:
+                continue
+            lower, upper = uppers[k - 1], uppers[k]
             product = jnp.dot(
-                jnp.concatenate(stack, axis=0), w_ref[:, :LANES],
-                preferred_element_type=jnp.float32)
-            lane = lax.broadcasted_iota(jnp.int32, (height, LANES), 1)
-            chosen = product[:height]
-            for i in range(1, len(stack)):
-                chosen = jnp.where(
-                    lane < uppers[narrow[i]], product[i * height:(i + 1) * height], chosen)
-            store(out_refs, chosen, first, 0, LANES, chip_rows)
+                band, rows_of(w_refs, lower, upper), preferred_element_type=jnp.float32)
+            store(others, product, first, lower, upper, chip_rows)
+        product = jnp.dot(
+            jnp.concatenate(stack, axis=0), rows_of(w_refs, 0, LANES),
+            preferred_element_type=jnp.float32)
+        lane = lax.broadcasted_iota(jnp.int32, (height, LANES), 1)
+        chosen = product[:height]
+        for i in range(1, len(stack)):
+            chosen = jnp.where(
+                lane < uppers[narrow[i]], product[i * height:(i + 1) * height], chosen)
+        store(others, chosen, first, 0, LANES, chip_rows)
 
 
 def store(out_refs, value, first_row, lower, upper, chip_rows):
@@ -453,17 +475,23 @@
 
     mine = jnp.where(lead, queries, documents)
     other = jnp.where(lead, documents, queries)
-    v = {(0, 0): mine, (0, 1): swap(other)}
-    w = {(0, 0): swap(mine), (0, 1): other}
+    got = swap(other)
+    small = WIDTHS * total * total * 4 <= 16 << 20
+    cut = own_rows - 16 if small and own_rows >= 32 else own_rows
+    v = {0: [mine, got]}
+    w = {0: [swap(mine), other]}
     for stage in reversed(range(stages)):
-        for j in [j for j in range(groups) if (j, 0) in v]:
-            for t in range(2):
-                v[j | 1 << stage, t] = along(v[j, t], stage)
-    for j, t in sorted(v):
-        if j:
-            w[j, t] = swap(v[j, t])
-    order = [(j, t) for j in range(groups) for t in range(2)]
-    v_list, w_list = [v[key] for key in order], [w[key] for key in order]
+        for j in sorted(v):
+            parts = v[j]
+            if j == 0 and stage == stages - 1 and cut < own_rows:
+                parts = [mine, got[:cut], got[cut:]]
+            v[j | 1 << stage] = [
+                along(part, stage) for part in parts]
+    for j in range(1, groups):
+        w[j] = [swap(part) for part in v[j]]
+    counts = [len(v[j]) for j in range(groups)]
+    v_list = [part for j in range(groups) for part in v[j]]
+    w_list = [part for j in range(groups) for part in w[j]]
 
     own_partner = partner.astype(jnp.float32).reshape(1, own_rows)
     far_partner = swap(own_partner)
@@ -488,7 +516,7 @@
             jax.ShapeDtypeStruct((chip_rows, columns), jnp.bfloat16 if j & 1 else jnp.float32)
             for j in range(groups)]
 
-    if WIDTHS * total * total * 4 > 16 << 20:
+    if not small:
         limit = 60 << 20
         stats = pl.pallas_call(
             functools.partial(stats_kernel, pieces, uppers),
@@ -525,7 +553,8 @@
 
         def tile(span, partner_row, earlier=()):
             first, end, left, right = extent([shapes[i] for i in span])
-            operands = v_list[2 * first:2 * end] + w_list[2 * left:2 * right]
+            operands = v_list[sum(counts[:first]):sum(counts[:end])]
+            operands += w_list[sum(counts[:left]):sum(counts[:right])]
             stat_shapes = [shape(STATS, total)] if earlier else [shape(1, chip_rows)]
             result, area = [], 0
             for i in span:
@@ -536,7 +565,7 @@
                            shape(STATS, wide), shape(STATS, wide)]
             *arrays, last_array = pl.pallas_call(
                 functools.partial(
-                    tile_kernel, span, groups, uppers, own_rows, len(earlier)),
+                    tile_kernel, span, counts, uppers, own_rows, len(earlier)),
                 out_shape=result + stat_shapes,
                 in_specs=[smem] + [vmem] * (1 + len(operands) + 4 * len(earlier)),
                 out_specs=[vmem] * (len(result) + 1),
@@ -548,35 +577,34 @@
             return [arrays[5 * i:5 * i + 5] for i in range(len(span))], last_array
 
         done, chip_partner = tile([0], chip_partner)
-        more, chip_partner = tile([1, 2], chip_partner)
-        done += more
-        more, chip_partner = tile([3], chip_partner)
-        done += more
+        for at in (1, 2, 3):
+            more, chip_partner = tile([at], chip_partner)
+            done += more
         more, stats = tile([4], chip_partner, done)
         done += more
         common = [me, *gathered(stats), *[t[0] for t in done], *[t[1] for t in done],
                   *[t[3] for t in done], *w_list]
-        last = WIDTHS - 1
-
-        def bands(widths, more, follows):
-            base = 0 if widths[-1] == 0 else uppers[widths[-1] - 1]
-            columns = uppers[widths[0]] - base
+        near = segments_of(groups)[-1][0]
+        widest = feature_dim - uppers[-2]
+
+        def bands(kernel, more, outs):
             return pl.pallas_call(
-                functools.partial(
-                    band_kernel, groups, uppers, widths, own_rows, document_masks, follows),
-                out_shape=gradient_shapes(columns) + ([] if follows else [shape(total, total)]),
+                functools.partial(kernel, groups, uppers, own_rows, document_masks),
+                out_shape=outs,
                 in_specs=[smem] + [vmem] * (len(common) - 1 + len(more)),
-                out_specs=[vmem] * (groups + (not follows)),
-                scratch_shapes=[pltpu.VMEM((total, columns), jnp.bfloat16)],
+                out_specs=[vmem] * len(outs),
                 compiler_params=params,
                 cost_estimate=pl.CostEstimate(
                     flops=2 * total * total * feature_dim, transcendentals=0,
                     bytes_accessed=4 * total * feature_dim),
             )(*common, *more)
 
-        *widest, running = bands([last], [], False)
-        others = bands(list(reversed(range(last))), [running], True)
-        chunks = [widest, others]
+        *far_ones, running = bands(
+            last_band_kernel, [],
+            gradient_shapes(widest)[near:] + [shape((groups - near) * chip_rows, total)])
+        rest = bands(
+            bands_kernel, [running], gradient_shapes(uppers[-2]) + gradient_shapes(widest)[:near])
+        chunks = [[*rest[groups:], *far_ones], rest[:groups]]
 
     mine_parts, other_parts = [], []
     for c, chunk in enumerate(chunks):

time: 70 us -> 74.6 us (1.066)
  the two profiles are of different devices: /device:TPU:1 before, /device:TPU:0 now
where the time goes in v2:
time: 74.6 us; the launch traced here: 73.8 us
  waiting for transfers between devices  31 us (42%)
  starting transfers between devices  27.2 us (36%)
  Pallas kernels  11.4 us (15%)
  other arithmetic  3.22 us (4%)
  between operations  0.87 us (1%)
    ppermute x31, waiting for transfers between devices, exchange(): return lax.ppermute(x, AXES, [(i, i ^ masks_of(i)) for i in range(devices)])  31 us
    ppermute x31, starting transfers between devices, exchange(): return lax.ppermute(x, AXES, [(i, i ^ masks_of(i)) for i in range(devices)])  27.2 us
    pallas_call x5, Pallas kernels, tile(): pl.pallas_call(functools.partial(tile_kernel, span, counts, uppers, own_r...  6.92 us
    pallas_call x2, Pallas kernels, bands(): pl.pallas_call(functools.partial(kernel, groups, uppers, own_rows, docume...  4.45 us
  transfers between devices with their start and end apart: 31, of which 11 were waited for; matrix products, arithmetic and copies ran while one was open for 2% of the time, Pallas kernels for 6%

profile of v2, /device:TPU:0, one launch (start us, length us, event | category | flops | bytes accessed | tf_op | source)
XLA Modules:
  0.0 73.8 jit_solution(3333132153071925805)
XLA Ops:
  2.3 2.6 %collective-permute-start.7 = (bf16[64,2048]{1,0:T(8,128)(2,1)S(1)}, bf16[64,2048]{1,0:T(8,128)(2,1)S(1)}, u32[]{:S(2)}, u32[]{:S(2)}) collective-permute-start(bf16[64,2048]{1,0:T(8,128)(2,1)S(1)} %get-tuple-element.87.refs_2_), channel_id=1, source_target_pairs={{0,8},{1,17},{2,10},{3,19},{4,12},{5,21},{6,14},{7,23},{8,0},{9,25... | collective-permute-start | bytes 786440 | tf_op jit(solution)/shard_map/ppermute | solution.py:468
  4.9 1.5 %collective-permute-start.2 = (bf16[64,2048]{1,0:T(8,128)(2,1)S(1)}, bf16[64,2048]{1,0:T(8,128)(2,1)S(1)}, u32[]{:S(2)}, u32[]{:S(2)}) collective-permute-start(bf16[64,2048]{1,0:T(8,128)(2,1)S(1)} %get-tuple-element.87.refs_2_), channel_id=1, source_target_pairs={{0,2},{1,5},{2,0},{3,7},{4,6},{5,1},{6,4},{7,3},{8,10},{9,13},{10,... | collective-permute-start | bytes 786440 | tf_op jit(solution)/shard_map/ppermute | solution.py:468
  7.3 1.5 %collective-permute-start.3 = (bf16[64,2048]{1,0:T(8,128)(2,1)S(1)}, bf16[64,2048]{1,0:T(8,128)(2,1)S(1)}, u32[]{:S(2)}, u32[]{:S(2)}) collective-permute-start(bf16[64,2048]{1,0:T(8,128)(2,1)S(1)} %collective-permute-done.1.refs_3_), channel_id=1, source_target_pairs={{0,2},{1,5},{2,0},{3,7},{4,6},{5,1},{6,4},{7,3},{8,10},{9,13},{10,... | collective-permute-start | bytes 786440 | tf_op jit(solution)/shard_map/ppermute | solution.py:468
  9.5 1.1 %collective-permute-done = f32[1,64]{1,0:T(1,128)S(1)} collective-permute-done((f32[1,64]{1,0:T(1,128)S(1)}, f32[1,64]{1,0:T(1,128)S(1)}, u32[]{:S(2)}, u32[]{:S(2)}) %collective-permute-start) | collective-permute-done | bytes 288 | tf_op jit(solution)/shard_map/ppermute | solution.py:468
  10.6 1.6 %collective-permute-start.8 = (bf16[48,2048]{1,0:T(8,128)(2,1)S(1)}, bf16[48,2048]{1,0:T(8,128)(2,1)S(1)}, u32[]{:S(2)}, u32[]{:S(2)}) collective-permute-start(bf16[48,2048]{1,0:T(8,128)(2,1)S(1)} %slice.32), channel_id=1, source_target_pairs={{0,8},{1,17},{2,10},{3,19},{4,12},{5,21},{6,14},{7,23},{8,0},{9,25... | collective-permute-start | bytes 589832 | tf_op jit(solution)/shard_map/ppermute | solution.py:468
  12.2 1.7 %collective-permute-start.13 = (bf16[64,2048]{1,0:T(8,128)(2,1)S(1)}, bf16[64,2048]{1,0:T(8,128)(2,1)S(1)}, u32[]{:S(2)}, u32[]{:S(2)}) collective-permute-start(bf16[64,2048]{1,0:T(8,128)(2,1)S(1)} %collective-permute-done.7.refs_2_.refs_6_), channel_id=1, source_target_pairs={{0,2},{1,5},{2,0},{3,7},{4,6},{5,1},{6,4},{7,3},{8,10},{9,13},{10,... | collective-permute-start | bytes 786440 | tf_op jit(solution)/shard_map/ppermute | solution.py:468
  13.9 2.0 %collective-permute-start.9 = (bf16[16,2048]{1,0:T(8,128)(2,1)S(1)}, bf16[16,2048]{1,0:T(8,128)(2,1)S(1)}, u32[]{:S(2)}, u32[]{:S(2)}) collective-permute-start(bf16[16,2048]{1,0:T(8,128)(2,1)S(1)} %slice.33), channel_id=1, source_target_pairs={{0,8},{1,17},{2,10},{3,19},{4,12},{5,21},{6,14},{7,23},{8,0},{9,25... | collective-permute-start | bytes 196616 | tf_op jit(solution)/shard_map/ppermute | solution.py:468
  16.3 3.6 %collective-permute-done.9.refs_4_.refs_8_ = bf16[16,2048]{1,0:T(8,128)(2,1)S(1)} collective-permute-done((bf16[16,2048]{1,0:T(8,128)(2,1)S(1)}, bf16[16,2048]{1,0:T(8,128)(2,1)S(1)}, u32[]{:S(2)}, u32[]{:S(2)}) %collective-permute-start.9) | collective-permute-done | bytes 65568 | tf_op jit(solution)/shard_map/ppermute | solution.py:468
  20.3 1.5 %collective-permute-start.14 = (bf16[48,2048]{1,0:T(8,128)(2,1)S(1)}, bf16[48,2048]{1,0:T(8,128)(2,1)S(1)}, u32[]{:S(2)}, u32[]{:S(2)}) collective-permute-start(bf16[48,2048]{1,0:T(8,128)(2,1)S(1)} %collective-permute-done.8.refs_3_.refs_7_), channel_id=1, source_target_pairs={{0,2},{1,5},{2,0},{3,7},{4,6},{5,1},{6,4},{7,3},{8,10},{9,13},{10,... | collective-permute-start | bytes 589832 | tf_op jit(solution)/shard_map/ppermute | solution.py:468
  21.8 2.2 %collective-permute-done.15.refs_4_.refs_11_ = bf16[16,2048]{1,0:T(8,128)(2,1)S(1)} collective-permute-done((bf16[16,2048]{1,0:T(8,128)(2,1)S(1)}, bf16[16,2048]{1,0:T(8,128)(2,1)S(1)}, u32[]{:S(2)}, u32[]{:S(2)}) %collective-permute-start.15) | collective-permute-done | bytes 65568 | tf_op jit(solution)/shard_map/ppermute | solution.py:468
  24.7 1.4 %collective-permute-done.14.refs_3_.refs_10_ = bf16[48,2048]{1,0:T(8,128)(2,1)S(1)} collective-permute-done((bf16[48,2048]{1,0:T(8,128)(2,1)S(1)}, bf16[48,2048]{1,0:T(8,128)(2,1)S(1)}, u32[]{:S(2)}, u32[]{:S(2)}) %collective-permute-start.14) | collective-permute-done | bytes 196640 | tf_op jit(solution)/shard_map/ppermute | solution.py:468
  28.6 1.4 %shard_map.52 = (f32[9,384,128]{2,1,0:T(8,128)S(1)}, f32[384,128]{1,0:T(8,128)S(1)}, f32[384,128]{1,0:T(8,128)S(1)}, f32[16,128]{1,0:T(8,128)S(1)}, f32[16,128]{1,0:T(8,128)S(1)}, /*index=5*/f32[1,128]{1,0:T(1,128)S(1)}) custom-call(s32[1]{0:T(128)} %bitcast.refs_0_, f32[1,128]{1,0:T(1,128)S(1)} %get-tuple-element.42.refs_1_, ...), custom_call_target="tpu_custom_call" | custom-call | flops 603979776 | bytes 2097152 | tf_op jit(solution)/shard_map/pallas_call | solution.py:566
  31.0 2.7 %shard_map.54 = (f32[9,512,128]{2,1,0:T(8,128)S(1)}, f32[512,128]{1,0:T(8,128)S(1)}, f32[512,128]{1,0:T(8,128)}, f32[16,128]{1,0:T(8,128)S(1)}, f32[16,128]{1,0:T(8,128)}, /*index=5*/f32[16,512]{1,0:T(8,128)S(1)}) custom-call(s32[1]{0:T(128)} %bitcast.refs_0_, f32[1,128]{1,0:T(1,128)S(1)} %get-tuple-element.44.refs_1_, ...), custom_call_target="tpu_custom_call" | custom-call | flops 805306368 | bytes 2097152 | tf_op jit(solution)/shard_map/pallas_call | solution.py:566
  33.8 1.7 %collective-permute-start.21 = (f32[16,512]{1,0:T(8,128)S(1)}, f32[16,512]{1,0:T(8,128)S(1)}, u32[]{:S(2)}, u32[]{:S(2)}) collective-permute-start(f32[16,512]{1,0:T(8,128)S(1)} %get-tuple-element.61.refs_1_), channel_id=1, source_target_pairs={{0,10},{1,11},{2,8},{3,9},{4,14},{5,15},{6,12},{7,13},{8,2},{9,3},... | collective-permute-start | bytes 98312 | tf_op jit(solution)/shard_map/ppermute | solution.py:468
  37.3 1.4 %collective-permute-done.21.refs_4_ = f32[16,512]{1,0:T(8,128)S(1)} collective-permute-done((f32[16,512]{1,0:T(8,128)S(1)}, f32[16,512]{1,0:T(8,128)S(1)}, u32[]{:S(2)}, u32[]{:S(2)}) %collective-permute-start.21) | collective-permute-done | bytes 32800 | tf_op jit(solution)/shard_map/ppermute | solution.py:468
  41.0 4.0 %shard_map.56 = (f32[128,1024]{1,0:T(8,128)S(1)}, bf16[128,1024]{1,0:T(8,128)(2,1)S(1)}, f32[128,1024]{1,0:T(8,128)S(1)}, bf16[128,1024]{1,0:T(8,128)(2,1)S(1)},...) custom-call(s32[1]{0:T(128)} %bitcast.refs_0_, ...), custom_call_target="tpu_custom_call" | custom-call | flops 1073741824 | bytes 4194304 | tf_op jit(solution)/shard_map/pallas_call | solution.py:591
  45.7 1.3 %collective-permute-start.23 = (bf16[128,1024]{1,0:T(8,128)(2,1)S(1)}, bf16[128,1024]{1,0:T(8,128)(2,1)S(1)}, u32[]{:S(2)}, u32[]{:S(2)}) collective-permute-start(bf16[128,1024]{1,0:T(8,128)(2,1)S(1)} %get-tuple-element.74), channel_id=1, source_target_pairs={{0,2},{1,5},{2,0},{3,7},{4,6},{5,1},{6,4},{7,3},{8,10},{9,13},{10,... | collective-permute-start | bytes 786440 | tf_op jit(solution)/shard_map/ppermute | solution.py:468
  47.7 1.3 %collective-permute-start.26 = (bf16[128,1024]{1,0:T(8,128)(2,1)S(1)}, bf16[128,1024]{1,0:T(8,128)(2,1)S(1)}, u32[]{:S(2)}, u32[]{:S(2)}) collective-permute-start(bf16[128,1024]{1,0:T(8,128)(2,1)S(1)} %get-tuple-element.78), channel_id=1, source_target_pairs={{0,2},{1,5},{2,0},{3,7},{4,6},{5,1},{6,4},{7,3},{8,10},{9,13},{10,... | collective-permute-start | bytes 786440 | tf_op jit(solution)/shard_map/ppermute | solution.py:468
  49.1 2.3 %collective-permute-done.22 = bf16[128,1024]{1,0:T(8,128)(2,1)S(1)} collective-permute-done((bf16[128,1024]{1,0:T(8,128)(2,1)S(1)}, bf16[128,1024]{1,0:T(8,128)(2,1)S(1)}, u32[]{:S(2)}, u32[]{:S(2)}) %collective-permute-start.22) | collective-permute-done | bytes 262176 | tf_op jit(solution)/shard_map/ppermute | solution.py:468
  51.6 8.2 %collective-permute-done.26 = bf16[128,1024]{1,0:T(8,128)(2,1)S(1)} collective-permute-done((bf16[128,1024]{1,0:T(8,128)(2,1)S(1)}, bf16[128,1024]{1,0:T(8,128)(2,1)S(1)}, u32[]{:S(2)}, u32[]{:S(2)}) %collective-permute-start.26) | collective-permute-done | bytes 262176 | tf_op jit(solution)/shard_map/ppermute | solution.py:468
  61.0 1.1 %collective-permute-start.24 = (bf16[64,1024]{1,0:T(8,128)(2,1)S(1)}, bf16[64,1024]{1,0:T(8,128)(2,1)S(1)}, u32[]{:S(2)}, u32[]{:S(2)}) collective-permute-start(bf16[64,1024]{1,0:T(8,128)(2,1)S(1)} %get-tuple-element.88), channel_id=1, source_target_pairs={{0,8},{1,17},{2,10},{3,19},{4,12},{5,21},{6,14},{7,23},{8,0},{9,25... | collective-permute-start | bytes 393224 | tf_op jit(solution)/shard_map/ppermute | solution.py:468
  62.2 5.5 %collective-permute-done.27 = bf16[128,1024]{1,0:T(8,128)(2,1)S(1)} collective-permute-done((bf16[128,1024]{1,0:T(8,128)(2,1)S(1)}, bf16[128,1024]{1,0:T(8,128)(2,1)S(1)}, u32[]{:S(2)}, u32[]{:S(2)}) %collective-permute-start.27) | collective-permute-done | bytes 262176 | tf_op jit(solution)/shard_map/ppermute | solution.py:468
  67.8 1.5 %collective-permute-start.30 = (f32[64,1024]{1,0:T(8,128)S(1)}, f32[64,1024]{1,0:T(8,128)S(1)}, u32[]{:S(2)}, u32[]{:S(2)}) collective-permute-start(f32[64,1024]{1,0:T(8,128)S(1)} %get-tuple-element.83), channel_id=1, source_target_pairs={{0,1},{1,0},{2,3},{3,2},{4,5},{5,4},{6,7},{7,6},{8,9},{9,8},{10,11... | collective-permute-start | bytes 786440 | tf_op jit(solution)/shard_map/ppermute | solution.py:468
  69.3 3.4 %collective-permute-done.24 = bf16[64,1024]{1,0:T(8,128)(2,1)S(1)} collective-permute-done((bf16[64,1024]{1,0:T(8,128)(2,1)S(1)}, bf16[64,1024]{1,0:T(8,128)(2,1)S(1)}, u32[]{:S(2)}, u32[]{:S(2)}) %collective-permute-start.24) | collective-permute-done | bytes 131104 | tf_op jit(solution)/shard_map/ppermute | solution.py:468
  (60 shorter events, 16.2 us)
Async XLA Ops:
  1.7 5.6 %collective-permute-start.1 = (bf16[64,2048]{1,0:T(8,128)(2,1)S(1)}, bf16[64,2048]{1,0:T(8,128)(2,1)S(1)}, u32[]{:S(2)}, u32[]{:S(2)}) collective-permute-start(bf16[64,2048]{1,0:T(8,128)(2,1)S(1)} %get-tuple-element.86.refs_7_.refs_6_.refs_21_), channel_id=1, source_target_pairs={{0,1},{1,0},{2,3},{3,2},{4,5},{5,4},{6,7},{7,6},{8,9},{9,8},{10,11... | collective-permute-start | bytes 786440 | tf_op jit(solution)/shard_map/ppermute | solution.py:468
  2.3 9.9 %collective-permute-start.7 = (bf16[64,2048]{1,0:T(8,128)(2,1)S(1)}, bf16[64,2048]{1,0:T(8,128)(2,1)S(1)}, u32[]{:S(2)}, u32[]{:S(2)}) collective-permute-start(bf16[64,2048]{1,0:T(8,128)(2,1)S(1)} %get-tuple-element.87.refs_2_), channel_id=1, source_target_pairs={{0,8},{1,17},{2,10},{3,19},{4,12},{5,21},{6,14},{7,23},{8,0},{9,25... | collective-permute-start | bytes 786440 | tf_op jit(solution)/shard_map/ppermute | solution.py:468
  4.9 9.0 %collective-permute-start.2 = (bf16[64,2048]{1,0:T(8,128)(2,1)S(1)}, bf16[64,2048]{1,0:T(8,128)(2,1)S(1)}, u32[]{:S(2)}, u32[]{:S(2)}) collective-permute-start(bf16[64,2048]{1,0:T(8,128)(2,1)S(1)} %get-tuple-element.87.refs_2_), channel_id=1, source_target_pairs={{0,2},{1,5},{2,0},{3,7},{4,6},{5,1},{6,4},{7,3},{8,10},{9,13},{10,... | collective-permute-start | bytes 786440 | tf_op jit(solution)/shard_map/ppermute | solution.py:468
  6.4 7.5 %collective-permute-start.4 = (bf16[64,2048]{1,0:T(8,128)(2,1)S(1)}, bf16[64,2048]{1,0:T(8,128)(2,1)S(1)}, u32[]{:S(2)}, u32[]{:S(2)}) collective-permute-start(bf16[64,2048]{1,0:T(8,128)(2,1)S(1)} %get-tuple-element.87.refs_2_), channel_id=1, source_target_pairs={{0,1},{1,0},{2,3},{3,2},{4,5},{5,4},{6,7},{7,6},{8,9},{9,8},{10,11... | collective-permute-start | bytes 786440 | tf_op jit(solution)/shard_map/ppermute | solution.py:468
  7.3 8.7 %collective-permute-start.3 = (bf16[64,2048]{1,0:T(8,128)(2,1)S(1)}, bf16[64,2048]{1,0:T(8,128)(2,1)S(1)}, u32[]{:S(2)}, u32[]{:S(2)}) collective-permute-start(bf16[64,2048]{1,0:T(8,128)(2,1)S(1)} %collective-permute-done.1.refs_3_), channel_id=1, source_target_pairs={{0,2},{1,5},{2,0},{3,7},{4,6},{5,1},{6,4},{7,3},{8,10},{9,13},{10,... | collective-permute-start | bytes 786440 | tf_op jit(solution)/shard_map/ppermute | solution.py:468
  10.6 9.7 %collective-permute-start.8 = (bf16[48,2048]{1,0:T(8,128)(2,1)S(1)}, bf16[48,2048]{1,0:T(8,128)(2,1)S(1)}, u32[]{:S(2)}, u32[]{:S(2)}) collective-permute-start(bf16[48,2048]{1,0:T(8,128)(2,1)S(1)} %slice.32), channel_id=1, source_target_pairs={{0,8},{1,17},{2,10},{3,19},{4,12},{5,21},{6,14},{7,23},{8,0},{9,25... | collective-permute-start | bytes 589832 | tf_op jit(solution)/shard_map/ppermute | solution.py:468
  12.2 11.9 %collective-permute-start.13 = (bf16[64,2048]{1,0:T(8,128)(2,1)S(1)}, bf16[64,2048]{1,0:T(8,128)(2,1)S(1)}, u32[]{:S(2)}, u32[]{:S(2)}) collective-permute-start(bf16[64,2048]{1,0:T(8,128)(2,1)S(1)} %collective-permute-done.7.refs_2_.refs_6_), channel_id=1, source_target_pairs={{0,2},{1,5},{2,0},{3,7},{4,6},{5,1},{6,4},{7,3},{8,10},{9,13},{10,... | collective-permute-start | bytes 786440 | tf_op jit(solution)/shard_map/ppermute | solution.py:468
  13.9 10.7 %collective-permute-start.5 = (bf16[64,2048]{1,0:T(8,128)(2,1)S(1)}, bf16[64,2048]{1,0:T(8,128)(2,1)S(1)}, u32[]{:S(2)}, u32[]{:S(2)}) collective-permute-start(bf16[64,2048]{1,0:T(8,128)(2,1)S(1)} %collective-permute-done.2.refs_4_), channel_id=1, source_target_pairs={{0,1},{1,0},{2,3},{3,2},{4,5},{5,4},{6,7},{7,6},{8,9},{9,8},{10,11... | collective-permute-start | bytes 786440 | tf_op jit(solution)/shard_map/ppermute | solution.py:468
  13.9 5.9 %collective-permute-start.9 = (bf16[16,2048]{1,0:T(8,128)(2,1)S(1)}, bf16[16,2048]{1,0:T(8,128)(2,1)S(1)}, u32[]{:S(2)}, u32[]{:S(2)}) collective-permute-start(bf16[16,2048]{1,0:T(8,128)(2,1)S(1)} %slice.33), channel_id=1, source_target_pairs={{0,8},{1,17},{2,10},{3,19},{4,12},{5,21},{6,14},{7,23},{8,0},{9,25... | collective-permute-start | bytes 196616 | tf_op jit(solution)/shard_map/ppermute | solution.py:468
  16.0 10.2 %collective-permute-start.6 = (bf16[64,2048]{1,0:T(8,128)(2,1)S(1)}, bf16[64,2048]{1,0:T(8,128)(2,1)S(1)}, u32[]{:S(2)}, u32[]{:S(2)}) collective-permute-start(bf16[64,2048]{1,0:T(8,128)(2,1)S(1)} %collective-permute-done.3.refs_5_), channel_id=1, source_target_pairs={{0,1},{1,0},{2,3},{3,2},{4,5},{5,4},{6,7},{7,6},{8,9},{9,8},{10,11... | collective-permute-start | bytes 786440 | tf_op jit(solution)/shard_map/ppermute | solution.py:468
  20.3 5.8 %collective-permute-start.14 = (bf16[48,2048]{1,0:T(8,128)(2,1)S(1)}, bf16[48,2048]{1,0:T(8,128)(2,1)S(1)}, u32[]{:S(2)}, u32[]{:S(2)}) collective-permute-start(bf16[48,2048]{1,0:T(8,128)(2,1)S(1)} %collective-permute-done.8.refs_3_.refs_7_), channel_id=1, source_target_pairs={{0,2},{1,5},{2,0},{3,7},{4,6},{5,1},{6,4},{7,3},{8,10},{9,13},{10,... | collective-permute-start | bytes 589832 | tf_op jit(solution)/shard_map/ppermute | solution.py:468
  24.1 4.5 %collective-permute-start.11 = (bf16[48,2048]{1,0:T(8,128)(2,1)S(1)}, bf16[48,2048]{1,0:T(8,128)(2,1)S(1)}, u32[]{:S(2)}, u32[]{:S(2)}) collective-permute-start(bf16[48,2048]{1,0:T(8,128)(2,1)S(1)} %collective-permute-done.8.refs_3_.refs_7_), channel_id=1, source_target_pairs={{0,1},{1,0},{2,3},{3,2},{4,5},{5,4},{6,7},{7,6},{8,9},{9,8},{10,11... | collective-permute-start | bytes 589832 | tf_op jit(solution)/shard_map/ppermute | solution.py:468
  24.6 6.4 %collective-permute-start.16 = (bf16[64,2048]{1,0:T(8,128)(2,1)S(1)}, bf16[64,2048]{1,0:T(8,128)(2,1)S(1)}, u32[]{:S(2)}, u32[]{:S(2)}) collective-permute-start(bf16[64,2048]{1,0:T(8,128)(2,1)S(1)} %collective-permute-done.13.refs_2_.refs_9_), channel_id=1, source_target_pairs={{0,1},{1,0},{2,3},{3,2},{4,5},{5,4},{6,7},{7,6},{8,9},{9,8},{10,11... | collective-permute-start | bytes 786440 | tf_op jit(solution)/shard_map/ppermute | solution.py:468
  26.2 4.8 %collective-permute-start.17 = (bf16[48,2048]{1,0:T(8,128)(2,1)S(1)}, bf16[48,2048]{1,0:T(8,128)(2,1)S(1)}, u32[]{:S(2)}, u32[]{:S(2)}) collective-permute-start(bf16[48,2048]{1,0:T(8,128)(2,1)S(1)} %collective-permute-done.14.refs_3_.refs_10_), channel_id=1, source_target_pairs={{0,1},{1,0},{2,3},{3,2},{4,5},{5,4},{6,7},{7,6},{8,9},{9,8},{10,11... | collective-permute-start | bytes 589832 | tf_op jit(solution)/shard_map/ppermute | solution.py:468
  33.8 4.9 %collective-permute-start.21 = (f32[16,512]{1,0:T(8,128)S(1)}, f32[16,512]{1,0:T(8,128)S(1)}, u32[]{:S(2)}, u32[]{:S(2)}) collective-permute-start(f32[16,512]{1,0:T(8,128)S(1)} %get-tuple-element.61.refs_1_), channel_id=1, source_target_pairs={{0,10},{1,11},{2,8},{3,9},{4,14},{5,15},{6,12},{7,13},{8,2},{9,3},... | collective-permute-start | bytes 98312 | tf_op jit(solution)/shard_map/ppermute | solution.py:468
  45.0 6.4 %collective-permute-start.22 = (bf16[128,1024]{1,0:T(8,128)(2,1)S(1)}, bf16[128,1024]{1,0:T(8,128)(2,1)S(1)}, u32[]{:S(2)}, u32[]{:S(2)}) collective-permute-start(bf16[128,1024]{1,0:T(8,128)(2,1)S(1)} %get-tuple-element.71), channel_id=1, source_target_pairs={{0,2},{1,5},{2,0},{3,7},{4,6},{5,1},{6,4},{7,3},{8,10},{9,13},{10,... | collective-permute-start | bytes 786440 | tf_op jit(solution)/shard_map/ppermute | solution.py:468
  45.7 15.2 %collective-permute-start.23 = (bf16[128,1024]{1,0:T(8,128)(2,1)S(1)}, bf16[128,1024]{1,0:T(8,128)(2,1)S(1)}, u32[]{:S(2)}, u32[]{:S(2)}) collective-permute-start(bf16[128,1024]{1,0:T(8,128)(2,1)S(1)} %get-tuple-element.74), channel_id=1, source_target_pairs={{0,2},{1,5},{2,0},{3,7},{4,6},{5,1},{6,4},{7,3},{8,10},{9,13},{10,... | collective-permute-start | bytes 786440 | tf_op jit(solution)/shard_map/ppermute | solution.py:468
  47.0 15.1 %collective-permute-start.25 = (bf16[128,1024]{1,0:T(8,128)(2,1)S(1)}, bf16[128,1024]{1,0:T(8,128)(2,1)S(1)}, u32[]{:S(2)}, u32[]{:S(2)}) collective-permute-start(bf16[128,1024]{1,0:T(8,128)(2,1)S(1)} %get-tuple-element.76), channel_id=1, source_target_pairs={{0,2},{1,5},{2,0},{3,7},{4,6},{5,1},{6,4},{7,3},{8,10},{9,13},{10,... | collective-permute-start | bytes 786440 | tf_op jit(solution)/shard_map/ppermute | solution.py:468
  47.7 12.1 %collective-permute-start.26 = (bf16[128,1024]{1,0:T(8,128)(2,1)S(1)}, bf16[128,1024]{1,0:T(8,128)(2,1)S(1)}, u32[]{:S(2)}, u32[]{:S(2)}) collective-permute-start(bf16[128,1024]{1,0:T(8,128)(2,1)S(1)} %get-tuple-element.78), channel_id=1, source_target_pairs={{0,2},{1,5},{2,0},{3,7},{4,6},{5,1},{6,4},{7,3},{8,10},{9,13},{10,... | collective-permute-start | bytes 786440 | tf_op jit(solution)/shard_map/ppermute | solution.py:468
  51.5 21.2 %collective-permute-start.28 = (f32[64,1024]{1,0:T(8,128)S(1)}, f32[64,1024]{1,0:T(8,128)S(1)}, u32[]{:S(2)}, u32[]{:S(2)}) collective-permute-start(f32[64,1024]{1,0:T(8,128)S(1)} %get-tuple-element.79), channel_id=1, source_target_pairs={{0,1},{1,0},{2,3},{3,2},{4,5},{5,4},{6,7},{7,6},{8,9},{9,8},{10,11... | collective-permute-start | bytes 786440 | tf_op jit(solution)/shard_map/ppermute | solution.py:468
  59.9 7.7 %collective-permute-start.27 = (bf16[128,1024]{1,0:T(8,128)(2,1)S(1)}, bf16[128,1024]{1,0:T(8,128)(2,1)S(1)}, u32[]{:S(2)}, u32[]{:S(2)}) collective-permute-start(bf16[128,1024]{1,0:T(8,128)(2,1)S(1)} %add_convert_fusion), channel_id=1, source_target_pairs={{0,8},{1,17},{2,10},{3,19},{4,12},{5,21},{6,14},{7,23},{8,0},{9,25... | collective-permute-start | bytes 786440 | tf_op jit(solution)/shard_map/ppermute | solution.py:468
  61.0 11.6 %collective-permute-start.24 = (bf16[64,1024]{1,0:T(8,128)(2,1)S(1)}, bf16[64,1024]{1,0:T(8,128)(2,1)S(1)}, u32[]{:S(2)}, u32[]{:S(2)}) collective-permute-start(bf16[64,1024]{1,0:T(8,128)(2,1)S(1)} %get-tuple-element.88), channel_id=1, source_target_pairs={{0,8},{1,17},{2,10},{3,19},{4,12},{5,21},{6,14},{7,23},{8,0},{9,25... | collective-permute-start | bytes 393224 | tf_op jit(solution)/shard_map/ppermute | solution.py:468
  62.2 10.5 %collective-permute-start.29 = (bf16[64,1024]{1,0:T(8,128)(2,1)S(1)}, bf16[64,1024]{1,0:T(8,128)(2,1)S(1)}, u32[]{:S(2)}, u32[]{:S(2)}) collective-permute-start(bf16[64,1024]{1,0:T(8,128)(2,1)S(1)} %get-tuple-element.89), channel_id=1, source_target_pairs={{0,9},{1,16},{2,11},{3,18},{4,13},{5,20},{6,15},{7,22},{8,1},{9,24... | collective-permute-start | bytes 393224 | tf_op jit(solution)/shard_map/ppermute | solution.py:468
  67.8 5.0 %collective-permute-start.30 = (f32[64,1024]{1,0:T(8,128)S(1)}, f32[64,1024]{1,0:T(8,128)S(1)}, u32[]{:S(2)}, u32[]{:S(2)}) collective-permute-start(f32[64,1024]{1,0:T(8,128)S(1)} %get-tuple-element.83), channel_id=1, source_target_pairs={{0,1},{1,0},{2,3},{3,2},{4,5},{5,4},{6,7},{7,6},{8,9},{9,8},{10,11... | collective-permute-start | bytes 786440 | tf_op jit(solution)/shard_map/ppermute | solution.py:468
  (7 other events, 22.6 us)

commit v3 on v2

--- a/solution.py
+++ b/solution.py
@@ -209,36 +209,35 @@
 
 
 def subtile(lead, v_refs, w_refs, uppers, refs):
-    power_ref, col_peak, col_mass, row_peak, row_mass = refs
+    power_ref, col_ref, line_ref = refs
     gains = [logit_gain * m ** -0.5 * LOG2E for m in uppers]
-    count = power_ref.shape[1]
+    count, across = power_ref.shape[1:]
 
     @pl.when(lead)
     def _():
         lane = lax.broadcasted_iota(jnp.int32, (count, LANES), 1)
-        peaks = jnp.zeros((count, LANES), jnp.float32)
-        masses = jnp.ones((count, LANES), jnp.float32)
+        both = jnp.where(lane < STATS, 0.0, 1.0)
         for k, s in enumerate(subtile_scores(v_refs, w_refs, uppers)):
             logits = s * gains[k]
             peak = jnp.max(logits, axis=1, keepdims=True)
             power = jnp.exp2(logits - peak)
             power_ref[k] = power
-            peaks = jnp.where(lane == k, peak, peaks)
-            masses = jnp.where(lane == k, jnp.sum(power, axis=1, keepdims=True), masses)
-        col_peak[...] = peaks
-        col_mass[...] = masses
+            both = jnp.where(lane == k, peak, both)
+            both = jnp.where(lane == STATS + k, jnp.sum(power, axis=1, keepdims=True), both)
+        col_ref[...] = both
+        line_ref[:, :count] = both.T[:2 * STATS]
 
     @pl.when(jnp.logical_not(lead))
     def _():
-        row_peak[...] = jnp.zeros_like(row_peak)
-        row_mass[...] = jnp.ones_like(row_mass)
+        line_ref[:STATS, :] = jnp.zeros((STATS, line_ref.shape[1]), jnp.float32)
+        line_ref[STATS:, :] = jnp.ones((STATS, line_ref.shape[1]), jnp.float32)
         for k, s in enumerate(subtile_scores(v_refs, w_refs, uppers)):
             logits = s * gains[k]
             peak = jnp.max(logits, axis=0, keepdims=True)
             power = jnp.exp2(logits - peak)
             power_ref[k] = power
-            row_peak[k:k + 1, :] = peak
-            row_mass[k:k + 1, :] = jnp.sum(power, axis=0, keepdims=True)
+            line_ref[k:k + 1, :across] = peak
+            line_ref[STATS + k:STATS + k + 1, :across] = jnp.sum(power, axis=0, keepdims=True)
 
 
 def log_sum(pairs):
@@ -257,43 +256,33 @@
     at = 2 + sum(counts[r0:r1])
     v_refs, w_refs = refs[2:at], refs[at:at + sum(counts[c0:c1])]
     at += sum(counts[c0:c1])
-    earlier = refs[at:at + 4 * finish]
-    outs = refs[at + 4 * finish:]
+    earlier = refs[at:at + finish]
+    outs = refs[at + finish:]
     lead = (me_ref[0] & 1) == 0
     for i, (t0, t1, u0, u1) in enumerate(tiles):
         subtile(
             lead, v_refs[sum(counts[r0:t0]):sum(counts[r0:t1])],
-            w_refs[sum(counts[c0:u0]):sum(counts[c0:u1])], uppers, outs[5 * i:5 * i + 5])
+            w_refs[sum(counts[c0:u0]):sum(counts[c0:u1])], uppers, outs[3 * i:3 * i + 3])
     if not finish:
         outs[-1][...] = partner_ref[...]
         return
     stats_ref = outs[-1]
-    every = [earlier[4 * i:4 * i + 4] for i in range(finish)]
-    every += [outs[5 * i + 1:5 * i + 5] for i in range(len(tiles))]
+    every = [*earlier, *outs[2:3 * len(tiles):3]]
     segments = segments_of(groups)
     chip_rows = 2 * own_rows
 
-    @pl.when(lead)
-    def _():
-        merged = []
+    def merge(axis):
         for s0, s1 in segments:
             pairs = []
-            for (r0, r1, _, _), tile in zip(shapes, every):
-                if r0 <= s0 and s1 <= r1:
-                    rows = slice((s0 - r0) * chip_rows, (s1 - r0) * chip_rows)
-                    pairs.append((tile[0][rows, :], tile[1][rows, :]))
-            merged.append(log_sum(pairs))
-        stats_ref[...] = jnp.concatenate(merged, axis=0).T[:STATS]
-
-    @pl.when(jnp.logical_not(lead))
-    def _():
-        for s0, s1 in segments:
-            pairs = []
-            for (_, _, c0, c1), tile in zip(shapes, every):
-                if c0 <= s0 and s1 <= c1:
-                    across = slice((s0 - c0) * chip_rows, (s1 - c0) * chip_rows)
-                    pairs.append((tile[2][:, across], tile[3][:, across]))
+            for shape, line in zip(shapes, every):
+                low, high = shape[axis:axis + 2]
+                if low <= s0 and s1 <= high:
+                    at = slice((s0 - low) * chip_rows, (s1 - low) * chip_rows)
+                    pairs.append((line[:STATS, at], line[STATS:, at]))
             stats_ref[:, s0 * chip_rows:s1 * chip_rows] = log_sum(pairs)
+
+    pl.when(lead)(lambda: merge(0))
+    pl.when(jnp.logical_not(lead))(lambda: merge(2))
 
     count = len(uppers)
     stats_ref[count:count + 1, :chip_rows] = partner_ref[...]
@@ -349,7 +338,7 @@
     chip_rows = totals.shape[1] // groups
     s0, s1 = segment
     strip = []
-    for (r0, r1, c0, c1), power, col_peak, row_peak in zip(
+    for (r0, r1, c0, c1), power, col_peak, line in zip(
             subtiles(groups), power_refs, col_refs, row_refs):
         if r0 <= s0 and s1 <= r1:
             inner = slice((s0 - r0) * chip_rows, (s1 - r0) * chip_rows)
@@ -358,7 +347,7 @@
             strip.append((
                 c0, power, inner,
                 jnp.where(lead, jnp.exp2(col_peak[inner, :] - cols[outer]), 1.0),
-                jnp.where(lead, 1.0, jnp.exp2(row_peak[...] - totals[:, across]))))
+                jnp.where(lead, 1.0, jnp.exp2(line[:STATS, :(c1 - c0) * chip_rows] - totals[:, across]))))
     strip.sort(key=lambda item: item[0])
     return lambda k: jnp.concatenate([
         power[k, inner] * col_gain[:, k:k + 1] * row_gain[k:k + 1, :]
@@ -561,20 +550,20 @@
                 r0, r1, c0, c1 = shapes[i]
                 tall, wide = (r1 - r0) * chip_rows, (c1 - c0) * chip_rows
                 area += tall * wide
-                result += [shape(WIDTHS, tall, wide), shape(tall, LANES), shape(tall, LANES),
-                           shape(STATS, wide), shape(STATS, wide)]
+                result += [shape(WIDTHS, tall, wide), shape(tall, LANES),
+                           shape(2 * STATS, max(tall, wide))]
             *arrays, last_array = pl.pallas_call(
                 functools.partial(
                     tile_kernel, span, counts, uppers, own_rows, len(earlier)),
                 out_shape=result + stat_shapes,
-                in_specs=[smem] + [vmem] * (1 + len(operands) + 4 * len(earlier)),
+                in_specs=[smem] + [vmem] * (1 + len(operands) + len(earlier)),
                 out_specs=[vmem] * (len(result) + 1),
                 compiler_params=params,
                 cost_estimate=pl.CostEstimate(
                     flops=6 * area * feature_dim, transcendentals=0,
                     bytes_accessed=2 * total * feature_dim),
-            )(me, partner_row, *operands, *[a for one in earlier for a in one[1:]])
-            return [arrays[5 * i:5 * i + 5] for i in range(len(span))], last_array
+            )(me, partner_row, *operands, *[one[2] for one in earlier])
+            return [arrays[3 * i:3 * i + 3] for i in range(len(span))], last_array
 
         done, chip_partner = tile([0], chip_partner)
         for at in (1, 2, 3):
@@ -583,7 +572,7 @@
         more, stats = tile([4], chip_partner, done)
         done += more
         common = [me, *gathered(stats), *[t[0] for t in done], *[t[1] for t in done],
-                  *[t[3] for t in done], *w_list]
+                  *[t[2] for t in done], *w_list]
         near = segments_of(groups)[-1][0]
         widest = feature_dim - uppers[-2]
 

time: 74.6 us -> 73.9 us (level)
  no operation moved by 1% of the time
where the time goes in v3:
time: 73.9 us; the launch traced here: 73.1 us
  waiting for transfers between devices  31 us (42%)
  starting transfers between devices  27.3 us (37%)
  Pallas kernels  10.7 us (14%)
  other arithmetic  3.16 us (4%)
  between operations  0.84 us (1%)
    ppermute x31, waiting for transfers between devices, exchange(): return lax.ppermute(x, AXES, [(i, i ^ masks_of(i)) for i in range(devices)])  31 us
    ppermute x31, starting transfers between devices, exchange(): return lax.ppermute(x, AXES, [(i, i ^ masks_of(i)) for i in range(devices)])  27.3 us
    pallas_call x5, Pallas kernels, tile(): pl.pallas_call(functools.partial(tile_kernel, span, counts, uppers, own_r...  6.26 us
    pallas_call x2, Pallas kernels, bands(): pl.pallas_call(functools.partial(kernel, groups, uppers, own_rows, docume...  4.42 us
  transfers between devices with their start and end apart: 31, of which 11 were waited for; matrix products, arithmetic and copies ran while one was open for 2% of the time, Pallas kernels for 6%

profile of v3, /device:TPU:0, one launch (start us, length us, event | category | flops | bytes accessed | tf_op | source)
XLA Modules:
  0.0 73.1 jit_solution(658888271691090452)
XLA Ops:
  2.3 2.6 %collective-permute-start.7 = (bf16[64,2048]{1,0:T(8,128)(2,1)S(1)}, bf16[64,2048]{1,0:T(8,128)(2,1)S(1)}, u32[]{:S(2)}, u32[]{:S(2)}) collective-permute-start(bf16[64,2048]{1,0:T(8,128)(2,1)S(1)} %get-tuple-element.71.refs_2_), channel_id=1, source_target_pairs={{0,8},{1,17},{2,10},{3,19},{4,12},{5,21},{6,14},{7,23},{8,0},{9,25... | collective-permute-start | bytes 786440 | tf_op jit(solution)/shard_map/ppermute | solution.py:457
  4.9 1.5 %collective-permute-start.2 = (bf16[64,2048]{1,0:T(8,128)(2,1)S(1)}, bf16[64,2048]{1,0:T(8,128)(2,1)S(1)}, u32[]{:S(2)}, u32[]{:S(2)}) collective-permute-start(bf16[64,2048]{1,0:T(8,128)(2,1)S(1)} %get-tuple-element.71.refs_2_), channel_id=1, source_target_pairs={{0,2},{1,5},{2,0},{3,7},{4,6},{5,1},{6,4},{7,3},{8,10},{9,13},{10,... | collective-permute-start | bytes 786440 | tf_op jit(solution)/shard_map/ppermute | solution.py:457
  7.3 1.5 %collective-permute-start.3 = (bf16[64,2048]{1,0:T(8,128)(2,1)S(1)}, bf16[64,2048]{1,0:T(8,128)(2,1)S(1)}, u32[]{:S(2)}, u32[]{:S(2)}) collective-permute-start(bf16[64,2048]{1,0:T(8,128)(2,1)S(1)} %collective-permute-done.1.refs_3_), channel_id=1, source_target_pairs={{0,2},{1,5},{2,0},{3,7},{4,6},{5,1},{6,4},{7,3},{8,10},{9,13},{10,... | collective-permute-start | bytes 786440 | tf_op jit(solution)/shard_map/ppermute | solution.py:457
  9.5 1.1 %collective-permute-done = f32[1,64]{1,0:T(1,128)S(1)} collective-permute-done((f32[1,64]{1,0:T(1,128)S(1)}, f32[1,64]{1,0:T(1,128)S(1)}, u32[]{:S(2)}, u32[]{:S(2)}) %collective-permute-start) | collective-permute-done | bytes 288 | tf_op jit(solution)/shard_map/ppermute | solution.py:457
  10.6 1.6 %collective-permute-start.8 = (bf16[48,2048]{1,0:T(8,128)(2,1)S(1)}, bf16[48,2048]{1,0:T(8,128)(2,1)S(1)}, u32[]{:S(2)}, u32[]{:S(2)}) collective-permute-start(bf16[48,2048]{1,0:T(8,128)(2,1)S(1)} %slice.32), channel_id=1, source_target_pairs={{0,8},{1,17},{2,10},{3,19},{4,12},{5,21},{6,14},{7,23},{8,0},{9,25... | collective-permute-start | bytes 589832 | tf_op jit(solution)/shard_map/ppermute | solution.py:457
  12.2 1.7 %collective-permute-start.13 = (bf16[64,2048]{1,0:T(8,128)(2,1)S(1)}, bf16[64,2048]{1,0:T(8,128)(2,1)S(1)}, u32[]{:S(2)}, u32[]{:S(2)}) collective-permute-start(bf16[64,2048]{1,0:T(8,128)(2,1)S(1)} %collective-permute-done.7.refs_2_.refs_6_), channel_id=1, source_target_pairs={{0,2},{1,5},{2,0},{3,7},{4,6},{5,1},{6,4},{7,3},{8,10},{9,13},{10,... | collective-permute-start | bytes 786440 | tf_op jit(solution)/shard_map/ppermute | solution.py:457
  13.9 2.0 %collective-permute-start.9 = (bf16[16,2048]{1,0:T(8,128)(2,1)S(1)}, bf16[16,2048]{1,0:T(8,128)(2,1)S(1)}, u32[]{:S(2)}, u32[]{:S(2)}) collective-permute-start(bf16[16,2048]{1,0:T(8,128)(2,1)S(1)} %slice.33), channel_id=1, source_target_pairs={{0,8},{1,17},{2,10},{3,19},{4,12},{5,21},{6,14},{7,23},{8,0},{9,25... | collective-permute-start | bytes 196616 | tf_op jit(solution)/shard_map/ppermute | solution.py:457
  16.3 3.6 %collective-permute-done.9.refs_4_.refs_8_ = bf16[16,2048]{1,0:T(8,128)(2,1)S(1)} collective-permute-done((bf16[16,2048]{1,0:T(8,128)(2,1)S(1)}, bf16[16,2048]{1,0:T(8,128)(2,1)S(1)}, u32[]{:S(2)}, u32[]{:S(2)}) %collective-permute-start.9) | collective-permute-done | bytes 65568 | tf_op jit(solution)/shard_map/ppermute | solution.py:457
  20.3 1.5 %collective-permute-start.14 = (bf16[48,2048]{1,0:T(8,128)(2,1)S(1)}, bf16[48,2048]{1,0:T(8,128)(2,1)S(1)}, u32[]{:S(2)}, u32[]{:S(2)}) collective-permute-start(bf16[48,2048]{1,0:T(8,128)(2,1)S(1)} %collective-permute-done.8.refs_3_.refs_7_), channel_id=1, source_target_pairs={{0,2},{1,5},{2,0},{3,7},{4,6},{5,1},{6,4},{7,3},{8,10},{9,13},{10,... | collective-permute-start | bytes 589832 | tf_op jit(solution)/shard_map/ppermute | solution.py:457
  21.8 2.2 %collective-permute-done.15.refs_4_.refs_11_ = bf16[16,2048]{1,0:T(8,128)(2,1)S(1)} collective-permute-done((bf16[16,2048]{1,0:T(8,128)(2,1)S(1)}, bf16[16,2048]{1,0:T(8,128)(2,1)S(1)}, u32[]{:S(2)}, u32[]{:S(2)}) %collective-permute-start.15) | collective-permute-done | bytes 65568 | tf_op jit(solution)/shard_map/ppermute | solution.py:457
  24.7 1.4 %collective-permute-done.14.refs_3_.refs_10_ = bf16[48,2048]{1,0:T(8,128)(2,1)S(1)} collective-permute-done((bf16[48,2048]{1,0:T(8,128)(2,1)S(1)}, bf16[48,2048]{1,0:T(8,128)(2,1)S(1)}, u32[]{:S(2)}, u32[]{:S(2)}) %collective-permute-start.14) | collective-permute-done | bytes 196640 | tf_op jit(solution)/shard_map/ppermute | solution.py:457
  28.6 1.5 %shard_map.52 = (f32[9,384,128]{2,1,0:T(8,128)S(1)}, f32[384,128]{1,0:T(8,128)S(1)}, f32[32,384]{1,0:T(8,128)S(1)}, f32[1,128]{1,0:T(1,128)S(1)}) custom-call(s32[1]{0:T(128)} %bitcast.refs_0_, f32[1,128]{1,0:T(1,128)S(1)} %get-tuple-element.34.refs_1_, bf16[64,2048]{1,0:T(8,128)(2,1)S(1)} %get-tuple-element.71.refs_2_, ...), custom_call_target="tpu_custom_call" | custom-call | flops 603979776 | bytes 2097152 | tf_op jit(solution)/shard_map/pallas_call | solution.py:555
  31.1 1.9 %shard_map.54 = (f32[9,512,128]{2,1,0:T(8,128)S(1)}, f32[512,128]{1,0:T(8,128)S(1)}, f32[32,512]{1,0:T(8,128)S(1)}, f32[16,512]{1,0:T(8,128)S(1)}) custom-call(s32[1]{0:T(128)} %bitcast.refs_0_, f32[1,128]{1,0:T(1,128)S(1)} %get-tuple-element.36.refs_1_, bf16[64,2048]{1,0:T(8,128)(2,1)S(1)} %get-tuple-element.71.refs_2_, ...), custom_call_target="tpu_custom_call" | custom-call | flops 805306368 | bytes 2097152 | tf_op jit(solution)/shard_map/pallas_call | solution.py:555
  33.1 1.8 %collective-permute-start.21 = (f32[16,512]{1,0:T(8,128)S(1)}, f32[16,512]{1,0:T(8,128)S(1)}, u32[]{:S(2)}, u32[]{:S(2)}) collective-permute-start(f32[16,512]{1,0:T(8,128)S(1)} %get-tuple-element.41.refs_1_), channel_id=1, source_target_pairs={{0,10},{1,11},{2,8},{3,9},{4,14},{5,15},{6,12},{7,13},{8,2},{9,3},... | collective-permute-start | bytes 98312 | tf_op jit(solution)/shard_map/ppermute | solution.py:457
  36.6 1.4 %collective-permute-done.21.refs_4_ = f32[16,512]{1,0:T(8,128)S(1)} collective-permute-done((f32[16,512]{1,0:T(8,128)S(1)}, f32[16,512]{1,0:T(8,128)S(1)}, u32[]{:S(2)}, u32[]{:S(2)}) %collective-permute-start.21) | collective-permute-done | bytes 32800 | tf_op jit(solution)/shard_map/ppermute | solution.py:457
  40.3 3.9 %shard_map.56 = (f32[128,1024]{1,0:T(8,128)S(1)}, bf16[128,1024]{1,0:T(8,128)(2,1)S(1)}, f32[128,1024]{1,0:T(8,128)S(1)}, bf16[128,1024]{1,0:T(8,128)(2,1)S(1)},...) custom-call(s32[1]{0:T(128)} %bitcast.refs_0_, ...), custom_call_target="tpu_custom_call" | custom-call | flops 1073741824 | bytes 4194304 | tf_op jit(solution)/shard_map/pallas_call | solution.py:580
  45.1 1.3 %collective-permute-start.23 = (bf16[128,1024]{1,0:T(8,128)(2,1)S(1)}, bf16[128,1024]{1,0:T(8,128)(2,1)S(1)}, u32[]{:S(2)}, u32[]{:S(2)}) collective-permute-start(bf16[128,1024]{1,0:T(8,128)(2,1)S(1)} %get-tuple-element.58), channel_id=1, source_target_pairs={{0,2},{1,5},{2,0},{3,7},{4,6},{5,1},{6,4},{7,3},{8,10},{9,13},{10,... | collective-permute-start | bytes 786440 | tf_op jit(solution)/shard_map/ppermute | solution.py:457
  47.1 1.3 %collective-permute-start.26 = (bf16[128,1024]{1,0:T(8,128)(2,1)S(1)}, bf16[128,1024]{1,0:T(8,128)(2,1)S(1)}, u32[]{:S(2)}, u32[]{:S(2)}) collective-permute-start(bf16[128,1024]{1,0:T(8,128)(2,1)S(1)} %get-tuple-element.62), channel_id=1, source_target_pairs={{0,2},{1,5},{2,0},{3,7},{4,6},{5,1},{6,4},{7,3},{8,10},{9,13},{10,... | collective-permute-start | bytes 786440 | tf_op jit(solution)/shard_map/ppermute | solution.py:457
  48.4 2.3 %collective-permute-done.22 = bf16[128,1024]{1,0:T(8,128)(2,1)S(1)} collective-permute-done((bf16[128,1024]{1,0:T(8,128)(2,1)S(1)}, bf16[128,1024]{1,0:T(8,128)(2,1)S(1)}, u32[]{:S(2)}, u32[]{:S(2)}) %collective-permute-start.22) | collective-permute-done | bytes 262176 | tf_op jit(solution)/shard_map/ppermute | solution.py:457
  50.9 8.2 %collective-permute-done.26 = bf16[128,1024]{1,0:T(8,128)(2,1)S(1)} collective-permute-done((bf16[128,1024]{1,0:T(8,128)(2,1)S(1)}, bf16[128,1024]{1,0:T(8,128)(2,1)S(1)}, u32[]{:S(2)}, u32[]{:S(2)}) %collective-permute-start.26) | collective-permute-done | bytes 262176 | tf_op jit(solution)/shard_map/ppermute | solution.py:457
  60.3 1.1 %collective-permute-start.24 = (bf16[64,1024]{1,0:T(8,128)(2,1)S(1)}, bf16[64,1024]{1,0:T(8,128)(2,1)S(1)}, u32[]{:S(2)}, u32[]{:S(2)}) collective-permute-start(bf16[64,1024]{1,0:T(8,128)(2,1)S(1)} %get-tuple-element.72), channel_id=1, source_target_pairs={{0,8},{1,17},{2,10},{3,19},{4,12},{5,21},{6,14},{7,23},{8,0},{9,25... | collective-permute-start | bytes 393224 | tf_op jit(solution)/shard_map/ppermute | solution.py:457
  61.5 5.5 %collective-permute-done.27 = bf16[128,1024]{1,0:T(8,128)(2,1)S(1)} collective-permute-done((bf16[128,1024]{1,0:T(8,128)(2,1)S(1)}, bf16[128,1024]{1,0:T(8,128)(2,1)S(1)}, u32[]{:S(2)}, u32[]{:S(2)}) %collective-permute-start.27) | collective-permute-done | bytes 262176 | tf_op jit(solution)/shard_map/ppermute | solution.py:457
  67.1 1.5 %collective-permute-start.30 = (f32[64,1024]{1,0:T(8,128)S(1)}, f32[64,1024]{1,0:T(8,128)S(1)}, u32[]{:S(2)}, u32[]{:S(2)}) collective-permute-start(f32[64,1024]{1,0:T(8,128)S(1)} %get-tuple-element.67), channel_id=1, source_target_pairs={{0,1},{1,0},{2,3},{3,2},{4,5},{5,4},{6,7},{7,6},{8,9},{9,8},{10,11... | collective-permute-start | bytes 786440 | tf_op jit(solution)/shard_map/ppermute | solution.py:457
  68.6 3.4 %collective-permute-done.24 = bf16[64,1024]{1,0:T(8,128)(2,1)S(1)} collective-permute-done((bf16[64,1024]{1,0:T(8,128)(2,1)S(1)}, bf16[64,1024]{1,0:T(8,128)(2,1)S(1)}, u32[]{:S(2)}, u32[]{:S(2)}) %collective-permute-start.24) | collective-permute-done | bytes 131104 | tf_op jit(solution)/shard_map/ppermute | solution.py:457
  (60 shorter events, 16.2 us)
Async XLA Ops:
  1.7 5.6 %collective-permute-start.1 = (bf16[64,2048]{1,0:T(8,128)(2,1)S(1)}, bf16[64,2048]{1,0:T(8,128)(2,1)S(1)}, u32[]{:S(2)}, u32[]{:S(2)}) collective-permute-start(bf16[64,2048]{1,0:T(8,128)(2,1)S(1)} %get-tuple-element.70.refs_7_.refs_6_.refs_21_), channel_id=1, source_target_pairs={{0,1},{1,0},{2,3},{3,2},{4,5},{5,4},{6,7},{7,6},{8,9},{9,8},{10,11... | collective-permute-start | bytes 786440 | tf_op jit(solution)/shard_map/ppermute | solution.py:457
  2.3 9.9 %collective-permute-start.7 = (bf16[64,2048]{1,0:T(8,128)(2,1)S(1)}, bf16[64,2048]{1,0:T(8,128)(2,1)S(1)}, u32[]{:S(2)}, u32[]{:S(2)}) collective-permute-start(bf16[64,2048]{1,0:T(8,128)(2,1)S(1)} %get-tuple-element.71.refs_2_), channel_id=1, source_target_pairs={{0,8},{1,17},{2,10},{3,19},{4,12},{5,21},{6,14},{7,23},{8,0},{9,25... | collective-permute-start | bytes 786440 | tf_op jit(solution)/shard_map/ppermute | solution.py:457
  4.9 9.0 %collective-permute-start.2 = (bf16[64,2048]{1,0:T(8,128)(2,1)S(1)}, bf16[64,2048]{1,0:T(8,128)(2,1)S(1)}, u32[]{:S(2)}, u32[]{:S(2)}) collective-permute-start(bf16[64,2048]{1,0:T(8,128)(2,1)S(1)} %get-tuple-element.71.refs_2_), channel_id=1, source_target_pairs={{0,2},{1,5},{2,0},{3,7},{4,6},{5,1},{6,4},{7,3},{8,10},{9,13},{10,... | collective-permute-start | bytes 786440 | tf_op jit(solution)/shard_map/ppermute | solution.py:457
  6.4 7.5 %collective-permute-start.4 = (bf16[64,2048]{1,0:T(8,128)(2,1)S(1)}, bf16[64,2048]{1,0:T(8,128)(2,1)S(1)}, u32[]{:S(2)}, u32[]{:S(2)}) collective-permute-start(bf16[64,2048]{1,0:T(8,128)(2,1)S(1)} %get-tuple-element.71.refs_2_), channel_id=1, source_target_pairs={{0,1},{1,0},{2,3},{3,2},{4,5},{5,4},{6,7},{7,6},{8,9},{9,8},{10,11... | collective-permute-start | bytes 786440 | tf_op jit(solution)/shard_map/ppermute | solution.py:457
  7.3 8.7 %collective-permute-start.3 = (bf16[64,2048]{1,0:T(8,128)(2,1)S(1)}, bf16[64,2048]{1,0:T(8,128)(2,1)S(1)}, u32[]{:S(2)}, u32[]{:S(2)}) collective-permute-start(bf16[64,2048]{1,0:T(8,128)(2,1)S(1)} %collective-permute-done.1.refs_3_), channel_id=1, source_target_pairs={{0,2},{1,5},{2,0},{3,7},{4,6},{5,1},{6,4},{7,3},{8,10},{9,13},{10,... | collective-permute-start | bytes 786440 | tf_op jit(solution)/shard_map/ppermute | solution.py:457
  10.6 9.7 %collective-permute-start.8 = (bf16[48,2048]{1,0:T(8,128)(2,1)S(1)}, bf16[48,2048]{1,0:T(8,128)(2,1)S(1)}, u32[]{:S(2)}, u32[]{:S(2)}) collective-permute-start(bf16[48,2048]{1,0:T(8,128)(2,1)S(1)} %slice.32), channel_id=1, source_target_pairs={{0,8},{1,17},{2,10},{3,19},{4,12},{5,21},{6,14},{7,23},{8,0},{9,25... | collective-permute-start | bytes 589832 | tf_op jit(solution)/shard_map/ppermute | solution.py:457
  12.2 11.9 %collective-permute-start.13 = (bf16[64,2048]{1,0:T(8,128)(2,1)S(1)}, bf16[64,2048]{1,0:T(8,128)(2,1)S(1)}, u32[]{:S(2)}, u32[]{:S(2)}) collective-permute-start(bf16[64,2048]{1,0:T(8,128)(2,1)S(1)} %collective-permute-done.7.refs_2_.refs_6_), channel_id=1, source_target_pairs={{0,2},{1,5},{2,0},{3,7},{4,6},{5,1},{6,4},{7,3},{8,10},{9,13},{10,... | collective-permute-start | bytes 786440 | tf_op jit(solution)/shard_map/ppermute | solution.py:457
  13.9 10.7 %collective-permute-start.5 = (bf16[64,2048]{1,0:T(8,128)(2,1)S(1)}, bf16[64,2048]{1,0:T(8,128)(2,1)S(1)}, u32[]{:S(2)}, u32[]{:S(2)}) collective-permute-start(bf16[64,2048]{1,0:T(8,128)(2,1)S(1)} %collective-permute-done.2.refs_4_), channel_id=1, source_target_pairs={{0,1},{1,0},{2,3},{3,2},{4,5},{5,4},{6,7},{7,6},{8,9},{9,8},{10,11... | collective-permute-start | bytes 786440 | tf_op jit(solution)/shard_map/ppermute | solution.py:457
  13.9 5.9 %collective-permute-start.9 = (bf16[16,2048]{1,0:T(8,128)(2,1)S(1)}, bf16[16,2048]{1,0:T(8,128)(2,1)S(1)}, u32[]{:S(2)}, u32[]{:S(2)}) collective-permute-start(bf16[16,2048]{1,0:T(8,128)(2,1)S(1)} %slice.33), channel_id=1, source_target_pairs={{0,8},{1,17},{2,10},{3,19},{4,12},{5,21},{6,14},{7,23},{8,0},{9,25... | collective-permute-start | bytes 196616 | tf_op jit(solution)/shard_map/ppermute | solution.py:457
  16.0 10.2 %collective-permute-start.6 = (bf16[64,2048]{1,0:T(8,128)(2,1)S(1)}, bf16[64,2048]{1,0:T(8,128)(2,1)S(1)}, u32[]{:S(2)}, u32[]{:S(2)}) collective-permute-start(bf16[64,2048]{1,0:T(8,128)(2,1)S(1)} %collective-permute-done.3.refs_5_), channel_id=1, source_target_pairs={{0,1},{1,0},{2,3},{3,2},{4,5},{5,4},{6,7},{7,6},{8,9},{9,8},{10,11... | collective-permute-start | bytes 786440 | tf_op jit(solution)/shard_map/ppermute | solution.py:457
  20.3 5.8 %collective-permute-start.14 = (bf16[48,2048]{1,0:T(8,128)(2,1)S(1)}, bf16[48,2048]{1,0:T(8,128)(2,1)S(1)}, u32[]{:S(2)}, u32[]{:S(2)}) collective-permute-start(bf16[48,2048]{1,0:T(8,128)(2,1)S(1)} %collective-permute-done.8.refs_3_.refs_7_), channel_id=1, source_target_pairs={{0,2},{1,5},{2,0},{3,7},{4,6},{5,1},{6,4},{7,3},{8,10},{9,13},{10,... | collective-permute-start | bytes 589832 | tf_op jit(solution)/shard_map/ppermute | solution.py:457
  24.1 4.5 %collective-permute-start.11 = (bf16[48,2048]{1,0:T(8,128)(2,1)S(1)}, bf16[48,2048]{1,0:T(8,128)(2,1)S(1)}, u32[]{:S(2)}, u32[]{:S(2)}) collective-permute-start(bf16[48,2048]{1,0:T(8,128)(2,1)S(1)} %collective-permute-done.8.refs_3_.refs_7_), channel_id=1, source_target_pairs={{0,1},{1,0},{2,3},{3,2},{4,5},{5,4},{6,7},{7,6},{8,9},{9,8},{10,11... | collective-permute-start | bytes 589832 | tf_op jit(solution)/shard_map/ppermute | solution.py:457
  24.6 6.5 %collective-permute-start.16 = (bf16[64,2048]{1,0:T(8,128)(2,1)S(1)}, bf16[64,2048]{1,0:T(8,128)(2,1)S(1)}, u32[]{:S(2)}, u32[]{:S(2)}) collective-permute-start(bf16[64,2048]{1,0:T(8,128)(2,1)S(1)} %collective-permute-done.13.refs_2_.refs_9_), channel_id=1, source_target_pairs={{0,1},{1,0},{2,3},{3,2},{4,5},{5,4},{6,7},{7,6},{8,9},{9,8},{10,11... | collective-permute-start | bytes 786440 | tf_op jit(solution)/shard_map/ppermute | solution.py:457
  26.2 4.9 %collective-permute-start.17 = (bf16[48,2048]{1,0:T(8,128)(2,1)S(1)}, bf16[48,2048]{1,0:T(8,128)(2,1)S(1)}, u32[]{:S(2)}, u32[]{:S(2)}) collective-permute-start(bf16[48,2048]{1,0:T(8,128)(2,1)S(1)} %collective-permute-done.14.refs_3_.refs_10_), channel_id=1, source_target_pairs={{0,1},{1,0},{2,3},{3,2},{4,5},{5,4},{6,7},{7,6},{8,9},{9,8},{10,11... | collective-permute-start | bytes 589832 | tf_op jit(solution)/shard_map/ppermute | solution.py:457
  33.1 5.0 %collective-permute-start.21 = (f32[16,512]{1,0:T(8,128)S(1)}, f32[16,512]{1,0:T(8,128)S(1)}, u32[]{:S(2)}, u32[]{:S(2)}) collective-permute-start(f32[16,512]{1,0:T(8,128)S(1)} %get-tuple-element.41.refs_1_), channel_id=1, source_target_pairs={{0,10},{1,11},{2,8},{3,9},{4,14},{5,15},{6,12},{7,13},{8,2},{9,3},... | collective-permute-start | bytes 98312 | tf_op jit(solution)/shard_map/ppermute | solution.py:457
  44.3 6.4 %collective-permute-start.22 = (bf16[128,1024]{1,0:T(8,128)(2,1)S(1)}, bf16[128,1024]{1,0:T(8,128)(2,1)S(1)}, u32[]{:S(2)}, u32[]{:S(2)}) collective-permute-start(bf16[128,1024]{1,0:T(8,128)(2,1)S(1)} %get-tuple-element.55), channel_id=1, source_target_pairs={{0,2},{1,5},{2,0},{3,7},{4,6},{5,1},{6,4},{7,3},{8,10},{9,13},{10,... | collective-permute-start | bytes 786440 | tf_op jit(solution)/shard_map/ppermute | solution.py:457
  45.1 15.2 %collective-permute-start.23 = (bf16[128,1024]{1,0:T(8,128)(2,1)S(1)}, bf16[128,1024]{1,0:T(8,128)(2,1)S(1)}, u32[]{:S(2)}, u32[]{:S(2)}) collective-permute-start(bf16[128,1024]{1,0:T(8,128)(2,1)S(1)} %get-tuple-element.58), channel_id=1, source_target_pairs={{0,2},{1,5},{2,0},{3,7},{4,6},{5,1},{6,4},{7,3},{8,10},{9,13},{10,... | collective-permute-start | bytes 786440 | tf_op jit(solution)/shard_map/ppermute | solution.py:457
  46.4 15.1 %collective-permute-start.25 = (bf16[128,1024]{1,0:T(8,128)(2,1)S(1)}, bf16[128,1024]{1,0:T(8,128)(2,1)S(1)}, u32[]{:S(2)}, u32[]{:S(2)}) collective-permute-start(bf16[128,1024]{1,0:T(8,128)(2,1)S(1)} %get-tuple-element.60), channel_id=1, source_target_pairs={{0,2},{1,5},{2,0},{3,7},{4,6},{5,1},{6,4},{7,3},{8,10},{9,13},{10,... | collective-permute-start | bytes 786440 | tf_op jit(solution)/shard_map/ppermute | solution.py:457
  47.1 12.1 %collective-permute-start.26 = (bf16[128,1024]{1,0:T(8,128)(2,1)S(1)}, bf16[128,1024]{1,0:T(8,128)(2,1)S(1)}, u32[]{:S(2)}, u32[]{:S(2)}) collective-permute-start(bf16[128,1024]{1,0:T(8,128)(2,1)S(1)} %get-tuple-element.62), channel_id=1, source_target_pairs={{0,2},{1,5},{2,0},{3,7},{4,6},{5,1},{6,4},{7,3},{8,10},{9,13},{10,... | collective-permute-start | bytes 786440 | tf_op jit(solution)/shard_map/ppermute | solution.py:457
  50.8 21.2 %collective-permute-start.28 = (f32[64,1024]{1,0:T(8,128)S(1)}, f32[64,1024]{1,0:T(8,128)S(1)}, u32[]{:S(2)}, u32[]{:S(2)}) collective-permute-start(f32[64,1024]{1,0:T(8,128)S(1)} %get-tuple-element.63), channel_id=1, source_target_pairs={{0,1},{1,0},{2,3},{3,2},{4,5},{5,4},{6,7},{7,6},{8,9},{9,8},{10,11... | collective-permute-start | bytes 786440 | tf_op jit(solution)/shard_map/ppermute | solution.py:457
  59.2 7.7 %collective-permute-start.27 = (bf16[128,1024]{1,0:T(8,128)(2,1)S(1)}, bf16[128,1024]{1,0:T(8,128)(2,1)S(1)}, u32[]{:S(2)}, u32[]{:S(2)}) collective-permute-start(bf16[128,1024]{1,0:T(8,128)(2,1)S(1)} %add_convert_fusion), channel_id=1, source_target_pairs={{0,8},{1,17},{2,10},{3,19},{4,12},{5,21},{6,14},{7,23},{8,0},{9,25... | collective-permute-start | bytes 786440 | tf_op jit(solution)/shard_map/ppermute | solution.py:457
  60.3 11.6 %collective-permute-start.24 = (bf16[64,1024]{1,0:T(8,128)(2,1)S(1)}, bf16[64,1024]{1,0:T(8,128)(2,1)S(1)}, u32[]{:S(2)}, u32[]{:S(2)}) collective-permute-start(bf16[64,1024]{1,0:T(8,128)(2,1)S(1)} %get-tuple-element.72), channel_id=1, source_target_pairs={{0,8},{1,17},{2,10},{3,19},{4,12},{5,21},{6,14},{7,23},{8,0},{9,25... | collective-permute-start | bytes 393224 | tf_op jit(solution)/shard_map/ppermute | solution.py:457
  61.5 10.5 %collective-permute-start.29 = (bf16[64,1024]{1,0:T(8,128)(2,1)S(1)}, bf16[64,1024]{1,0:T(8,128)(2,1)S(1)}, u32[]{:S(2)}, u32[]{:S(2)}) collective-permute-start(bf16[64,1024]{1,0:T(8,128)(2,1)S(1)} %get-tuple-element.73), channel_id=1, source_target_pairs={{0,9},{1,16},{2,11},{3,18},{4,13},{5,20},{6,15},{7,22},{8,1},{9,24... | collective-permute-start | bytes 393224 | tf_op jit(solution)/shard_map/ppermute | solution.py:457
  67.1 5.0 %collective-permute-start.30 = (f32[64,1024]{1,0:T(8,128)S(1)}, f32[64,1024]{1,0:T(8,128)S(1)}, u32[]{:S(2)}, u32[]{:S(2)}) collective-permute-start(f32[64,1024]{1,0:T(8,128)S(1)} %get-tuple-element.67), channel_id=1, source_target_pairs={{0,1},{1,0},{2,3},{3,2},{4,5},{5,4},{6,7},{7,6},{8,9},{9,8},{10,11... | collective-permute-start | bytes 786440 | tf_op jit(solution)/shard_map/ppermute | solution.py:457
  (7 other events, 22.7 us)

commit v4 on v3

--- a/solution.py
+++ b/solution.py
@@ -252,9 +252,9 @@
     shapes = subtiles(groups)
     tiles = [shapes[i] for i in span]
     r0, r1, c0, c1 = extent(tiles)
-    me_ref, partner_ref = refs[:2]
-    at = 2 + sum(counts[r0:r1])
-    v_refs, w_refs = refs[2:at], refs[at:at + sum(counts[c0:c1])]
+    me_ref, partner_ref, far_ref = refs[:3]
+    at = 3 + sum(counts[r0:r1])
+    v_refs, w_refs = refs[3:at], refs[at:at + sum(counts[c0:c1])]
     at += sum(counts[c0:c1])
     earlier = refs[at:at + finish]
     outs = refs[at + finish:]
@@ -264,7 +264,12 @@
             lead, v_refs[sum(counts[r0:t0]):sum(counts[r0:t1])],
             w_refs[sum(counts[c0:u0]):sum(counts[c0:u1])], uppers, outs[3 * i:3 * i + 3])
     if not finish:
-        outs[-1][...] = partner_ref[...]
+        if span[0] == 0:
+            near, far = partner_ref[...].astype(jnp.float32), far_ref[...].astype(jnp.float32)
+            outs[-1][:, :own_rows] = jnp.where(lead, near, far)
+            outs[-1][:, own_rows:] = jnp.where(lead, far, near)
+        else:
+            outs[-1][...] = partner_ref[...]
         return
     stats_ref = outs[-1]
     every = [*earlier, *outs[2:3 * len(tiles):3]]
@@ -310,11 +315,13 @@
     chip_rows = total // groups
     me = me_ref[0]
     lead = (me & 1) == 0
+    own, first, second, swapped = [ref[...] for ref in stat_refs]
+    values = [own, jnp.where(lead, swapped, first), second, jnp.where(lead, first, swapped)]
     parts, partners = [], []
-    for j, ref in enumerate(stat_refs):
+    for j, value in enumerate(values):
         parts.append(jnp.concatenate(
-            [ref[:, (i ^ j) * chip_rows:((i ^ j) + 1) * chip_rows] for i in range(groups)], axis=1))
-        partners.append(ref[count:count + 1, :chip_rows])
+            [value[:, (i ^ j) * chip_rows:((i ^ j) + 1) * chip_rows] for i in range(groups)], axis=1))
+        partners.append(value[count:count + 1, :chip_rows])
     peak = functools.reduce(jnp.maximum, parts)
     mass = functools.reduce(lambda a, b: a + b, [jnp.exp2(part - peak) for part in parts])
     partner_row = jnp.concatenate(partners, axis=1)
@@ -465,15 +472,15 @@
     mine = jnp.where(lead, queries, documents)
     other = jnp.where(lead, documents, queries)
     got = swap(other)
-    small = WIDTHS * total * total * 4 <= 16 << 20
+    small = groups == 4 and WIDTHS * total * total * 4 <= 16 << 20
     cut = own_rows - 16 if small and own_rows >= 32 else own_rows
     v = {0: [mine, got]}
     w = {0: [swap(mine), other]}
     for stage in reversed(range(stages)):
         for j in sorted(v):
             parts = v[j]
-            if j == 0 and stage == stages - 1 and cut < own_rows:
-                parts = [mine, got[:cut], got[cut:]]
+            if small and j == 0:
+                parts = [mine, got[:cut], got[cut:]] if stage else [jnp.concatenate(v[0], axis=0)]
             v[j | 1 << stage] = [
                 along(part, stage) for part in parts]
     for j in range(1, groups):
@@ -482,12 +489,8 @@
     v_list = [part for j in range(groups) for part in v[j]]
     w_list = [part for j in range(groups) for part in w[j]]
 
-    own_partner = partner.astype(jnp.float32).reshape(1, own_rows)
+    own_partner = partner.reshape(1, own_rows)
     far_partner = swap(own_partner)
-    chip_partner = jnp.where(
-        lead,
-        jnp.concatenate([own_partner, far_partner], axis=1),
-        jnp.concatenate([far_partner, own_partner], axis=1))
 
     vmem = pl.BlockSpec(memory_space=pltpu.VMEM)
     smem = pl.BlockSpec(memory_space=pltpu.SMEM)
@@ -506,6 +509,9 @@
             for j in range(groups)]
 
     if not small:
+        near, far = own_partner.astype(jnp.float32), far_partner.astype(jnp.float32)
+        chip_partner = jnp.where(
+            lead, jnp.concatenate([near, far], axis=1), jnp.concatenate([far, near], axis=1))
         limit = 60 << 20
         stats = pl.pallas_call(
             functools.partial(stats_kernel, pieces, uppers),
@@ -540,7 +546,7 @@
         limit = 20 << 20
         params = pltpu.CompilerParams(vmem_limit_bytes=limit)
 
-        def tile(span, partner_row, earlier=()):
+        def tile(span, partner_row, far_row, earlier=()):
             first, end, left, right = extent([shapes[i] for i in span])
             operands = v_list[sum(counts[:first]):sum(counts[:end])]
             operands += w_list[sum(counts[:left]):sum(counts[:right])]
@@ -556,22 +562,26 @@
                 functools.partial(
                     tile_kernel, span, counts, uppers, own_rows, len(earlier)),
                 out_shape=result + stat_shapes,
-                in_specs=[smem] + [vmem] * (1 + len(operands) + len(earlier)),
+                in_specs=[smem] + [vmem] * (2 + len(operands) + len(earlier)),
                 out_specs=[vmem] * (len(result) + 1),
                 compiler_params=params,
                 cost_estimate=pl.CostEstimate(
                     flops=6 * area * feature_dim, transcendentals=0,
                     bytes_accessed=2 * total * feature_dim),
-            )(me, partner_row, *operands, *[one[2] for one in earlier])
+            )(me, partner_row, far_row, *operands, *[one[2] for one in earlier])
             return [arrays[3 * i:3 * i + 3] for i in range(len(span))], last_array
 
-        done, chip_partner = tile([0], chip_partner)
+        done, chip_partner = tile([0], own_partner, far_partner)
         for at in (1, 2, 3):
-            more, chip_partner = tile([at], chip_partner)
+            more, chip_partner = tile([at], chip_partner, far_partner)
             done += more
-        more, stats = tile([4], chip_partner, done)
+        more, stats = tile([4], chip_partner, far_partner, done)
         done += more
-        common = [me, *gathered(stats), *[t[0] for t in done], *[t[1] for t in done],
+        first = exchange(
+            stats, lambda i: query_mask(1) if i & 1 else query_mask(3))
+        second = exchange(stats, lambda i: query_mask(2))
+        swapped = swap(first)
+        common = [me, stats, first, second, swapped, *[t[0] for t in done], *[t[1] for t in done],
                   *[t[2] for t in done], *w_list]
         near = segments_of(groups)[-1][0]
         widest = feature_dim - uppers[-2]

time: 73.9 us -> 78.9 us (1.068)
  waiting for transfers between devices: 31 us -> 35.8 us
  Pallas kernels: 10.7 us -> 12.6 us
    ppermute x31 -> x29, waiting for transfers between devices: 31 us -> 35.8 us  [exchange(): return lax.ppermute(x, AXES, [(i, i ^ masks_of(i)) for i in range(devices)])]
    pallas_call x5, Pallas kernels: 6.26 us -> 8.27 us  [tile(): pl.pallas_call(functools.partial(tile_kernel, span, counts, uppers, own_r...]
    ppermute x31 -> x29, starting transfers between devices: 27.3 us -> 26.8 us  [exchange(): return lax.ppermute(x, AXES, [(i, i ^ masks_of(i)) for i in range(devices)])]
  transfers between devices with their start and end apart: 31 -> 29, of which waited for: 11 -> 13; matrix products, arithmetic and copies ran while one was open for 2% -> 1% of each run, Pallas kernels for 6% -> 7%
where the time goes in v4:
time: 78.9 us; the launch traced here: 78.7 us
  waiting for transfers between devices  35.8 us (45%)
  starting transfers between devices  26.8 us (34%)
  Pallas kernels  12.6 us (16%)
  other arithmetic  2.47 us (3%)
  between operations  0.83 us (1%)
    ppermute x29, waiting for transfers between devices, exchange(): return lax.ppermute(x, AXES, [(i, i ^ masks_of(i)) for i in range(devices)])  35.8 us
    ppermute x29, starting transfers between devices, exchange(): return lax.ppermute(x, AXES, [(i, i ^ masks_of(i)) for i in range(devices)])  26.8 us
    pallas_call x5, Pallas kernels, tile(): pl.pallas_call(functools.partial(tile_kernel, span, counts, uppers, own_r...  8.27 us
    pallas_call x2, Pallas kernels, bands(): pl.pallas_call(functools.partial(kernel, groups, uppers, own_rows, docume...  4.37 us
  transfers between devices with their start and end apart: 29, of which 13 were waited for; matrix products, arithmetic and copies ran while one was open for 1% of the time, Pallas kernels for 7%

profile of v4, /device:TPU:0, one launch (start us, length us, event | category | flops | bytes accessed | tf_op | source)
XLA Modules:
  0.0 78.7 jit_solution(9666805365668881567)
XLA Ops:
  2.3 1.2 %collective-permute-done.1.refs_4_ = bf16[64,2048]{1,0:T(8,128)(2,1)S(1)} collective-permute-done((bf16[64,2048]{1,0:T(8,128)(2,1)S(1)}, bf16[64,2048]{1,0:T(8,128)(2,1)S(1)}, u32[]{:S(2)}, u32[]{:S(2)}) %collective-permute-start.1) | collective-permute-done | bytes 262176 | tf_op jit(solution)/shard_map/ppermute | solution.py:464
  3.5 2.9 %collective-permute-start.2 = (bf16[128,2048]{1,0:T(8,128)(2,1)S(1)}, bf16[128,2048]{1,0:T(8,128)(2,1)S(1)}, u32[]{:S(2)}, u32[]{:S(2)}) collective-permute-start(bf16[128,2048]{1,0:T(8,128)(2,1)S(1)} %pad_maximum_fusion), channel_id=1, source_target_pairs={{0,2},{1,5},{2,0},{3,7},{4,6},{5,1},{6,4},{7,3},{8,10},{9,13},{10,... | collective-permute-start | bytes 1572872 | tf_op jit(solution)/shard_map/ppermute | solution.py:464
  6.4 1.6 %collective-permute-start.5 = (bf16[64,2048]{1,0:T(8,128)(2,1)S(1)}, bf16[64,2048]{1,0:T(8,128)(2,1)S(1)}, u32[]{:S(2)}, u32[]{:S(2)}) collective-permute-start(bf16[64,2048]{1,0:T(8,128)(2,1)S(1)} %get-tuple-element.71.refs_3_), channel_id=1, source_target_pairs={{0,8},{1,17},{2,10},{3,19},{4,12},{5,21},{6,14},{7,23},{8,0},{9,25... | collective-permute-start | bytes 786440 | tf_op jit(solution)/shard_map/ppermute | solution.py:464
  8.0 5.6 %collective-permute-done.2.refs_5_ = bf16[128,2048]{1,0:T(8,128)(2,1)S(1)} collective-permute-done((bf16[128,2048]{1,0:T(8,128)(2,1)S(1)}, bf16[128,2048]{1,0:T(8,128)(2,1)S(1)}, u32[]{:S(2)}, u32[]{:S(2)}) %collective-permute-start.2) | collective-permute-done | bytes 524320 | tf_op jit(solution)/shard_map/ppermute | solution.py:464
  14.1 2.2 %collective-permute-start.6 = (bf16[48,2048]{1,0:T(8,128)(2,1)S(1)}, bf16[48,2048]{1,0:T(8,128)(2,1)S(1)}, u32[]{:S(2)}, u32[]{:S(2)}) collective-permute-start(bf16[48,2048]{1,0:T(8,128)(2,1)S(1)} %slice.32), channel_id=1, source_target_pairs={{0,8},{1,17},{2,10},{3,19},{4,12},{5,21},{6,14},{7,23},{8,0},{9,25... | collective-permute-start | bytes 589832 | tf_op jit(solution)/shard_map/ppermute | solution.py:464
  16.3 1.5 %collective-permute-start.11 = (bf16[64,2048]{1,0:T(8,128)(2,1)S(1)}, bf16[64,2048]{1,0:T(8,128)(2,1)}, u32[]{:S(2)}, u32[]{:S(2)}) collective-permute-start(bf16[64,2048]{1,0:T(8,128)(2,1)S(1)} %collective-permute-done.5.refs_3_.refs_6_), channel_id=1, source_target_pairs={{0,2},{1,5},{2,0},{3,7},{4,6},{5,1},{6,4},{7,3},{8,10},{9,13},{10,... | collective-permute-start | bytes 786440 | tf_op jit(solution)/shard_map/ppermute | solution.py:464
  19.1 1.6 %collective-permute-start.7 = (bf16[16,2048]{1,0:T(8,128)(2,1)S(1)}, bf16[16,2048]{1,0:T(8,128)(2,1)S(1)}, u32[]{:S(2)}, u32[]{:S(2)}) collective-permute-start(bf16[16,2048]{1,0:T(8,128)(2,1)S(1)} %slice.33), channel_id=1, source_target_pairs={{0,8},{1,17},{2,10},{3,19},{4,12},{5,21},{6,14},{7,23},{8,0},{9,25... | collective-permute-start | bytes 196616 | tf_op jit(solution)/shard_map/ppermute | solution.py:464
  21.7 2.2 %collective-permute-start.12 = (bf16[48,2048]{1,0:T(8,128)(2,1)S(1)}, bf16[48,2048]{1,0:T(8,128)(2,1)S(1)}, u32[]{:S(2)}, u32[]{:S(2)}) collective-permute-start(bf16[48,2048]{1,0:T(8,128)(2,1)S(1)} %collective-permute-done.6.refs_4_.refs_7_), channel_id=1, source_target_pairs={{0,2},{1,5},{2,0},{3,7},{4,6},{5,1},{6,4},{7,3},{8,10},{9,13},{10,... | collective-permute-start | bytes 589832 | tf_op jit(solution)/shard_map/ppermute | solution.py:464
  24.0 1.5 %collective-permute-start.13 = (bf16[16,2048]{1,0:T(8,128)(2,1)S(1)}, bf16[16,2048]{1,0:T(8,128)(2,1)}, u32[]{:S(2)}, u32[]{:S(2)}) collective-permute-start(bf16[16,2048]{1,0:T(8,128)(2,1)S(1)} %collective-permute-done.7.refs_5_.refs_8_), channel_id=1, source_target_pairs={{0,2},{1,5},{2,0},{3,7},{4,6},{5,1},{6,4},{7,3},{8,10},{9,13},{10,... | collective-permute-start | bytes 196616 | tf_op jit(solution)/shard_map/ppermute | solution.py:464
  25.5 2.9 %collective-permute-done.13.refs_5_.refs_11_ = bf16[16,2048]{1,0:T(8,128)(2,1)} collective-permute-done((bf16[16,2048]{1,0:T(8,128)(2,1)S(1)}, bf16[16,2048]{1,0:T(8,128)(2,1)}, u32[]{:S(2)}, u32[]{:S(2)}) %collective-permute-start.13) | collective-permute-done | bytes 65568 | tf_op jit(solution)/shard_map/ppermute | solution.py:464
  31.5 1.5 %shard_map.52 = (f32[9,384,128]{2,1,0:T(8,128)S(1)}, f32[384,128]{1,0:T(8,128)S(1)}, f32[32,384]{1,0:T(8,128)S(1)}, f32[1,128]{1,0:T(1,128)S(1)}) custom-call(s32[1]{0:T(128)} %bitcast.refs_0_, f32[1,128]{1,0:T(1,128)S(1)} %get-tuple-element.34.refs_1_, s32[1,64]{1,0:T(1,128)S(1)} %collective-permute-done.refs_2_, ...), custom_call_target="tpu_custom_call" | custom-call | flops 603979776 | bytes 2097152 | tf_op jit(solution)/shard_map/pallas_call | solution.py:561
  32.9 2.0 %shard_map.53 = (f32[9,128,384]{2,1,0:T(8,128)S(1)}, f32[128,128]{1,0:T(8,128)S(1)}, f32[32,384]{1,0:T(8,128)S(1)}, f32[1,128]{1,0:T(1,128)S(1)}) custom-call(s32[1]{0:T(128)} %bitcast.refs_0_, f32[1,128]{1,0:T(1,128)S(1)} %get-tuple-element.35.refs_1_, s32[1,64]{1,0:T(1,128)S(1)} %collective-permute-done.refs_2_, ...), custom_call_target="tpu_custom_call" | custom-call | flops 603979776 | bytes 2097152 | tf_op jit(solution)/shard_map/pallas_call | solution.py:561
  34.9 2.9 %shard_map.54 = (f32[9,512,128]{2,1,0:T(8,128)S(1)}, f32[512,128]{1,0:T(8,128)S(1)}, f32[32,512]{1,0:T(8,128)S(1)}, f32[16,512]{1,0:T(8,128)S(1)}) custom-call(s32[1]{0:T(128)} %bitcast.refs_0_, f32[1,128]{1,0:T(1,128)S(1)} %get-tuple-element.36.refs_1_, s32[1,64]{1,0:T(1,128)S(1)} %collective-permute-done.refs_2_, ...), custom_call_target="tpu_custom_call" | custom-call | flops 805306368 | bytes 2097152 | tf_op jit(solution)/shard_map/pallas_call | solution.py:561
  37.8 3.1 %collective-permute-start.17 = (f32[16,512]{1,0:T(8,128)S(1)}, f32[16,512]{1,0:T(8,128)S(1)}, u32[]{:S(2)}, u32[]{:S(2)}) collective-permute-start(f32[16,512]{1,0:T(8,128)S(1)} %get-tuple-element.41.refs_1_), channel_id=1, source_target_pairs={{0,10},{1,3},{2,8},{3,1},{4,14},{5,7},{6,12},{7,5},{8,2},{9,11},{1... | collective-permute-start | bytes 98312 | tf_op jit(solution)/shard_map/ppermute | solution.py:464
  41.3 1.5 %collective-permute-done.17.refs_2_ = f32[16,512]{1,0:T(8,128)S(1)} collective-permute-done((f32[16,512]{1,0:T(8,128)S(1)}, f32[16,512]{1,0:T(8,128)S(1)}, u32[]{:S(2)}, u32[]{:S(2)}) %collective-permute-start.17) | collective-permute-done | bytes 32800 | tf_op jit(solution)/shard_map/ppermute | solution.py:464
  42.8 2.0 %collective-permute-done.18.refs_3_ = f32[16,512]{1,0:T(8,128)S(1)} collective-permute-done((f32[16,512]{1,0:T(8,128)S(1)}, f32[16,512]{1,0:T(8,128)S(1)}, u32[]{:S(2)}, u32[]{:S(2)}) %collective-permute-start.18) | collective-permute-done | bytes 32800 | tf_op jit(solution)/shard_map/ppermute | solution.py:464
  45.3 3.9 %shard_map.56 = (f32[128,1024]{1,0:T(8,128)S(1)}, bf16[128,1024]{1,0:T(8,128)(2,1)S(1)}, f32[128,1024]{1,0:T(8,128)S(1)}, bf16[128,1024]{1,0:T(8,128)(2,1)S(1)},...) custom-call(s32[1]{0:T(128)} %bitcast.refs_0_, ...), custom_call_target="tpu_custom_call" | custom-call | flops 1073741824 | bytes 4194304 | tf_op jit(solution)/shard_map/pallas_call | solution.py:590
  49.2 1.1 %collective-permute-start.20 = (bf16[128,1024]{1,0:T(8,128)(2,1)S(1)}, bf16[128,1024]{1,0:T(8,128)(2,1)S(1)}, u32[]{:S(2)}, u32[]{:S(2)}) collective-permute-start(bf16[128,1024]{1,0:T(8,128)(2,1)S(1)} %get-tuple-element.55), channel_id=1, source_target_pairs={{0,2},{1,5},{2,0},{3,7},{4,6},{5,1},{6,4},{7,3},{8,10},{9,13},{10,... | collective-permute-start | bytes 786440 | tf_op jit(solution)/shard_map/ppermute | solution.py:464
  53.3 2.3 %collective-permute-done.20 = bf16[128,1024]{1,0:T(8,128)(2,1)S(1)} collective-permute-done((bf16[128,1024]{1,0:T(8,128)(2,1)S(1)}, bf16[128,1024]{1,0:T(8,128)(2,1)S(1)}, u32[]{:S(2)}, u32[]{:S(2)}) %collective-permute-start.20) | collective-permute-done | bytes 262176 | tf_op jit(solution)/shard_map/ppermute | solution.py:464
  55.8 8.2 %collective-permute-done.24 = bf16[128,1024]{1,0:T(8,128)(2,1)S(1)} collective-permute-done((bf16[128,1024]{1,0:T(8,128)(2,1)S(1)}, bf16[128,1024]{1,0:T(8,128)(2,1)S(1)}, u32[]{:S(2)}, u32[]{:S(2)}) %collective-permute-start.24) | collective-permute-done | bytes 262176 | tf_op jit(solution)/shard_map/ppermute | solution.py:464
  64.1 1.2 %collective-permute-start.25 = (bf16[128,1024]{1,0:T(8,128)(2,1)S(1)}, bf16[128,1024]{1,0:T(8,128)(2,1)S(1)}, u32[]{:S(2)}, u32[]{:S(2)}) collective-permute-start(bf16[128,1024]{1,0:T(8,128)(2,1)S(1)} %add_convert_fusion), channel_id=1, source_target_pairs={{0,8},{1,17},{2,10},{3,19},{4,12},{5,21},{6,14},{7,23},{8,0},{9,25... | collective-permute-start | bytes 786440 | tf_op jit(solution)/shard_map/ppermute | solution.py:464
  67.1 5.0 %collective-permute-done.25 = bf16[128,1024]{1,0:T(8,128)(2,1)S(1)} collective-permute-done((bf16[128,1024]{1,0:T(8,128)(2,1)S(1)}, bf16[128,1024]{1,0:T(8,128)(2,1)S(1)}, u32[]{:S(2)}, u32[]{:S(2)}) %collective-permute-start.25) | collective-permute-done | bytes 262176 | tf_op jit(solution)/shard_map/ppermute | solution.py:464
  72.5 2.4 %collective-permute-done.22 = bf16[64,1024]{1,0:T(8,128)(2,1)S(1)} collective-permute-done((bf16[64,1024]{1,0:T(8,128)(2,1)S(1)}, bf16[64,1024]{1,0:T(8,128)(2,1)S(1)}, u32[]{:S(2)}, u32[]{:S(2)}) %collective-permute-start.22) | collective-permute-done | bytes 131104 | tf_op jit(solution)/shard_map/ppermute | solution.py:464
  74.9 2.7 %collective-permute-done.27 = bf16[64,1024]{1,0:T(8,128)(2,1)S(1)} collective-permute-done((bf16[64,1024]{1,0:T(8,128)(2,1)S(1)}, bf16[64,1024]{1,0:T(8,128)(2,1)S(1)}, u32[]{:S(2)}, u32[]{:S(2)}) %collective-permute-start.27) | collective-permute-done | bytes 131104 | tf_op jit(solution)/shard_map/ppermute | solution.py:464
  (57 shorter events, 15.0 us)
Async XLA Ops:
  3.5 10.1 %collective-permute-start.2 = (bf16[128,2048]{1,0:T(8,128)(2,1)S(1)}, bf16[128,2048]{1,0:T(8,128)(2,1)S(1)}, u32[]{:S(2)}, u32[]{:S(2)}) collective-permute-start(bf16[128,2048]{1,0:T(8,128)(2,1)S(1)} %pad_maximum_fusion), channel_id=1, source_target_pairs={{0,2},{1,5},{2,0},{3,7},{4,6},{5,1},{6,4},{7,3},{8,10},{9,13},{10,... | collective-permute-start | bytes 1572872 | tf_op jit(solution)/shard_map/ppermute | solution.py:464
  6.4 9.9 %collective-permute-start.5 = (bf16[64,2048]{1,0:T(8,128)(2,1)S(1)}, bf16[64,2048]{1,0:T(8,128)(2,1)S(1)}, u32[]{:S(2)}, u32[]{:S(2)}) collective-permute-start(bf16[64,2048]{1,0:T(8,128)(2,1)S(1)} %get-tuple-element.71.refs_3_), channel_id=1, source_target_pairs={{0,8},{1,17},{2,10},{3,19},{4,12},{5,21},{6,14},{7,23},{8,0},{9,25... | collective-permute-start | bytes 786440 | tf_op jit(solution)/shard_map/ppermute | solution.py:464
  13.6 15.4 %collective-permute-start.4 = (bf16[128,2048]{1,0:T(8,128)(2,1)S(1)}, bf16[128,2048]{1,0:T(8,128)(2,1)S(1)}, u32[]{:S(2)}, u32[]{:S(2)}) collective-permute-start(bf16[128,2048]{1,0:T(8,128)(2,1)S(1)} %collective-permute-done.2.refs_5_), channel_id=1, source_target_pairs={{0,1},{1,0},{2,3},{3,2},{4,5},{5,4},{6,7},{7,6},{8,9},{9,8},{10,11... | collective-permute-start | bytes 1572872 | tf_op jit(solution)/shard_map/ppermute | solution.py:464
  13.6 10.3 %collective-permute-start.3 = (bf16[64,2048]{1,0:T(8,128)(2,1)S(1)}, bf16[64,2048]{1,0:T(8,128)(2,1)S(1)}, u32[]{:S(2)}, u32[]{:S(2)}) collective-permute-start(bf16[64,2048]{1,0:T(8,128)(2,1)S(1)} %get-tuple-element.71.refs_3_), channel_id=1, source_target_pairs={{0,1},{1,0},{2,3},{3,2},{4,5},{5,4},{6,7},{7,6},{8,9},{9,8},{10,11... | collective-permute-start | bytes 786440 | tf_op jit(solution)/shard_map/ppermute | solution.py:464
  14.1 7.6 %collective-permute-start.6 = (bf16[48,2048]{1,0:T(8,128)(2,1)S(1)}, bf16[48,2048]{1,0:T(8,128)(2,1)S(1)}, u32[]{:S(2)}, u32[]{:S(2)}) collective-permute-start(bf16[48,2048]{1,0:T(8,128)(2,1)S(1)} %slice.32), channel_id=1, source_target_pairs={{0,8},{1,17},{2,10},{3,19},{4,12},{5,21},{6,14},{7,23},{8,0},{9,25... | collective-permute-start | bytes 589832 | tf_op jit(solution)/shard_map/ppermute | solution.py:464
  16.3 12.1 %collective-permute-start.11 = (bf16[64,2048]{1,0:T(8,128)(2,1)S(1)}, bf16[64,2048]{1,0:T(8,128)(2,1)}, u32[]{:S(2)}, u32[]{:S(2)}) collective-permute-start(bf16[64,2048]{1,0:T(8,128)(2,1)S(1)} %collective-permute-done.5.refs_3_.refs_6_), channel_id=1, source_target_pairs={{0,2},{1,5},{2,0},{3,7},{4,6},{5,1},{6,4},{7,3},{8,10},{9,13},{10,... | collective-permute-start | bytes 786440 | tf_op jit(solution)/shard_map/ppermute | solution.py:464
  19.1 5.0 %collective-permute-start.7 = (bf16[16,2048]{1,0:T(8,128)(2,1)S(1)}, bf16[16,2048]{1,0:T(8,128)(2,1)S(1)}, u32[]{:S(2)}, u32[]{:S(2)}) collective-permute-start(bf16[16,2048]{1,0:T(8,128)(2,1)S(1)} %slice.33), channel_id=1, source_target_pairs={{0,8},{1,17},{2,10},{3,19},{4,12},{5,21},{6,14},{7,23},{8,0},{9,25... | collective-permute-start | bytes 196616 | tf_op jit(solution)/shard_map/ppermute | solution.py:464
  21.7 7.2 %collective-permute-start.12 = (bf16[48,2048]{1,0:T(8,128)(2,1)S(1)}, bf16[48,2048]{1,0:T(8,128)(2,1)S(1)}, u32[]{:S(2)}, u32[]{:S(2)}) collective-permute-start(bf16[48,2048]{1,0:T(8,128)(2,1)S(1)} %collective-permute-done.6.refs_4_.refs_7_), channel_id=1, source_target_pairs={{0,2},{1,5},{2,0},{3,7},{4,6},{5,1},{6,4},{7,3},{8,10},{9,13},{10,... | collective-permute-start | bytes 589832 | tf_op jit(solution)/shard_map/ppermute | solution.py:464
  23.9 7.5 %collective-permute-start.8 = (bf16[64,2048]{1,0:T(8,128)(2,1)S(1)}, bf16[64,2048]{1,0:T(8,128)(2,1)S(1)}, u32[]{:S(2)}, u32[]{:S(2)}) collective-permute-start(bf16[64,2048]{1,0:T(8,128)(2,1)S(1)} %collective-permute-done.5.refs_3_.refs_6_), channel_id=1, source_target_pairs={{0,1},{1,0},{2,3},{3,2},{4,5},{5,4},{6,7},{7,6},{8,9},{9,8},{10,11... | collective-permute-start | bytes 786440 | tf_op jit(solution)/shard_map/ppermute | solution.py:464
  24.0 4.4 %collective-permute-start.13 = (bf16[16,2048]{1,0:T(8,128)(2,1)S(1)}, bf16[16,2048]{1,0:T(8,128)(2,1)}, u32[]{:S(2)}, u32[]{:S(2)}) collective-permute-start(bf16[16,2048]{1,0:T(8,128)(2,1)S(1)} %collective-permute-done.7.refs_5_.refs_8_), channel_id=1, source_target_pairs={{0,2},{1,5},{2,0},{3,7},{4,6},{5,1},{6,4},{7,3},{8,10},{9,13},{10,... | collective-permute-start | bytes 196616 | tf_op jit(solution)/shard_map/ppermute | solution.py:464
  28.4 6.5 %collective-permute-start.14 = (bf16[64,2048]{1,0:T(8,128)(2,1)}, bf16[64,2048]{1,0:T(8,128)(2,1)S(1)}, u32[]{:S(2)}, u32[]{:S(2)}) collective-permute-start(bf16[64,2048]{1,0:T(8,128)(2,1)} %collective-permute-done.11.refs_3_.refs_9_), channel_id=1, source_target_pairs={{0,1},{1,0},{2,3},{3,2},{4,5},{5,4},{6,7},{7,6},{8,9},{9,8},{10,11... | collective-permute-start | bytes 786440 | tf_op jit(solution)/shard_map/ppermute | solution.py:464
  29.0 5.9 %collective-permute-start.15 = (bf16[48,2048]{1,0:T(8,128)(2,1)S(1)}, bf16[48,2048]{1,0:T(8,128)(2,1)S(1)}, u32[]{:S(2)}, u32[]{:S(2)}) collective-permute-start(bf16[48,2048]{1,0:T(8,128)(2,1)S(1)} %collective-permute-done.12.refs_4_.refs_10_), channel_id=1, source_target_pairs={{0,1},{1,0},{2,3},{3,2},{4,5},{5,4},{6,7},{7,6},{8,9},{9,8},{10,11... | collective-permute-start | bytes 589832 | tf_op jit(solution)/shard_map/ppermute | solution.py:464
  31.4 3.5 %collective-permute-start.16 = (bf16[16,2048]{1,0:T(8,128)(2,1)}, bf16[16,2048]{1,0:T(8,128)(2,1)S(1)}, u32[]{:S(2)}, u32[]{:S(2)}) collective-permute-start(bf16[16,2048]{1,0:T(8,128)(2,1)} %collective-permute-done.13.refs_5_.refs_11_), channel_id=1, source_target_pairs={{0,1},{1,0},{2,3},{3,2},{4,5},{5,4},{6,7},{7,6},{8,9},{9,8},{10,11... | collective-permute-start | bytes 196616 | tf_op jit(solution)/shard_map/ppermute | solution.py:464
  37.8 5.0 %collective-permute-start.17 = (f32[16,512]{1,0:T(8,128)S(1)}, f32[16,512]{1,0:T(8,128)S(1)}, u32[]{:S(2)}, u32[]{:S(2)}) collective-permute-start(f32[16,512]{1,0:T(8,128)S(1)} %get-tuple-element.41.refs_1_), channel_id=1, source_target_pairs={{0,10},{1,3},{2,8},{3,1},{4,14},{5,7},{6,12},{7,5},{8,2},{9,11},{1... | collective-permute-start | bytes 98312 | tf_op jit(solution)/shard_map/ppermute | solution.py:464
  40.9 3.9 %collective-permute-start.18 = (f32[16,512]{1,0:T(8,128)S(1)}, f32[16,512]{1,0:T(8,128)S(1)}, u32[]{:S(2)}, u32[]{:S(2)}) collective-permute-start(f32[16,512]{1,0:T(8,128)S(1)} %get-tuple-element.41.refs_1_), channel_id=1, source_target_pairs={{0,8},{1,9},{2,10},{3,11},{4,12},{5,13},{6,14},{7,15},{8,0},{9,1},... | collective-permute-start | bytes 98312 | tf_op jit(solution)/shard_map/ppermute | solution.py:464
  49.2 6.4 %collective-permute-start.20 = (bf16[128,1024]{1,0:T(8,128)(2,1)S(1)}, bf16[128,1024]{1,0:T(8,128)(2,1)S(1)}, u32[]{:S(2)}, u32[]{:S(2)}) collective-permute-start(bf16[128,1024]{1,0:T(8,128)(2,1)S(1)} %get-tuple-element.55), channel_id=1, source_target_pairs={{0,2},{1,5},{2,0},{3,7},{4,6},{5,1},{6,4},{7,3},{8,10},{9,13},{10,... | collective-permute-start | bytes 786440 | tf_op jit(solution)/shard_map/ppermute | solution.py:464
  50.3 15.0 %collective-permute-start.21 = (bf16[128,1024]{1,0:T(8,128)(2,1)S(1)}, bf16[128,1024]{1,0:T(8,128)(2,1)S(1)}, u32[]{:S(2)}, u32[]{:S(2)}) collective-permute-start(bf16[128,1024]{1,0:T(8,128)(2,1)S(1)} %get-tuple-element.58), channel_id=1, source_target_pairs={{0,2},{1,5},{2,0},{3,7},{4,6},{5,1},{6,4},{7,3},{8,10},{9,13},{10,... | collective-permute-start | bytes 786440 | tf_op jit(solution)/shard_map/ppermute | solution.py:464
  51.3 15.8 %collective-permute-start.23 = (bf16[128,1024]{1,0:T(8,128)(2,1)S(1)}, bf16[128,1024]{1,0:T(8,128)(2,1)S(1)}, u32[]{:S(2)}, u32[]{:S(2)}) collective-permute-start(bf16[128,1024]{1,0:T(8,128)(2,1)S(1)} %get-tuple-element.60), channel_id=1, source_target_pairs={{0,2},{1,5},{2,0},{3,7},{4,6},{5,1},{6,4},{7,3},{8,10},{9,13},{10,... | collective-permute-start | bytes 786440 | tf_op jit(solution)/shard_map/ppermute | solution.py:464
  52.4 11.7 %collective-permute-start.24 = (bf16[128,1024]{1,0:T(8,128)(2,1)S(1)}, bf16[128,1024]{1,0:T(8,128)(2,1)S(1)}, u32[]{:S(2)}, u32[]{:S(2)}) collective-permute-start(bf16[128,1024]{1,0:T(8,128)(2,1)S(1)} %get-tuple-element.62), channel_id=1, source_target_pairs={{0,2},{1,5},{2,0},{3,7},{4,6},{5,1},{6,4},{7,3},{8,10},{9,13},{10,... | collective-permute-start | bytes 786440 | tf_op jit(solution)/shard_map/ppermute | solution.py:464
  55.7 21.8 %collective-permute-start.26 = (f32[64,1024]{1,0:T(8,128)S(1)}, f32[64,1024]{1,0:T(8,128)S(1)}, u32[]{:S(2)}, u32[]{:S(2)}) collective-permute-start(f32[64,1024]{1,0:T(8,128)S(1)} %get-tuple-element.63), channel_id=1, source_target_pairs={{0,1},{1,0},{2,3},{3,2},{4,5},{5,4},{6,7},{7,6},{8,9},{9,8},{10,11... | collective-permute-start | bytes 786440 | tf_op jit(solution)/shard_map/ppermute | solution.py:464
  64.1 7.9 %collective-permute-start.25 = (bf16[128,1024]{1,0:T(8,128)(2,1)S(1)}, bf16[128,1024]{1,0:T(8,128)(2,1)S(1)}, u32[]{:S(2)}, u32[]{:S(2)}) collective-permute-start(bf16[128,1024]{1,0:T(8,128)(2,1)S(1)} %add_convert_fusion), channel_id=1, source_target_pairs={{0,8},{1,17},{2,10},{3,19},{4,12},{5,21},{6,14},{7,23},{8,0},{9,25... | collective-permute-start | bytes 786440 | tf_op jit(solution)/shard_map/ppermute | solution.py:464
  65.5 9.4 %collective-permute-start.22 = (bf16[64,1024]{1,0:T(8,128)(2,1)S(1)}, bf16[64,1024]{1,0:T(8,128)(2,1)S(1)}, u32[]{:S(2)}, u32[]{:S(2)}) collective-permute-start(bf16[64,1024]{1,0:T(8,128)(2,1)S(1)} %get-tuple-element.72), channel_id=1, source_target_pairs={{0,8},{1,17},{2,10},{3,19},{4,12},{5,21},{6,14},{7,23},{8,0},{9,25... | collective-permute-start | bytes 393224 | tf_op jit(solution)/shard_map/ppermute | solution.py:464
  66.4 11.2 %collective-permute-start.27 = (bf16[64,1024]{1,0:T(8,128)(2,1)S(1)}, bf16[64,1024]{1,0:T(8,128)(2,1)S(1)}, u32[]{:S(2)}, u32[]{:S(2)}) collective-permute-start(bf16[64,1024]{1,0:T(8,128)(2,1)S(1)} %get-tuple-element.73), channel_id=1, source_target_pairs={{0,9},{1,16},{2,11},{3,18},{4,13},{5,20},{6,15},{7,22},{8,1},{9,24... | collective-permute-start | bytes 393224 | tf_op jit(solution)/shard_map/ppermute | solution.py:464
  72.2 5.4 %collective-permute-start.28 = (f32[64,1024]{1,0:T(8,128)S(1)}, f32[64,1024]{1,0:T(8,128)S(1)}, u32[]{:S(2)}, u32[]{:S(2)}) collective-permute-start(f32[64,1024]{1,0:T(8,128)S(1)} %get-tuple-element.67), channel_id=1, source_target_pairs={{0,1},{1,0},{2,3},{3,2},{4,5},{5,4},{6,7},{7,6},{8,9},{9,8},{10,11... | collective-permute-start | bytes 786440 | tf_op jit(solution)/shard_map/ppermute | solution.py:464
  (6 other events, 27.7 us)

commit v5 on v4

--- a/solution.py
+++ b/solution.py
@@ -316,7 +316,7 @@
     me = me_ref[0]
     lead = (me & 1) == 0
     own, first, second, swapped = [ref[...] for ref in stat_refs]
-    values = [own, jnp.where(lead, swapped, first), second, jnp.where(lead, first, swapped)]
+    values = [own, jnp.where(lead, first, swapped), second, jnp.where(lead, swapped, first)]
     parts, partners = [], []
     for j, value in enumerate(values):
         parts.append(jnp.concatenate(
@@ -479,8 +479,8 @@
     for stage in reversed(range(stages)):
         for j in sorted(v):
             parts = v[j]
-            if small and j == 0:
-                parts = [mine, got[:cut], got[cut:]] if stage else [jnp.concatenate(v[0], axis=0)]
+            if small and j == 0 and stage:
+                parts = [mine, got[:cut], got[cut:]]
             v[j | 1 << stage] = [
                 along(part, stage) for part in parts]
     for j in range(1, groups):
@@ -578,7 +578,7 @@
         more, stats = tile([4], chip_partner, far_partner, done)
         done += more
         first = exchange(
-            stats, lambda i: query_mask(1) if i & 1 else query_mask(3))
+            stats, lambda i: query_mask(3) if i & 1 else query_mask(1))
         second = exchange(stats, lambda i: query_mask(2))
         swapped = swap(first)
         common = [me, stats, first, second, swapped, *[t[0] for t in done], *[t[1] for t in done],

time: 78.9 us -> 75.3 us (0.954)
  waiting for transfers between devices: 35.8 us -> 32.1 us
    ppermute x29 -> x31, waiting for transfers between devices: 35.8 us -> 32.1 us  [exchange(): return lax.ppermute(x, AXES, [(i, i ^ masks_of(i)) for i in range(devices)])]
    ppermute x29 -> x31, starting transfers between devices: 26.8 us -> 26.4 us  [exchange(): return lax.ppermute(x, AXES, [(i, i ^ masks_of(i)) for i in range(devices)])]
  transfers between devices with their start and end apart: 29 -> 31, of which waited for: 13 -> 12; matrix products, arithmetic and copies ran while one was open for 1% -> 1% of each run, Pallas kernels for 7% -> 7%
where the time goes in v5:
time: 75.3 us; the launch traced here: 75.2 us
  waiting for transfers between devices  32.1 us (43%)
  starting transfers between devices  26.4 us (35%)
  Pallas kernels  12.7 us (17%)
  other arithmetic  2.43 us (3%)
  between operations  0.83 us (1%)
  local copies, waits for them, and re-layouts  0.78 us (1%)
    ppermute x31, waiting for transfers between devices, exchange(): return lax.ppermute(x, AXES, [(i, i ^ masks_of(i)) for i in range(devices)])  32.1 us
    ppermute x31, starting transfers between devices, exchange(): return lax.ppermute(x, AXES, [(i, i ^ masks_of(i)) for i in range(devices)])  26.4 us
    pallas_call x5, Pallas kernels, tile(): pl.pallas_call(functools.partial(tile_kernel, span, counts, uppers, own_r...  8.28 us
    pallas_call x2, Pallas kernels, bands(): pl.pallas_call(functools.partial(kernel, groups, uppers, own_rows, docume...  4.37 us
  transfers between devices with their start and end apart: 31, of which 12 were waited for; matrix products, arithmetic and copies ran while one was open for 1% of the time, Pallas kernels for 7%

profile of v5, /device:TPU:0, one launch (start us, length us, event | category | flops | bytes accessed | tf_op | source)
XLA Modules:
  0.0 75.2 jit_solution(18264750988392064440)
XLA Ops:
  2.3 2.6 %collective-permute-start.7 = (bf16[64,2048]{1,0:T(8,128)(2,1)S(1)}, bf16[64,2048]{1,0:T(8,128)(2,1)S(1)}, u32[]{:S(2)}, u32[]{:S(2)}) collective-permute-start(bf16[64,2048]{1,0:T(8,128)(2,1)S(1)} %get-tuple-element.71.refs_3_), channel_id=1, source_target_pairs={{0,8},{1,17},{2,10},{3,19},{4,12},{5,21},{6,14},{7,23},{8,0},{9,25... | collective-permute-start | bytes 786440 | tf_op jit(solution)/shard_map/ppermute | solution.py:464
  4.9 1.5 %collective-permute-start.2 = (bf16[64,2048]{1,0:T(8,128)(2,1)S(1)}, bf16[64,2048]{1,0:T(8,128)(2,1)S(1)}, u32[]{:S(2)}, u32[]{:S(2)}) collective-permute-start(bf16[64,2048]{1,0:T(8,128)(2,1)S(1)} %get-tuple-element.71.refs_3_), channel_id=1, source_target_pairs={{0,2},{1,5},{2,0},{3,7},{4,6},{5,1},{6,4},{7,3},{8,10},{9,13},{10,... | collective-permute-start | bytes 786440 | tf_op jit(solution)/shard_map/ppermute | solution.py:464
  7.3 1.5 %collective-permute-start.3 = (bf16[64,2048]{1,0:T(8,128)(2,1)S(1)}, bf16[64,2048]{1,0:T(8,128)(2,1)S(1)}, u32[]{:S(2)}, u32[]{:S(2)}) collective-permute-start(bf16[64,2048]{1,0:T(8,128)(2,1)S(1)} %collective-permute-done.1.refs_4_), channel_id=1, source_target_pairs={{0,2},{1,5},{2,0},{3,7},{4,6},{5,1},{6,4},{7,3},{8,10},{9,13},{10,... | collective-permute-start | bytes 786440 | tf_op jit(solution)/shard_map/ppermute | solution.py:464
  8.8 1.3 %collective-permute-done.refs_2_ = s32[1,64]{1,0:T(1,128)S(1)} collective-permute-done((s32[1,64]{1,0:T(1,128)}, s32[1,64]{1,0:T(1,128)S(1)}, u32[]{:S(2)}, u32[]{:S(2)}) %collective-permute-start) | collective-permute-done | bytes 288 | tf_op jit(solution)/shard_map/ppermute | solution.py:464
  10.1 1.6 %collective-permute-start.8 = (bf16[48,2048]{1,0:T(8,128)(2,1)S(1)}, bf16[48,2048]{1,0:T(8,128)(2,1)S(1)}, u32[]{:S(2)}, u32[]{:S(2)}) collective-permute-start(bf16[48,2048]{1,0:T(8,128)(2,1)S(1)} %slice.32), channel_id=1, source_target_pairs={{0,8},{1,17},{2,10},{3,19},{4,12},{5,21},{6,14},{7,23},{8,0},{9,25... | collective-permute-start | bytes 589832 | tf_op jit(solution)/shard_map/ppermute | solution.py:464
  11.7 2.2 %collective-permute-start.13 = (bf16[64,2048]{1,0:T(8,128)(2,1)S(1)}, bf16[64,2048]{1,0:T(8,128)(2,1)}, u32[]{:S(2)}, u32[]{:S(2)}) collective-permute-start(bf16[64,2048]{1,0:T(8,128)(2,1)S(1)} %collective-permute-done.7.refs_3_.refs_7_), channel_id=1, source_target_pairs={{0,2},{1,5},{2,0},{3,7},{4,6},{5,1},{6,4},{7,3},{8,10},{9,13},{10,... | collective-permute-start | bytes 786440 | tf_op jit(solution)/shard_map/ppermute | solution.py:464
  13.9 1.6 %collective-permute-start.9 = (bf16[16,2048]{1,0:T(8,128)(2,1)S(1)}, bf16[16,2048]{1,0:T(8,128)(2,1)S(1)}, u32[]{:S(2)}, u32[]{:S(2)}) collective-permute-start(bf16[16,2048]{1,0:T(8,128)(2,1)S(1)} %slice.33), channel_id=1, source_target_pairs={{0,8},{1,17},{2,10},{3,19},{4,12},{5,21},{6,14},{7,23},{8,0},{9,25... | collective-permute-start | bytes 196616 | tf_op jit(solution)/shard_map/ppermute | solution.py:464
  16.3 2.9 %collective-permute-done.9.refs_5_.refs_9_ = bf16[16,2048]{1,0:T(8,128)(2,1)S(1)} collective-permute-done((bf16[16,2048]{1,0:T(8,128)(2,1)S(1)}, bf16[16,2048]{1,0:T(8,128)(2,1)S(1)}, u32[]{:S(2)}, u32[]{:S(2)}) %collective-permute-start.9) | collective-permute-done | bytes 65568 | tf_op jit(solution)/shard_map/ppermute | solution.py:464
  21.2 2.3 %collective-permute-done.15.refs_5_.refs_12_ = bf16[16,2048]{1,0:T(8,128)(2,1)} collective-permute-done((bf16[16,2048]{1,0:T(8,128)(2,1)S(1)}, bf16[16,2048]{1,0:T(8,128)(2,1)}, u32[]{:S(2)}, u32[]{:S(2)}) %collective-permute-start.15) | collective-permute-done | bytes 65568 | tf_op jit(solution)/shard_map/ppermute | solution.py:464
  24.1 1.7 %collective-permute-done.14.refs_4_.refs_11_ = bf16[48,2048]{1,0:T(8,128)(2,1)S(1)} collective-permute-done((bf16[48,2048]{1,0:T(8,128)(2,1)S(1)}, bf16[48,2048]{1,0:T(8,128)(2,1)S(1)}, u32[]{:S(2)}, u32[]{:S(2)}) %collective-permute-start.14) | collective-permute-done | bytes 196640 | tf_op jit(solution)/shard_map/ppermute | solution.py:464
  27.0 1.1 %shard_map.50 = (f32[9,256,256]{2,1,0:T(8,128)S(1)}, f32[256,128]{1,0:T(8,128)S(1)}, f32[32,256]{1,0:T(8,128)S(1)}, f32[1,128]{1,0:T(1,128)S(1)}) custom-call(s32[1]{0:T(128)} %bitcast.refs_0_, s32[1,64]{1,0:T(1,128)S(1)} %bitcast.3, s32[1,64]{1,0:T(1,128)S(1)} %collective-permute-done.refs_2_, bf16[64,2048]{1,0:T(8,128)(2,1)S(1)} %get-tuple-element.71.refs_3_, ...), custom_call_target="tpu_custom_call" | custom-call | flops 805306368 | bytes 2097152 | tf_op jit(solution)/shard_map/pallas_call | solution.py:561
  29.1 1.5 %shard_map.52 = (f32[9,384,128]{2,1,0:T(8,128)S(1)}, f32[384,128]{1,0:T(8,128)S(1)}, f32[32,384]{1,0:T(8,128)S(1)}, f32[1,128]{1,0:T(1,128)S(1)}) custom-call(s32[1]{0:T(128)} %bitcast.refs_0_, f32[1,128]{1,0:T(1,128)S(1)} %get-tuple-element.34.refs_1_, s32[1,64]{1,0:T(1,128)S(1)} %collective-permute-done.refs_2_, ...), custom_call_target="tpu_custom_call" | custom-call | flops 603979776 | bytes 2097152 | tf_op jit(solution)/shard_map/pallas_call | solution.py:561
  30.5 2.0 %shard_map.53 = (f32[9,128,384]{2,1,0:T(8,128)S(1)}, f32[128,128]{1,0:T(8,128)S(1)}, f32[32,384]{1,0:T(8,128)S(1)}, f32[1,128]{1,0:T(1,128)S(1)}) custom-call(s32[1]{0:T(128)} %bitcast.refs_0_, f32[1,128]{1,0:T(1,128)S(1)} %get-tuple-element.35.refs_1_, s32[1,64]{1,0:T(1,128)S(1)} %collective-permute-done.refs_2_, ...), custom_call_target="tpu_custom_call" | custom-call | flops 603979776 | bytes 2097152 | tf_op jit(solution)/shard_map/pallas_call | solution.py:561
  32.5 2.9 %shard_map.54 = (f32[9,512,128]{2,1,0:T(8,128)S(1)}, f32[512,128]{1,0:T(8,128)S(1)}, f32[32,512]{1,0:T(8,128)S(1)}, f32[16,512]{1,0:T(8,128)S(1)}) custom-call(s32[1]{0:T(128)} %bitcast.refs_0_, f32[1,128]{1,0:T(1,128)S(1)} %get-tuple-element.36.refs_1_, s32[1,64]{1,0:T(1,128)S(1)} %collective-permute-done.refs_2_, ...), custom_call_target="tpu_custom_call" | custom-call | flops 805306368 | bytes 2097152 | tf_op jit(solution)/shard_map/pallas_call | solution.py:561
  36.5 1.3 %collective-permute-start.20 = (f32[16,512]{1,0:T(8,128)S(1)}, f32[16,512]{1,0:T(8,128)S(1)}, u32[]{:S(2)}, u32[]{:S(2)}) collective-permute-start(f32[16,512]{1,0:T(8,128)S(1)} %get-tuple-element.41.refs_1_), channel_id=1, source_target_pairs={{0,8},{1,9},{2,10},{3,11},{4,12},{5,13},{6,14},{7,15},{8,0},{9,1},... | collective-permute-start | bytes 98312 | tf_op jit(solution)/shard_map/ppermute | solution.py:464
  37.8 1.6 %collective-permute-done.19.refs_2_ = f32[16,512]{1,0:T(8,128)S(1)} collective-permute-done((f32[16,512]{1,0:T(8,128)S(1)}, f32[16,512]{1,0:T(8,128)S(1)}, u32[]{:S(2)}, u32[]{:S(2)}) %collective-permute-start.19) | collective-permute-done | bytes 32800 | tf_op jit(solution)/shard_map/ppermute | solution.py:464
  41.1 3.9 %shard_map.56 = (f32[128,1024]{1,0:T(8,128)S(1)}, bf16[128,1024]{1,0:T(8,128)(2,1)S(1)}, f32[128,1024]{1,0:T(8,128)S(1)}, bf16[128,1024]{1,0:T(8,128)(2,1)S(1)},...) custom-call(s32[1]{0:T(128)} %bitcast.refs_0_, ...), custom_call_target="tpu_custom_call" | custom-call | flops 1073741824 | bytes 4194304 | tf_op jit(solution)/shard_map/pallas_call | solution.py:590
  49.1 2.3 %collective-permute-done.22 = bf16[128,1024]{1,0:T(8,128)(2,1)S(1)} collective-permute-done((bf16[128,1024]{1,0:T(8,128)(2,1)S(1)}, bf16[128,1024]{1,0:T(8,128)(2,1)S(1)}, u32[]{:S(2)}, u32[]{:S(2)}) %collective-permute-start.22) | collective-permute-done | bytes 262176 | tf_op jit(solution)/shard_map/ppermute | solution.py:464
  51.6 8.2 %collective-permute-done.26 = bf16[128,1024]{1,0:T(8,128)(2,1)S(1)} collective-permute-done((bf16[128,1024]{1,0:T(8,128)(2,1)S(1)}, bf16[128,1024]{1,0:T(8,128)(2,1)S(1)}, u32[]{:S(2)}, u32[]{:S(2)}) %collective-permute-start.26) | collective-permute-done | bytes 262176 | tf_op jit(solution)/shard_map/ppermute | solution.py:464
  59.9 1.2 %collective-permute-start.27 = (bf16[128,1024]{1,0:T(8,128)(2,1)S(1)}, bf16[128,1024]{1,0:T(8,128)(2,1)S(1)}, u32[]{:S(2)}, u32[]{:S(2)}) collective-permute-start(bf16[128,1024]{1,0:T(8,128)(2,1)S(1)} %add_convert_fusion), channel_id=1, source_target_pairs={{0,8},{1,17},{2,10},{3,19},{4,12},{5,21},{6,14},{7,23},{8,0},{9,25... | collective-permute-start | bytes 786440 | tf_op jit(solution)/shard_map/ppermute | solution.py:464
  62.2 1.1 %collective-permute-start.29 = (bf16[64,1024]{1,0:T(8,128)(2,1)S(1)}, bf16[64,1024]{1,0:T(8,128)(2,1)S(1)}, u32[]{:S(2)}, u32[]{:S(2)}) collective-permute-start(bf16[64,1024]{1,0:T(8,128)(2,1)S(1)} %get-tuple-element.73), channel_id=1, source_target_pairs={{0,9},{1,16},{2,11},{3,18},{4,13},{5,20},{6,15},{7,22},{8,1},{9,24... | collective-permute-start | bytes 393224 | tf_op jit(solution)/shard_map/ppermute | solution.py:464
  63.3 5.1 %collective-permute-done.27 = bf16[128,1024]{1,0:T(8,128)(2,1)S(1)} collective-permute-done((bf16[128,1024]{1,0:T(8,128)(2,1)S(1)}, bf16[128,1024]{1,0:T(8,128)(2,1)S(1)}, u32[]{:S(2)}, u32[]{:S(2)}) %collective-permute-start.27) | collective-permute-done | bytes 262176 | tf_op jit(solution)/shard_map/ppermute | solution.py:464
  68.6 2.6 %collective-permute-done.24 = bf16[64,1024]{1,0:T(8,128)(2,1)S(1)} collective-permute-done((bf16[64,1024]{1,0:T(8,128)(2,1)S(1)}, bf16[64,1024]{1,0:T(8,128)(2,1)S(1)}, u32[]{:S(2)}, u32[]{:S(2)}) %collective-permute-start.24) | collective-permute-done | bytes 131104 | tf_op jit(solution)/shard_map/ppermute | solution.py:464
  71.3 2.8 %collective-permute-done.29 = bf16[64,1024]{1,0:T(8,128)(2,1)S(1)} collective-permute-done((bf16[64,1024]{1,0:T(8,128)(2,1)S(1)}, bf16[64,1024]{1,0:T(8,128)(2,1)S(1)}, u32[]{:S(2)}, u32[]{:S(2)}) %collective-permute-start.29) | collective-permute-done | bytes 131104 | tf_op jit(solution)/shard_map/ppermute | solution.py:464
  (60 shorter events, 17.5 us)
Async XLA Ops:
  1.7 5.6 %collective-permute-start.1 = (bf16[64,2048]{1,0:T(8,128)(2,1)S(1)}, bf16[64,2048]{1,0:T(8,128)(2,1)S(1)}, u32[]{:S(2)}, u32[]{:S(2)}) collective-permute-start(bf16[64,2048]{1,0:T(8,128)(2,1)S(1)} %get-tuple-element.70.refs_8_.refs_7_.refs_21_), channel_id=1, source_target_pairs={{0,1},{1,0},{2,3},{3,2},{4,5},{5,4},{6,7},{7,6},{8,9},{9,8},{10,11... | collective-permute-start | bytes 786440 | tf_op jit(solution)/shard_map/ppermute | solution.py:464
  2.3 9.4 %collective-permute-start.7 = (bf16[64,2048]{1,0:T(8,128)(2,1)S(1)}, bf16[64,2048]{1,0:T(8,128)(2,1)S(1)}, u32[]{:S(2)}, u32[]{:S(2)}) collective-permute-start(bf16[64,2048]{1,0:T(8,128)(2,1)S(1)} %get-tuple-element.71.refs_3_), channel_id=1, source_target_pairs={{0,8},{1,17},{2,10},{3,19},{4,12},{5,21},{6,14},{7,23},{8,0},{9,25... | collective-permute-start | bytes 786440 | tf_op jit(solution)/shard_map/ppermute | solution.py:464
  4.9 9.0 %collective-permute-start.2 = (bf16[64,2048]{1,0:T(8,128)(2,1)S(1)}, bf16[64,2048]{1,0:T(8,128)(2,1)S(1)}, u32[]{:S(2)}, u32[]{:S(2)}) collective-permute-start(bf16[64,2048]{1,0:T(8,128)(2,1)S(1)} %get-tuple-element.71.refs_3_), channel_id=1, source_target_pairs={{0,2},{1,5},{2,0},{3,7},{4,6},{5,1},{6,4},{7,3},{8,10},{9,13},{10,... | collective-permute-start | bytes 786440 | tf_op jit(solution)/shard_map/ppermute | solution.py:464
  6.4 7.5 %collective-permute-start.4 = (bf16[64,2048]{1,0:T(8,128)(2,1)S(1)}, bf16[64,2048]{1,0:T(8,128)(2,1)S(1)}, u32[]{:S(2)}, u32[]{:S(2)}) collective-permute-start(bf16[64,2048]{1,0:T(8,128)(2,1)S(1)} %get-tuple-element.71.refs_3_), channel_id=1, source_target_pairs={{0,1},{1,0},{2,3},{3,2},{4,5},{5,4},{6,7},{7,6},{8,9},{9,8},{10,11... | collective-permute-start | bytes 786440 | tf_op jit(solution)/shard_map/ppermute | solution.py:464
  7.3 8.3 %collective-permute-start.3 = (bf16[64,2048]{1,0:T(8,128)(2,1)S(1)}, bf16[64,2048]{1,0:T(8,128)(2,1)S(1)}, u32[]{:S(2)}, u32[]{:S(2)}) collective-permute-start(bf16[64,2048]{1,0:T(8,128)(2,1)S(1)} %collective-permute-done.1.refs_4_), channel_id=1, source_target_pairs={{0,2},{1,5},{2,0},{3,7},{4,6},{5,1},{6,4},{7,3},{8,10},{9,13},{10,... | collective-permute-start | bytes 786440 | tf_op jit(solution)/shard_map/ppermute | solution.py:464
  10.1 10.1 %collective-permute-start.8 = (bf16[48,2048]{1,0:T(8,128)(2,1)S(1)}, bf16[48,2048]{1,0:T(8,128)(2,1)S(1)}, u32[]{:S(2)}, u32[]{:S(2)}) collective-permute-start(bf16[48,2048]{1,0:T(8,128)(2,1)S(1)} %slice.32), channel_id=1, source_target_pairs={{0,8},{1,17},{2,10},{3,19},{4,12},{5,21},{6,14},{7,23},{8,0},{9,25... | collective-permute-start | bytes 589832 | tf_op jit(solution)/shard_map/ppermute | solution.py:464
  11.7 11.9 %collective-permute-start.13 = (bf16[64,2048]{1,0:T(8,128)(2,1)S(1)}, bf16[64,2048]{1,0:T(8,128)(2,1)}, u32[]{:S(2)}, u32[]{:S(2)}) collective-permute-start(bf16[64,2048]{1,0:T(8,128)(2,1)S(1)} %collective-permute-done.7.refs_3_.refs_7_), channel_id=1, source_target_pairs={{0,2},{1,5},{2,0},{3,7},{4,6},{5,1},{6,4},{7,3},{8,10},{9,13},{10,... | collective-permute-start | bytes 786440 | tf_op jit(solution)/shard_map/ppermute | solution.py:464
  13.9 10.2 %collective-permute-start.5 = (bf16[64,2048]{1,0:T(8,128)(2,1)S(1)}, bf16[64,2048]{1,0:T(8,128)(2,1)S(1)}, u32[]{:S(2)}, u32[]{:S(2)}) collective-permute-start(bf16[64,2048]{1,0:T(8,128)(2,1)S(1)} %collective-permute-done.2.refs_5_), channel_id=1, source_target_pairs={{0,1},{1,0},{2,3},{3,2},{4,5},{5,4},{6,7},{7,6},{8,9},{9,8},{10,11... | collective-permute-start | bytes 786440 | tf_op jit(solution)/shard_map/ppermute | solution.py:464
  13.9 5.2 %collective-permute-start.9 = (bf16[16,2048]{1,0:T(8,128)(2,1)S(1)}, bf16[16,2048]{1,0:T(8,128)(2,1)S(1)}, u32[]{:S(2)}, u32[]{:S(2)}) collective-permute-start(bf16[16,2048]{1,0:T(8,128)(2,1)S(1)} %slice.33), channel_id=1, source_target_pairs={{0,8},{1,17},{2,10},{3,19},{4,12},{5,21},{6,14},{7,23},{8,0},{9,25... | collective-permute-start | bytes 196616 | tf_op jit(solution)/shard_map/ppermute | solution.py:464
  15.6 10.3 %collective-permute-start.6 = (bf16[64,2048]{1,0:T(8,128)(2,1)S(1)}, bf16[64,2048]{1,0:T(8,128)(2,1)S(1)}, u32[]{:S(2)}, u32[]{:S(2)}) collective-permute-start(bf16[64,2048]{1,0:T(8,128)(2,1)S(1)} %collective-permute-done.3.refs_6_), channel_id=1, source_target_pairs={{0,1},{1,0},{2,3},{3,2},{4,5},{5,4},{6,7},{7,6},{8,9},{9,8},{10,11... | collective-permute-start | bytes 786440 | tf_op jit(solution)/shard_map/ppermute | solution.py:464
  20.2 5.7 %collective-permute-start.14 = (bf16[48,2048]{1,0:T(8,128)(2,1)S(1)}, bf16[48,2048]{1,0:T(8,128)(2,1)S(1)}, u32[]{:S(2)}, u32[]{:S(2)}) collective-permute-start(bf16[48,2048]{1,0:T(8,128)(2,1)S(1)} %collective-permute-done.8.refs_4_.refs_8_), channel_id=1, source_target_pairs={{0,2},{1,5},{2,0},{3,7},{4,6},{5,1},{6,4},{7,3},{8,10},{9,13},{10,... | collective-permute-start | bytes 589832 | tf_op jit(solution)/shard_map/ppermute | solution.py:464
  23.6 5.5 %collective-permute-start.10 = (bf16[64,2048]{1,0:T(8,128)(2,1)S(1)}, bf16[64,2048]{1,0:T(8,128)(2,1)S(1)}, u32[]{:S(2)}, u32[]{:S(2)}) collective-permute-start(bf16[64,2048]{1,0:T(8,128)(2,1)S(1)} %collective-permute-done.7.refs_3_.refs_7_), channel_id=1, source_target_pairs={{0,1},{1,0},{2,3},{3,2},{4,5},{5,4},{6,7},{7,6},{8,9},{9,8},{10,11... | collective-permute-start | bytes 786440 | tf_op jit(solution)/shard_map/ppermute | solution.py:464
  23.6 5.5 %collective-permute-start.11 = (bf16[48,2048]{1,0:T(8,128)(2,1)S(1)}, bf16[48,2048]{1,0:T(8,128)(2,1)S(1)}, u32[]{:S(2)}, u32[]{:S(2)}) collective-permute-start(bf16[48,2048]{1,0:T(8,128)(2,1)S(1)} %collective-permute-done.8.refs_4_.refs_8_), channel_id=1, source_target_pairs={{0,1},{1,0},{2,3},{3,2},{4,5},{5,4},{6,7},{7,6},{8,9},{9,8},{10,11... | collective-permute-start | bytes 589832 | tf_op jit(solution)/shard_map/ppermute | solution.py:464
  24.1 8.4 %collective-permute-start.16 = (bf16[64,2048]{1,0:T(8,128)(2,1)}, bf16[64,2048]{1,0:T(8,128)(2,1)S(1)}, u32[]{:S(2)}, u32[]{:S(2)}) collective-permute-start(bf16[64,2048]{1,0:T(8,128)(2,1)} %collective-permute-done.13.refs_3_.refs_10_), channel_id=1, source_target_pairs={{0,1},{1,0},{2,3},{3,2},{4,5},{5,4},{6,7},{7,6},{8,9},{9,8},{10,11... | collective-permute-start | bytes 786440 | tf_op jit(solution)/shard_map/ppermute | solution.py:464
  25.9 6.7 %collective-permute-start.17 = (bf16[48,2048]{1,0:T(8,128)(2,1)S(1)}, bf16[48,2048]{1,0:T(8,128)(2,1)S(1)}, u32[]{:S(2)}, u32[]{:S(2)}) collective-permute-start(bf16[48,2048]{1,0:T(8,128)(2,1)S(1)} %collective-permute-done.14.refs_4_.refs_11_), channel_id=1, source_target_pairs={{0,1},{1,0},{2,3},{3,2},{4,5},{5,4},{6,7},{7,6},{8,9},{9,8},{10,11... | collective-permute-start | bytes 589832 | tf_op jit(solution)/shard_map/ppermute | solution.py:464
  45.0 6.4 %collective-permute-start.22 = (bf16[128,1024]{1,0:T(8,128)(2,1)S(1)}, bf16[128,1024]{1,0:T(8,128)(2,1)S(1)}, u32[]{:S(2)}, u32[]{:S(2)}) collective-permute-start(bf16[128,1024]{1,0:T(8,128)(2,1)S(1)} %get-tuple-element.55), channel_id=1, source_target_pairs={{0,2},{1,5},{2,0},{3,7},{4,6},{5,1},{6,4},{7,3},{8,10},{9,13},{10,... | collective-permute-start | bytes 786440 | tf_op jit(solution)/shard_map/ppermute | solution.py:464
  46.1 15.0 %collective-permute-start.23 = (bf16[128,1024]{1,0:T(8,128)(2,1)S(1)}, bf16[128,1024]{1,0:T(8,128)(2,1)S(1)}, u32[]{:S(2)}, u32[]{:S(2)}) collective-permute-start(bf16[128,1024]{1,0:T(8,128)(2,1)S(1)} %get-tuple-element.58), channel_id=1, source_target_pairs={{0,2},{1,5},{2,0},{3,7},{4,6},{5,1},{6,4},{7,3},{8,10},{9,13},{10,... | collective-permute-start | bytes 786440 | tf_op jit(solution)/shard_map/ppermute | solution.py:464
  47.1 16.2 %collective-permute-start.25 = (bf16[128,1024]{1,0:T(8,128)(2,1)S(1)}, bf16[128,1024]{1,0:T(8,128)(2,1)S(1)}, u32[]{:S(2)}, u32[]{:S(2)}) collective-permute-start(bf16[128,1024]{1,0:T(8,128)(2,1)S(1)} %get-tuple-element.60), channel_id=1, source_target_pairs={{0,2},{1,5},{2,0},{3,7},{4,6},{5,1},{6,4},{7,3},{8,10},{9,13},{10,... | collective-permute-start | bytes 786440 | tf_op jit(solution)/shard_map/ppermute | solution.py:464
  48.1 11.8 %collective-permute-start.26 = (bf16[128,1024]{1,0:T(8,128)(2,1)S(1)}, bf16[128,1024]{1,0:T(8,128)(2,1)S(1)}, u32[]{:S(2)}, u32[]{:S(2)}) collective-permute-start(bf16[128,1024]{1,0:T(8,128)(2,1)S(1)} %get-tuple-element.62), channel_id=1, source_target_pairs={{0,2},{1,5},{2,0},{3,7},{4,6},{5,1},{6,4},{7,3},{8,10},{9,13},{10,... | collective-permute-start | bytes 786440 | tf_op jit(solution)/shard_map/ppermute | solution.py:464
  51.6 22.5 %collective-permute-start.28 = (f32[64,1024]{1,0:T(8,128)S(1)}, f32[64,1024]{1,0:T(8,128)S(1)}, u32[]{:S(2)}, u32[]{:S(2)}) collective-permute-start(f32[64,1024]{1,0:T(8,128)S(1)} %get-tuple-element.63), channel_id=1, source_target_pairs={{0,1},{1,0},{2,3},{3,2},{4,5},{5,4},{6,7},{7,6},{8,9},{9,8},{10,11... | collective-permute-start | bytes 786440 | tf_op jit(solution)/shard_map/ppermute | solution.py:464
  59.9 8.5 %collective-permute-start.27 = (bf16[128,1024]{1,0:T(8,128)(2,1)S(1)}, bf16[128,1024]{1,0:T(8,128)(2,1)S(1)}, u32[]{:S(2)}, u32[]{:S(2)}) collective-permute-start(bf16[128,1024]{1,0:T(8,128)(2,1)S(1)} %add_convert_fusion), channel_id=1, source_target_pairs={{0,8},{1,17},{2,10},{3,19},{4,12},{5,21},{6,14},{7,23},{8,0},{9,25... | collective-permute-start | bytes 786440 | tf_op jit(solution)/shard_map/ppermute | solution.py:464
  61.2 10.0 %collective-permute-start.24 = (bf16[64,1024]{1,0:T(8,128)(2,1)S(1)}, bf16[64,1024]{1,0:T(8,128)(2,1)S(1)}, u32[]{:S(2)}, u32[]{:S(2)}) collective-permute-start(bf16[64,1024]{1,0:T(8,128)(2,1)S(1)} %get-tuple-element.72), channel_id=1, source_target_pairs={{0,8},{1,17},{2,10},{3,19},{4,12},{5,21},{6,14},{7,23},{8,0},{9,25... | collective-permute-start | bytes 393224 | tf_op jit(solution)/shard_map/ppermute | solution.py:464
  62.2 11.9 %collective-permute-start.29 = (bf16[64,1024]{1,0:T(8,128)(2,1)S(1)}, bf16[64,1024]{1,0:T(8,128)(2,1)S(1)}, u32[]{:S(2)}, u32[]{:S(2)}) collective-permute-start(bf16[64,1024]{1,0:T(8,128)(2,1)S(1)} %get-tuple-element.73), channel_id=1, source_target_pairs={{0,9},{1,16},{2,11},{3,18},{4,13},{5,20},{6,15},{7,22},{8,1},{9,24... | collective-permute-start | bytes 393224 | tf_op jit(solution)/shard_map/ppermute | solution.py:464
  68.5 5.5 %collective-permute-start.30 = (f32[64,1024]{1,0:T(8,128)S(1)}, f32[64,1024]{1,0:T(8,128)S(1)}, u32[]{:S(2)}, u32[]{:S(2)}) collective-permute-start(f32[64,1024]{1,0:T(8,128)S(1)} %get-tuple-element.67), channel_id=1, source_target_pairs={{0,1},{1,0},{2,3},{3,2},{4,5},{5,4},{6,7},{7,6},{8,9},{9,8},{10,11... | collective-permute-start | bytes 786440 | tf_op jit(solution)/shard_map/ppermute | solution.py:464
  (8 other events, 22.1 us)

commit v6 on v3

--- a/solution.py
+++ b/solution.py
@@ -310,11 +310,13 @@
     chip_rows = total // groups
     me = me_ref[0]
     lead = (me & 1) == 0
+    own, first, second, swapped = [ref[...] for ref in stat_refs]
+    values = [own, jnp.where(lead, first, swapped), second, jnp.where(lead, swapped, first)]
     parts, partners = [], []
-    for j, ref in enumerate(stat_refs):
+    for j, value in enumerate(values):
         parts.append(jnp.concatenate(
-            [ref[:, (i ^ j) * chip_rows:((i ^ j) + 1) * chip_rows] for i in range(groups)], axis=1))
-        partners.append(ref[count:count + 1, :chip_rows])
+            [value[:, (i ^ j) * chip_rows:((i ^ j) + 1) * chip_rows] for i in range(groups)], axis=1))
+        partners.append(value[count:count + 1, :chip_rows])
     peak = functools.reduce(jnp.maximum, parts)
     mass = functools.reduce(lambda a, b: a + b, [jnp.exp2(part - peak) for part in parts])
     partner_row = jnp.concatenate(partners, axis=1)
@@ -375,57 +377,58 @@
     store(out_refs, product, 0, 0, uppers[k] - uppers[k - 1], chip_rows)
 
 
-def bands_kernel(groups, uppers, own_rows, masks, *refs):
+def bands_kernel(groups, uppers, own_rows, masks, *refs, block):
     tiles = len(subtiles(groups))
     setup = band_setup(groups, uppers, own_rows, masks, refs[0], refs[1:1 + groups])
     at = 1 + groups
     power_refs, col_refs, row_refs = [refs[at + i * tiles:at + (i + 1) * tiles] for i in range(3)]
-    segments = segments_of(groups)
-    outs = groups + segments[-1][0]
-    before_ref = refs[-outs - 1]
-    w_refs, others, widest = refs[at + 3 * tiles:-outs - 1], refs[-outs:-outs + groups], refs[-outs + groups:]
+    at += 3 * tiles
+    far = segments_of(groups)[-1]
+    height = block[-1][1] - block[0][0]
+    fresh = far[0] - block[0][0] if block[-1] == far else height
+    outs = refs[len(refs) - height - fresh:]
+    others, widest = outs[:height], outs[height:]
+    inputs = refs[at:len(refs) - height - fresh]
+    before_ref = inputs[-1] if fresh < height else None
+    w_refs = inputs[:-1] if fresh < height else inputs
     _, totals, _, id_row, id_col = setup
     chip_rows = totals.shape[1] // groups
+    height, fresh = height * chip_rows, fresh * chip_rows
+    first = block[0][0] * chip_rows
     scales = [logit_gain * m ** -0.5 for m in uppers]
     last = len(uppers) - 1
     narrow = [k for k in range(last, -1, -1) if uppers[k] <= LANES]
-    for block in (segments[1:], segments[:1]):
-        first = block[0][0] * chip_rows
-        rows = slice(first, block[-1][1] * chip_rows)
-        height = rows.stop - first
-        hit = id_col[rows] == id_row
-        weights = [
-            weights_of(segment, groups, setup, power_refs, col_refs, row_refs) for segment in block]
-        tall = (block[0][1] - block[0][0]) * chip_rows
-        running = weights[0](last) - jnp.where(hit[:tall], scales[last], 0.0)
-        lower, upper = uppers[last - 1], uppers[last]
-        product = jnp.dot(
-            running.astype(jnp.bfloat16), rows_of(w_refs, lower, upper),
-            preferred_element_type=jnp.float32)
-        store(widest, product, first, 0, upper - lower, chip_rows)
-        if len(block) > 1:
-            running = jnp.concatenate([running, before_ref[...]], axis=0)
-        stack = []
-        for k in range(last - 1, -1, -1):
-            weight = jnp.concatenate([part(k) for part in weights], axis=0)
-            running = running + (weight - jnp.where(hit, scales[k], 0.0))
-            band = running.astype(jnp.bfloat16)
-            if k in narrow:
-                stack.append(band)
-                continue
-            lower, upper = uppers[k - 1], uppers[k]
-            product = jnp.dot(
-                band, rows_of(w_refs, lower, upper), preferred_element_type=jnp.float32)
-            store(others, product, first, lower, upper, chip_rows)
-        product = jnp.dot(
-            jnp.concatenate(stack, axis=0), rows_of(w_refs, 0, LANES),
-            preferred_element_type=jnp.float32)
-        lane = lax.broadcasted_iota(jnp.int32, (height, LANES), 1)
-        chosen = product[:height]
-        for i in range(1, len(stack)):
-            chosen = jnp.where(
-                lane < uppers[narrow[i]], product[i * height:(i + 1) * height], chosen)
-        store(others, chosen, first, 0, LANES, chip_rows)
+    hit = id_col[first:first + height] == id_row
+    weights = [
+        weights_of(segment, groups, setup, power_refs, col_refs, row_refs) for segment in block]
+    running = weights[0](last) - jnp.where(hit[:fresh], scales[last], 0.0)
+    lower, upper = uppers[last - 1], uppers[last]
+    product = jnp.dot(
+        running.astype(jnp.bfloat16), rows_of(w_refs, lower, upper),
+        preferred_element_type=jnp.float32)
+    store(widest, product, 0, 0, upper - lower, chip_rows)
+    if before_ref is not None:
+        running = jnp.concatenate([running, before_ref[...]], axis=0)
+    stack = []
+    for k in range(last - 1, -1, -1):
+        weight = jnp.concatenate([part(k) for part in weights], axis=0)
+        running = running + (weight - jnp.where(hit, scales[k], 0.0))
+        band = running.astype(jnp.bfloat16)
+        if k in narrow:
+            stack.append(band)
+            continue
+        lower, upper = uppers[k - 1], uppers[k]
+        product = jnp.dot(band, rows_of(w_refs, lower, upper), preferred_element_type=jnp.float32)
+        store(others, product, 0, lower, upper, chip_rows)
+    product = jnp.dot(
+        jnp.concatenate(stack, axis=0), rows_of(w_refs, 0, LANES),
+        preferred_element_type=jnp.float32)
+    lane = lax.broadcasted_iota(jnp.int32, (height, LANES), 1)
+    chosen = product[:height]
+    for i in range(1, len(stack)):
+        chosen = jnp.where(
+            lane < uppers[narrow[i]], product[i * height:(i + 1) * height], chosen)
+    store(others, chosen, 0, 0, LANES, chip_rows)
 
 
 def store(out_refs, value, first_row, lower, upper, chip_rows):
@@ -465,14 +468,14 @@
     mine = jnp.where(lead, queries, documents)
     other = jnp.where(lead, documents, queries)
     got = swap(other)
-    small = WIDTHS * total * total * 4 <= 16 << 20
-    cut = own_rows - 16 if small and own_rows >= 32 else own_rows
+    small = groups == 4 and WIDTHS * total * total * 4 <= 16 << 20
+    cut = own_rows // 2 if small and own_rows % 32 == 0 else own_rows
     v = {0: [mine, got]}
     w = {0: [swap(mine), other]}
     for stage in reversed(range(stages)):
         for j in sorted(v):
             parts = v[j]
-            if j == 0 and stage == stages - 1 and cut < own_rows:
+            if cut < own_rows and j == 0 and stage:
                 parts = [mine, got[:cut], got[cut:]]
             v[j | 1 << stage] = [
                 along(part, stage) for part in parts]
@@ -571,7 +574,11 @@
             done += more
         more, stats = tile([4], chip_partner, done)
         done += more
-        common = [me, *gathered(stats), *[t[0] for t in done], *[t[1] for t in done],
+        first = exchange(
+            stats, lambda i: query_mask(3) if i & 1 else query_mask(1))
+        second = exchange(stats, lambda i: query_mask(2))
+        swapped = swap(first)
+        common = [me, stats, first, second, swapped, *[t[0] for t in done], *[t[1] for t in done],
                   *[t[2] for t in done], *w_list]
         near = segments_of(groups)[-1][0]
         widest = feature_dim - uppers[-2]
@@ -591,9 +598,24 @@
         *far_ones, running = bands(
             last_band_kernel, [],
             gradient_shapes(widest)[near:] + [shape((groups - near) * chip_rows, total)])
-        rest = bands(
-            bands_kernel, [running], gradient_shapes(uppers[-2]) + gradient_shapes(widest)[:near])
-        chunks = [[*rest[groups:], *far_ones], rest[:groups]]
+        narrow_ones = gradient_shapes(uppers[-2])
+        wide_ones = gradient_shapes(widest)
+        middle = segments_of(groups)[1]
+
+        def block_of_bands(block, more):
+            span = slice(block[0][0], block[-1][1])
+            fresh = slice(block[0][0], min(block[-1][1], near))
+            result = bands(
+                functools.partial(bands_kernel, block=block), more,
+                narrow_ones[span] + wide_ones[fresh])
+            return result[:span.stop - span.start], result[span.stop - span.start:]
+
+        far_narrow, middle_wide = block_of_bands([middle, (near, groups)], [running])
+        next_narrow, next_wide = block_of_bands([(1, 2)], [])
+        own_narrow, own_wide = block_of_bands([(0, 1)], [])
+        chunks = [
+            [*own_wide, *next_wide, *middle_wide, *far_ones],
+            [*own_narrow, *next_narrow, *far_narrow]]
 
     mine_parts, other_parts = [], []
     for c, chunk in enumerate(chunks):

time: 73.9 us -> 65.9 us (0.89)
  waiting for transfers between devices: 31 us -> 24.3 us
  starting transfers between devices: 27.3 us -> 25.9 us
    ppermute x31, waiting for transfers between devices: 31 us -> 24.3 us  [exchange(): return lax.ppermute(x, AXES, [(i, i ^ masks_of(i)) for i in range(devices)])]
    ppermute x31, starting transfers between devices: 27.3 us -> 25.9 us  [exchange(): return lax.ppermute(x, AXES, [(i, i ^ masks_of(i)) for i in range(devices)])]
    pallas_call x2 -> x4, Pallas kernels: 4.42 us -> 5.17 us  [bands(): pl.pallas_call(functools.partial(kernel, groups, uppers, own_rows, docume...]
  transfers between devices with their start and end apart: 31 -> 31, of which waited for: 11 -> 9; matrix products, arithmetic and copies ran while one was open for 2% -> 2% of each run, Pallas kernels for 6% -> 14%
where the time goes in v6:
time: 65.9 us; the launch traced here: 65.8 us
  starting transfers between devices  25.9 us (39%)
  waiting for transfers between devices  24.3 us (37%)
  Pallas kernels  11.4 us (17%)
  other arithmetic  3.23 us (5%)
  between operations  0.82 us (1%)
    ppermute x31, starting transfers between devices, exchange(): return lax.ppermute(x, AXES, [(i, i ^ masks_of(i)) for i in range(devices)])  25.9 us
    ppermute x31, waiting for transfers between devices, exchange(): return lax.ppermute(x, AXES, [(i, i ^ masks_of(i)) for i in range(devices)])  24.3 us
    pallas_call x5, Pallas kernels, tile(): pl.pallas_call(functools.partial(tile_kernel, span, counts, uppers, own_r...  6.27 us
    pallas_call x4, Pallas kernels, bands(): pl.pallas_call(functools.partial(kernel, groups, uppers, own_rows, docume...  5.17 us
  transfers between devices with their start and end apart: 31, of which 9 were waited for; matrix products, arithmetic and copies ran while one was open for 2% of the time, Pallas kernels for 14%

profile of v6, /device:TPU:0, one launch (start us, length us, event | category | flops | bytes accessed | tf_op | source)
XLA Modules:
  0.0 65.8 jit_solution(8559405382573848585)
XLA Ops:
  2.3 2.6 %collective-permute-start.2 = (bf16[64,2048]{1,0:T(8,128)(2,1)S(1)}, bf16[64,2048]{1,0:T(8,128)(2,1)S(1)}, u32[]{:S(2)}, u32[]{:S(2)}) collective-permute-start(bf16[64,2048]{1,0:T(8,128)(2,1)S(1)} %get-tuple-element.71.refs_2_), channel_id=1, source_target_pairs={{0,2},{1,5},{2,0},{3,7},{4,6},{5,1},{6,4},{7,3},{8,10},{9,13},{10,... | collective-permute-start | bytes 786440 | tf_op jit(solution)/shard_map/ppermute | solution.py:460
  5.0 1.6 %collective-permute-start.7 = (bf16[64,2048]{1,0:T(8,128)(2,1)S(1)}, bf16[64,2048]{1,0:T(8,128)(2,1)S(1)}, u32[]{:S(2)}, u32[]{:S(2)}) collective-permute-start(bf16[64,2048]{1,0:T(8,128)(2,1)S(1)} %get-tuple-element.71.refs_2_), channel_id=1, source_target_pairs={{0,8},{1,17},{2,10},{3,19},{4,12},{5,21},{6,14},{7,23},{8,0},{9,25... | collective-permute-start | bytes 786440 | tf_op jit(solution)/shard_map/ppermute | solution.py:460
  9.5 1.6 %collective-permute-start.8 = (bf16[32,2048]{1,0:T(8,128)(2,1)S(1)}, bf16[32,2048]{1,0:T(8,128)(2,1)S(1)}, u32[]{:S(2)}, u32[]{:S(2)}) collective-permute-start(bf16[32,2048]{1,0:T(8,128)(2,1)S(1)} %get-tuple-element.75), channel_id=1, source_target_pairs={{0,8},{1,17},{2,10},{3,19},{4,12},{5,21},{6,14},{7,23},{8,0},{9,25... | collective-permute-start | bytes 393224 | tf_op jit(solution)/shard_map/ppermute | solution.py:460
  11.2 2.9 %collective-permute-done.7.refs_2_.refs_6_ = bf16[64,2048]{1,0:T(8,128)(2,1)S(1)} collective-permute-done((bf16[64,2048]{1,0:T(8,128)(2,1)S(1)}, bf16[64,2048]{1,0:T(8,128)(2,1)S(1)}, u32[]{:S(2)}, u32[]{:S(2)}) %collective-permute-start.7) | collective-permute-done | bytes 262176 | tf_op jit(solution)/shard_map/ppermute | solution.py:460
  14.1 1.5 %collective-permute-start.13 = (bf16[64,2048]{1,0:T(8,128)(2,1)S(1)}, bf16[64,2048]{1,0:T(8,128)(2,1)S(1)}, u32[]{:S(2)}, u32[]{:S(2)}) collective-permute-start(bf16[64,2048]{1,0:T(8,128)(2,1)S(1)} %collective-permute-done.7.refs_2_.refs_6_), channel_id=1, source_target_pairs={{0,2},{1,5},{2,0},{3,7},{4,6},{5,1},{6,4},{7,3},{8,10},{9,13},{10,... | collective-permute-start | bytes 786440 | tf_op jit(solution)/shard_map/ppermute | solution.py:460
  15.7 1.2 %collective-permute-done.8.refs_3_.refs_7_ = bf16[32,2048]{1,0:T(8,128)(2,1)S(1)} collective-permute-done((bf16[32,2048]{1,0:T(8,128)(2,1)S(1)}, bf16[32,2048]{1,0:T(8,128)(2,1)S(1)}, u32[]{:S(2)}, u32[]{:S(2)}) %collective-permute-start.8) | collective-permute-done | bytes 131104 | tf_op jit(solution)/shard_map/ppermute | solution.py:460
  16.9 1.3 %collective-permute-start.9 = (bf16[32,2048]{1,0:T(8,128)(2,1)S(1)}, bf16[32,2048]{1,0:T(8,128)(2,1)S(1)}, u32[]{:S(2)}, u32[]{:S(2)}) collective-permute-start(bf16[32,2048]{1,0:T(8,128)(2,1)S(1)} %get-tuple-element.74), channel_id=1, source_target_pairs={{0,8},{1,17},{2,10},{3,19},{4,12},{5,21},{6,14},{7,23},{8,0},{9,25... | collective-permute-start | bytes 393224 | tf_op jit(solution)/shard_map/ppermute | solution.py:460
  18.2 5.0 %collective-permute-done.9.refs_4_.refs_8_ = bf16[32,2048]{1,0:T(8,128)(2,1)S(1)} collective-permute-done((bf16[32,2048]{1,0:T(8,128)(2,1)S(1)}, bf16[32,2048]{1,0:T(8,128)(2,1)S(1)}, u32[]{:S(2)}, u32[]{:S(2)}) %collective-permute-start.9) | collective-permute-done | bytes 131104 | tf_op jit(solution)/shard_map/ppermute | solution.py:460
  23.2 1.3 %collective-permute-start.14 = (bf16[32,2048]{1,0:T(8,128)(2,1)S(1)}, bf16[32,2048]{1,0:T(8,128)(2,1)S(1)}, u32[]{:S(2)}, u32[]{:S(2)}) collective-permute-start(bf16[32,2048]{1,0:T(8,128)(2,1)S(1)} %collective-permute-done.8.refs_3_.refs_7_), channel_id=1, source_target_pairs={{0,2},{1,5},{2,0},{3,7},{4,6},{5,1},{6,4},{7,3},{8,10},{9,13},{10,... | collective-permute-start | bytes 393224 | tf_op jit(solution)/shard_map/ppermute | solution.py:460
  26.6 1.6 %collective-permute-done.14.refs_3_.refs_10_ = bf16[32,2048]{1,0:T(8,128)(2,1)S(1)} collective-permute-done((bf16[32,2048]{1,0:T(8,128)(2,1)S(1)}, bf16[32,2048]{1,0:T(8,128)(2,1)S(1)}, u32[]{:S(2)}, u32[]{:S(2)}) %collective-permute-start.14) | collective-permute-done | bytes 131104 | tf_op jit(solution)/shard_map/ppermute | solution.py:460
  28.2 1.6 %collective-permute-done.15.refs_4_.refs_11_ = bf16[32,2048]{1,0:T(8,128)(2,1)S(1)} collective-permute-done((bf16[32,2048]{1,0:T(8,128)(2,1)S(1)}, bf16[32,2048]{1,0:T(8,128)(2,1)S(1)}, u32[]{:S(2)}, u32[]{:S(2)}) %collective-permute-start.15) | collective-permute-done | bytes 131104 | tf_op jit(solution)/shard_map/ppermute | solution.py:460
  30.6 1.5 %shard_map.52 = (f32[9,384,128]{2,1,0:T(8,128)S(1)}, f32[384,128]{1,0:T(8,128)S(1)}, f32[32,384]{1,0:T(8,128)S(1)}, f32[1,128]{1,0:T(1,128)S(1)}) custom-call(s32[1]{0:T(128)} %bitcast.refs_0_, f32[1,128]{1,0:T(1,128)S(1)} %get-tuple-element.34.refs_1_, bf16[64,2048]{1,0:T(8,128)(2,1)S(1)} %get-tuple-element.71.refs_2_, ...), custom_call_target="tpu_custom_call" | custom-call | flops 603979776 | bytes 2097152 | tf_op jit(solution)/shard_map/pallas_call | solution.py:558
  33.1 1.9 %shard_map.54 = (f32[9,512,128]{2,1,0:T(8,128)S(1)}, f32[512,128]{1,0:T(8,128)S(1)}, f32[32,512]{1,0:T(8,128)S(1)}, f32[16,512]{1,0:T(8,128)S(1)}) custom-call(s32[1]{0:T(128)} %bitcast.refs_0_, f32[1,128]{1,0:T(1,128)S(1)} %get-tuple-element.36.refs_1_, bf16[64,2048]{1,0:T(8,128)(2,1)S(1)} %get-tuple-element.71.refs_2_, ...), custom_call_target="tpu_custom_call" | custom-call | flops 805306368 | bytes 2097152 | tf_op jit(solution)/shard_map/pallas_call | solution.py:558
  35.0 1.2 %collective-permute-start.19 = (f32[16,512]{1,0:T(8,128)S(1)}, f32[16,512]{1,0:T(8,128)S(1)}, u32[]{:S(2)}, u32[]{:S(2)}) collective-permute-start(f32[16,512]{1,0:T(8,128)S(1)} %get-tuple-element.41.refs_1_), channel_id=1, source_target_pairs={{0,2},{1,11},{2,0},{3,9},{4,6},{5,15},{6,4},{7,13},{8,10},{9,3},{1... | collective-permute-start | bytes 98312 | tf_op jit(solution)/shard_map/ppermute | solution.py:460
  36.3 1.7 %collective-permute-start.20 = (f32[16,512]{1,0:T(8,128)S(1)}, f32[16,512]{1,0:T(8,128)S(1)}, u32[]{:S(2)}, u32[]{:S(2)}) collective-permute-start(f32[16,512]{1,0:T(8,128)S(1)} %get-tuple-element.41.refs_1_), channel_id=1, source_target_pairs={{0,8},{1,9},{2,10},{3,11},{4,12},{5,13},{6,14},{7,15},{8,0},{9,1},... | collective-permute-start | bytes 98312 | tf_op jit(solution)/shard_map/ppermute | solution.py:460
  40.7 1.2 %collective-permute-start.26 = (bf16[128,1024]{1,0:T(8,128)(2,1)S(1)}, bf16[128,1024]{1,0:T(8,128)(2,1)S(1)}, u32[]{:S(2)}, u32[]{:S(2)}) collective-permute-start(bf16[128,1024]{1,0:T(8,128)(2,1)S(1)} %get-tuple-element.62), channel_id=1, source_target_pairs={{0,2},{1,5},{2,0},{3,7},{4,6},{5,1},{6,4},{7,3},{8,10},{9,13},{10,... | collective-permute-start | bytes 786440 | tf_op jit(solution)/shard_map/ppermute | solution.py:460
  41.9 1.3 %shard_map.56 = (bf16[128,1024]{1,0:T(8,128)(2,1)S(1)}, bf16[128,1024]{1,0:T(8,128)(2,1)S(1)}) custom-call(s32[1]{0:T(128)} %bitcast.refs_0_, f32[16,512]{1,0:T(8,128)S(1)} %get-tuple-element.41.refs_1_, f32[16,512]{1,0:T(8,128)S(1)} %collective-permute-done.19.refs_2_, f32[16,512]{1,0:T(8,128)S(1)} %collective-permute-done.20.refs_3_, ...), custom_call_target="tpu_custom_call" | custom-call | flops 1073741824 | bytes 4194304 | tf_op jit(solution)/shard_map/pallas_call | solution.py:587
  44.2 1.2 %collective-permute-start.22 = (bf16[128,1024]{1,0:T(8,128)(2,1)S(1)}, bf16[128,1024]{1,0:T(8,128)(2,1)S(1)}, u32[]{:S(2)}, u32[]{:S(2)}) collective-permute-start(bf16[128,1024]{1,0:T(8,128)(2,1)S(1)} %get-tuple-element.54), channel_id=1, source_target_pairs={{0,2},{1,5},{2,0},{3,7},{4,6},{5,1},{6,4},{7,3},{8,10},{9,13},{10,... | collective-permute-start | bytes 786440 | tf_op jit(solution)/shard_map/ppermute | solution.py:460
  45.3 2.1 %shard_map.58 = (f32[128,1024]{1,0:T(8,128)S(1)}, bf16[128,1024]{1,0:T(8,128)(2,1)S(1)}, f32[128,1024]{1,0:T(8,128)S(1)}) custom-call(s32[1]{0:T(128)} %bitcast.refs_0_, f32[16,512]{1,0:T(8,128)S(1)} %get-tuple-element.41.refs_1_, f32[16,512]{1,0:T(8,128)S(1)} %collective-permute-done.19.refs_2_, f32[16,512]{1,0:T(8,128)S(1)} %collective-permute-done.20.refs_3_, ...), custom_call_target="tpu_custom_call" | custom-call | flops 1073741824 | bytes 4194304 | tf_op jit(solution)/shard_map/pallas_call | solution.py:587
  48.4 1.3 %shard_map.55 = (f32[128,1024]{1,0:T(8,128)S(1)}, f32[128,1024]{1,0:T(8,128)S(1)}) custom-call(s32[1]{0:T(128)} %bitcast.refs_0_, f32[16,512]{1,0:T(8,128)S(1)} %get-tuple-element.41.refs_1_, f32[16,512]{1,0:T(8,128)S(1)} %collective-permute-done.19.refs_2_, f32[16,512]{1,0:T(8,128)S(1)} %collective-permute-done.20.refs_3_, ...), custom_call_target="tpu_custom_call" | custom-call | flops 1073741824 | bytes 4194304 | tf_op jit(solution)/shard_map/pallas_call | solution.py:587
  49.7 1.8 %collective-permute-start.27 = (bf16[128,1024]{1,0:T(8,128)(2,1)S(1)}, bf16[128,1024]{1,0:T(8,128)(2,1)S(1)}, u32[]{:S(2)}, u32[]{:S(2)}) collective-permute-start(bf16[128,1024]{1,0:T(8,128)(2,1)S(1)} %add_convert_fusion), channel_id=1, source_target_pairs={{0,8},{1,17},{2,10},{3,19},{4,12},{5,21},{6,14},{7,23},{8,0},{9,25... | collective-permute-start | bytes 786440 | tf_op jit(solution)/shard_map/ppermute | solution.py:460
  51.5 4.1 %collective-permute-done.23 = bf16[128,1024]{1,0:T(8,128)(2,1)S(1)} collective-permute-done((bf16[128,1024]{1,0:T(8,128)(2,1)S(1)}, bf16[128,1024]{1,0:T(8,128)(2,1)S(1)}, u32[]{:S(2)}, u32[]{:S(2)}) %collective-permute-start.23) | collective-permute-done | bytes 262176 | tf_op jit(solution)/shard_map/ppermute | solution.py:460
  56.2 1.3 %collective-permute-start.24 = (bf16[64,1024]{1,0:T(8,128)(2,1)S(1)}, bf16[64,1024]{1,0:T(8,128)(2,1)S(1)}, u32[]{:S(2)}, u32[]{:S(2)}) collective-permute-start(bf16[64,1024]{1,0:T(8,128)(2,1)S(1)} %get-tuple-element.72), channel_id=1, source_target_pairs={{0,8},{1,17},{2,10},{3,19},{4,12},{5,21},{6,14},{7,23},{8,0},{9,25... | collective-permute-start | bytes 393224 | tf_op jit(solution)/shard_map/ppermute | solution.py:460
  58.9 5.7 %collective-permute-done.24 = bf16[64,1024]{1,0:T(8,128)(2,1)S(1)} collective-permute-done((bf16[64,1024]{1,0:T(8,128)(2,1)S(1)}, bf16[64,1024]{1,0:T(8,128)(2,1)S(1)}, u32[]{:S(2)}, u32[]{:S(2)}) %collective-permute-start.24) | collective-permute-done | bytes 131104 | tf_op jit(solution)/shard_map/ppermute | solution.py:460
  (60 shorter events, 16.5 us)
Async XLA Ops:
  1.7 6.6 %collective-permute-start.1 = (bf16[64,2048]{1,0:T(8,128)(2,1)S(1)}, bf16[64,2048]{1,0:T(8,128)(2,1)S(1)}, u32[]{:S(2)}, u32[]{:S(2)}) collective-permute-start(bf16[64,2048]{1,0:T(8,128)(2,1)S(1)} %get-tuple-element.70.refs_7_.refs_6_.refs_21_), channel_id=1, source_target_pairs={{0,1},{1,0},{2,3},{3,2},{4,5},{5,4},{6,7},{7,6},{8,9},{9,8},{10,11... | collective-permute-start | bytes 786440 | tf_op jit(solution)/shard_map/ppermute | solution.py:460
  2.3 8.9 %collective-permute-start.2 = (bf16[64,2048]{1,0:T(8,128)(2,1)S(1)}, bf16[64,2048]{1,0:T(8,128)(2,1)S(1)}, u32[]{:S(2)}, u32[]{:S(2)}) collective-permute-start(bf16[64,2048]{1,0:T(8,128)(2,1)S(1)} %get-tuple-element.71.refs_2_), channel_id=1, source_target_pairs={{0,2},{1,5},{2,0},{3,7},{4,6},{5,1},{6,4},{7,3},{8,10},{9,13},{10,... | collective-permute-start | bytes 786440 | tf_op jit(solution)/shard_map/ppermute | solution.py:460
  4.8 9.3 %collective-permute-start.4 = (bf16[64,2048]{1,0:T(8,128)(2,1)S(1)}, bf16[64,2048]{1,0:T(8,128)(2,1)S(1)}, u32[]{:S(2)}, u32[]{:S(2)}) collective-permute-start(bf16[64,2048]{1,0:T(8,128)(2,1)S(1)} %get-tuple-element.71.refs_2_), channel_id=1, source_target_pairs={{0,1},{1,0},{2,3},{3,2},{4,5},{5,4},{6,7},{7,6},{8,9},{9,8},{10,11... | collective-permute-start | bytes 786440 | tf_op jit(solution)/shard_map/ppermute | solution.py:460
  5.0 9.1 %collective-permute-start.7 = (bf16[64,2048]{1,0:T(8,128)(2,1)S(1)}, bf16[64,2048]{1,0:T(8,128)(2,1)S(1)}, u32[]{:S(2)}, u32[]{:S(2)}) collective-permute-start(bf16[64,2048]{1,0:T(8,128)(2,1)S(1)} %get-tuple-element.71.refs_2_), channel_id=1, source_target_pairs={{0,8},{1,17},{2,10},{3,19},{4,12},{5,21},{6,14},{7,23},{8,0},{9,25... | collective-permute-start | bytes 786440 | tf_op jit(solution)/shard_map/ppermute | solution.py:460
  8.3 7.3 %collective-permute-start.3 = (bf16[64,2048]{1,0:T(8,128)(2,1)S(1)}, bf16[64,2048]{1,0:T(8,128)(2,1)S(1)}, u32[]{:S(2)}, u32[]{:S(2)}) collective-permute-start(bf16[64,2048]{1,0:T(8,128)(2,1)S(1)} %collective-permute-done.1.refs_3_), channel_id=1, source_target_pairs={{0,2},{1,5},{2,0},{3,7},{4,6},{5,1},{6,4},{7,3},{8,10},{9,13},{10,... | collective-permute-start | bytes 786440 | tf_op jit(solution)/shard_map/ppermute | solution.py:460
  9.5 7.4 %collective-permute-start.8 = (bf16[32,2048]{1,0:T(8,128)(2,1)S(1)}, bf16[32,2048]{1,0:T(8,128)(2,1)S(1)}, u32[]{:S(2)}, u32[]{:S(2)}) collective-permute-start(bf16[32,2048]{1,0:T(8,128)(2,1)S(1)} %get-tuple-element.75), channel_id=1, source_target_pairs={{0,8},{1,17},{2,10},{3,19},{4,12},{5,21},{6,14},{7,23},{8,0},{9,25... | collective-permute-start | bytes 393224 | tf_op jit(solution)/shard_map/ppermute | solution.py:460
  11.1 12.1 %collective-permute-start.5 = (bf16[64,2048]{1,0:T(8,128)(2,1)S(1)}, bf16[64,2048]{1,0:T(8,128)(2,1)S(1)}, u32[]{:S(2)}, u32[]{:S(2)}) collective-permute-start(bf16[64,2048]{1,0:T(8,128)(2,1)S(1)} %collective-permute-done.2.refs_4_), channel_id=1, source_target_pairs={{0,1},{1,0},{2,3},{3,2},{4,5},{5,4},{6,7},{7,6},{8,9},{9,8},{10,11... | collective-permute-start | bytes 786440 | tf_op jit(solution)/shard_map/ppermute | solution.py:460
  14.1 10.5 %collective-permute-start.10 = (bf16[64,2048]{1,0:T(8,128)(2,1)S(1)}, bf16[64,2048]{1,0:T(8,128)(2,1)S(1)}, u32[]{:S(2)}, u32[]{:S(2)}) collective-permute-start(bf16[64,2048]{1,0:T(8,128)(2,1)S(1)} %collective-permute-done.7.refs_2_.refs_6_), channel_id=1, source_target_pairs={{0,1},{1,0},{2,3},{3,2},{4,5},{5,4},{6,7},{7,6},{8,9},{9,8},{10,11... | collective-permute-start | bytes 786440 | tf_op jit(solution)/shard_map/ppermute | solution.py:460
  14.1 10.7 %collective-permute-start.13 = (bf16[64,2048]{1,0:T(8,128)(2,1)S(1)}, bf16[64,2048]{1,0:T(8,128)(2,1)S(1)}, u32[]{:S(2)}, u32[]{:S(2)}) collective-permute-start(bf16[64,2048]{1,0:T(8,128)(2,1)S(1)} %collective-permute-done.7.refs_2_.refs_6_), channel_id=1, source_target_pairs={{0,2},{1,5},{2,0},{3,7},{4,6},{5,1},{6,4},{7,3},{8,10},{9,13},{10,... | collective-permute-start | bytes 786440 | tf_op jit(solution)/shard_map/ppermute | solution.py:460
  15.6 9.8 %collective-permute-start.6 = (bf16[64,2048]{1,0:T(8,128)(2,1)S(1)}, bf16[64,2048]{1,0:T(8,128)(2,1)S(1)}, u32[]{:S(2)}, u32[]{:S(2)}) collective-permute-start(bf16[64,2048]{1,0:T(8,128)(2,1)S(1)} %collective-permute-done.3.refs_5_), channel_id=1, source_target_pairs={{0,1},{1,0},{2,3},{3,2},{4,5},{5,4},{6,7},{7,6},{8,9},{9,8},{10,11... | collective-permute-start | bytes 786440 | tf_op jit(solution)/shard_map/ppermute | solution.py:460
  16.9 6.3 %collective-permute-start.9 = (bf16[32,2048]{1,0:T(8,128)(2,1)S(1)}, bf16[32,2048]{1,0:T(8,128)(2,1)S(1)}, u32[]{:S(2)}, u32[]{:S(2)}) collective-permute-start(bf16[32,2048]{1,0:T(8,128)(2,1)S(1)} %get-tuple-element.74), channel_id=1, source_target_pairs={{0,8},{1,17},{2,10},{3,19},{4,12},{5,21},{6,14},{7,23},{8,0},{9,25... | collective-permute-start | bytes 393224 | tf_op jit(solution)/shard_map/ppermute | solution.py:460
  23.2 7.3 %collective-permute-start.11 = (bf16[32,2048]{1,0:T(8,128)(2,1)S(1)}, bf16[32,2048]{1,0:T(8,128)(2,1)S(1)}, u32[]{:S(2)}, u32[]{:S(2)}) collective-permute-start(bf16[32,2048]{1,0:T(8,128)(2,1)S(1)} %collective-permute-done.8.refs_3_.refs_7_), channel_id=1, source_target_pairs={{0,1},{1,0},{2,3},{3,2},{4,5},{5,4},{6,7},{7,6},{8,9},{9,8},{10,11... | collective-permute-start | bytes 393224 | tf_op jit(solution)/shard_map/ppermute | solution.py:460
  23.2 5.0 %collective-permute-start.14 = (bf16[32,2048]{1,0:T(8,128)(2,1)S(1)}, bf16[32,2048]{1,0:T(8,128)(2,1)S(1)}, u32[]{:S(2)}, u32[]{:S(2)}) collective-permute-start(bf16[32,2048]{1,0:T(8,128)(2,1)S(1)} %collective-permute-done.8.refs_3_.refs_7_), channel_id=1, source_target_pairs={{0,2},{1,5},{2,0},{3,7},{4,6},{5,1},{6,4},{7,3},{8,10},{9,13},{10,... | collective-permute-start | bytes 393224 | tf_op jit(solution)/shard_map/ppermute | solution.py:460
  24.6 6.0 %collective-permute-start.12 = (bf16[32,2048]{1,0:T(8,128)(2,1)S(1)}, bf16[32,2048]{1,0:T(8,128)(2,1)S(1)}, u32[]{:S(2)}, u32[]{:S(2)}) collective-permute-start(bf16[32,2048]{1,0:T(8,128)(2,1)S(1)} %collective-permute-done.9.refs_4_.refs_8_), channel_id=1, source_target_pairs={{0,1},{1,0},{2,3},{3,2},{4,5},{5,4},{6,7},{7,6},{8,9},{9,8},{10,11... | collective-permute-start | bytes 393224 | tf_op jit(solution)/shard_map/ppermute | solution.py:460
  25.4 7.6 %collective-permute-start.16 = (bf16[64,2048]{1,0:T(8,128)(2,1)S(1)}, bf16[64,2048]{1,0:T(8,128)(2,1)S(1)}, u32[]{:S(2)}, u32[]{:S(2)}) collective-permute-start(bf16[64,2048]{1,0:T(8,128)(2,1)S(1)} %collective-permute-done.13.refs_2_.refs_9_), channel_id=1, source_target_pairs={{0,1},{1,0},{2,3},{3,2},{4,5},{5,4},{6,7},{7,6},{8,9},{9,8},{10,11... | collective-permute-start | bytes 786440 | tf_op jit(solution)/shard_map/ppermute | solution.py:460
  40.7 9.0 %collective-permute-start.26 = (bf16[128,1024]{1,0:T(8,128)(2,1)S(1)}, bf16[128,1024]{1,0:T(8,128)(2,1)S(1)}, u32[]{:S(2)}, u32[]{:S(2)}) collective-permute-start(bf16[128,1024]{1,0:T(8,128)(2,1)S(1)} %get-tuple-element.62), channel_id=1, source_target_pairs={{0,2},{1,5},{2,0},{3,7},{4,6},{5,1},{6,4},{7,3},{8,10},{9,13},{10,... | collective-permute-start | bytes 786440 | tf_op jit(solution)/shard_map/ppermute | solution.py:460
  43.3 14.3 %collective-permute-start.25 = (bf16[128,1024]{1,0:T(8,128)(2,1)S(1)}, bf16[128,1024]{1,0:T(8,128)(2,1)S(1)}, u32[]{:S(2)}, u32[]{:S(2)}) collective-permute-start(bf16[128,1024]{1,0:T(8,128)(2,1)S(1)} %get-tuple-element.60), channel_id=1, source_target_pairs={{0,2},{1,5},{2,0},{3,7},{4,6},{5,1},{6,4},{7,3},{8,10},{9,13},{10,... | collective-permute-start | bytes 786440 | tf_op jit(solution)/shard_map/ppermute | solution.py:460
  44.2 13.3 %collective-permute-start.22 = (bf16[128,1024]{1,0:T(8,128)(2,1)S(1)}, bf16[128,1024]{1,0:T(8,128)(2,1)S(1)}, u32[]{:S(2)}, u32[]{:S(2)}) collective-permute-start(bf16[128,1024]{1,0:T(8,128)(2,1)S(1)} %get-tuple-element.54), channel_id=1, source_target_pairs={{0,2},{1,5},{2,0},{3,7},{4,6},{5,1},{6,4},{7,3},{8,10},{9,13},{10,... | collective-permute-start | bytes 786440 | tf_op jit(solution)/shard_map/ppermute | solution.py:460
  47.5 8.1 %collective-permute-start.23 = (bf16[128,1024]{1,0:T(8,128)(2,1)S(1)}, bf16[128,1024]{1,0:T(8,128)(2,1)S(1)}, u32[]{:S(2)}, u32[]{:S(2)}) collective-permute-start(bf16[128,1024]{1,0:T(8,128)(2,1)S(1)} %get-tuple-element.58), channel_id=1, source_target_pairs={{0,2},{1,5},{2,0},{3,7},{4,6},{5,1},{6,4},{7,3},{8,10},{9,13},{10,... | collective-permute-start | bytes 786440 | tf_op jit(solution)/shard_map/ppermute | solution.py:460
  49.7 7.8 %collective-permute-start.27 = (bf16[128,1024]{1,0:T(8,128)(2,1)S(1)}, bf16[128,1024]{1,0:T(8,128)(2,1)S(1)}, u32[]{:S(2)}, u32[]{:S(2)}) collective-permute-start(bf16[128,1024]{1,0:T(8,128)(2,1)S(1)} %add_convert_fusion), channel_id=1, source_target_pairs={{0,8},{1,17},{2,10},{3,19},{4,12},{5,21},{6,14},{7,23},{8,0},{9,25... | collective-permute-start | bytes 786440 | tf_op jit(solution)/shard_map/ppermute | solution.py:460
  55.7 9.0 %collective-permute-start.29 = (bf16[64,1024]{1,0:T(8,128)(2,1)S(1)}, bf16[64,1024]{1,0:T(8,128)(2,1)S(1)}, u32[]{:S(2)}, u32[]{:S(2)}) collective-permute-start(bf16[64,1024]{1,0:T(8,128)(2,1)S(1)} %get-tuple-element.73), channel_id=1, source_target_pairs={{0,9},{1,16},{2,11},{3,18},{4,13},{5,20},{6,15},{7,22},{8,1},{9,24... | collective-permute-start | bytes 393224 | tf_op jit(solution)/shard_map/ppermute | solution.py:460
  56.2 8.4 %collective-permute-start.24 = (bf16[64,1024]{1,0:T(8,128)(2,1)S(1)}, bf16[64,1024]{1,0:T(8,128)(2,1)S(1)}, u32[]{:S(2)}, u32[]{:S(2)}) collective-permute-start(bf16[64,1024]{1,0:T(8,128)(2,1)S(1)} %get-tuple-element.72), channel_id=1, source_target_pairs={{0,8},{1,17},{2,10},{3,19},{4,12},{5,21},{6,14},{7,23},{8,0},{9,25... | collective-permute-start | bytes 393224 | tf_op jit(solution)/shard_map/ppermute | solution.py:460
  57.8 6.9 %collective-permute-start.28 = (f32[64,1024]{1,0:T(8,128)S(1)}, f32[64,1024]{1,0:T(8,128)S(1)}, u32[]{:S(2)}, u32[]{:S(2)}) collective-permute-start(f32[64,1024]{1,0:T(8,128)S(1)} %get-tuple-element.63), channel_id=1, source_target_pairs={{0,1},{1,0},{2,3},{3,2},{4,5},{5,4},{6,7},{7,6},{8,9},{9,8},{10,11... | collective-permute-start | bytes 786440 | tf_op jit(solution)/shard_map/ppermute | solution.py:460
  58.8 5.8 %collective-permute-start.30 = (f32[64,1024]{1,0:T(8,128)S(1)}, f32[64,1024]{1,0:T(8,128)S(1)}, u32[]{:S(2)}, u32[]{:S(2)}) collective-permute-start(f32[64,1024]{1,0:T(8,128)S(1)} %get-tuple-element.67), channel_id=1, source_target_pairs={{0,1},{1,0},{2,3},{3,2},{4,5},{5,4},{6,7},{7,6},{8,9},{9,8},{10,11... | collective-permute-start | bytes 786440 | tf_op jit(solution)/shard_map/ppermute | solution.py:460
  (7 other events, 24.5 us)

commit v7 on v6

--- a/solution.py
+++ b/solution.py
@@ -356,7 +356,7 @@
         for _, power, inner, col_gain, row_gain in strip], axis=1)
 
 
-def last_band_kernel(groups, uppers, own_rows, masks, *refs):
+def last_band_kernel(groups, uppers, own_rows, masks, split, *refs):
     tiles = len(subtiles(groups))
     setup = band_setup(groups, uppers, own_rows, masks, refs[0], refs[1:1 + groups])
     at = 1 + groups
@@ -372,12 +372,12 @@
     weight = weight - jnp.where(id_col[rows] == id_row, logit_gain * uppers[k] ** -0.5, 0.0)
     after_ref[...] = weight
     product = jnp.dot(
-        weight.astype(jnp.bfloat16), rows_of(w_refs, uppers[k - 1], uppers[k]),
+        weight.astype(jnp.bfloat16), rows_of(w_refs, split, uppers[k]),
         preferred_element_type=jnp.float32)
-    store(out_refs, product, 0, 0, uppers[k] - uppers[k - 1], chip_rows)
-
-
-def bands_kernel(groups, uppers, own_rows, masks, *refs, block):
+    store(out_refs, product, 0, 0, uppers[k] - split, chip_rows)
+
+
+def bands_kernel(groups, uppers, own_rows, masks, split, *refs, block):
     tiles = len(subtiles(groups))
     setup = band_setup(groups, uppers, own_rows, masks, refs[0], refs[1:1 + groups])
     at = 1 + groups
@@ -402,13 +402,16 @@
     weights = [
         weights_of(segment, groups, setup, power_refs, col_refs, row_refs) for segment in block]
     running = weights[0](last) - jnp.where(hit[:fresh], scales[last], 0.0)
-    lower, upper = uppers[last - 1], uppers[last]
     product = jnp.dot(
-        running.astype(jnp.bfloat16), rows_of(w_refs, lower, upper),
+        running.astype(jnp.bfloat16), rows_of(w_refs, split, uppers[last]),
         preferred_element_type=jnp.float32)
-    store(widest, product, 0, 0, upper - lower, chip_rows)
+    store(widest, product, 0, 0, uppers[last] - split, chip_rows)
     if before_ref is not None:
         running = jnp.concatenate([running, before_ref[...]], axis=0)
+    product = jnp.dot(
+        running.astype(jnp.bfloat16), rows_of(w_refs, uppers[last - 1], split),
+        preferred_element_type=jnp.float32)
+    store(others, product, 0, uppers[last - 1], split, chip_rows)
     stack = []
     for k in range(last - 1, -1, -1):
         weight = jnp.concatenate([part(k) for part in weights], axis=0)
@@ -581,11 +584,12 @@
         common = [me, stats, first, second, swapped, *[t[0] for t in done], *[t[1] for t in done],
                   *[t[2] for t in done], *w_list]
         near = segments_of(groups)[-1][0]
-        widest = feature_dim - uppers[-2]
+        split = uppers[-2] + (feature_dim - uppers[-2]) // 4
+        widest = feature_dim - split
 
         def bands(kernel, more, outs):
             return pl.pallas_call(
-                functools.partial(kernel, groups, uppers, own_rows, document_masks),
+                functools.partial(kernel, groups, uppers, own_rows, document_masks, split),
                 out_shape=outs,
                 in_specs=[smem] + [vmem] * (len(common) - 1 + len(more)),
                 out_specs=[vmem] * len(outs),
@@ -598,7 +602,7 @@
         *far_ones, running = bands(
             last_band_kernel, [],
             gradient_shapes(widest)[near:] + [shape((groups - near) * chip_rows, total)])
-        narrow_ones = gradient_shapes(uppers[-2])
+        narrow_ones = gradient_shapes(split)
         wide_ones = gradient_shapes(widest)
         middle = segments_of(groups)[1]
 

time: 65.9 us -> 66.1 us (level)
  transfers between devices with their start and end apart: 31 -> 31, of which waited for: 9 -> 12; matrix products, arithmetic and copies ran while one was open for 2% -> 2% of each run, Pallas kernels for 14% -> 10%
where the time goes in v7:
time: 66.1 us; the launch traced here: 66 us
  starting transfers between devices  26.4 us (40%)
  waiting for transfers between devices  24.1 us (36%)
  Pallas kernels  11.4 us (17%)
  other arithmetic  3.17 us (5%)
  between operations  0.8 us (1%)
    ppermute x31, starting transfers between devices, exchange(): return lax.ppermute(x, AXES, [(i, i ^ masks_of(i)) for i in range(devices)])  26.4 us
    ppermute x31, waiting for transfers between devices, exchange(): return lax.ppermute(x, AXES, [(i, i ^ masks_of(i)) for i in range(devices)])  24.1 us
    pallas_call x5, Pallas kernels, tile(): pl.pallas_call(functools.partial(tile_kernel, span, counts, uppers, own_r...  6.26 us
    pallas_call x4, Pallas kernels, bands(): pl.pallas_call(functools.partial(kernel, groups, uppers, own_rows, docume...  5.12 us
  transfers between devices with their start and end apart: 31, of which 12 were waited for; matrix products, arithmetic and copies ran while one was open for 2% of the time, Pallas kernels for 10%

profile of v7, /device:TPU:0, one launch (start us, length us, event | category | flops | bytes accessed | tf_op | source)
XLA Modules:
  0.0 66.0 jit_solution(14693379755006074879)
XLA Ops:
  2.3 2.6 %collective-permute-start.2 = (bf16[64,2048]{1,0:T(8,128)(2,1)S(1)}, bf16[64,2048]{1,0:T(8,128)(2,1)S(1)}, u32[]{:S(2)}, u32[]{:S(2)}) collective-permute-start(bf16[64,2048]{1,0:T(8,128)(2,1)S(1)} %get-tuple-element.69.refs_2_), channel_id=1, source_target_pairs={{0,2},{1,5},{2,0},{3,7},{4,6},{5,1},{6,4},{7,3},{8,10},{9,13},{10,... | collective-permute-start | bytes 786440 | tf_op jit(solution)/shard_map/ppermute | solution.py:463
  5.0 1.6 %collective-permute-start.7 = (bf16[64,2048]{1,0:T(8,128)(2,1)S(1)}, bf16[64,2048]{1,0:T(8,128)(2,1)S(1)}, u32[]{:S(2)}, u32[]{:S(2)}) collective-permute-start(bf16[64,2048]{1,0:T(8,128)(2,1)S(1)} %get-tuple-element.69.refs_2_), channel_id=1, source_target_pairs={{0,8},{1,17},{2,10},{3,19},{4,12},{5,21},{6,14},{7,23},{8,0},{9,25... | collective-permute-start | bytes 786440 | tf_op jit(solution)/shard_map/ppermute | solution.py:463
  9.6 1.6 %collective-permute-start.8 = (bf16[32,2048]{1,0:T(8,128)(2,1)S(1)}, bf16[32,2048]{1,0:T(8,128)(2,1)S(1)}, u32[]{:S(2)}, u32[]{:S(2)}) collective-permute-start(bf16[32,2048]{1,0:T(8,128)(2,1)S(1)} %get-tuple-element.75), channel_id=1, source_target_pairs={{0,8},{1,17},{2,10},{3,19},{4,12},{5,21},{6,14},{7,23},{8,0},{9,25... | collective-permute-start | bytes 393224 | tf_op jit(solution)/shard_map/ppermute | solution.py:463
  11.3 2.8 %collective-permute-done.7.refs_2_.refs_6_ = bf16[64,2048]{1,0:T(8,128)(2,1)S(1)} collective-permute-done((bf16[64,2048]{1,0:T(8,128)(2,1)S(1)}, bf16[64,2048]{1,0:T(8,128)(2,1)S(1)}, u32[]{:S(2)}, u32[]{:S(2)}) %collective-permute-start.7) | collective-permute-done | bytes 262176 | tf_op jit(solution)/shard_map/ppermute | solution.py:463
  14.1 1.5 %collective-permute-start.13 = (bf16[64,2048]{1,0:T(8,128)(2,1)S(1)}, bf16[64,2048]{1,0:T(8,128)(2,1)S(1)}, u32[]{:S(2)}, u32[]{:S(2)}) collective-permute-start(bf16[64,2048]{1,0:T(8,128)(2,1)S(1)} %collective-permute-done.7.refs_2_.refs_6_), channel_id=1, source_target_pairs={{0,2},{1,5},{2,0},{3,7},{4,6},{5,1},{6,4},{7,3},{8,10},{9,13},{10,... | collective-permute-start | bytes 786440 | tf_op jit(solution)/shard_map/ppermute | solution.py:463
  15.6 1.6 %collective-permute-start.9 = (bf16[32,2048]{1,0:T(8,128)(2,1)S(1)}, bf16[32,2048]{1,0:T(8,128)(2,1)S(1)}, u32[]{:S(2)}, u32[]{:S(2)}) collective-permute-start(bf16[32,2048]{1,0:T(8,128)(2,1)S(1)} %get-tuple-element.74), channel_id=1, source_target_pairs={{0,8},{1,17},{2,10},{3,19},{4,12},{5,21},{6,14},{7,23},{8,0},{9,25... | collective-permute-start | bytes 393224 | tf_op jit(solution)/shard_map/ppermute | solution.py:463
  17.9 4.2 %collective-permute-done.9.refs_4_.refs_8_ = bf16[32,2048]{1,0:T(8,128)(2,1)S(1)} collective-permute-done((bf16[32,2048]{1,0:T(8,128)(2,1)S(1)}, bf16[32,2048]{1,0:T(8,128)(2,1)S(1)}, u32[]{:S(2)}, u32[]{:S(2)}) %collective-permute-start.9) | collective-permute-done | bytes 131104 | tf_op jit(solution)/shard_map/ppermute | solution.py:463
  22.8 1.4 %collective-permute-start.15 = (bf16[32,2048]{1,0:T(8,128)(2,1)S(1)}, bf16[32,2048]{1,0:T(8,128)(2,1)S(1)}, u32[]{:S(2)}, u32[]{:S(2)}) collective-permute-start(bf16[32,2048]{1,0:T(8,128)(2,1)S(1)} %collective-permute-done.9.refs_4_.refs_8_), channel_id=1, source_target_pairs={{0,2},{1,5},{2,0},{3,7},{4,6},{5,1},{6,4},{7,3},{8,10},{9,13},{10,... | collective-permute-start | bytes 393224 | tf_op jit(solution)/shard_map/ppermute | solution.py:463
  25.5 1.6 %collective-permute-done.14.refs_3_.refs_10_ = bf16[32,2048]{1,0:T(8,128)(2,1)S(1)} collective-permute-done((bf16[32,2048]{1,0:T(8,128)(2,1)S(1)}, bf16[32,2048]{1,0:T(8,128)(2,1)S(1)}, u32[]{:S(2)}, u32[]{:S(2)}) %collective-permute-start.14) | collective-permute-done | bytes 131104 | tf_op jit(solution)/shard_map/ppermute | solution.py:463
  27.1 1.4 %collective-permute-done.15.refs_4_.refs_11_ = bf16[32,2048]{1,0:T(8,128)(2,1)S(1)} collective-permute-done((bf16[32,2048]{1,0:T(8,128)(2,1)S(1)}, bf16[32,2048]{1,0:T(8,128)(2,1)S(1)}, u32[]{:S(2)}, u32[]{:S(2)}) %collective-permute-start.15) | collective-permute-done | bytes 131104 | tf_op jit(solution)/shard_map/ppermute | solution.py:463
  29.3 1.4 %shard_map.52 = (f32[9,384,128]{2,1,0:T(8,128)S(1)}, f32[384,128]{1,0:T(8,128)S(1)}, f32[32,384]{1,0:T(8,128)S(1)}, f32[1,128]{1,0:T(1,128)S(1)}) custom-call(s32[1]{0:T(128)} %bitcast.refs_0_, f32[1,128]{1,0:T(1,128)S(1)} %get-tuple-element.34.refs_1_, bf16[64,2048]{1,0:T(8,128)(2,1)S(1)} %get-tuple-element.69.refs_2_, ...), custom_call_target="tpu_custom_call" | custom-call | flops 603979776 | bytes 2097152 | tf_op jit(solution)/shard_map/pallas_call | solution.py:561
  31.8 1.9 %shard_map.54 = (f32[9,512,128]{2,1,0:T(8,128)S(1)}, f32[512,128]{1,0:T(8,128)S(1)}, f32[32,512]{1,0:T(8,128)S(1)}, f32[16,512]{1,0:T(8,128)S(1)}) custom-call(s32[1]{0:T(128)} %bitcast.refs_0_, f32[1,128]{1,0:T(1,128)S(1)} %get-tuple-element.36.refs_1_, bf16[64,2048]{1,0:T(8,128)(2,1)S(1)} %get-tuple-element.69.refs_2_, ...), custom_call_target="tpu_custom_call" | custom-call | flops 805306368 | bytes 2097152 | tf_op jit(solution)/shard_map/pallas_call | solution.py:561
  34.5 1.5 %collective-permute-start.20 = (f32[16,512]{1,0:T(8,128)S(1)}, f32[16,512]{1,0:T(8,128)S(1)}, u32[]{:S(2)}, u32[]{:S(2)}) collective-permute-start(f32[16,512]{1,0:T(8,128)S(1)} %get-tuple-element.41.refs_1_), channel_id=1, source_target_pairs={{0,8},{1,9},{2,10},{3,11},{4,12},{5,13},{6,14},{7,15},{8,0},{9,1},... | collective-permute-start | bytes 98312 | tf_op jit(solution)/shard_map/ppermute | solution.py:463
  36.0 1.7 %collective-permute-done.19.refs_2_ = f32[16,512]{1,0:T(8,128)S(1)} collective-permute-done((f32[16,512]{1,0:T(8,128)S(1)}, f32[16,512]{1,0:T(8,128)S(1)}, u32[]{:S(2)}, u32[]{:S(2)}) %collective-permute-start.19) | collective-permute-done | bytes 32800 | tf_op jit(solution)/shard_map/ppermute | solution.py:463
  39.4 2.1 %shard_map.58 = (f32[128,1280]{1,0:T(8,128)S(1)}, bf16[128,1280]{1,0:T(8,128)(2,1)S(1)}, f32[128,768]{1,0:T(8,128)S(1)}) custom-call(s32[1]{0:T(128)} %bitcast.refs_0_, f32[16,512]{1,0:T(8,128)S(1)} %get-tuple-element.41.refs_1_, f32[16,512]{1,0:T(8,128)S(1)} %collective-permute-done.19.refs_2_, f32[16,512]{1,0:T(8,128)S(1)} %collective-permute-done.20.refs_3_, ...), custom_call_target="tpu_custom_call" | custom-call | flops 1073741824 | bytes 4194304 | tf_op jit(solution)/shard_map/pallas_call | solution.py:591
  42.3 1.2 %collective-permute-start.26 = (bf16[128,768]{1,0:T(8,128)(2,1)S(1)}, bf16[128,768]{1,0:T(8,128)(2,1)S(1)}, u32[]{:S(2)}, u32[]{:S(2)}) collective-permute-start(bf16[128,768]{1,0:T(8,128)(2,1)S(1)} %get-tuple-element.62), channel_id=1, source_target_pairs={{0,2},{1,5},{2,0},{3,7},{4,6},{5,1},{6,4},{7,3},{8,10},{9,13},{10,... | collective-permute-start | bytes 589832 | tf_op jit(solution)/shard_map/ppermute | solution.py:463
  43.6 1.3 %shard_map.56 = (bf16[128,1280]{1,0:T(8,128)(2,1)S(1)}, bf16[128,768]{1,0:T(8,128)(2,1)S(1)}) custom-call(s32[1]{0:T(128)} %bitcast.refs_0_, f32[16,512]{1,0:T(8,128)S(1)} %get-tuple-element.41.refs_1_, f32[16,512]{1,0:T(8,128)S(1)} %collective-permute-done.19.refs_2_, f32[16,512]{1,0:T(8,128)S(1)} %collective-permute-done.20.refs_3_, ...), custom_call_target="tpu_custom_call" | custom-call | flops 1073741824 | bytes 4194304 | tf_op jit(solution)/shard_map/pallas_call | solution.py:591
  47.0 1.3 %shard_map.55 = (f32[128,1280]{1,0:T(8,128)S(1)}, f32[128,768]{1,0:T(8,128)S(1)}) custom-call(s32[1]{0:T(128)} %bitcast.refs_0_, f32[16,512]{1,0:T(8,128)S(1)} %get-tuple-element.41.refs_1_, f32[16,512]{1,0:T(8,128)S(1)} %collective-permute-done.19.refs_2_, f32[16,512]{1,0:T(8,128)S(1)} %collective-permute-done.20.refs_3_, ...), custom_call_target="tpu_custom_call" | custom-call | flops 1073741824 | bytes 4194304 | tf_op jit(solution)/shard_map/pallas_call | solution.py:591
  48.2 2.5 %collective-permute-done.26 = bf16[128,768]{1,0:T(8,128)(2,1)S(1)} collective-permute-done((bf16[128,768]{1,0:T(8,128)(2,1)S(1)}, bf16[128,768]{1,0:T(8,128)(2,1)S(1)}, u32[]{:S(2)}, u32[]{:S(2)}) %collective-permute-start.26) | collective-permute-done | bytes 196640 | tf_op jit(solution)/shard_map/ppermute | solution.py:463
  50.7 1.6 %collective-permute-start.27 = (bf16[128,768]{1,0:T(8,128)(2,1)S(1)}, bf16[128,768]{1,0:T(8,128)(2,1)S(1)}, u32[]{:S(2)}, u32[]{:S(2)}) collective-permute-start(bf16[128,768]{1,0:T(8,128)(2,1)S(1)} %add_convert_fusion.1), channel_id=1, source_target_pairs={{0,8},{1,17},{2,10},{3,19},{4,12},{5,21},{6,14},{7,23},{8,0},{9,25... | collective-permute-start | bytes 589832 | tf_op jit(solution)/shard_map/ppermute | solution.py:463
  53.0 1.2 %collective-permute-done.22 = bf16[128,1280]{1,0:T(8,128)(2,1)S(1)} collective-permute-done((bf16[128,1280]{1,0:T(8,128)(2,1)S(1)}, bf16[128,1280]{1,0:T(8,128)(2,1)S(1)}, u32[]{:S(2)}, u32[]{:S(2)}) %collective-permute-start.22) | collective-permute-done | bytes 327712 | tf_op jit(solution)/shard_map/ppermute | solution.py:463
  54.8 1.9 %collective-permute-start.28 = (f32[64,1280]{1,0:T(8,128)S(1)}, f32[64,1280]{1,0:T(8,128)S(1)}, u32[]{:S(2)}, u32[]{:S(2)}) collective-permute-start(f32[64,1280]{1,0:T(8,128)S(1)} %get-tuple-element.63), channel_id=1, source_target_pairs={{0,1},{1,0},{2,3},{3,2},{4,5},{5,4},{6,7},{7,6},{8,9},{9,8},{10,11... | collective-permute-start | bytes 983048 | tf_op jit(solution)/shard_map/ppermute | solution.py:463
  58.2 3.0 %collective-permute-done.24 = bf16[64,1280]{1,0:T(8,128)(2,1)S(1)} collective-permute-done((bf16[64,1280]{1,0:T(8,128)(2,1)S(1)}, bf16[64,1280]{1,0:T(8,128)(2,1)S(1)}, u32[]{:S(2)}, u32[]{:S(2)}) %collective-permute-start.24) | collective-permute-done | bytes 163872 | tf_op jit(solution)/shard_map/ppermute | solution.py:463
  61.2 3.7 %collective-permute-done.29 = bf16[64,1280]{1,0:T(8,128)(2,1)S(1)} collective-permute-done((bf16[64,1280]{1,0:T(8,128)(2,1)S(1)}, bf16[64,1280]{1,0:T(8,128)(2,1)S(1)}, u32[]{:S(2)}, u32[]{:S(2)}) %collective-permute-start.29) | collective-permute-done | bytes 163872 | tf_op jit(solution)/shard_map/ppermute | solution.py:463
  (61 shorter events, 18.8 us)
Async XLA Ops:
  1.7 6.6 %collective-permute-start.1 = (bf16[64,2048]{1,0:T(8,128)(2,1)S(1)}, bf16[64,2048]{1,0:T(8,128)(2,1)S(1)}, u32[]{:S(2)}, u32[]{:S(2)}) collective-permute-start(bf16[64,2048]{1,0:T(8,128)(2,1)S(1)} %get-tuple-element.68.refs_7_.refs_6_.refs_21_), channel_id=1, source_target_pairs={{0,1},{1,0},{2,3},{3,2},{4,5},{5,4},{6,7},{7,6},{8,9},{9,8},{10,11... | collective-permute-start | bytes 786440 | tf_op jit(solution)/shard_map/ppermute | solution.py:463
  2.3 7.2 %collective-permute-start.2 = (bf16[64,2048]{1,0:T(8,128)(2,1)S(1)}, bf16[64,2048]{1,0:T(8,128)(2,1)S(1)}, u32[]{:S(2)}, u32[]{:S(2)}) collective-permute-start(bf16[64,2048]{1,0:T(8,128)(2,1)S(1)} %get-tuple-element.69.refs_2_), channel_id=1, source_target_pairs={{0,2},{1,5},{2,0},{3,7},{4,6},{5,1},{6,4},{7,3},{8,10},{9,13},{10,... | collective-permute-start | bytes 786440 | tf_op jit(solution)/shard_map/ppermute | solution.py:463
  4.8 10.8 %collective-permute-start.4 = (bf16[64,2048]{1,0:T(8,128)(2,1)S(1)}, bf16[64,2048]{1,0:T(8,128)(2,1)S(1)}, u32[]{:S(2)}, u32[]{:S(2)}) collective-permute-start(bf16[64,2048]{1,0:T(8,128)(2,1)S(1)} %get-tuple-element.69.refs_2_), channel_id=1, source_target_pairs={{0,1},{1,0},{2,3},{3,2},{4,5},{5,4},{6,7},{7,6},{8,9},{9,8},{10,11... | collective-permute-start | bytes 786440 | tf_op jit(solution)/shard_map/ppermute | solution.py:463
  5.0 9.1 %collective-permute-start.7 = (bf16[64,2048]{1,0:T(8,128)(2,1)S(1)}, bf16[64,2048]{1,0:T(8,128)(2,1)S(1)}, u32[]{:S(2)}, u32[]{:S(2)}) collective-permute-start(bf16[64,2048]{1,0:T(8,128)(2,1)S(1)} %get-tuple-element.69.refs_2_), channel_id=1, source_target_pairs={{0,8},{1,17},{2,10},{3,19},{4,12},{5,21},{6,14},{7,23},{8,0},{9,25... | collective-permute-start | bytes 786440 | tf_op jit(solution)/shard_map/ppermute | solution.py:463
  8.3 7.3 %collective-permute-start.3 = (bf16[64,2048]{1,0:T(8,128)(2,1)S(1)}, bf16[64,2048]{1,0:T(8,128)(2,1)S(1)}, u32[]{:S(2)}, u32[]{:S(2)}) collective-permute-start(bf16[64,2048]{1,0:T(8,128)(2,1)S(1)} %collective-permute-done.1.refs_3_), channel_id=1, source_target_pairs={{0,2},{1,5},{2,0},{3,7},{4,6},{5,1},{6,4},{7,3},{8,10},{9,13},{10,... | collective-permute-start | bytes 786440 | tf_op jit(solution)/shard_map/ppermute | solution.py:463
  9.5 12.6 %collective-permute-start.5 = (bf16[64,2048]{1,0:T(8,128)(2,1)S(1)}, bf16[64,2048]{1,0:T(8,128)(2,1)S(1)}, u32[]{:S(2)}, u32[]{:S(2)}) collective-permute-start(bf16[64,2048]{1,0:T(8,128)(2,1)S(1)} %collective-permute-done.2.refs_4_), channel_id=1, source_target_pairs={{0,1},{1,0},{2,3},{3,2},{4,5},{5,4},{6,7},{7,6},{8,9},{9,8},{10,11... | collective-permute-start | bytes 786440 | tf_op jit(solution)/shard_map/ppermute | solution.py:463
  9.6 7.6 %collective-permute-start.8 = (bf16[32,2048]{1,0:T(8,128)(2,1)S(1)}, bf16[32,2048]{1,0:T(8,128)(2,1)S(1)}, u32[]{:S(2)}, u32[]{:S(2)}) collective-permute-start(bf16[32,2048]{1,0:T(8,128)(2,1)S(1)} %get-tuple-element.75), channel_id=1, source_target_pairs={{0,8},{1,17},{2,10},{3,19},{4,12},{5,21},{6,14},{7,23},{8,0},{9,25... | collective-permute-start | bytes 393224 | tf_op jit(solution)/shard_map/ppermute | solution.py:463
  14.1 8.7 %collective-permute-start.13 = (bf16[64,2048]{1,0:T(8,128)(2,1)S(1)}, bf16[64,2048]{1,0:T(8,128)(2,1)S(1)}, u32[]{:S(2)}, u32[]{:S(2)}) collective-permute-start(bf16[64,2048]{1,0:T(8,128)(2,1)S(1)} %collective-permute-done.7.refs_2_.refs_6_), channel_id=1, source_target_pairs={{0,2},{1,5},{2,0},{3,7},{4,6},{5,1},{6,4},{7,3},{8,10},{9,13},{10,... | collective-permute-start | bytes 786440 | tf_op jit(solution)/shard_map/ppermute | solution.py:463
  15.6 8.6 %collective-permute-start.6 = (bf16[64,2048]{1,0:T(8,128)(2,1)S(1)}, bf16[64,2048]{1,0:T(8,128)(2,1)S(1)}, u32[]{:S(2)}, u32[]{:S(2)}) collective-permute-start(bf16[64,2048]{1,0:T(8,128)(2,1)S(1)} %collective-permute-done.3.refs_5_), channel_id=1, source_target_pairs={{0,1},{1,0},{2,3},{3,2},{4,5},{5,4},{6,7},{7,6},{8,9},{9,8},{10,11... | collective-permute-start | bytes 786440 | tf_op jit(solution)/shard_map/ppermute | solution.py:463
  15.6 6.4 %collective-permute-start.9 = (bf16[32,2048]{1,0:T(8,128)(2,1)S(1)}, bf16[32,2048]{1,0:T(8,128)(2,1)S(1)}, u32[]{:S(2)}, u32[]{:S(2)}) collective-permute-start(bf16[32,2048]{1,0:T(8,128)(2,1)S(1)} %get-tuple-element.74), channel_id=1, source_target_pairs={{0,8},{1,17},{2,10},{3,19},{4,12},{5,21},{6,14},{7,23},{8,0},{9,25... | collective-permute-start | bytes 393224 | tf_op jit(solution)/shard_map/ppermute | solution.py:463
  17.3 5.5 %collective-permute-start.11 = (bf16[32,2048]{1,0:T(8,128)(2,1)S(1)}, bf16[32,2048]{1,0:T(8,128)(2,1)S(1)}, u32[]{:S(2)}, u32[]{:S(2)}) collective-permute-start(bf16[32,2048]{1,0:T(8,128)(2,1)S(1)} %collective-permute-done.8.refs_3_.refs_7_), channel_id=1, source_target_pairs={{0,1},{1,0},{2,3},{3,2},{4,5},{5,4},{6,7},{7,6},{8,9},{9,8},{10,11... | collective-permute-start | bytes 393224 | tf_op jit(solution)/shard_map/ppermute | solution.py:463
  22.1 7.2 %collective-permute-start.10 = (bf16[64,2048]{1,0:T(8,128)(2,1)S(1)}, bf16[64,2048]{1,0:T(8,128)(2,1)S(1)}, u32[]{:S(2)}, u32[]{:S(2)}) collective-permute-start(bf16[64,2048]{1,0:T(8,128)(2,1)S(1)} %collective-permute-done.7.refs_2_.refs_6_), channel_id=1, source_target_pairs={{0,1},{1,0},{2,3},{3,2},{4,5},{5,4},{6,7},{7,6},{8,9},{9,8},{10,11... | collective-permute-start | bytes 786440 | tf_op jit(solution)/shard_map/ppermute | solution.py:463
  22.8 6.5 %collective-permute-start.12 = (bf16[32,2048]{1,0:T(8,128)(2,1)S(1)}, bf16[32,2048]{1,0:T(8,128)(2,1)S(1)}, u32[]{:S(2)}, u32[]{:S(2)}) collective-permute-start(bf16[32,2048]{1,0:T(8,128)(2,1)S(1)} %collective-permute-done.9.refs_4_.refs_8_), channel_id=1, source_target_pairs={{0,1},{1,0},{2,3},{3,2},{4,5},{5,4},{6,7},{7,6},{8,9},{9,8},{10,11... | collective-permute-start | bytes 393224 | tf_op jit(solution)/shard_map/ppermute | solution.py:463
  22.8 5.6 %collective-permute-start.15 = (bf16[32,2048]{1,0:T(8,128)(2,1)S(1)}, bf16[32,2048]{1,0:T(8,128)(2,1)S(1)}, u32[]{:S(2)}, u32[]{:S(2)}) collective-permute-start(bf16[32,2048]{1,0:T(8,128)(2,1)S(1)} %collective-permute-done.9.refs_4_.refs_8_), channel_id=1, source_target_pairs={{0,2},{1,5},{2,0},{3,7},{4,6},{5,1},{6,4},{7,3},{8,10},{9,13},{10,... | collective-permute-start | bytes 393224 | tf_op jit(solution)/shard_map/ppermute | solution.py:463
  24.2 7.6 %collective-permute-start.16 = (bf16[64,2048]{1,0:T(8,128)(2,1)S(1)}, bf16[64,2048]{1,0:T(8,128)(2,1)S(1)}, u32[]{:S(2)}, u32[]{:S(2)}) collective-permute-start(bf16[64,2048]{1,0:T(8,128)(2,1)S(1)} %collective-permute-done.13.refs_2_.refs_9_), channel_id=1, source_target_pairs={{0,1},{1,0},{2,3},{3,2},{4,5},{5,4},{6,7},{7,6},{8,9},{9,8},{10,11... | collective-permute-start | bytes 786440 | tf_op jit(solution)/shard_map/ppermute | solution.py:463
  41.5 10.9 %collective-permute-start.23 = (bf16[128,1280]{1,0:T(8,128)(2,1)S(1)}, bf16[128,1280]{1,0:T(8,128)(2,1)S(1)}, u32[]{:S(2)}, u32[]{:S(2)}) collective-permute-start(bf16[128,1280]{1,0:T(8,128)(2,1)S(1)} %get-tuple-element.58), channel_id=1, source_target_pairs={{0,2},{1,5},{2,0},{3,7},{4,6},{5,1},{6,4},{7,3},{8,10},{9,13},{10,... | collective-permute-start | bytes 983048 | tf_op jit(solution)/shard_map/ppermute | solution.py:463
  42.3 8.4 %collective-permute-start.26 = (bf16[128,768]{1,0:T(8,128)(2,1)S(1)}, bf16[128,768]{1,0:T(8,128)(2,1)S(1)}, u32[]{:S(2)}, u32[]{:S(2)}) collective-permute-start(bf16[128,768]{1,0:T(8,128)(2,1)S(1)} %get-tuple-element.62), channel_id=1, source_target_pairs={{0,2},{1,5},{2,0},{3,7},{4,6},{5,1},{6,4},{7,3},{8,10},{9,13},{10,... | collective-permute-start | bytes 589832 | tf_op jit(solution)/shard_map/ppermute | solution.py:463
  44.9 9.4 %collective-permute-start.22 = (bf16[128,1280]{1,0:T(8,128)(2,1)S(1)}, bf16[128,1280]{1,0:T(8,128)(2,1)S(1)}, u32[]{:S(2)}, u32[]{:S(2)}) collective-permute-start(bf16[128,1280]{1,0:T(8,128)(2,1)S(1)} %get-tuple-element.54), channel_id=1, source_target_pairs={{0,2},{1,5},{2,0},{3,7},{4,6},{5,1},{6,4},{7,3},{8,10},{9,13},{10,... | collective-permute-start | bytes 983048 | tf_op jit(solution)/shard_map/ppermute | solution.py:463
  45.8 10.9 %collective-permute-start.25 = (bf16[128,768]{1,0:T(8,128)(2,1)S(1)}, bf16[128,768]{1,0:T(8,128)(2,1)S(1)}, u32[]{:S(2)}, u32[]{:S(2)}) collective-permute-start(bf16[128,768]{1,0:T(8,128)(2,1)S(1)} %get-tuple-element.60), channel_id=1, source_target_pairs={{0,2},{1,5},{2,0},{3,7},{4,6},{5,1},{6,4},{7,3},{8,10},{9,13},{10,... | collective-permute-start | bytes 589832 | tf_op jit(solution)/shard_map/ppermute | solution.py:463
  50.7 6.9 %collective-permute-start.27 = (bf16[128,768]{1,0:T(8,128)(2,1)S(1)}, bf16[128,768]{1,0:T(8,128)(2,1)S(1)}, u32[]{:S(2)}, u32[]{:S(2)}) collective-permute-start(bf16[128,768]{1,0:T(8,128)(2,1)S(1)} %add_convert_fusion.1), channel_id=1, source_target_pairs={{0,8},{1,17},{2,10},{3,19},{4,12},{5,21},{6,14},{7,23},{8,0},{9,25... | collective-permute-start | bytes 589832 | tf_op jit(solution)/shard_map/ppermute | solution.py:463
  52.4 8.7 %collective-permute-start.24 = (bf16[64,1280]{1,0:T(8,128)(2,1)S(1)}, bf16[64,1280]{1,0:T(8,128)(2,1)S(1)}, u32[]{:S(2)}, u32[]{:S(2)}) collective-permute-start(bf16[64,1280]{1,0:T(8,128)(2,1)S(1)} %get-tuple-element.72), channel_id=1, source_target_pairs={{0,8},{1,17},{2,10},{3,19},{4,12},{5,21},{6,14},{7,23},{8,0},{9,25... | collective-permute-start | bytes 491528 | tf_op jit(solution)/shard_map/ppermute | solution.py:463
  54.3 10.5 %collective-permute-start.29 = (bf16[64,1280]{1,0:T(8,128)(2,1)S(1)}, bf16[64,1280]{1,0:T(8,128)(2,1)S(1)}, u32[]{:S(2)}, u32[]{:S(2)}) collective-permute-start(bf16[64,1280]{1,0:T(8,128)(2,1)S(1)} %get-tuple-element.73), channel_id=1, source_target_pairs={{0,9},{1,16},{2,11},{3,18},{4,13},{5,20},{6,15},{7,22},{8,1},{9,24... | collective-permute-start | bytes 491528 | tf_op jit(solution)/shard_map/ppermute | solution.py:463
  54.8 10.0 %collective-permute-start.28 = (f32[64,1280]{1,0:T(8,128)S(1)}, f32[64,1280]{1,0:T(8,128)S(1)}, u32[]{:S(2)}, u32[]{:S(2)}) collective-permute-start(f32[64,1280]{1,0:T(8,128)S(1)} %get-tuple-element.63), channel_id=1, source_target_pairs={{0,1},{1,0},{2,3},{3,2},{4,5},{5,4},{6,7},{7,6},{8,9},{9,8},{10,11... | collective-permute-start | bytes 983048 | tf_op jit(solution)/shard_map/ppermute | solution.py:463
  57.7 7.2 %collective-permute-start.30 = (f32[64,768]{1,0:T(8,128)S(1)}, f32[64,768]{1,0:T(8,128)S(1)}, u32[]{:S(2)}, u32[]{:S(2)}) collective-permute-start(f32[64,768]{1,0:T(8,128)S(1)} %get-tuple-element.71), channel_id=1, source_target_pairs={{0,1},{1,0},{2,3},{3,2},{4,5},{5,4},{6,7},{7,6},{8,9},{9,8},{10,11... | collective-permute-start | bytes 589832 | tf_op jit(solution)/shard_map/ppermute | solution.py:463
  (7 other events, 24.5 us)

commit v8 on v3

--- a/solution.py
+++ b/solution.py
@@ -310,11 +310,13 @@
     chip_rows = total // groups
     me = me_ref[0]
     lead = (me & 1) == 0
+    own, first, second, swapped = [ref[...] for ref in stat_refs]
+    values = [own, jnp.where(lead, first, swapped), second, jnp.where(lead, swapped, first)]
     parts, partners = [], []
-    for j, ref in enumerate(stat_refs):
+    for j, value in enumerate(values):
         parts.append(jnp.concatenate(
-            [ref[:, (i ^ j) * chip_rows:((i ^ j) + 1) * chip_rows] for i in range(groups)], axis=1))
-        partners.append(ref[count:count + 1, :chip_rows])
+            [value[:, (i ^ j) * chip_rows:((i ^ j) + 1) * chip_rows] for i in range(groups)], axis=1))
+        partners.append(value[count:count + 1, :chip_rows])
     peak = functools.reduce(jnp.maximum, parts)
     mass = functools.reduce(lambda a, b: a + b, [jnp.exp2(part - peak) for part in parts])
     partner_row = jnp.concatenate(partners, axis=1)
@@ -465,14 +467,14 @@
     mine = jnp.where(lead, queries, documents)
     other = jnp.where(lead, documents, queries)
     got = swap(other)
-    small = WIDTHS * total * total * 4 <= 16 << 20
-    cut = own_rows - 16 if small and own_rows >= 32 else own_rows
+    small = groups == 4 and WIDTHS * total * total * 4 <= 16 << 20
+    cut = own_rows // 2 if small and own_rows % 32 == 0 else own_rows
     v = {0: [mine, got]}
     w = {0: [swap(mine), other]}
     for stage in reversed(range(stages)):
         for j in sorted(v):
             parts = v[j]
-            if j == 0 and stage == stages - 1 and cut < own_rows:
+            if cut < own_rows and j == 0 and stage:
                 parts = [mine, got[:cut], got[cut:]]
             v[j | 1 << stage] = [
                 along(part, stage) for part in parts]
@@ -571,7 +573,11 @@
             done += more
         more, stats = tile([4], chip_partner, done)
         done += more
-        common = [me, *gathered(stats), *[t[0] for t in done], *[t[1] for t in done],
+        first = exchange(
+            stats, lambda i: query_mask(3) if i & 1 else query_mask(1))
+        second = exchange(stats, lambda i: query_mask(2))
+        swapped = swap(first)
+        common = [me, stats, first, second, swapped, *[t[0] for t in done], *[t[1] for t in done],
                   *[t[2] for t in done], *w_list]
         near = segments_of(groups)[-1][0]
         widest = feature_dim - uppers[-2]

time: 73.9 us -> 72.4 us (0.980)
  starting transfers between devices: 27.3 us -> 26.4 us
    ppermute x31, starting transfers between devices: 27.3 us -> 26.4 us  [exchange(): return lax.ppermute(x, AXES, [(i, i ^ masks_of(i)) for i in range(devices)])]
  transfers between devices with their start and end apart: 31 -> 31, of which waited for: 11 -> 12; matrix products, arithmetic and copies ran while one was open for 2% -> 2% of each run, Pallas kernels for 6% -> 6%
where the time goes in v8:
time: 72.4 us; the launch traced here: 72.3 us
  waiting for transfers between devices  31.1 us (43%)
  starting transfers between devices  26.4 us (36%)
  Pallas kernels  10.7 us (15%)
  other arithmetic  3.18 us (4%)
  between operations  0.81 us (1%)
    ppermute x31, waiting for transfers between devices, exchange(): return lax.ppermute(x, AXES, [(i, i ^ masks_of(i)) for i in range(devices)])  31.1 us
    ppermute x31, starting transfers between devices, exchange(): return lax.ppermute(x, AXES, [(i, i ^ masks_of(i)) for i in range(devices)])  26.4 us
    pallas_call x5, Pallas kernels, tile(): pl.pallas_call(functools.partial(tile_kernel, span, counts, uppers, own_r...  6.27 us
    pallas_call x2, Pallas kernels, bands(): pl.pallas_call(functools.partial(kernel, groups, uppers, own_rows, docume...  4.45 us
  transfers between devices with their start and end apart: 31, of which 12 were waited for; matrix products, arithmetic and copies ran while one was open for 2% of the time, Pallas kernels for 6%

profile of v8, /device:TPU:0, one launch (start us, length us, event | category | flops | bytes accessed | tf_op | source)
XLA Modules:
  0.0 72.3 jit_solution(7274888070890183061)
XLA Ops:
  2.3 2.6 %collective-permute-start.7 = (bf16[64,2048]{1,0:T(8,128)(2,1)S(1)}, bf16[64,2048]{1,0:T(8,128)(2,1)S(1)}, u32[]{:S(2)}, u32[]{:S(2)}) collective-permute-start(bf16[64,2048]{1,0:T(8,128)(2,1)S(1)} %get-tuple-element.71.refs_2_), channel_id=1, source_target_pairs={{0,8},{1,17},{2,10},{3,19},{4,12},{5,21},{6,14},{7,23},{8,0},{9,25... | collective-permute-start | bytes 786440 | tf_op jit(solution)/shard_map/ppermute | solution.py:459
  6.1 1.5 %collective-permute-start.2 = (bf16[64,2048]{1,0:T(8,128)(2,1)S(1)}, bf16[64,2048]{1,0:T(8,128)(2,1)S(1)}, u32[]{:S(2)}, u32[]{:S(2)}) collective-permute-start(bf16[64,2048]{1,0:T(8,128)(2,1)S(1)} %get-tuple-element.71.refs_2_), channel_id=1, source_target_pairs={{0,2},{1,5},{2,0},{3,7},{4,6},{5,1},{6,4},{7,3},{8,10},{9,13},{10,... | collective-permute-start | bytes 786440 | tf_op jit(solution)/shard_map/ppermute | solution.py:459
  8.2 1.2 %collective-permute-start.3 = (bf16[64,2048]{1,0:T(8,128)(2,1)S(1)}, bf16[64,2048]{1,0:T(8,128)(2,1)S(1)}, u32[]{:S(2)}, u32[]{:S(2)}) collective-permute-start(bf16[64,2048]{1,0:T(8,128)(2,1)S(1)} %collective-permute-done.1.refs_3_), channel_id=1, source_target_pairs={{0,2},{1,5},{2,0},{3,7},{4,6},{5,1},{6,4},{7,3},{8,10},{9,13},{10,... | collective-permute-start | bytes 786440 | tf_op jit(solution)/shard_map/ppermute | solution.py:459
  9.5 1.6 %collective-permute-start.9 = (bf16[32,2048]{1,0:T(8,128)(2,1)S(1)}, bf16[32,2048]{1,0:T(8,128)(2,1)S(1)}, u32[]{:S(2)}, u32[]{:S(2)}) collective-permute-start(bf16[32,2048]{1,0:T(8,128)(2,1)S(1)} %get-tuple-element.74), channel_id=1, source_target_pairs={{0,8},{1,17},{2,10},{3,19},{4,12},{5,21},{6,14},{7,23},{8,0},{9,25... | collective-permute-start | bytes 393224 | tf_op jit(solution)/shard_map/ppermute | solution.py:459
  11.6 2.3 %collective-permute-start.13 = (bf16[64,2048]{1,0:T(8,128)(2,1)S(1)}, bf16[64,2048]{1,0:T(8,128)(2,1)S(1)}, u32[]{:S(2)}, u32[]{:S(2)}) collective-permute-start(bf16[64,2048]{1,0:T(8,128)(2,1)S(1)} %collective-permute-done.7.refs_2_.refs_6_), channel_id=1, source_target_pairs={{0,2},{1,5},{2,0},{3,7},{4,6},{5,1},{6,4},{7,3},{8,10},{9,13},{10,... | collective-permute-start | bytes 786440 | tf_op jit(solution)/shard_map/ppermute | solution.py:459
  13.9 1.3 %collective-permute-done.3.refs_5_ = bf16[64,2048]{1,0:T(8,128)(2,1)S(1)} collective-permute-done((bf16[64,2048]{1,0:T(8,128)(2,1)S(1)}, bf16[64,2048]{1,0:T(8,128)(2,1)S(1)}, u32[]{:S(2)}, u32[]{:S(2)}) %collective-permute-start.3) | collective-permute-done | bytes 262176 | tf_op jit(solution)/shard_map/ppermute | solution.py:459
  15.3 1.6 %collective-permute-start.8 = (bf16[32,2048]{1,0:T(8,128)(2,1)S(1)}, bf16[32,2048]{1,0:T(8,128)(2,1)S(1)}, u32[]{:S(2)}, u32[]{:S(2)}) collective-permute-start(bf16[32,2048]{1,0:T(8,128)(2,1)S(1)} %get-tuple-element.75), channel_id=1, source_target_pairs={{0,8},{1,17},{2,10},{3,19},{4,12},{5,21},{6,14},{7,23},{8,0},{9,25... | collective-permute-start | bytes 393224 | tf_op jit(solution)/shard_map/ppermute | solution.py:459
  16.8 1.5 %collective-permute-start.15 = (bf16[32,2048]{1,0:T(8,128)(2,1)S(1)}, bf16[32,2048]{1,0:T(8,128)(2,1)S(1)}, u32[]{:S(2)}, u32[]{:S(2)}) collective-permute-start(bf16[32,2048]{1,0:T(8,128)(2,1)S(1)} %collective-permute-done.9.refs_4_.refs_8_), channel_id=1, source_target_pairs={{0,2},{1,5},{2,0},{3,7},{4,6},{5,1},{6,4},{7,3},{8,10},{9,13},{10,... | collective-permute-start | bytes 393224 | tf_op jit(solution)/shard_map/ppermute | solution.py:459
  18.3 3.3 %collective-permute-done.8.refs_3_.refs_7_ = bf16[32,2048]{1,0:T(8,128)(2,1)S(1)} collective-permute-done((bf16[32,2048]{1,0:T(8,128)(2,1)S(1)}, bf16[32,2048]{1,0:T(8,128)(2,1)S(1)}, u32[]{:S(2)}, u32[]{:S(2)}) %collective-permute-start.8) | collective-permute-done | bytes 131104 | tf_op jit(solution)/shard_map/ppermute | solution.py:459
  22.1 1.5 %collective-permute-start.14 = (bf16[32,2048]{1,0:T(8,128)(2,1)S(1)}, bf16[32,2048]{1,0:T(8,128)(2,1)S(1)}, u32[]{:S(2)}, u32[]{:S(2)}) collective-permute-start(bf16[32,2048]{1,0:T(8,128)(2,1)S(1)} %collective-permute-done.8.refs_3_.refs_7_), channel_id=1, source_target_pairs={{0,2},{1,5},{2,0},{3,7},{4,6},{5,1},{6,4},{7,3},{8,10},{9,13},{10,... | collective-permute-start | bytes 393224 | tf_op jit(solution)/shard_map/ppermute | solution.py:459
  25.4 1.8 %collective-permute-done.14.refs_3_.refs_10_ = bf16[32,2048]{1,0:T(8,128)(2,1)S(1)} collective-permute-done((bf16[32,2048]{1,0:T(8,128)(2,1)S(1)}, bf16[32,2048]{1,0:T(8,128)(2,1)S(1)}, u32[]{:S(2)}, u32[]{:S(2)}) %collective-permute-start.14) | collective-permute-done | bytes 131104 | tf_op jit(solution)/shard_map/ppermute | solution.py:459
  27.9 1.4 %shard_map.52 = (f32[9,384,128]{2,1,0:T(8,128)S(1)}, f32[384,128]{1,0:T(8,128)S(1)}, f32[32,384]{1,0:T(8,128)S(1)}, f32[1,128]{1,0:T(1,128)S(1)}) custom-call(s32[1]{0:T(128)} %bitcast.refs_0_, f32[1,128]{1,0:T(1,128)S(1)} %get-tuple-element.34.refs_1_, bf16[64,2048]{1,0:T(8,128)(2,1)S(1)} %get-tuple-element.71.refs_2_, ...), custom_call_target="tpu_custom_call" | custom-call | flops 603979776 | bytes 2097152 | tf_op jit(solution)/shard_map/pallas_call | solution.py:557
  30.4 1.9 %shard_map.54 = (f32[9,512,128]{2,1,0:T(8,128)S(1)}, f32[512,128]{1,0:T(8,128)S(1)}, f32[32,512]{1,0:T(8,128)S(1)}, f32[16,512]{1,0:T(8,128)S(1)}) custom-call(s32[1]{0:T(128)} %bitcast.refs_0_, f32[1,128]{1,0:T(1,128)S(1)} %get-tuple-element.36.refs_1_, bf16[64,2048]{1,0:T(8,128)(2,1)S(1)} %get-tuple-element.71.refs_2_, ...), custom_call_target="tpu_custom_call" | custom-call | flops 805306368 | bytes 2097152 | tf_op jit(solution)/shard_map/pallas_call | solution.py:557
  32.4 1.6 %collective-permute-start.19 = (f32[16,512]{1,0:T(8,128)S(1)}, f32[16,512]{1,0:T(8,128)S(1)}, u32[]{:S(2)}, u32[]{:S(2)}) collective-permute-start(f32[16,512]{1,0:T(8,128)S(1)} %get-tuple-element.41.refs_1_), channel_id=1, source_target_pairs={{0,2},{1,11},{2,0},{3,9},{4,6},{5,15},{6,4},{7,13},{8,10},{9,3},{1... | collective-permute-start | bytes 98312 | tf_op jit(solution)/shard_map/ppermute | solution.py:459
  34.9 1.5 %collective-permute-done.19.refs_2_ = f32[16,512]{1,0:T(8,128)S(1)} collective-permute-done((f32[16,512]{1,0:T(8,128)S(1)}, f32[16,512]{1,0:T(8,128)S(1)}, u32[]{:S(2)}, u32[]{:S(2)}) %collective-permute-start.19) | collective-permute-done | bytes 32800 | tf_op jit(solution)/shard_map/ppermute | solution.py:459
  36.4 1.5 %collective-permute-done.20.refs_3_ = f32[16,512]{1,0:T(8,128)S(1)} collective-permute-done((f32[16,512]{1,0:T(8,128)S(1)}, f32[16,512]{1,0:T(8,128)S(1)}, u32[]{:S(2)}, u32[]{:S(2)}) %collective-permute-start.20) | collective-permute-done | bytes 32800 | tf_op jit(solution)/shard_map/ppermute | solution.py:459
  38.4 4.0 %shard_map.56 = (f32[128,1024]{1,0:T(8,128)S(1)}, bf16[128,1024]{1,0:T(8,128)(2,1)S(1)}, f32[128,1024]{1,0:T(8,128)S(1)}, bf16[128,1024]{1,0:T(8,128)(2,1)S(1)},...) custom-call(s32[1]{0:T(128)} %bitcast.refs_0_, ...), custom_call_target="tpu_custom_call" | custom-call | flops 1073741824 | bytes 4194304 | tf_op jit(solution)/shard_map/pallas_call | solution.py:586
  42.3 1.3 %collective-permute-start.22 = (bf16[128,1024]{1,0:T(8,128)(2,1)S(1)}, bf16[128,1024]{1,0:T(8,128)(2,1)S(1)}, u32[]{:S(2)}, u32[]{:S(2)}) collective-permute-start(bf16[128,1024]{1,0:T(8,128)(2,1)S(1)} %get-tuple-element.55), channel_id=1, source_target_pairs={{0,2},{1,5},{2,0},{3,7},{4,6},{5,1},{6,4},{7,3},{8,10},{9,13},{10,... | collective-permute-start | bytes 786440 | tf_op jit(solution)/shard_map/ppermute | solution.py:459
  44.4 1.2 %collective-permute-start.25 = (bf16[128,1024]{1,0:T(8,128)(2,1)S(1)}, bf16[128,1024]{1,0:T(8,128)(2,1)S(1)}, u32[]{:S(2)}, u32[]{:S(2)}) collective-permute-start(bf16[128,1024]{1,0:T(8,128)(2,1)S(1)} %get-tuple-element.60), channel_id=1, source_target_pairs={{0,2},{1,5},{2,0},{3,7},{4,6},{5,1},{6,4},{7,3},{8,10},{9,13},{10,... | collective-permute-start | bytes 786440 | tf_op jit(solution)/shard_map/ppermute | solution.py:459
  46.5 2.3 %collective-permute-done.22 = bf16[128,1024]{1,0:T(8,128)(2,1)S(1)} collective-permute-done((bf16[128,1024]{1,0:T(8,128)(2,1)S(1)}, bf16[128,1024]{1,0:T(8,128)(2,1)S(1)}, u32[]{:S(2)}, u32[]{:S(2)}) %collective-permute-start.22) | collective-permute-done | bytes 262176 | tf_op jit(solution)/shard_map/ppermute | solution.py:459
  49.0 8.2 %collective-permute-done.26 = bf16[128,1024]{1,0:T(8,128)(2,1)S(1)} collective-permute-done((bf16[128,1024]{1,0:T(8,128)(2,1)S(1)}, bf16[128,1024]{1,0:T(8,128)(2,1)S(1)}, u32[]{:S(2)}, u32[]{:S(2)}) %collective-permute-start.26) | collective-permute-done | bytes 262176 | tf_op jit(solution)/shard_map/ppermute | solution.py:459
  59.7 5.6 %collective-permute-done.27 = bf16[128,1024]{1,0:T(8,128)(2,1)S(1)} collective-permute-done((bf16[128,1024]{1,0:T(8,128)(2,1)S(1)}, bf16[128,1024]{1,0:T(8,128)(2,1)S(1)}, u32[]{:S(2)}, u32[]{:S(2)}) %collective-permute-start.27) | collective-permute-done | bytes 262176 | tf_op jit(solution)/shard_map/ppermute | solution.py:459
  66.3 1.9 %collective-permute-done.24 = bf16[64,1024]{1,0:T(8,128)(2,1)S(1)} collective-permute-done((bf16[64,1024]{1,0:T(8,128)(2,1)S(1)}, bf16[64,1024]{1,0:T(8,128)(2,1)S(1)}, u32[]{:S(2)}, u32[]{:S(2)}) %collective-permute-start.24) | collective-permute-done | bytes 131104 | tf_op jit(solution)/shard_map/ppermute | solution.py:459
  68.2 3.0 %collective-permute-done.29 = bf16[64,1024]{1,0:T(8,128)(2,1)S(1)} collective-permute-done((bf16[64,1024]{1,0:T(8,128)(2,1)S(1)}, bf16[64,1024]{1,0:T(8,128)(2,1)S(1)}, u32[]{:S(2)}, u32[]{:S(2)}) %collective-permute-start.29) | collective-permute-done | bytes 131104 | tf_op jit(solution)/shard_map/ppermute | solution.py:459
  (59 shorter events, 15.9 us)
Async XLA Ops:
  1.7 6.5 %collective-permute-start.1 = (bf16[64,2048]{1,0:T(8,128)(2,1)S(1)}, bf16[64,2048]{1,0:T(8,128)(2,1)S(1)}, u32[]{:S(2)}, u32[]{:S(2)}) collective-permute-start(bf16[64,2048]{1,0:T(8,128)(2,1)S(1)} %get-tuple-element.70.refs_7_.refs_6_.refs_21_), channel_id=1, source_target_pairs={{0,1},{1,0},{2,3},{3,2},{4,5},{5,4},{6,7},{7,6},{8,9},{9,8},{10,11... | collective-permute-start | bytes 786440 | tf_op jit(solution)/shard_map/ppermute | solution.py:459
  2.3 9.4 %collective-permute-start.7 = (bf16[64,2048]{1,0:T(8,128)(2,1)S(1)}, bf16[64,2048]{1,0:T(8,128)(2,1)S(1)}, u32[]{:S(2)}, u32[]{:S(2)}) collective-permute-start(bf16[64,2048]{1,0:T(8,128)(2,1)S(1)} %get-tuple-element.71.refs_2_), channel_id=1, source_target_pairs={{0,8},{1,17},{2,10},{3,19},{4,12},{5,21},{6,14},{7,23},{8,0},{9,25... | collective-permute-start | bytes 786440 | tf_op jit(solution)/shard_map/ppermute | solution.py:459
  4.9 10.4 %collective-permute-start.4 = (bf16[64,2048]{1,0:T(8,128)(2,1)S(1)}, bf16[64,2048]{1,0:T(8,128)(2,1)S(1)}, u32[]{:S(2)}, u32[]{:S(2)}) collective-permute-start(bf16[64,2048]{1,0:T(8,128)(2,1)S(1)} %get-tuple-element.71.refs_2_), channel_id=1, source_target_pairs={{0,1},{1,0},{2,3},{3,2},{4,5},{5,4},{6,7},{7,6},{8,9},{9,8},{10,11... | collective-permute-start | bytes 786440 | tf_op jit(solution)/shard_map/ppermute | solution.py:459
  6.1 7.8 %collective-permute-start.2 = (bf16[64,2048]{1,0:T(8,128)(2,1)S(1)}, bf16[64,2048]{1,0:T(8,128)(2,1)S(1)}, u32[]{:S(2)}, u32[]{:S(2)}) collective-permute-start(bf16[64,2048]{1,0:T(8,128)(2,1)S(1)} %get-tuple-element.71.refs_2_), channel_id=1, source_target_pairs={{0,2},{1,5},{2,0},{3,7},{4,6},{5,1},{6,4},{7,3},{8,10},{9,13},{10,... | collective-permute-start | bytes 786440 | tf_op jit(solution)/shard_map/ppermute | solution.py:459
  8.2 7.0 %collective-permute-start.3 = (bf16[64,2048]{1,0:T(8,128)(2,1)S(1)}, bf16[64,2048]{1,0:T(8,128)(2,1)S(1)}, u32[]{:S(2)}, u32[]{:S(2)}) collective-permute-start(bf16[64,2048]{1,0:T(8,128)(2,1)S(1)} %collective-permute-done.1.refs_3_), channel_id=1, source_target_pairs={{0,2},{1,5},{2,0},{3,7},{4,6},{5,1},{6,4},{7,3},{8,10},{9,13},{10,... | collective-permute-start | bytes 786440 | tf_op jit(solution)/shard_map/ppermute | solution.py:459
  9.5 7.3 %collective-permute-start.9 = (bf16[32,2048]{1,0:T(8,128)(2,1)S(1)}, bf16[32,2048]{1,0:T(8,128)(2,1)S(1)}, u32[]{:S(2)}, u32[]{:S(2)}) collective-permute-start(bf16[32,2048]{1,0:T(8,128)(2,1)S(1)} %get-tuple-element.74), channel_id=1, source_target_pairs={{0,8},{1,17},{2,10},{3,19},{4,12},{5,21},{6,14},{7,23},{8,0},{9,25... | collective-permute-start | bytes 393224 | tf_op jit(solution)/shard_map/ppermute | solution.py:459
  11.6 10.5 %collective-permute-start.13 = (bf16[64,2048]{1,0:T(8,128)(2,1)S(1)}, bf16[64,2048]{1,0:T(8,128)(2,1)S(1)}, u32[]{:S(2)}, u32[]{:S(2)}) collective-permute-start(bf16[64,2048]{1,0:T(8,128)(2,1)S(1)} %collective-permute-done.7.refs_2_.refs_6_), channel_id=1, source_target_pairs={{0,2},{1,5},{2,0},{3,7},{4,6},{5,1},{6,4},{7,3},{8,10},{9,13},{10,... | collective-permute-start | bytes 786440 | tf_op jit(solution)/shard_map/ppermute | solution.py:459
  13.9 9.7 %collective-permute-start.5 = (bf16[64,2048]{1,0:T(8,128)(2,1)S(1)}, bf16[64,2048]{1,0:T(8,128)(2,1)S(1)}, u32[]{:S(2)}, u32[]{:S(2)}) collective-permute-start(bf16[64,2048]{1,0:T(8,128)(2,1)S(1)} %collective-permute-done.2.refs_4_), channel_id=1, source_target_pairs={{0,1},{1,0},{2,3},{3,2},{4,5},{5,4},{6,7},{7,6},{8,9},{9,8},{10,11... | collective-permute-start | bytes 786440 | tf_op jit(solution)/shard_map/ppermute | solution.py:459
  15.3 8.4 %collective-permute-start.6 = (bf16[64,2048]{1,0:T(8,128)(2,1)S(1)}, bf16[64,2048]{1,0:T(8,128)(2,1)S(1)}, u32[]{:S(2)}, u32[]{:S(2)}) collective-permute-start(bf16[64,2048]{1,0:T(8,128)(2,1)S(1)} %collective-permute-done.3.refs_5_), channel_id=1, source_target_pairs={{0,1},{1,0},{2,3},{3,2},{4,5},{5,4},{6,7},{7,6},{8,9},{9,8},{10,11... | collective-permute-start | bytes 786440 | tf_op jit(solution)/shard_map/ppermute | solution.py:459
  15.3 6.4 %collective-permute-start.8 = (bf16[32,2048]{1,0:T(8,128)(2,1)S(1)}, bf16[32,2048]{1,0:T(8,128)(2,1)S(1)}, u32[]{:S(2)}, u32[]{:S(2)}) collective-permute-start(bf16[32,2048]{1,0:T(8,128)(2,1)S(1)} %get-tuple-element.75), channel_id=1, source_target_pairs={{0,8},{1,17},{2,10},{3,19},{4,12},{5,21},{6,14},{7,23},{8,0},{9,25... | collective-permute-start | bytes 393224 | tf_op jit(solution)/shard_map/ppermute | solution.py:459
  16.8 5.0 %collective-permute-start.15 = (bf16[32,2048]{1,0:T(8,128)(2,1)S(1)}, bf16[32,2048]{1,0:T(8,128)(2,1)S(1)}, u32[]{:S(2)}, u32[]{:S(2)}) collective-permute-start(bf16[32,2048]{1,0:T(8,128)(2,1)S(1)} %collective-permute-done.9.refs_4_.refs_8_), channel_id=1, source_target_pairs={{0,2},{1,5},{2,0},{3,7},{4,6},{5,1},{6,4},{7,3},{8,10},{9,13},{10,... | collective-permute-start | bytes 393224 | tf_op jit(solution)/shard_map/ppermute | solution.py:459
  21.6 6.3 %collective-permute-start.10 = (bf16[64,2048]{1,0:T(8,128)(2,1)S(1)}, bf16[64,2048]{1,0:T(8,128)(2,1)S(1)}, u32[]{:S(2)}, u32[]{:S(2)}) collective-permute-start(bf16[64,2048]{1,0:T(8,128)(2,1)S(1)} %collective-permute-done.7.refs_2_.refs_6_), channel_id=1, source_target_pairs={{0,1},{1,0},{2,3},{3,2},{4,5},{5,4},{6,7},{7,6},{8,9},{9,8},{10,11... | collective-permute-start | bytes 786440 | tf_op jit(solution)/shard_map/ppermute | solution.py:459
  22.1 5.0 %collective-permute-start.14 = (bf16[32,2048]{1,0:T(8,128)(2,1)S(1)}, bf16[32,2048]{1,0:T(8,128)(2,1)S(1)}, u32[]{:S(2)}, u32[]{:S(2)}) collective-permute-start(bf16[32,2048]{1,0:T(8,128)(2,1)S(1)} %collective-permute-done.8.refs_3_.refs_7_), channel_id=1, source_target_pairs={{0,2},{1,5},{2,0},{3,7},{4,6},{5,1},{6,4},{7,3},{8,10},{9,13},{10,... | collective-permute-start | bytes 393224 | tf_op jit(solution)/shard_map/ppermute | solution.py:459
  23.7 6.8 %collective-permute-start.16 = (bf16[64,2048]{1,0:T(8,128)(2,1)S(1)}, bf16[64,2048]{1,0:T(8,128)(2,1)S(1)}, u32[]{:S(2)}, u32[]{:S(2)}) collective-permute-start(bf16[64,2048]{1,0:T(8,128)(2,1)S(1)} %collective-permute-done.13.refs_2_.refs_9_), channel_id=1, source_target_pairs={{0,1},{1,0},{2,3},{3,2},{4,5},{5,4},{6,7},{7,6},{8,9},{9,8},{10,11... | collective-permute-start | bytes 786440 | tf_op jit(solution)/shard_map/ppermute | solution.py:459
  25.3 5.1 %collective-permute-start.18 = (bf16[32,2048]{1,0:T(8,128)(2,1)S(1)}, bf16[32,2048]{1,0:T(8,128)(2,1)S(1)}, u32[]{:S(2)}, u32[]{:S(2)}) collective-permute-start(bf16[32,2048]{1,0:T(8,128)(2,1)S(1)} %collective-permute-done.15.refs_4_.refs_11_), channel_id=1, source_target_pairs={{0,1},{1,0},{2,3},{3,2},{4,5},{5,4},{6,7},{7,6},{8,9},{9,8},{10,11... | collective-permute-start | bytes 393224 | tf_op jit(solution)/shard_map/ppermute | solution.py:459
  42.3 6.4 %collective-permute-start.22 = (bf16[128,1024]{1,0:T(8,128)(2,1)S(1)}, bf16[128,1024]{1,0:T(8,128)(2,1)S(1)}, u32[]{:S(2)}, u32[]{:S(2)}) collective-permute-start(bf16[128,1024]{1,0:T(8,128)(2,1)S(1)} %get-tuple-element.55), channel_id=1, source_target_pairs={{0,2},{1,5},{2,0},{3,7},{4,6},{5,1},{6,4},{7,3},{8,10},{9,13},{10,... | collective-permute-start | bytes 786440 | tf_op jit(solution)/shard_map/ppermute | solution.py:459
  43.6 14.7 %collective-permute-start.23 = (bf16[128,1024]{1,0:T(8,128)(2,1)S(1)}, bf16[128,1024]{1,0:T(8,128)(2,1)S(1)}, u32[]{:S(2)}, u32[]{:S(2)}) collective-permute-start(bf16[128,1024]{1,0:T(8,128)(2,1)S(1)} %get-tuple-element.58), channel_id=1, source_target_pairs={{0,2},{1,5},{2,0},{3,7},{4,6},{5,1},{6,4},{7,3},{8,10},{9,13},{10,... | collective-permute-start | bytes 786440 | tf_op jit(solution)/shard_map/ppermute | solution.py:459
  44.4 15.3 %collective-permute-start.25 = (bf16[128,1024]{1,0:T(8,128)(2,1)S(1)}, bf16[128,1024]{1,0:T(8,128)(2,1)S(1)}, u32[]{:S(2)}, u32[]{:S(2)}) collective-permute-start(bf16[128,1024]{1,0:T(8,128)(2,1)S(1)} %get-tuple-element.60), channel_id=1, source_target_pairs={{0,2},{1,5},{2,0},{3,7},{4,6},{5,1},{6,4},{7,3},{8,10},{9,13},{10,... | collective-permute-start | bytes 786440 | tf_op jit(solution)/shard_map/ppermute | solution.py:459
  45.6 11.6 %collective-permute-start.26 = (bf16[128,1024]{1,0:T(8,128)(2,1)S(1)}, bf16[128,1024]{1,0:T(8,128)(2,1)S(1)}, u32[]{:S(2)}, u32[]{:S(2)}) collective-permute-start(bf16[128,1024]{1,0:T(8,128)(2,1)S(1)} %get-tuple-element.62), channel_id=1, source_target_pairs={{0,2},{1,5},{2,0},{3,7},{4,6},{5,1},{6,4},{7,3},{8,10},{9,13},{10,... | collective-permute-start | bytes 786440 | tf_op jit(solution)/shard_map/ppermute | solution.py:459
  48.9 22.3 %collective-permute-start.28 = (f32[64,1024]{1,0:T(8,128)S(1)}, f32[64,1024]{1,0:T(8,128)S(1)}, u32[]{:S(2)}, u32[]{:S(2)}) collective-permute-start(f32[64,1024]{1,0:T(8,128)S(1)} %get-tuple-element.63), channel_id=1, source_target_pairs={{0,1},{1,0},{2,3},{3,2},{4,5},{5,4},{6,7},{7,6},{8,9},{9,8},{10,11... | collective-permute-start | bytes 786440 | tf_op jit(solution)/shard_map/ppermute | solution.py:459
  57.3 8.1 %collective-permute-start.27 = (bf16[128,1024]{1,0:T(8,128)(2,1)S(1)}, bf16[128,1024]{1,0:T(8,128)(2,1)S(1)}, u32[]{:S(2)}, u32[]{:S(2)}) collective-permute-start(bf16[128,1024]{1,0:T(8,128)(2,1)S(1)} %add_convert_fusion), channel_id=1, source_target_pairs={{0,8},{1,17},{2,10},{3,19},{4,12},{5,21},{6,14},{7,23},{8,0},{9,25... | collective-permute-start | bytes 786440 | tf_op jit(solution)/shard_map/ppermute | solution.py:459
  58.4 9.8 %collective-permute-start.24 = (bf16[64,1024]{1,0:T(8,128)(2,1)S(1)}, bf16[64,1024]{1,0:T(8,128)(2,1)S(1)}, u32[]{:S(2)}, u32[]{:S(2)}) collective-permute-start(bf16[64,1024]{1,0:T(8,128)(2,1)S(1)} %get-tuple-element.72), channel_id=1, source_target_pairs={{0,8},{1,17},{2,10},{3,19},{4,12},{5,21},{6,14},{7,23},{8,0},{9,25... | collective-permute-start | bytes 393224 | tf_op jit(solution)/shard_map/ppermute | solution.py:459
  59.5 11.7 %collective-permute-start.29 = (bf16[64,1024]{1,0:T(8,128)(2,1)S(1)}, bf16[64,1024]{1,0:T(8,128)(2,1)S(1)}, u32[]{:S(2)}, u32[]{:S(2)}) collective-permute-start(bf16[64,1024]{1,0:T(8,128)(2,1)S(1)} %get-tuple-element.73), channel_id=1, source_target_pairs={{0,9},{1,16},{2,11},{3,18},{4,13},{5,20},{6,15},{7,22},{8,1},{9,24... | collective-permute-start | bytes 393224 | tf_op jit(solution)/shard_map/ppermute | solution.py:459
  65.5 5.7 %collective-permute-start.30 = (f32[64,1024]{1,0:T(8,128)S(1)}, f32[64,1024]{1,0:T(8,128)S(1)}, u32[]{:S(2)}, u32[]{:S(2)}) collective-permute-start(f32[64,1024]{1,0:T(8,128)S(1)} %get-tuple-element.67), channel_id=1, source_target_pairs={{0,1},{1,0},{2,3},{3,2},{4,5},{5,4},{6,7},{7,6},{8,9},{9,8},{10,11... | collective-permute-start | bytes 786440 | tf_op jit(solution)/shard_map/ppermute | solution.py:459
  (7 other events, 21.7 us)

commit v9 on v8

--- a/solution.py
+++ b/solution.py
@@ -17,6 +17,15 @@
 
 
 logit_gain = 3.0
+QUERY_CORE = 1
+
+
+def leads(device):
+    return (device & 1) == QUERY_CORE
+
+
+def other_core(device):
+    return (device & -2) | (1 - QUERY_CORE)
 
 
 def width_list(feature_dim):
@@ -67,7 +76,7 @@
     own = partner_ref.shape[1]
     out_ref[...] = jnp.zeros_like(out_ref)
 
-    @pl.when((role_ref[0] & 1) == 0)
+    @pl.when(leads(role_ref[0]))
     def _():
         for step in range(steps):
             rows = pl.ds(step * block, block)
@@ -79,7 +88,7 @@
                 col_ref[rows, k:k + 1] = peak + jnp.log(mass) * LOG2E
         out_ref[...] = col_ref[...].T[:STATS]
 
-    @pl.when((role_ref[0] & 1) != 0)
+    @pl.when(jnp.logical_not(leads(role_ref[0])))
     def _():
         peaks, masses = [None] * len(uppers), [None] * len(uppers)
         for step in range(steps):
@@ -125,7 +134,7 @@
     count = len(uppers)
     scales = [logit_gain * m ** -0.5 for m in uppers]
     me = me_ref[0]
-    lead = (me & 1) == 0
+    lead = leads(me)
 
     parts = []
     partners = []
@@ -141,7 +150,7 @@
         [totals[:count], partner_row, jnp.zeros((LANES - count - 1, total), jnp.float32)], axis=0)
     col_ref[...] = packed.T
     zero_or = lambda keep, x: jnp.where(keep, x, jnp.zeros_like(x))
-    document_row = document_ids((1, total), 1, me | 1, own_rows, masks)
+    document_row = document_ids((1, total), 1, other_core(me), own_rows, masks)
     id_row = jnp.where(lead, document_row, partner_row)
     shifts = [math.log2(s) for s in scales]
     total_rows = [zero_or(jnp.logical_not(lead), totals[k:k + 1]) - shifts[k] for k in range(count)]
@@ -149,7 +158,7 @@
     narrow = [m for m in uppers if m <= LANES]
     for step in range(total // block):
         rows = pl.ds(step * block, block)
-        document_col = document_ids((block, 1), 0, me | 1, own_rows, masks, step * block)
+        document_col = document_ids((block, 1), 0, other_core(me), own_rows, masks, step * block)
         id_col = jnp.where(lead, col_ref[rows, count:count + 1], document_col)
         hit = id_col == id_row
         for k, s in enumerate(prefix_scores(v_ref, w_ref, rows, uppers)):
@@ -258,7 +267,7 @@
     at += sum(counts[c0:c1])
     earlier = refs[at:at + finish]
     outs = refs[at + finish:]
-    lead = (me_ref[0] & 1) == 0
+    lead = leads(me_ref[0])
     for i, (t0, t1, u0, u1) in enumerate(tiles):
         subtile(
             lead, v_refs[sum(counts[r0:t0]):sum(counts[r0:t1])],
@@ -309,9 +318,10 @@
     total = stat_refs[0].shape[1]
     chip_rows = total // groups
     me = me_ref[0]
-    lead = (me & 1) == 0
+    lead = leads(me)
     own, first, second, swapped = [ref[...] for ref in stat_refs]
-    values = [own, jnp.where(lead, first, swapped), second, jnp.where(lead, swapped, first)]
+    odd = (me & 1) == 1
+    values = [own, jnp.where(odd, swapped, first), second, jnp.where(odd, first, swapped)]
     parts, partners = [], []
     for j, value in enumerate(values):
         parts.append(jnp.concatenate(
@@ -328,10 +338,10 @@
         [totals[:count], partner_row, jnp.zeros((LANES - count - 1, total), jnp.float32)], axis=0)
     cols = packed.T
     id_row = jnp.where(
-        lead, document_ids((1, total), 1, me | 1, own_rows, masks), partner_row)
+        lead, document_ids((1, total), 1, other_core(me), own_rows, masks), partner_row)
     id_col = jnp.where(
         lead, cols[:, count:count + 1],
-        document_ids((total, 1), 0, me | 1, own_rows, masks))
+        document_ids((total, 1), 0, other_core(me), own_rows, masks))
     return lead, totals, cols, id_row, id_col
 
 
@@ -436,6 +446,25 @@
         ref[:, lower:upper] = value[at:at + chip_rows].astype(ref.dtype)
 
 
+def put_kernel(columns, me_ref, *refs):
+    kept_ref, near_ref, given_ref, far_ref = refs[:4]
+    queries_ref, documents_ref, ours_ref, theirs_ref, sems = refs[-5:]
+    ours_ref[...] = kept_ref[...] + near_ref[...].astype(jnp.float32)
+    theirs_ref[...] = given_ref[...] + far_ref[...].astype(jnp.float32)
+
+    def write(first, second):
+        copies = [pltpu.make_async_copy(ours_ref, first.at[:, columns], sems.at[0]),
+                  pltpu.make_async_copy(theirs_ref, second.at[:, columns], sems.at[1])]
+        for copy in copies:
+            copy.start()
+        for copy in copies:
+            copy.wait()
+
+    lead = leads(me_ref[0])
+    pl.when(lead)(lambda: write(queries_ref, documents_ref))
+    pl.when(jnp.logical_not(lead))(lambda: write(documents_ref, queries_ref))
+
+
 def on_device(queries, documents, partner):
     own_rows, feature_dim = queries.shape
     uppers = width_list(feature_dim)
@@ -453,7 +482,7 @@
 
     role = lax.axis_index("rep")
     me = (lax.axis_index("dp") * rep_size + role).astype(jnp.int32).reshape(1)
-    lead = role == 0
+    lead = leads(role)
 
     def exchange(x, masks_of):
         return lax.ppermute(x, AXES, [(i, i ^ masks_of(i)) for i in range(devices)])
@@ -462,8 +491,11 @@
         return exchange(x, lambda i: 1)
 
     def along(x, stage):
-        return exchange(x, lambda i: document_masks[stage] if i & 1 else query_masks[stage])
-
+        return exchange(x, lambda i: query_masks[stage] if leads(i) else document_masks[stage])
+
+    vmem = pl.BlockSpec(memory_space=pltpu.VMEM)
+    smem = pl.BlockSpec(memory_space=pltpu.SMEM)
+    hbm = pl.BlockSpec(memory_space=pltpu.HBM)
     mine = jnp.where(lead, queries, documents)
     other = jnp.where(lead, documents, queries)
     got = swap(other)
@@ -490,9 +522,6 @@
         lead,
         jnp.concatenate([own_partner, far_partner], axis=1),
         jnp.concatenate([far_partner, own_partner], axis=1))
-
-    vmem = pl.BlockSpec(memory_space=pltpu.VMEM)
-    smem = pl.BlockSpec(memory_space=pltpu.SMEM)
 
     def query_mask(j):
         return sum(mask for s, mask in enumerate(query_masks) if j >> s & 1)
@@ -601,7 +630,20 @@
             bands_kernel, [running], gradient_shapes(uppers[-2]) + gradient_shapes(widest)[:near])
         chunks = [[*rest[groups:], *far_ones], rest[:groups]]
 
-    mine_parts, other_parts = [], []
+    def put(columns, parts, before):
+        return pl.pallas_call(
+            functools.partial(put_kernel, columns),
+            out_shape=[jax.ShapeDtypeStruct(queries.shape, jnp.float32)] * 2,
+            in_specs=[smem] + [vmem] * 4 + [hbm] * len(before),
+            out_specs=[hbm, hbm],
+            scratch_shapes=[pltpu.VMEM(parts[0].shape, jnp.float32)] * 2
+            + [pltpu.SemaphoreType.DMA((2,))],
+            input_output_aliases={5 + i: i for i in range(len(before))},
+            compiler_params=pltpu.CompilerParams(vmem_limit_bytes=8 << 20),
+            cost_estimate=pl.CostEstimate(flops=1000, transcendentals=0, bytes_accessed=1000),
+        )(me, *parts, *before)
+
+    gradients, end = [], feature_dim
     for c, chunk in enumerate(chunks):
         partial = dict(enumerate(chunk))
         for stage in range(stages - 1):
@@ -614,22 +656,21 @@
         stage = stages - 1
         outgoing = partial[1 << stage]
         kept = partial[0]
+        start = end - kept.shape[1]
         if c < len(chunks) - 1:
             arrived = along(outgoing, stage)
-            kept = kept + arrived.astype(jnp.float32)
-            mine_parts.append(kept[:own_rows])
-            other_parts.append(swap(kept[own_rows:]))
+            near = arrived[:own_rows]
+            theirs = kept[own_rows:] + arrived[own_rows:].astype(jnp.float32)
+            parts = [kept[:own_rows], near, swap(theirs), jnp.zeros_like(near)]
         else:
-            far = lambda i: document_masks[stage] ^ 1 if i & 1 else query_masks[stage] ^ 1
+            far = lambda i: 1 ^ (query_masks[stage] if leads(i) else document_masks[stage])
             near_arrived = along(outgoing[:own_rows], stage)
             far_arrived = exchange(outgoing[own_rows:], far)
             ours, theirs = lax.optimization_barrier((kept[:own_rows], kept[own_rows:]))
-            mine_parts.append(ours + near_arrived.astype(jnp.float32))
-            other_parts.append(swap(theirs) + far_arrived.astype(jnp.float32))
-    mine_parts, other_parts = mine_parts[::-1], other_parts[::-1]
-    ours = jnp.concatenate(mine_parts, axis=1)
-    theirs = jnp.concatenate(other_parts, axis=1)
-    return jnp.where(lead, ours, theirs), jnp.where(lead, theirs, ours)
+            parts = [ours, near_arrived, swap(theirs), far_arrived]
+        gradients = put(slice(start, end), parts, gradients)
+        end = start
+    return tuple(gradients)
 
 
 def solution(mesh):

time: 72.4 us -> 70.2 us (0.970)
  the two profiles are of different devices: /device:TPU:0 before, /device:TPU:1 now
where the time goes in v9:
time: 70.2 us; the launch traced here: 70 us
  starting transfers between devices  35.6 us (51%)
  waiting for transfers between devices  18.9 us (27%)
  Pallas kernels  12.4 us (18%)
  other arithmetic  2.09 us (3%)
  between operations  0.99 us (1%)
    ppermute x31, starting transfers between devices, exchange(): return lax.ppermute(x, AXES, [(i, i ^ masks_of(i)) for i in range(devices)])  35.6 us
    ppermute x31, waiting for transfers between devices, exchange(): return lax.ppermute(x, AXES, [(i, i ^ masks_of(i)) for i in range(devices)])  18.9 us
    pallas_call x5, Pallas kernels, tile(): pl.pallas_call(functools.partial(tile_kernel, span, counts, uppers, own_r...  6.27 us
    pallas_call x2, Pallas kernels, bands(): pl.pallas_call(functools.partial(kernel, groups, uppers, own_rows, docume...  4.42 us
    pallas_call x2, Pallas kernels, put(): pl.pallas_call(functools.partial(put_kernel, columns), out_shape=[jax.Sha...  1.7 us
  transfers between devices with their start and end apart: 31, of which 8 were waited for; matrix products, arithmetic and copies ran while one was open for 2% of the time, Pallas kernels for 13%

profile of v9, /device:TPU:1, one launch (start us, length us, event | category | flops | bytes accessed | tf_op | source)
XLA Modules:
  0.0 70.0 jit_solution(9465338024908051479)
XLA Ops:
  1.8 2.7 %collective-permute-start.2 = (bf16[64,2048]{1,0:T(8,128)(2,1)S(1)}, bf16[64,2048]{1,0:T(8,128)(2,1)S(1)}, u32[]{:S(2)}, u32[]{:S(2)}) collective-permute-start(bf16[64,2048]{1,0:T(8,128)(2,1)S(1)} %get-tuple-element.73.refs_2_), channel_id=1, source_target_pairs={{0,4},{1,3},{2,6},{3,1},{4,0},{5,7},{6,2},{7,5},{8,12},{9,11},{10,... | collective-permute-start | bytes 786440 | tf_op jit(solution)/shard_map/ppermute | solution.py:488
  4.9 1.3 %collective-permute-start.7 = (bf16[64,2048]{1,0:T(8,128)(2,1)S(1)}, bf16[64,2048]{1,0:T(8,128)(2,1)S(1)}, u32[]{:S(2)}, u32[]{:S(2)}) collective-permute-start(bf16[64,2048]{1,0:T(8,128)(2,1)S(1)} %get-tuple-element.73.refs_2_), channel_id=1, source_target_pairs={{0,16},{1,9},{2,18},{3,11},{4,20},{5,13},{6,22},{7,15},{8,24},{9,1... | collective-permute-start | bytes 786440 | tf_op jit(solution)/shard_map/ppermute | solution.py:488
  6.8 1.4 %collective-permute-start = (f32[1,64]{1,0:T(1,128)S(1)}, f32[1,64]{1,0:T(1,128)S(1)}, u32[]{:S(2)}, u32[]{:S(2)}) collective-permute-start(f32[1,64]{1,0:T(1,128)S(1)} %convert_bitcast_fusion), channel_id=1, source_target_pairs={{0,1},{1,0},{2,3},{3,2},{4,5},{5,4},{6,7},{7,6},{8,9},{9,8},{10,11... | collective-permute-start | bytes 776 | tf_op jit(solution)/shard_map/ppermute | solution.py:488
  9.9 1.3 %collective-permute-start.8 = (bf16[32,2048]{1,0:T(8,128)(2,1)S(1)}, bf16[32,2048]{1,0:T(8,128)(2,1)S(1)}, u32[]{:S(2)}, u32[]{:S(2)}) collective-permute-start(bf16[32,2048]{1,0:T(8,128)(2,1)S(1)} %get-tuple-element.77), channel_id=1, source_target_pairs={{0,16},{1,9},{2,18},{3,11},{4,20},{5,13},{6,22},{7,15},{8,24},{9,1... | collective-permute-start | bytes 393224 | tf_op jit(solution)/shard_map/ppermute | solution.py:488
  11.2 1.5 %collective-permute-done.7.refs_2_.refs_6_ = bf16[64,2048]{1,0:T(8,128)(2,1)S(1)} collective-permute-done((bf16[64,2048]{1,0:T(8,128)(2,1)S(1)}, bf16[64,2048]{1,0:T(8,128)(2,1)S(1)}, u32[]{:S(2)}, u32[]{:S(2)}) %collective-permute-start.7) | collective-permute-done | bytes 262176 | tf_op jit(solution)/shard_map/ppermute | solution.py:488
  12.6 1.3 %collective-permute-start.13 = (bf16[64,2048]{1,0:T(8,128)(2,1)S(1)}, bf16[64,2048]{1,0:T(8,128)(2,1)S(1)}, u32[]{:S(2)}, u32[]{:S(2)}) collective-permute-start(bf16[64,2048]{1,0:T(8,128)(2,1)S(1)} %collective-permute-done.7.refs_2_.refs_6_), channel_id=1, source_target_pairs={{0,4},{1,3},{2,6},{3,1},{4,0},{5,7},{6,2},{7,5},{8,12},{9,11},{10,... | collective-permute-start | bytes 786440 | tf_op jit(solution)/shard_map/ppermute | solution.py:488
  14.0 1.7 %collective-permute-start.6 = (bf16[64,2048]{1,0:T(8,128)(2,1)S(1)}, bf16[64,2048]{1,0:T(8,128)(2,1)S(1)}, u32[]{:S(2)}, u32[]{:S(2)}) collective-permute-start(bf16[64,2048]{1,0:T(8,128)(2,1)S(1)} %collective-permute-done.3.refs_5_), channel_id=1, source_target_pairs={{0,1},{1,0},{2,3},{3,2},{4,5},{5,4},{6,7},{7,6},{8,9},{9,8},{10,11... | collective-permute-start | bytes 786440 | tf_op jit(solution)/shard_map/ppermute | solution.py:488
  15.7 2.8 %collective-permute-start.9 = (bf16[32,2048]{1,0:T(8,128)(2,1)S(1)}, bf16[32,2048]{1,0:T(8,128)(2,1)S(1)}, u32[]{:S(2)}, u32[]{:S(2)}) collective-permute-start(bf16[32,2048]{1,0:T(8,128)(2,1)S(1)} %get-tuple-element.76), channel_id=1, source_target_pairs={{0,16},{1,9},{2,18},{3,11},{4,20},{5,13},{6,22},{7,15},{8,24},{9,1... | collective-permute-start | bytes 393224 | tf_op jit(solution)/shard_map/ppermute | solution.py:488
  18.5 3.8 %collective-permute-done.9.refs_4_.refs_8_ = bf16[32,2048]{1,0:T(8,128)(2,1)S(1)} collective-permute-done((bf16[32,2048]{1,0:T(8,128)(2,1)S(1)}, bf16[32,2048]{1,0:T(8,128)(2,1)S(1)}, u32[]{:S(2)}, u32[]{:S(2)}) %collective-permute-start.9) | collective-permute-done | bytes 131104 | tf_op jit(solution)/shard_map/ppermute | solution.py:488
  26.4 1.4 %collective-permute-start.17 = (bf16[32,2048]{1,0:T(8,128)(2,1)S(1)}, bf16[32,2048]{1,0:T(8,128)(2,1)S(1)}, u32[]{:S(2)}, u32[]{:S(2)}) collective-permute-start(bf16[32,2048]{1,0:T(8,128)(2,1)S(1)} %collective-permute-done.14.refs_3_.refs_10_), channel_id=1, source_target_pairs={{0,1},{1,0},{2,3},{3,2},{4,5},{5,4},{6,7},{7,6},{8,9},{9,8},{10,11... | collective-permute-start | bytes 393224 | tf_op jit(solution)/shard_map/ppermute | solution.py:488
  27.8 1.4 %collective-permute-start.18 = (bf16[32,2048]{1,0:T(8,128)(2,1)S(1)}, bf16[32,2048]{1,0:T(8,128)(2,1)S(1)}, u32[]{:S(2)}, u32[]{:S(2)}) collective-permute-start(bf16[32,2048]{1,0:T(8,128)(2,1)S(1)} %collective-permute-done.15.refs_4_.refs_11_), channel_id=1, source_target_pairs={{0,1},{1,0},{2,3},{3,2},{4,5},{5,4},{6,7},{7,6},{8,9},{9,8},{10,11... | collective-permute-start | bytes 393224 | tf_op jit(solution)/shard_map/ppermute | solution.py:488
  29.9 1.4 %shard_map.52 = (f32[9,384,128]{2,1,0:T(8,128)S(1)}, f32[384,128]{1,0:T(8,128)S(1)}, f32[32,384]{1,0:T(8,128)S(1)}, f32[1,128]{1,0:T(1,128)S(1)}) custom-call(s32[1]{0:T(128)} %bitcast.refs_0_.me_ref, f32[1,128]{1,0:T(1,128)S(1)} %get-tuple-element.36.refs_1_, bf16[64,2048]{1,0:T(8,128)(2,1)S(1)} %get-tuple-element.73.refs_2_, ...), custom_call_target="tpu_custom_call" | custom-call | flops 603979776 | bytes 2097152 | tf_op jit(solution)/shard_map/pallas_call | solution.py:586
  32.4 1.9 %shard_map.54 = (f32[9,512,128]{2,1,0:T(8,128)S(1)}, f32[512,128]{1,0:T(8,128)S(1)}, f32[32,512]{1,0:T(8,128)S(1)}, f32[16,512]{1,0:T(8,128)S(1)}) custom-call(s32[1]{0:T(128)} %bitcast.refs_0_.me_ref, f32[1,128]{1,0:T(1,128)S(1)} %get-tuple-element.38.refs_1_, bf16[64,2048]{1,0:T(8,128)(2,1)S(1)} %get-tuple-element.73.refs_2_, ...), custom_call_target="tpu_custom_call" | custom-call | flops 805306368 | bytes 2097152 | tf_op jit(solution)/shard_map/pallas_call | solution.py:586
  34.4 3.6 %collective-permute-start.19 = (f32[16,512]{1,0:T(8,128)S(1)}, f32[16,512]{1,0:T(8,128)S(1)}, u32[]{:S(2)}, u32[]{:S(2)}) collective-permute-start(f32[16,512]{1,0:T(8,128)S(1)} %get-tuple-element.43.refs_1_), channel_id=1, source_target_pairs={{0,2},{1,11},{2,0},{3,9},{4,6},{5,15},{6,4},{7,13},{8,10},{9,3},{1... | collective-permute-start | bytes 98312 | tf_op jit(solution)/shard_map/ppermute | solution.py:488
  38.0 1.5 %collective-permute-done.19.refs_2_ = f32[16,512]{1,0:T(8,128)S(1)} collective-permute-done((f32[16,512]{1,0:T(8,128)S(1)}, f32[16,512]{1,0:T(8,128)S(1)}, u32[]{:S(2)}, u32[]{:S(2)}) %collective-permute-start.19) | collective-permute-done | bytes 32800 | tf_op jit(solution)/shard_map/ppermute | solution.py:488
  39.5 1.3 %collective-permute-done.20.refs_3_ = f32[16,512]{1,0:T(8,128)S(1)} collective-permute-done((f32[16,512]{1,0:T(8,128)S(1)}, f32[16,512]{1,0:T(8,128)S(1)}, u32[]{:S(2)}, u32[]{:S(2)}) %collective-permute-start.20) | collective-permute-done | bytes 32800 | tf_op jit(solution)/shard_map/ppermute | solution.py:488
  42.2 3.9 %shard_map.56 = (f32[128,1024]{1,0:T(8,128)S(1)}, bf16[128,1024]{1,0:T(8,128)(2,1)S(1)}, f32[128,1024]{1,0:T(8,128)S(1)}, bf16[128,1024]{1,0:T(8,128)(2,1)S(1)},...) custom-call(s32[1]{0:T(128)} %bitcast.refs_0_.me_ref, ...), custom_call_target="tpu_custom_call" | custom-call | flops 1073741824 | bytes 4194304 | tf_op jit(solution)/shard_map/pallas_call | solution.py:615
  48.3 2.1 %collective-permute-start.29 = (bf16[128,1024]{1,0:T(8,128)(2,1)S(1)}, bf16[128,1024]{1,0:T(8,128)(2,1)S(1)}, u32[]{:S(2)}, u32[]{:S(2)}) collective-permute-start(bf16[128,1024]{1,0:T(8,128)(2,1)S(1)} %add_convert_fusion), channel_id=1, source_target_pairs={{0,16},{1,9},{2,18},{3,11},{4,20},{5,13},{6,22},{7,15},{8,24},{9,1... | collective-permute-start | bytes 786440 | tf_op jit(solution)/shard_map/ppermute | solution.py:488
  50.4 1.3 %collective-permute-done.22 = bf16[128,1024]{1,0:T(8,128)(2,1)S(1)} collective-permute-done((bf16[128,1024]{1,0:T(8,128)(2,1)S(1)}, bf16[128,1024]{1,0:T(8,128)(2,1)S(1)}, u32[]{:S(2)}, u32[]{:S(2)}) %collective-permute-start.22) | collective-permute-done | bytes 262176 | tf_op jit(solution)/shard_map/ppermute | solution.py:488
  51.8 1.2 %collective-permute-start.25 = (f32[64,1024]{1,0:T(8,128)S(1)}, f32[64,1024]{1,0:T(8,128)S(1)}, u32[]{:S(2)}, u32[]{:S(2)}) collective-permute-start(f32[64,1024]{1,0:T(8,128)S(1)} %get-tuple-element.61), channel_id=1, source_target_pairs={{0,1},{1,0},{2,3},{3,2},{4,5},{5,4},{6,7},{7,6},{8,9},{9,8},{10,11... | collective-permute-start | bytes 786440 | tf_op jit(solution)/shard_map/ppermute | solution.py:488
  53.0 4.3 %collective-permute-done.23 = bf16[128,1024]{1,0:T(8,128)(2,1)S(1)} collective-permute-done((bf16[128,1024]{1,0:T(8,128)(2,1)S(1)}, bf16[128,1024]{1,0:T(8,128)(2,1)S(1)}, u32[]{:S(2)}, u32[]{:S(2)}) %collective-permute-start.23) | collective-permute-done | bytes 262176 | tf_op jit(solution)/shard_map/ppermute | solution.py:488
  57.6 2.3 %collective-permute-start.30 = (f32[64,1024]{1,0:T(8,128)S(1)}, f32[64,1024]{1,0:T(8,128)S(1)}, u32[]{:S(2)}, u32[]{:S(2)}) collective-permute-start(f32[64,1024]{1,0:T(8,128)S(1)} %get-tuple-element.68), channel_id=1, source_target_pairs={{0,1},{1,0},{2,3},{3,2},{4,5},{5,4},{6,7},{7,6},{8,9},{9,8},{10,11... | collective-permute-start | bytes 786440 | tf_op jit(solution)/shard_map/ppermute | solution.py:488
  60.6 2.8 %collective-permute-start.26 = (bf16[64,1024]{1,0:T(8,128)(2,1)S(1)}, bf16[64,1024]{1,0:T(8,128)(2,1)S(1)}, u32[]{:S(2)}, u32[]{:S(2)}) collective-permute-start(bf16[64,1024]{1,0:T(8,128)(2,1)S(1)} %get-tuple-element.74), channel_id=1, source_target_pairs={{0,17},{1,8},{2,19},{3,10},{4,21},{5,12},{6,23},{7,14},{8,25},{9,0... | collective-permute-start | bytes 393224 | tf_op jit(solution)/shard_map/ppermute | solution.py:488
  64.3 4.8 %collective-permute-done.26.refs_3_ = bf16[64,1024]{1,0:T(8,128)(2,1)S(1)} collective-permute-done((bf16[64,1024]{1,0:T(8,128)(2,1)S(1)}, bf16[64,1024]{1,0:T(8,128)(2,1)S(1)}, u32[]{:S(2)}, u32[]{:S(2)}) %collective-permute-start.26) | collective-permute-done | bytes 131104 | tf_op jit(solution)/shard_map/ppermute | solution.py:488
  (60 shorter events, 16.1 us)
Async XLA Ops:
  1.7 6.5 %collective-permute-start.1 = (bf16[64,2048]{1,0:T(8,128)(2,1)S(1)}, bf16[64,2048]{1,0:T(8,128)(2,1)S(1)}, u32[]{:S(2)}, u32[]{:S(2)}) collective-permute-start(bf16[64,2048]{1,0:T(8,128)(2,1)S(1)} %get-tuple-element.72.refs_7_.refs_6_.refs_21_), channel_id=1, source_target_pairs={{0,1},{1,0},{2,3},{3,2},{4,5},{5,4},{6,7},{7,6},{8,9},{9,8},{10,11... | collective-permute-start | bytes 786440 | tf_op jit(solution)/shard_map/ppermute | solution.py:488
  1.8 7.6 %collective-permute-start.2 = (bf16[64,2048]{1,0:T(8,128)(2,1)S(1)}, bf16[64,2048]{1,0:T(8,128)(2,1)S(1)}, u32[]{:S(2)}, u32[]{:S(2)}) collective-permute-start(bf16[64,2048]{1,0:T(8,128)(2,1)S(1)} %get-tuple-element.73.refs_2_), channel_id=1, source_target_pairs={{0,4},{1,3},{2,6},{3,1},{4,0},{5,7},{6,2},{7,5},{8,12},{9,11},{10,... | collective-permute-start | bytes 786440 | tf_op jit(solution)/shard_map/ppermute | solution.py:488
  4.5 11.2 %collective-permute-start.4 = (bf16[64,2048]{1,0:T(8,128)(2,1)S(1)}, bf16[64,2048]{1,0:T(8,128)(2,1)S(1)}, u32[]{:S(2)}, u32[]{:S(2)}) collective-permute-start(bf16[64,2048]{1,0:T(8,128)(2,1)S(1)} %get-tuple-element.73.refs_2_), channel_id=1, source_target_pairs={{0,1},{1,0},{2,3},{3,2},{4,5},{5,4},{6,7},{7,6},{8,9},{9,8},{10,11... | collective-permute-start | bytes 786440 | tf_op jit(solution)/shard_map/ppermute | solution.py:488
  4.9 7.8 %collective-permute-start.7 = (bf16[64,2048]{1,0:T(8,128)(2,1)S(1)}, bf16[64,2048]{1,0:T(8,128)(2,1)S(1)}, u32[]{:S(2)}, u32[]{:S(2)}) collective-permute-start(bf16[64,2048]{1,0:T(8,128)(2,1)S(1)} %get-tuple-element.73.refs_2_), channel_id=1, source_target_pairs={{0,16},{1,9},{2,18},{3,11},{4,20},{5,13},{6,22},{7,15},{8,24},{9,1... | collective-permute-start | bytes 786440 | tf_op jit(solution)/shard_map/ppermute | solution.py:488
  8.2 5.7 %collective-permute-start.3 = (bf16[64,2048]{1,0:T(8,128)(2,1)S(1)}, bf16[64,2048]{1,0:T(8,128)(2,1)S(1)}, u32[]{:S(2)}, u32[]{:S(2)}) collective-permute-start(bf16[64,2048]{1,0:T(8,128)(2,1)S(1)} %collective-permute-done.1.refs_3_), channel_id=1, source_target_pairs={{0,4},{1,3},{2,6},{3,1},{4,0},{5,7},{6,2},{7,5},{8,12},{9,11},{10,... | collective-permute-start | bytes 786440 | tf_op jit(solution)/shard_map/ppermute | solution.py:488
  9.4 12.9 %collective-permute-start.5 = (bf16[64,2048]{1,0:T(8,128)(2,1)S(1)}, bf16[64,2048]{1,0:T(8,128)(2,1)S(1)}, u32[]{:S(2)}, u32[]{:S(2)}) collective-permute-start(bf16[64,2048]{1,0:T(8,128)(2,1)S(1)} %collective-permute-done.2.refs_4_), channel_id=1, source_target_pairs={{0,1},{1,0},{2,3},{3,2},{4,5},{5,4},{6,7},{7,6},{8,9},{9,8},{10,11... | collective-permute-start | bytes 786440 | tf_op jit(solution)/shard_map/ppermute | solution.py:488
  9.9 8.6 %collective-permute-start.8 = (bf16[32,2048]{1,0:T(8,128)(2,1)S(1)}, bf16[32,2048]{1,0:T(8,128)(2,1)S(1)}, u32[]{:S(2)}, u32[]{:S(2)}) collective-permute-start(bf16[32,2048]{1,0:T(8,128)(2,1)S(1)} %get-tuple-element.77), channel_id=1, source_target_pairs={{0,16},{1,9},{2,18},{3,11},{4,20},{5,13},{6,22},{7,15},{8,24},{9,1... | collective-permute-start | bytes 393224 | tf_op jit(solution)/shard_map/ppermute | solution.py:488
  12.6 10.6 %collective-permute-start.13 = (bf16[64,2048]{1,0:T(8,128)(2,1)S(1)}, bf16[64,2048]{1,0:T(8,128)(2,1)S(1)}, u32[]{:S(2)}, u32[]{:S(2)}) collective-permute-start(bf16[64,2048]{1,0:T(8,128)(2,1)S(1)} %collective-permute-done.7.refs_2_.refs_6_), channel_id=1, source_target_pairs={{0,4},{1,3},{2,6},{3,1},{4,0},{5,7},{6,2},{7,5},{8,12},{9,11},{10,... | collective-permute-start | bytes 786440 | tf_op jit(solution)/shard_map/ppermute | solution.py:488
  14.0 9.8 %collective-permute-start.6 = (bf16[64,2048]{1,0:T(8,128)(2,1)S(1)}, bf16[64,2048]{1,0:T(8,128)(2,1)S(1)}, u32[]{:S(2)}, u32[]{:S(2)}) collective-permute-start(bf16[64,2048]{1,0:T(8,128)(2,1)S(1)} %collective-permute-done.3.refs_5_), channel_id=1, source_target_pairs={{0,1},{1,0},{2,3},{3,2},{4,5},{5,4},{6,7},{7,6},{8,9},{9,8},{10,11... | collective-permute-start | bytes 786440 | tf_op jit(solution)/shard_map/ppermute | solution.py:488
  15.7 6.6 %collective-permute-start.9 = (bf16[32,2048]{1,0:T(8,128)(2,1)S(1)}, bf16[32,2048]{1,0:T(8,128)(2,1)S(1)}, u32[]{:S(2)}, u32[]{:S(2)}) collective-permute-start(bf16[32,2048]{1,0:T(8,128)(2,1)S(1)} %get-tuple-element.76), channel_id=1, source_target_pairs={{0,16},{1,9},{2,18},{3,11},{4,20},{5,13},{6,22},{7,15},{8,24},{9,1... | collective-permute-start | bytes 393224 | tf_op jit(solution)/shard_map/ppermute | solution.py:488
  22.2 7.7 %collective-permute-start.10 = (bf16[64,2048]{1,0:T(8,128)(2,1)S(1)}, bf16[64,2048]{1,0:T(8,128)(2,1)S(1)}, u32[]{:S(2)}, u32[]{:S(2)}) collective-permute-start(bf16[64,2048]{1,0:T(8,128)(2,1)S(1)} %collective-permute-done.7.refs_2_.refs_6_), channel_id=1, source_target_pairs={{0,1},{1,0},{2,3},{3,2},{4,5},{5,4},{6,7},{7,6},{8,9},{9,8},{10,11... | collective-permute-start | bytes 786440 | tf_op jit(solution)/shard_map/ppermute | solution.py:488
  22.3 7.7 %collective-permute-start.12 = (bf16[32,2048]{1,0:T(8,128)(2,1)S(1)}, bf16[32,2048]{1,0:T(8,128)(2,1)S(1)}, u32[]{:S(2)}, u32[]{:S(2)}) collective-permute-start(bf16[32,2048]{1,0:T(8,128)(2,1)S(1)} %collective-permute-done.9.refs_4_.refs_8_), channel_id=1, source_target_pairs={{0,1},{1,0},{2,3},{3,2},{4,5},{5,4},{6,7},{7,6},{8,9},{9,8},{10,11... | collective-permute-start | bytes 393224 | tf_op jit(solution)/shard_map/ppermute | solution.py:488
  23.8 8.6 %collective-permute-start.16 = (bf16[64,2048]{1,0:T(8,128)(2,1)S(1)}, bf16[64,2048]{1,0:T(8,128)(2,1)S(1)}, u32[]{:S(2)}, u32[]{:S(2)}) collective-permute-start(bf16[64,2048]{1,0:T(8,128)(2,1)S(1)} %collective-permute-done.13.refs_2_.refs_9_), channel_id=1, source_target_pairs={{0,1},{1,0},{2,3},{3,2},{4,5},{5,4},{6,7},{7,6},{8,9},{9,8},{10,11... | collective-permute-start | bytes 786440 | tf_op jit(solution)/shard_map/ppermute | solution.py:488
  26.4 6.1 %collective-permute-start.17 = (bf16[32,2048]{1,0:T(8,128)(2,1)S(1)}, bf16[32,2048]{1,0:T(8,128)(2,1)S(1)}, u32[]{:S(2)}, u32[]{:S(2)}) collective-permute-start(bf16[32,2048]{1,0:T(8,128)(2,1)S(1)} %collective-permute-done.14.refs_3_.refs_10_), channel_id=1, source_target_pairs={{0,1},{1,0},{2,3},{3,2},{4,5},{5,4},{6,7},{7,6},{8,9},{9,8},{10,11... | collective-permute-start | bytes 393224 | tf_op jit(solution)/shard_map/ppermute | solution.py:488
  27.8 4.7 %collective-permute-start.18 = (bf16[32,2048]{1,0:T(8,128)(2,1)S(1)}, bf16[32,2048]{1,0:T(8,128)(2,1)S(1)}, u32[]{:S(2)}, u32[]{:S(2)}) collective-permute-start(bf16[32,2048]{1,0:T(8,128)(2,1)S(1)} %collective-permute-done.15.refs_4_.refs_11_), channel_id=1, source_target_pairs={{0,1},{1,0},{2,3},{3,2},{4,5},{5,4},{6,7},{7,6},{8,9},{9,8},{10,11... | collective-permute-start | bytes 393224 | tf_op jit(solution)/shard_map/ppermute | solution.py:488
  34.4 5.1 %collective-permute-start.19 = (f32[16,512]{1,0:T(8,128)S(1)}, f32[16,512]{1,0:T(8,128)S(1)}, u32[]{:S(2)}, u32[]{:S(2)}) collective-permute-start(f32[16,512]{1,0:T(8,128)S(1)} %get-tuple-element.43.refs_1_), channel_id=1, source_target_pairs={{0,2},{1,11},{2,0},{3,9},{4,6},{5,15},{6,4},{7,13},{8,10},{9,3},{1... | collective-permute-start | bytes 98312 | tf_op jit(solution)/shard_map/ppermute | solution.py:488
  41.3 7.0 %collective-permute-start.28 = (bf16[128,1024]{1,0:T(8,128)(2,1)S(1)}, bf16[128,1024]{1,0:T(8,128)(2,1)S(1)}, u32[]{:S(2)}, u32[]{:S(2)}) collective-permute-start(bf16[128,1024]{1,0:T(8,128)(2,1)S(1)} %get-tuple-element.65), channel_id=1, source_target_pairs={{0,4},{1,3},{2,6},{3,1},{4,0},{5,7},{6,2},{7,5},{8,12},{9,11},{10,... | collective-permute-start | bytes 786440 | tf_op jit(solution)/shard_map/ppermute | solution.py:488
  46.2 5.6 %collective-permute-start.22 = (bf16[128,1024]{1,0:T(8,128)(2,1)S(1)}, bf16[128,1024]{1,0:T(8,128)(2,1)S(1)}, u32[]{:S(2)}, u32[]{:S(2)}) collective-permute-start(bf16[128,1024]{1,0:T(8,128)(2,1)S(1)} %get-tuple-element.57), channel_id=1, source_target_pairs={{0,4},{1,3},{2,6},{3,1},{4,0},{5,7},{6,2},{7,5},{8,12},{9,11},{10,... | collective-permute-start | bytes 786440 | tf_op jit(solution)/shard_map/ppermute | solution.py:488
  46.8 10.6 %collective-permute-start.27 = (bf16[128,1024]{1,0:T(8,128)(2,1)S(1)}, bf16[128,1024]{1,0:T(8,128)(2,1)S(1)}, u32[]{:S(2)}, u32[]{:S(2)}) collective-permute-start(bf16[128,1024]{1,0:T(8,128)(2,1)S(1)} %get-tuple-element.63), channel_id=1, source_target_pairs={{0,4},{1,3},{2,6},{3,1},{4,0},{5,7},{6,2},{7,5},{8,12},{9,11},{10,... | collective-permute-start | bytes 786440 | tf_op jit(solution)/shard_map/ppermute | solution.py:488
  47.7 9.7 %collective-permute-start.23 = (bf16[128,1024]{1,0:T(8,128)(2,1)S(1)}, bf16[128,1024]{1,0:T(8,128)(2,1)S(1)}, u32[]{:S(2)}, u32[]{:S(2)}) collective-permute-start(bf16[128,1024]{1,0:T(8,128)(2,1)S(1)} %get-tuple-element.60), channel_id=1, source_target_pairs={{0,4},{1,3},{2,6},{3,1},{4,0},{5,7},{6,2},{7,5},{8,12},{9,11},{10,... | collective-permute-start | bytes 786440 | tf_op jit(solution)/shard_map/ppermute | solution.py:488
  48.3 9.1 %collective-permute-start.29 = (bf16[128,1024]{1,0:T(8,128)(2,1)S(1)}, bf16[128,1024]{1,0:T(8,128)(2,1)S(1)}, u32[]{:S(2)}, u32[]{:S(2)}) collective-permute-start(bf16[128,1024]{1,0:T(8,128)(2,1)S(1)} %add_convert_fusion), channel_id=1, source_target_pairs={{0,16},{1,9},{2,18},{3,11},{4,20},{5,13},{6,22},{7,15},{8,24},{9,1... | collective-permute-start | bytes 786440 | tf_op jit(solution)/shard_map/ppermute | solution.py:488
  51.8 17.2 %collective-permute-start.25 = (f32[64,1024]{1,0:T(8,128)S(1)}, f32[64,1024]{1,0:T(8,128)S(1)}, u32[]{:S(2)}, u32[]{:S(2)}) collective-permute-start(f32[64,1024]{1,0:T(8,128)S(1)} %get-tuple-element.61), channel_id=1, source_target_pairs={{0,1},{1,0},{2,3},{3,2},{4,5},{5,4},{6,7},{7,6},{8,9},{9,8},{10,11... | collective-permute-start | bytes 786440 | tf_op jit(solution)/shard_map/ppermute | solution.py:488
  57.6 5.8 %collective-permute-start.30 = (f32[64,1024]{1,0:T(8,128)S(1)}, f32[64,1024]{1,0:T(8,128)S(1)}, u32[]{:S(2)}, u32[]{:S(2)}) collective-permute-start(f32[64,1024]{1,0:T(8,128)S(1)} %get-tuple-element.68), channel_id=1, source_target_pairs={{0,1},{1,0},{2,3},{3,2},{4,5},{5,4},{6,7},{7,6},{8,9},{9,8},{10,11... | collective-permute-start | bytes 786440 | tf_op jit(solution)/shard_map/ppermute | solution.py:488
  60.6 8.5 %collective-permute-start.26 = (bf16[64,1024]{1,0:T(8,128)(2,1)S(1)}, bf16[64,1024]{1,0:T(8,128)(2,1)S(1)}, u32[]{:S(2)}, u32[]{:S(2)}) collective-permute-start(bf16[64,1024]{1,0:T(8,128)(2,1)S(1)} %get-tuple-element.74), channel_id=1, source_target_pairs={{0,17},{1,8},{2,19},{3,10},{4,21},{5,12},{6,23},{7,14},{8,25},{9,0... | collective-permute-start | bytes 393224 | tf_op jit(solution)/shard_map/ppermute | solution.py:488
  (7 other events, 23.9 us)

commit v10 on v9

--- a/solution.py
+++ b/solution.py
@@ -17,15 +17,6 @@
 
 
 logit_gain = 3.0
-QUERY_CORE = 1
-
-
-def leads(device):
-    return (device & 1) == QUERY_CORE
-
-
-def other_core(device):
-    return (device & -2) | (1 - QUERY_CORE)
 
 
 def width_list(feature_dim):
@@ -76,7 +67,7 @@
     own = partner_ref.shape[1]
     out_ref[...] = jnp.zeros_like(out_ref)
 
-    @pl.when(leads(role_ref[0]))
+    @pl.when((role_ref[0] & 1) == 0)
     def _():
         for step in range(steps):
             rows = pl.ds(step * block, block)
@@ -88,7 +79,7 @@
                 col_ref[rows, k:k + 1] = peak + jnp.log(mass) * LOG2E
         out_ref[...] = col_ref[...].T[:STATS]
 
-    @pl.when(jnp.logical_not(leads(role_ref[0])))
+    @pl.when((role_ref[0] & 1) != 0)
     def _():
         peaks, masses = [None] * len(uppers), [None] * len(uppers)
         for step in range(steps):
@@ -134,7 +125,7 @@
     count = len(uppers)
     scales = [logit_gain * m ** -0.5 for m in uppers]
     me = me_ref[0]
-    lead = leads(me)
+    lead = (me & 1) == 0
 
     parts = []
     partners = []
@@ -150,7 +141,7 @@
         [totals[:count], partner_row, jnp.zeros((LANES - count - 1, total), jnp.float32)], axis=0)
     col_ref[...] = packed.T
     zero_or = lambda keep, x: jnp.where(keep, x, jnp.zeros_like(x))
-    document_row = document_ids((1, total), 1, other_core(me), own_rows, masks)
+    document_row = document_ids((1, total), 1, me | 1, own_rows, masks)
     id_row = jnp.where(lead, document_row, partner_row)
     shifts = [math.log2(s) for s in scales]
     total_rows = [zero_or(jnp.logical_not(lead), totals[k:k + 1]) - shifts[k] for k in range(count)]
@@ -158,7 +149,7 @@
     narrow = [m for m in uppers if m <= LANES]
     for step in range(total // block):
         rows = pl.ds(step * block, block)
-        document_col = document_ids((block, 1), 0, other_core(me), own_rows, masks, step * block)
+        document_col = document_ids((block, 1), 0, me | 1, own_rows, masks, step * block)
         id_col = jnp.where(lead, col_ref[rows, count:count + 1], document_col)
         hit = id_col == id_row
         for k, s in enumerate(prefix_scores(v_ref, w_ref, rows, uppers)):
@@ -267,7 +258,7 @@
     at += sum(counts[c0:c1])
     earlier = refs[at:at + finish]
     outs = refs[at + finish:]
-    lead = leads(me_ref[0])
+    lead = (me_ref[0] & 1) == 0
     for i, (t0, t1, u0, u1) in enumerate(tiles):
         subtile(
             lead, v_refs[sum(counts[r0:t0]):sum(counts[r0:t1])],
@@ -318,10 +309,9 @@
     total = stat_refs[0].shape[1]
     chip_rows = total // groups
     me = me_ref[0]
-    lead = leads(me)
+    lead = (me & 1) == 0
     own, first, second, swapped = [ref[...] for ref in stat_refs]
-    odd = (me & 1) == 1
-    values = [own, jnp.where(odd, swapped, first), second, jnp.where(odd, first, swapped)]
+    values = [own, jnp.where(lead, first, swapped), second, jnp.where(lead, swapped, first)]
     parts, partners = [], []
     for j, value in enumerate(values):
         parts.append(jnp.concatenate(
@@ -338,10 +328,10 @@
         [totals[:count], partner_row, jnp.zeros((LANES - count - 1, total), jnp.float32)], axis=0)
     cols = packed.T
     id_row = jnp.where(
-        lead, document_ids((1, total), 1, other_core(me), own_rows, masks), partner_row)
+        lead, document_ids((1, total), 1, me | 1, own_rows, masks), partner_row)
     id_col = jnp.where(
         lead, cols[:, count:count + 1],
-        document_ids((total, 1), 0, other_core(me), own_rows, masks))
+        document_ids((total, 1), 0, me | 1, own_rows, masks))
     return lead, totals, cols, id_row, id_col
 
 
@@ -460,7 +450,7 @@
         for copy in copies:
             copy.wait()
 
-    lead = leads(me_ref[0])
+    lead = (me_ref[0] & 1) == 0
     pl.when(lead)(lambda: write(queries_ref, documents_ref))
     pl.when(jnp.logical_not(lead))(lambda: write(documents_ref, queries_ref))
 
@@ -482,7 +472,7 @@
 
     role = lax.axis_index("rep")
     me = (lax.axis_index("dp") * rep_size + role).astype(jnp.int32).reshape(1)
-    lead = leads(role)
+    lead = role == 0
 
     def exchange(x, masks_of):
         return lax.ppermute(x, AXES, [(i, i ^ masks_of(i)) for i in range(devices)])
@@ -491,7 +481,7 @@
         return exchange(x, lambda i: 1)
 
     def along(x, stage):
-        return exchange(x, lambda i: query_masks[stage] if leads(i) else document_masks[stage])
+        return exchange(x, lambda i: document_masks[stage] if i & 1 else query_masks[stage])
 
     vmem = pl.BlockSpec(memory_space=pltpu.VMEM)
     smem = pl.BlockSpec(memory_space=pltpu.SMEM)
@@ -663,7 +653,7 @@
             theirs = kept[own_rows:] + arrived[own_rows:].astype(jnp.float32)
             parts = [kept[:own_rows], near, swap(theirs), jnp.zeros_like(near)]
         else:
-            far = lambda i: 1 ^ (query_masks[stage] if leads(i) else document_masks[stage])
+            far = lambda i: document_masks[stage] ^ 1 if i & 1 else query_masks[stage] ^ 1
             near_arrived = along(outgoing[:own_rows], stage)
             far_arrived = exchange(outgoing[own_rows:], far)
             ours, theirs = lax.optimization_barrier((kept[:own_rows], kept[own_rows:]))

time: 70.2 us -> 66.6 us (0.949)
  the two profiles are of different devices: /device:TPU:1 before, /device:TPU:0 now
where the time goes in v10:
time: 66.6 us; the launch traced here: 66.4 us
  starting transfers between devices  27.4 us (41%)
  waiting for transfers between devices  23.4 us (35%)
  Pallas kernels  12.4 us (19%)
  other arithmetic  2.09 us (3%)
  between operations  0.99 us (1%)
    ppermute x31, starting transfers between devices, exchange(): return lax.ppermute(x, AXES, [(i, i ^ masks_of(i)) for i in range(devices)])  27.4 us
    ppermute x31, waiting for transfers between devices, exchange(): return lax.ppermute(x, AXES, [(i, i ^ masks_of(i)) for i in range(devices)])  23.4 us
    pallas_call x5, Pallas kernels, tile(): pl.pallas_call(functools.partial(tile_kernel, span, counts, uppers, own_r...  6.26 us
    pallas_call x2, Pallas kernels, bands(): pl.pallas_call(functools.partial(kernel, groups, uppers, own_rows, docume...  4.41 us
    pallas_call x2, Pallas kernels, put(): pl.pallas_call(functools.partial(put_kernel, columns), out_shape=[jax.Sha...  1.7 us
  transfers between devices with their start and end apart: 31, of which 11 were waited for; matrix products, arithmetic and copies ran while one was open for 2% of the time, Pallas kernels for 14%

profile of v10, /device:TPU:0, one launch (start us, length us, event | category | flops | bytes accessed | tf_op | source)
XLA Modules:
  0.0 66.4 jit_solution(6757135003969183905)
XLA Ops:
  2.3 2.6 %collective-permute-start.2 = (bf16[64,2048]{1,0:T(8,128)(2,1)S(1)}, bf16[64,2048]{1,0:T(8,128)(2,1)S(1)}, u32[]{:S(2)}, u32[]{:S(2)}) collective-permute-start(bf16[64,2048]{1,0:T(8,128)(2,1)S(1)} %get-tuple-element.73.refs_2_), channel_id=1, source_target_pairs={{0,2},{1,5},{2,0},{3,7},{4,6},{5,1},{6,4},{7,3},{8,10},{9,13},{10,... | collective-permute-start | bytes 786440 | tf_op jit(solution)/shard_map/ppermute | solution.py:478
  5.0 1.6 %collective-permute-start.7 = (bf16[64,2048]{1,0:T(8,128)(2,1)S(1)}, bf16[64,2048]{1,0:T(8,128)(2,1)S(1)}, u32[]{:S(2)}, u32[]{:S(2)}) collective-permute-start(bf16[64,2048]{1,0:T(8,128)(2,1)S(1)} %get-tuple-element.73.refs_2_), channel_id=1, source_target_pairs={{0,8},{1,17},{2,10},{3,19},{4,12},{5,21},{6,14},{7,23},{8,0},{9,25... | collective-permute-start | bytes 786440 | tf_op jit(solution)/shard_map/ppermute | solution.py:478
  9.6 1.6 %collective-permute-start.8 = (bf16[32,2048]{1,0:T(8,128)(2,1)S(1)}, bf16[32,2048]{1,0:T(8,128)(2,1)S(1)}, u32[]{:S(2)}, u32[]{:S(2)}) collective-permute-start(bf16[32,2048]{1,0:T(8,128)(2,1)S(1)} %get-tuple-element.77), channel_id=1, source_target_pairs={{0,8},{1,17},{2,10},{3,19},{4,12},{5,21},{6,14},{7,23},{8,0},{9,25... | collective-permute-start | bytes 393224 | tf_op jit(solution)/shard_map/ppermute | solution.py:478
  11.3 2.8 %collective-permute-done.7.refs_2_.refs_6_ = bf16[64,2048]{1,0:T(8,128)(2,1)S(1)} collective-permute-done((bf16[64,2048]{1,0:T(8,128)(2,1)S(1)}, bf16[64,2048]{1,0:T(8,128)(2,1)S(1)}, u32[]{:S(2)}, u32[]{:S(2)}) %collective-permute-start.7) | collective-permute-done | bytes 262176 | tf_op jit(solution)/shard_map/ppermute | solution.py:478
  14.1 1.5 %collective-permute-start.13 = (bf16[64,2048]{1,0:T(8,128)(2,1)S(1)}, bf16[64,2048]{1,0:T(8,128)(2,1)S(1)}, u32[]{:S(2)}, u32[]{:S(2)}) collective-permute-start(bf16[64,2048]{1,0:T(8,128)(2,1)S(1)} %collective-permute-done.7.refs_2_.refs_6_), channel_id=1, source_target_pairs={{0,2},{1,5},{2,0},{3,7},{4,6},{5,1},{6,4},{7,3},{8,10},{9,13},{10,... | collective-permute-start | bytes 786440 | tf_op jit(solution)/shard_map/ppermute | solution.py:478
  15.6 1.6 %collective-permute-start.9 = (bf16[32,2048]{1,0:T(8,128)(2,1)S(1)}, bf16[32,2048]{1,0:T(8,128)(2,1)S(1)}, u32[]{:S(2)}, u32[]{:S(2)}) collective-permute-start(bf16[32,2048]{1,0:T(8,128)(2,1)S(1)} %get-tuple-element.76), channel_id=1, source_target_pairs={{0,8},{1,17},{2,10},{3,19},{4,12},{5,21},{6,14},{7,23},{8,0},{9,25... | collective-permute-start | bytes 393224 | tf_op jit(solution)/shard_map/ppermute | solution.py:478
  17.9 4.2 %collective-permute-done.9.refs_4_.refs_8_ = bf16[32,2048]{1,0:T(8,128)(2,1)S(1)} collective-permute-done((bf16[32,2048]{1,0:T(8,128)(2,1)S(1)}, bf16[32,2048]{1,0:T(8,128)(2,1)S(1)}, u32[]{:S(2)}, u32[]{:S(2)}) %collective-permute-start.9) | collective-permute-done | bytes 131104 | tf_op jit(solution)/shard_map/ppermute | solution.py:478
  22.8 1.4 %collective-permute-start.15 = (bf16[32,2048]{1,0:T(8,128)(2,1)S(1)}, bf16[32,2048]{1,0:T(8,128)(2,1)S(1)}, u32[]{:S(2)}, u32[]{:S(2)}) collective-permute-start(bf16[32,2048]{1,0:T(8,128)(2,1)S(1)} %collective-permute-done.9.refs_4_.refs_8_), channel_id=1, source_target_pairs={{0,2},{1,5},{2,0},{3,7},{4,6},{5,1},{6,4},{7,3},{8,10},{9,13},{10,... | collective-permute-start | bytes 393224 | tf_op jit(solution)/shard_map/ppermute | solution.py:478
  25.5 1.6 %collective-permute-done.14.refs_3_.refs_10_ = bf16[32,2048]{1,0:T(8,128)(2,1)S(1)} collective-permute-done((bf16[32,2048]{1,0:T(8,128)(2,1)S(1)}, bf16[32,2048]{1,0:T(8,128)(2,1)S(1)}, u32[]{:S(2)}, u32[]{:S(2)}) %collective-permute-start.14) | collective-permute-done | bytes 131104 | tf_op jit(solution)/shard_map/ppermute | solution.py:478
  27.1 1.4 %collective-permute-done.15.refs_4_.refs_11_ = bf16[32,2048]{1,0:T(8,128)(2,1)S(1)} collective-permute-done((bf16[32,2048]{1,0:T(8,128)(2,1)S(1)}, bf16[32,2048]{1,0:T(8,128)(2,1)S(1)}, u32[]{:S(2)}, u32[]{:S(2)}) %collective-permute-start.15) | collective-permute-done | bytes 131104 | tf_op jit(solution)/shard_map/ppermute | solution.py:478
  29.3 1.4 %shard_map.52 = (f32[9,384,128]{2,1,0:T(8,128)S(1)}, f32[384,128]{1,0:T(8,128)S(1)}, f32[32,384]{1,0:T(8,128)S(1)}, f32[1,128]{1,0:T(1,128)S(1)}) custom-call(s32[1]{0:T(128)} %bitcast.refs_0_.me_ref, f32[1,128]{1,0:T(1,128)S(1)} %get-tuple-element.36.refs_1_, bf16[64,2048]{1,0:T(8,128)(2,1)S(1)} %get-tuple-element.73.refs_2_, ...), custom_call_target="tpu_custom_call" | custom-call | flops 603979776 | bytes 2097152 | tf_op jit(solution)/shard_map/pallas_call | solution.py:576
  31.8 1.9 %shard_map.54 = (f32[9,512,128]{2,1,0:T(8,128)S(1)}, f32[512,128]{1,0:T(8,128)S(1)}, f32[32,512]{1,0:T(8,128)S(1)}, f32[16,512]{1,0:T(8,128)S(1)}) custom-call(s32[1]{0:T(128)} %bitcast.refs_0_.me_ref, f32[1,128]{1,0:T(1,128)S(1)} %get-tuple-element.38.refs_1_, bf16[64,2048]{1,0:T(8,128)(2,1)S(1)} %get-tuple-element.73.refs_2_, ...), custom_call_target="tpu_custom_call" | custom-call | flops 805306368 | bytes 2097152 | tf_op jit(solution)/shard_map/pallas_call | solution.py:576
  34.5 1.5 %collective-permute-start.20 = (f32[16,512]{1,0:T(8,128)S(1)}, f32[16,512]{1,0:T(8,128)S(1)}, u32[]{:S(2)}, u32[]{:S(2)}) collective-permute-start(f32[16,512]{1,0:T(8,128)S(1)} %get-tuple-element.43.refs_1_), channel_id=1, source_target_pairs={{0,8},{1,9},{2,10},{3,11},{4,12},{5,13},{6,14},{7,15},{8,0},{9,1},... | collective-permute-start | bytes 98312 | tf_op jit(solution)/shard_map/ppermute | solution.py:478
  36.0 1.7 %collective-permute-done.19.refs_2_ = f32[16,512]{1,0:T(8,128)S(1)} collective-permute-done((f32[16,512]{1,0:T(8,128)S(1)}, f32[16,512]{1,0:T(8,128)S(1)}, u32[]{:S(2)}, u32[]{:S(2)}) %collective-permute-start.19) | collective-permute-done | bytes 32800 | tf_op jit(solution)/shard_map/ppermute | solution.py:478
  40.3 3.9 %shard_map.56 = (f32[128,1024]{1,0:T(8,128)S(1)}, bf16[128,1024]{1,0:T(8,128)(2,1)S(1)}, f32[128,1024]{1,0:T(8,128)S(1)}, bf16[128,1024]{1,0:T(8,128)(2,1)S(1)},...) custom-call(s32[1]{0:T(128)} %bitcast.refs_0_.me_ref, ...), custom_call_target="tpu_custom_call" | custom-call | flops 1073741824 | bytes 4194304 | tf_op jit(solution)/shard_map/pallas_call | solution.py:605
  44.2 1.3 %collective-permute-start.22 = (bf16[128,1024]{1,0:T(8,128)(2,1)S(1)}, bf16[128,1024]{1,0:T(8,128)(2,1)S(1)}, u32[]{:S(2)}, u32[]{:S(2)}) collective-permute-start(bf16[128,1024]{1,0:T(8,128)(2,1)S(1)} %get-tuple-element.57), channel_id=1, source_target_pairs={{0,2},{1,5},{2,0},{3,7},{4,6},{5,1},{6,4},{7,3},{8,10},{9,13},{10,... | collective-permute-start | bytes 786440 | tf_op jit(solution)/shard_map/ppermute | solution.py:478
  46.3 1.2 %collective-permute-start.23 = (bf16[128,1024]{1,0:T(8,128)(2,1)S(1)}, bf16[128,1024]{1,0:T(8,128)(2,1)S(1)}, u32[]{:S(2)}, u32[]{:S(2)}) collective-permute-start(bf16[128,1024]{1,0:T(8,128)(2,1)S(1)} %get-tuple-element.60), channel_id=1, source_target_pairs={{0,2},{1,5},{2,0},{3,7},{4,6},{5,1},{6,4},{7,3},{8,10},{9,13},{10,... | collective-permute-start | bytes 786440 | tf_op jit(solution)/shard_map/ppermute | solution.py:478
  47.6 1.6 %collective-permute-start.29 = (bf16[128,1024]{1,0:T(8,128)(2,1)S(1)}, bf16[128,1024]{1,0:T(8,128)(2,1)S(1)}, u32[]{:S(2)}, u32[]{:S(2)}) collective-permute-start(bf16[128,1024]{1,0:T(8,128)(2,1)S(1)} %add_convert_fusion), channel_id=1, source_target_pairs={{0,8},{1,17},{2,10},{3,19},{4,12},{5,21},{6,14},{7,23},{8,0},{9,25... | collective-permute-start | bytes 786440 | tf_op jit(solution)/shard_map/ppermute | solution.py:478
  49.2 1.5 %collective-permute-done.22 = bf16[128,1024]{1,0:T(8,128)(2,1)S(1)} collective-permute-done((bf16[128,1024]{1,0:T(8,128)(2,1)S(1)}, bf16[128,1024]{1,0:T(8,128)(2,1)S(1)}, u32[]{:S(2)}, u32[]{:S(2)}) %collective-permute-start.22) | collective-permute-done | bytes 262176 | tf_op jit(solution)/shard_map/ppermute | solution.py:478
  50.9 5.4 %collective-permute-done.23 = bf16[128,1024]{1,0:T(8,128)(2,1)S(1)} collective-permute-done((bf16[128,1024]{1,0:T(8,128)(2,1)S(1)}, bf16[128,1024]{1,0:T(8,128)(2,1)S(1)}, u32[]{:S(2)}, u32[]{:S(2)}) %collective-permute-start.23) | collective-permute-done | bytes 262176 | tf_op jit(solution)/shard_map/ppermute | solution.py:478
  56.6 1.6 %collective-permute-start.24 = (bf16[64,1024]{1,0:T(8,128)(2,1)S(1)}, bf16[64,1024]{1,0:T(8,128)(2,1)S(1)}, u32[]{:S(2)}, u32[]{:S(2)}) collective-permute-start(bf16[64,1024]{1,0:T(8,128)(2,1)S(1)} %get-tuple-element.75), channel_id=1, source_target_pairs={{0,8},{1,17},{2,10},{3,19},{4,12},{5,21},{6,14},{7,23},{8,0},{9,25... | collective-permute-start | bytes 393224 | tf_op jit(solution)/shard_map/ppermute | solution.py:478
  58.2 2.6 %collective-permute-start.26 = (bf16[64,1024]{1,0:T(8,128)(2,1)S(1)}, bf16[64,1024]{1,0:T(8,128)(2,1)S(1)}, u32[]{:S(2)}, u32[]{:S(2)}) collective-permute-start(bf16[64,1024]{1,0:T(8,128)(2,1)S(1)} %get-tuple-element.74), channel_id=1, source_target_pairs={{0,9},{1,16},{2,11},{3,18},{4,13},{5,20},{6,15},{7,22},{8,1},{9,24... | collective-permute-start | bytes 393224 | tf_op jit(solution)/shard_map/ppermute | solution.py:478
  61.7 1.7 %collective-permute-done.24.refs_1_ = bf16[64,1024]{1,0:T(8,128)(2,1)S(1)} collective-permute-done((bf16[64,1024]{1,0:T(8,128)(2,1)S(1)}, bf16[64,1024]{1,0:T(8,128)(2,1)S(1)}, u32[]{:S(2)}, u32[]{:S(2)}) %collective-permute-start.24) | collective-permute-done | bytes 131104 | tf_op jit(solution)/shard_map/ppermute | solution.py:478
  63.5 1.9 %collective-permute-done.26.refs_3_ = bf16[64,1024]{1,0:T(8,128)(2,1)S(1)} collective-permute-done((bf16[64,1024]{1,0:T(8,128)(2,1)S(1)}, bf16[64,1024]{1,0:T(8,128)(2,1)S(1)}, u32[]{:S(2)}, u32[]{:S(2)}) %collective-permute-start.26) | collective-permute-done | bytes 131104 | tf_op jit(solution)/shard_map/ppermute | solution.py:478
  (60 shorter events, 15.8 us)
Async XLA Ops:
  1.7 6.6 %collective-permute-start.1 = (bf16[64,2048]{1,0:T(8,128)(2,1)S(1)}, bf16[64,2048]{1,0:T(8,128)(2,1)S(1)}, u32[]{:S(2)}, u32[]{:S(2)}) collective-permute-start(bf16[64,2048]{1,0:T(8,128)(2,1)S(1)} %get-tuple-element.72.refs_7_.refs_6_.refs_21_), channel_id=1, source_target_pairs={{0,1},{1,0},{2,3},{3,2},{4,5},{5,4},{6,7},{7,6},{8,9},{9,8},{10,11... | collective-permute-start | bytes 786440 | tf_op jit(solution)/shard_map/ppermute | solution.py:478
  2.3 7.2 %collective-permute-start.2 = (bf16[64,2048]{1,0:T(8,128)(2,1)S(1)}, bf16[64,2048]{1,0:T(8,128)(2,1)S(1)}, u32[]{:S(2)}, u32[]{:S(2)}) collective-permute-start(bf16[64,2048]{1,0:T(8,128)(2,1)S(1)} %get-tuple-element.73.refs_2_), channel_id=1, source_target_pairs={{0,2},{1,5},{2,0},{3,7},{4,6},{5,1},{6,4},{7,3},{8,10},{9,13},{10,... | collective-permute-start | bytes 786440 | tf_op jit(solution)/shard_map/ppermute | solution.py:478
  4.8 10.8 %collective-permute-start.4 = (bf16[64,2048]{1,0:T(8,128)(2,1)S(1)}, bf16[64,2048]{1,0:T(8,128)(2,1)S(1)}, u32[]{:S(2)}, u32[]{:S(2)}) collective-permute-start(bf16[64,2048]{1,0:T(8,128)(2,1)S(1)} %get-tuple-element.73.refs_2_), channel_id=1, source_target_pairs={{0,1},{1,0},{2,3},{3,2},{4,5},{5,4},{6,7},{7,6},{8,9},{9,8},{10,11... | collective-permute-start | bytes 786440 | tf_op jit(solution)/shard_map/ppermute | solution.py:478
  5.0 9.1 %collective-permute-start.7 = (bf16[64,2048]{1,0:T(8,128)(2,1)S(1)}, bf16[64,2048]{1,0:T(8,128)(2,1)S(1)}, u32[]{:S(2)}, u32[]{:S(2)}) collective-permute-start(bf16[64,2048]{1,0:T(8,128)(2,1)S(1)} %get-tuple-element.73.refs_2_), channel_id=1, source_target_pairs={{0,8},{1,17},{2,10},{3,19},{4,12},{5,21},{6,14},{7,23},{8,0},{9,25... | collective-permute-start | bytes 786440 | tf_op jit(solution)/shard_map/ppermute | solution.py:478
  8.3 7.3 %collective-permute-start.3 = (bf16[64,2048]{1,0:T(8,128)(2,1)S(1)}, bf16[64,2048]{1,0:T(8,128)(2,1)S(1)}, u32[]{:S(2)}, u32[]{:S(2)}) collective-permute-start(bf16[64,2048]{1,0:T(8,128)(2,1)S(1)} %collective-permute-done.1.refs_3_), channel_id=1, source_target_pairs={{0,2},{1,5},{2,0},{3,7},{4,6},{5,1},{6,4},{7,3},{8,10},{9,13},{10,... | collective-permute-start | bytes 786440 | tf_op jit(solution)/shard_map/ppermute | solution.py:478
  9.5 12.6 %collective-permute-start.5 = (bf16[64,2048]{1,0:T(8,128)(2,1)S(1)}, bf16[64,2048]{1,0:T(8,128)(2,1)S(1)}, u32[]{:S(2)}, u32[]{:S(2)}) collective-permute-start(bf16[64,2048]{1,0:T(8,128)(2,1)S(1)} %collective-permute-done.2.refs_4_), channel_id=1, source_target_pairs={{0,1},{1,0},{2,3},{3,2},{4,5},{5,4},{6,7},{7,6},{8,9},{9,8},{10,11... | collective-permute-start | bytes 786440 | tf_op jit(solution)/shard_map/ppermute | solution.py:478
  9.6 7.6 %collective-permute-start.8 = (bf16[32,2048]{1,0:T(8,128)(2,1)S(1)}, bf16[32,2048]{1,0:T(8,128)(2,1)S(1)}, u32[]{:S(2)}, u32[]{:S(2)}) collective-permute-start(bf16[32,2048]{1,0:T(8,128)(2,1)S(1)} %get-tuple-element.77), channel_id=1, source_target_pairs={{0,8},{1,17},{2,10},{3,19},{4,12},{5,21},{6,14},{7,23},{8,0},{9,25... | collective-permute-start | bytes 393224 | tf_op jit(solution)/shard_map/ppermute | solution.py:478
  14.1 8.7 %collective-permute-start.13 = (bf16[64,2048]{1,0:T(8,128)(2,1)S(1)}, bf16[64,2048]{1,0:T(8,128)(2,1)S(1)}, u32[]{:S(2)}, u32[]{:S(2)}) collective-permute-start(bf16[64,2048]{1,0:T(8,128)(2,1)S(1)} %collective-permute-done.7.refs_2_.refs_6_), channel_id=1, source_target_pairs={{0,2},{1,5},{2,0},{3,7},{4,6},{5,1},{6,4},{7,3},{8,10},{9,13},{10,... | collective-permute-start | bytes 786440 | tf_op jit(solution)/shard_map/ppermute | solution.py:478
  15.6 8.6 %collective-permute-start.6 = (bf16[64,2048]{1,0:T(8,128)(2,1)S(1)}, bf16[64,2048]{1,0:T(8,128)(2,1)S(1)}, u32[]{:S(2)}, u32[]{:S(2)}) collective-permute-start(bf16[64,2048]{1,0:T(8,128)(2,1)S(1)} %collective-permute-done.3.refs_5_), channel_id=1, source_target_pairs={{0,1},{1,0},{2,3},{3,2},{4,5},{5,4},{6,7},{7,6},{8,9},{9,8},{10,11... | collective-permute-start | bytes 786440 | tf_op jit(solution)/shard_map/ppermute | solution.py:478
  15.6 6.4 %collective-permute-start.9 = (bf16[32,2048]{1,0:T(8,128)(2,1)S(1)}, bf16[32,2048]{1,0:T(8,128)(2,1)S(1)}, u32[]{:S(2)}, u32[]{:S(2)}) collective-permute-start(bf16[32,2048]{1,0:T(8,128)(2,1)S(1)} %get-tuple-element.76), channel_id=1, source_target_pairs={{0,8},{1,17},{2,10},{3,19},{4,12},{5,21},{6,14},{7,23},{8,0},{9,25... | collective-permute-start | bytes 393224 | tf_op jit(solution)/shard_map/ppermute | solution.py:478
  17.3 5.5 %collective-permute-start.11 = (bf16[32,2048]{1,0:T(8,128)(2,1)S(1)}, bf16[32,2048]{1,0:T(8,128)(2,1)S(1)}, u32[]{:S(2)}, u32[]{:S(2)}) collective-permute-start(bf16[32,2048]{1,0:T(8,128)(2,1)S(1)} %collective-permute-done.8.refs_3_.refs_7_), channel_id=1, source_target_pairs={{0,1},{1,0},{2,3},{3,2},{4,5},{5,4},{6,7},{7,6},{8,9},{9,8},{10,11... | collective-permute-start | bytes 393224 | tf_op jit(solution)/shard_map/ppermute | solution.py:478
  22.1 7.2 %collective-permute-start.10 = (bf16[64,2048]{1,0:T(8,128)(2,1)S(1)}, bf16[64,2048]{1,0:T(8,128)(2,1)S(1)}, u32[]{:S(2)}, u32[]{:S(2)}) collective-permute-start(bf16[64,2048]{1,0:T(8,128)(2,1)S(1)} %collective-permute-done.7.refs_2_.refs_6_), channel_id=1, source_target_pairs={{0,1},{1,0},{2,3},{3,2},{4,5},{5,4},{6,7},{7,6},{8,9},{9,8},{10,11... | collective-permute-start | bytes 786440 | tf_op jit(solution)/shard_map/ppermute | solution.py:478
  22.1 5.0 %collective-permute-start.14 = (bf16[32,2048]{1,0:T(8,128)(2,1)S(1)}, bf16[32,2048]{1,0:T(8,128)(2,1)S(1)}, u32[]{:S(2)}, u32[]{:S(2)}) collective-permute-start(bf16[32,2048]{1,0:T(8,128)(2,1)S(1)} %collective-permute-done.8.refs_3_.refs_7_), channel_id=1, source_target_pairs={{0,2},{1,5},{2,0},{3,7},{4,6},{5,1},{6,4},{7,3},{8,10},{9,13},{10,... | collective-permute-start | bytes 393224 | tf_op jit(solution)/shard_map/ppermute | solution.py:478
  22.8 6.5 %collective-permute-start.12 = (bf16[32,2048]{1,0:T(8,128)(2,1)S(1)}, bf16[32,2048]{1,0:T(8,128)(2,1)S(1)}, u32[]{:S(2)}, u32[]{:S(2)}) collective-permute-start(bf16[32,2048]{1,0:T(8,128)(2,1)S(1)} %collective-permute-done.9.refs_4_.refs_8_), channel_id=1, source_target_pairs={{0,1},{1,0},{2,3},{3,2},{4,5},{5,4},{6,7},{7,6},{8,9},{9,8},{10,11... | collective-permute-start | bytes 393224 | tf_op jit(solution)/shard_map/ppermute | solution.py:478
  22.8 5.6 %collective-permute-start.15 = (bf16[32,2048]{1,0:T(8,128)(2,1)S(1)}, bf16[32,2048]{1,0:T(8,128)(2,1)S(1)}, u32[]{:S(2)}, u32[]{:S(2)}) collective-permute-start(bf16[32,2048]{1,0:T(8,128)(2,1)S(1)} %collective-permute-done.9.refs_4_.refs_8_), channel_id=1, source_target_pairs={{0,2},{1,5},{2,0},{3,7},{4,6},{5,1},{6,4},{7,3},{8,10},{9,13},{10,... | collective-permute-start | bytes 393224 | tf_op jit(solution)/shard_map/ppermute | solution.py:478
  24.2 7.6 %collective-permute-start.16 = (bf16[64,2048]{1,0:T(8,128)(2,1)S(1)}, bf16[64,2048]{1,0:T(8,128)(2,1)S(1)}, u32[]{:S(2)}, u32[]{:S(2)}) collective-permute-start(bf16[64,2048]{1,0:T(8,128)(2,1)S(1)} %collective-permute-done.13.refs_2_.refs_9_), channel_id=1, source_target_pairs={{0,1},{1,0},{2,3},{3,2},{4,5},{5,4},{6,7},{7,6},{8,9},{9,8},{10,11... | collective-permute-start | bytes 786440 | tf_op jit(solution)/shard_map/ppermute | solution.py:478
  39.4 8.1 %collective-permute-start.28 = (bf16[128,1024]{1,0:T(8,128)(2,1)S(1)}, bf16[128,1024]{1,0:T(8,128)(2,1)S(1)}, u32[]{:S(2)}, u32[]{:S(2)}) collective-permute-start(bf16[128,1024]{1,0:T(8,128)(2,1)S(1)} %get-tuple-element.65), channel_id=1, source_target_pairs={{0,2},{1,5},{2,0},{3,7},{4,6},{5,1},{6,4},{7,3},{8,10},{9,13},{10,... | collective-permute-start | bytes 786440 | tf_op jit(solution)/shard_map/ppermute | solution.py:478
  44.2 6.4 %collective-permute-start.22 = (bf16[128,1024]{1,0:T(8,128)(2,1)S(1)}, bf16[128,1024]{1,0:T(8,128)(2,1)S(1)}, u32[]{:S(2)}, u32[]{:S(2)}) collective-permute-start(bf16[128,1024]{1,0:T(8,128)(2,1)S(1)} %get-tuple-element.57), channel_id=1, source_target_pairs={{0,2},{1,5},{2,0},{3,7},{4,6},{5,1},{6,4},{7,3},{8,10},{9,13},{10,... | collective-permute-start | bytes 786440 | tf_op jit(solution)/shard_map/ppermute | solution.py:478
  45.5 10.9 %collective-permute-start.27 = (bf16[128,1024]{1,0:T(8,128)(2,1)S(1)}, bf16[128,1024]{1,0:T(8,128)(2,1)S(1)}, u32[]{:S(2)}, u32[]{:S(2)}) collective-permute-start(bf16[128,1024]{1,0:T(8,128)(2,1)S(1)} %get-tuple-element.63), channel_id=1, source_target_pairs={{0,2},{1,5},{2,0},{3,7},{4,6},{5,1},{6,4},{7,3},{8,10},{9,13},{10,... | collective-permute-start | bytes 786440 | tf_op jit(solution)/shard_map/ppermute | solution.py:478
  46.3 10.0 %collective-permute-start.23 = (bf16[128,1024]{1,0:T(8,128)(2,1)S(1)}, bf16[128,1024]{1,0:T(8,128)(2,1)S(1)}, u32[]{:S(2)}, u32[]{:S(2)}) collective-permute-start(bf16[128,1024]{1,0:T(8,128)(2,1)S(1)} %get-tuple-element.60), channel_id=1, source_target_pairs={{0,2},{1,5},{2,0},{3,7},{4,6},{5,1},{6,4},{7,3},{8,10},{9,13},{10,... | collective-permute-start | bytes 786440 | tf_op jit(solution)/shard_map/ppermute | solution.py:478
  47.6 8.8 %collective-permute-start.29 = (bf16[128,1024]{1,0:T(8,128)(2,1)S(1)}, bf16[128,1024]{1,0:T(8,128)(2,1)S(1)}, u32[]{:S(2)}, u32[]{:S(2)}) collective-permute-start(bf16[128,1024]{1,0:T(8,128)(2,1)S(1)} %add_convert_fusion), channel_id=1, source_target_pairs={{0,8},{1,17},{2,10},{3,19},{4,12},{5,21},{6,14},{7,23},{8,0},{9,25... | collective-permute-start | bytes 786440 | tf_op jit(solution)/shard_map/ppermute | solution.py:478
  50.8 14.6 %collective-permute-start.25 = (f32[64,1024]{1,0:T(8,128)S(1)}, f32[64,1024]{1,0:T(8,128)S(1)}, u32[]{:S(2)}, u32[]{:S(2)}) collective-permute-start(f32[64,1024]{1,0:T(8,128)S(1)} %get-tuple-element.61), channel_id=1, source_target_pairs={{0,1},{1,0},{2,3},{3,2},{4,5},{5,4},{6,7},{7,6},{8,9},{9,8},{10,11... | collective-permute-start | bytes 786440 | tf_op jit(solution)/shard_map/ppermute | solution.py:478
  56.6 6.9 %collective-permute-start.24 = (bf16[64,1024]{1,0:T(8,128)(2,1)S(1)}, bf16[64,1024]{1,0:T(8,128)(2,1)S(1)}, u32[]{:S(2)}, u32[]{:S(2)}) collective-permute-start(bf16[64,1024]{1,0:T(8,128)(2,1)S(1)} %get-tuple-element.75), channel_id=1, source_target_pairs={{0,8},{1,17},{2,10},{3,19},{4,12},{5,21},{6,14},{7,23},{8,0},{9,25... | collective-permute-start | bytes 393224 | tf_op jit(solution)/shard_map/ppermute | solution.py:478
  58.2 7.2 %collective-permute-start.26 = (bf16[64,1024]{1,0:T(8,128)(2,1)S(1)}, bf16[64,1024]{1,0:T(8,128)(2,1)S(1)}, u32[]{:S(2)}, u32[]{:S(2)}) collective-permute-start(bf16[64,1024]{1,0:T(8,128)(2,1)S(1)} %get-tuple-element.74), channel_id=1, source_target_pairs={{0,9},{1,16},{2,11},{3,18},{4,13},{5,20},{6,15},{7,22},{8,1},{9,24... | collective-permute-start | bytes 393224 | tf_op jit(solution)/shard_map/ppermute | solution.py:478
  (7 other events, 23.9 us)
